TPU v7x, 32 devices: a whole 2x2x4 slice. The times are simulated.
32 devices in a mesh: expert: 8 (over z, x), weight: 4 (over y, core).
Axes of the slice: x: 2, y: 2, z: 4, core: 2. Of those that a mesh axis runs over, the one named last changes fastest.
Arguments:
- tokens: bfloat16 [5120, 2048], P(('expert', 'weight')), may hold values from -6 to 6
- cotangent: bfloat16 [5120, 2048], P(('expert', 'weight')), may hold values from -6 to 6
- segments: int32 [8, 640], P('expert'), may hold values from 0 to 2, never falling along the last dimension, each value on 1 to 512 neighbouring positions
- routes: int32 [5120, 6], P(('expert', 'weight')), may hold values from 0 to 63, all different within a row; in each aligned block of 160 rows (0 to 159, 160 to 319, ...) at most 20 rows name the same one
- first_gain: float32 [2048], replicated, may hold values from 0.1 to 1.9
- query_weight: bfloat16 [2048, 3072], P(None, 'weight'), may hold values from -0.125 to 0.125
- latent_weight: bfloat16 [2048, 576], replicated, may hold values from -0.125 to 0.125
- latent_gain: float32 [512], replicated, may hold values from 0.1 to 1.9
- expand_weight: bfloat16 [512, 4096], P(None, 'weight'), may hold values from -0.25 to 0.25
- output_weight: bfloat16 [2048, 2048], P('weight'), may hold values from -0.5 to 0.5
- second_gain: float32 [2048], replicated, may hold values from 0.1 to 1.9
- router_weight: bfloat16 [2048, 64], replicated, may hold values from -0.125 to 0.125
- shared_gate: bfloat16 [2048, 2816], P(None, 'weight'), may hold values from -0.125 to 0.125
- shared_up: bfloat16 [2048, 2816], P(None, 'weight'), may hold values from -0.125 to 0.125
- shared_down: bfloat16 [2816, 2048], P('weight'), may hold values from -0.109375 to 0.109375
- expert_gate: bfloat16 [64, 2048, 1408], P('expert', None, 'weight'), may hold values from -0.125 to 0.125
- expert_up: bfloat16 [64, 2048, 1408], P('expert', None, 'weight'), may hold values from -0.125 to 0.125
- expert_down: bfloat16 [64, 1408, 2048], P('expert', 'weight'), may hold values from -0.15625 to 0.15625
Outputs:
- layer_out: bfloat16 [5120, 2048], P(('expert', 'weight'))
- token_gradient: float32 [5120, 2048], P(('expert', 'weight'))
- first_gain_gradient: float32 [2048], replicated
- query_gradient: float32 [2048, 3072], P('expert', 'weight')
- latent_weight_gradient: float32 [2048, 576], replicated
- latent_gain_gradient: float32 [512], replicated
- expand_gradient: float32 [512, 4096], P('expert', 'weight')
- output_gradient: float32 [2048, 2048], P('weight', 'expert')
- second_gain_gradient: float32 [2048], replicated
- router_gradient: float32 [2048, 64], replicated
- shared_gate_gradient: float32 [2048, 2816], P('expert', 'weight')
- shared_up_gradient: float32 [2048, 2816], P('expert', 'weight')
- shared_down_gradient: float32 [2816, 2048], P('weight', 'expert')
- expert_gate_gradient: float32 [64, 2048, 1408], P('expert', None, 'weight')
- expert_up_gradient: float32 [64, 2048, 1408], P('expert', None, 'weight')
- expert_down_gradient: float32 [64, 1408, 2048], P('expert', 'weight')
Inputs may be any that keep to these rules, and one draw needn't show every extreme that they name: `segments`: ids never fall along a row; each of the 3 sequences of an index of expert is present, and the longest has 512 tokens. `routes`: each token names 6 different experts; no expert is named by more than 20 of one device's tokens, a bound that some device's tokens reach.
All inputs are finite; a program needn't handle non-finite values.
Results may differ from a plain program's by a relative error of at most 0.02.
Values may be sent and summed in bfloat16 or wider, within the bound.
A program may use at most 512 MiB of HBM per device.

v0:
```python
import jax
import jax.numpy as jnp
from jax import lax
from jax.sharding import PartitionSpec as P

NOPE = 128
ROPE = 64
VDIM = 128
LATENT = 512
TOPK = 6
CAP = 20


eps = 1e-06
route_scale = 2.446
rope_base = 50000.0
highest = lax.Precision.HIGHEST


def matmul(left, right):
    return jnp.dot(left, right, preferred_element_type=jnp.float32)


def trans_times(left, right):
    return lax.dot_general(
        left, right, (((0,), (0,)), ((), ())), preferred_element_type=jnp.float32
    )


def times_trans(left, right):
    return lax.dot_general(
        left, right, (((1,), (1,)), ((), ())), preferred_element_type=jnp.float32
    )


def inv_rms(value):
    return lax.rsqrt(jnp.mean(value * value, axis=-1, keepdims=True) + eps)


def norm_back(grad_out, value, scale, gain):
    scaled = grad_out * gain
    grad_in = scale * scaled - value * scale**3 * jnp.mean(scaled * value, axis=-1, keepdims=True)
    gain_grad = jnp.sum(grad_out * value * scale, axis=0)
    return (grad_in, gain_grad)


def rope_tables(seg):
    size = seg.shape[0]
    index = jnp.arange(size, dtype=jnp.int32)
    fresh = jnp.concatenate([jnp.ones((1,), dtype=bool), seg[1:] != seg[:-1]])
    first = lax.cummax(jnp.where(fresh, index, jnp.zeros_like(index)), axis=0)
    place = (index - first).astype(jnp.float32)
    half = ROPE // 2
    freqs = rope_base ** (-(jnp.arange(half, dtype=jnp.float32) * 2.0 / ROPE))
    angle = place[:, None] * freqs[None, :]
    return (jnp.cos(angle), jnp.sin(angle))


def attention_mask(seg):
    index = jnp.arange(seg.shape[0], dtype=jnp.int32)
    return (seg[:, None] == seg[None, :]) & (index[None, :] <= index[:, None])


def rotate(value, cosine, sine):
    half = value.shape[-1] // 2
    first, second = (value[..., :half], value[..., half:])
    return jnp.concatenate(
        [first * cosine - second * sine, second * cosine + first * sine], axis=-1
    )


def unrotate(value, cosine, sine):
    half = value.shape[-1] // 2
    first, second = (value[..., :half], value[..., half:])
    return jnp.concatenate(
        [first * cosine + second * sine, second * cosine - first * sine], axis=-1
    )


def shared_pass(inputs, grads, gate_matrix, up_matrix, down_matrix):
    gate = matmul(inputs, gate_matrix)
    lift = matmul(inputs, up_matrix)
    sigma = jax.nn.sigmoid(gate)
    active = gate * sigma
    hidden = (active * lift).astype(jnp.bfloat16)
    back = times_trans(grads, down_matrix)
    gate_grad = (back * lift * sigma * (1.0 + gate * (1.0 - sigma))).astype(jnp.bfloat16)
    lift_grad = (back * active).astype(jnp.bfloat16)
    return (
        hidden,
        gate_grad,
        lift_grad,
        (
            trans_times(inputs, gate_grad),
            trans_times(inputs, lift_grad),
            trans_times(hidden, grads),
        ),
    )


def shared_rows(hidden, gate_grad, lift_grad, gate_matrix, up_matrix, down_matrix):
    return (
        matmul(hidden, down_matrix),
        times_trans(gate_grad, gate_matrix) + times_trans(lift_grad, up_matrix),
    )


def expert_pass(inputs, grads, gate_matrix, up_matrix, down_matrix):
    gate = jnp.einsum("sjcd,jdf->sjcf", inputs, gate_matrix, preferred_element_type=jnp.float32)
    lift = jnp.einsum("sjcd,jdf->sjcf", inputs, up_matrix, preferred_element_type=jnp.float32)
    sigma = jax.nn.sigmoid(gate)
    active = gate * sigma
    hidden = (active * lift).astype(jnp.bfloat16)
    back = jnp.einsum("sjcd,jfd->sjcf", grads, down_matrix, preferred_element_type=jnp.float32)
    gate_grad = (back * lift * sigma * (1.0 + gate * (1.0 - sigma))).astype(jnp.bfloat16)
    lift_grad = (back * active).astype(jnp.bfloat16)
    weight_grads = (
        jnp.einsum("sjcd,sjcf->jdf", inputs, gate_grad, preferred_element_type=jnp.float32),
        jnp.einsum("sjcd,sjcf->jdf", inputs, lift_grad, preferred_element_type=jnp.float32),
        jnp.einsum("sjcf,sjcd->jfd", hidden, grads, preferred_element_type=jnp.float32),
    )
    return (hidden, gate_grad, lift_grad, weight_grads)


def expert_rows(hidden, gate_grad, lift_grad, gate_matrix, up_matrix, down_matrix):
    produced = jnp.einsum("sjcf,jfd->sjcd", hidden, down_matrix, preferred_element_type=jnp.float32)
    returned = jnp.einsum(
        "sjcf,jdf->sjcd", gate_grad, gate_matrix, preferred_element_type=jnp.float32
    )
    returned = returned + jnp.einsum(
        "sjcf,jdf->sjcd", lift_grad, up_matrix, preferred_element_type=jnp.float32
    )
    return (produced, returned)


def per_device(
    tokens,
    cotangent,
    segments,
    routes,
    first_gain,
    query_weight,
    latent_weight,
    latent_gain,
    expand_weight,
    output_weight,
    second_gain,
    router_weight,
    shared_gate,
    shared_up,
    shared_down,
    expert_gate,
    expert_up,
    expert_down,
):
    weight_count = lax.axis_size("weight")
    token_rows = tokens.shape[0]
    width = tokens.shape[1]
    group_rows = token_rows * weight_count
    query_width = NOPE + ROPE
    heads_here = query_weight.shape[1] // query_width
    expert_count = router_weight.shape[1]
    local_experts = expert_gate.shape[0]
    score_scale = query_width ** (-0.5)
    activations = tokens.astype(jnp.float32)
    first_scale = inv_rms(activations)
    normed = (activations * first_scale * first_gain).astype(jnp.bfloat16)
    normed_all = lax.all_gather(normed, "weight", axis=0, tiled=True)
    cosine, sine = rope_tables(segments[0])
    allowed = attention_mask(segments[0])
    query_full = matmul(normed_all, query_weight).reshape(group_rows, heads_here, query_width)
    query = jnp.concatenate(
        [
            query_full[..., :NOPE],
            rotate(query_full[..., NOPE:], cosine[:, None, :], sine[:, None, :]),
        ],
        axis=-1,
    ).astype(jnp.bfloat16)
    compressed = matmul(normed_all, latent_weight)
    latent = compressed[:, :LATENT]
    latent_scale = inv_rms(latent)
    latent_normed = (latent * latent_scale * latent_gain).astype(jnp.bfloat16)
    key_rope = rotate(compressed[:, LATENT:], cosine, sine).astype(jnp.bfloat16)
    expanded = (
        matmul(latent_normed, expand_weight)
        .astype(jnp.bfloat16)
        .reshape(group_rows, heads_here, NOPE + VDIM)
    )
    key_nope = expanded[..., :NOPE]
    values = expanded[..., NOPE:]

    def score_block():
        raw = jnp.einsum(
            "ihd,jhd->hij", query[..., :NOPE], key_nope, preferred_element_type=jnp.float32
        )
        raw = raw + jnp.einsum(
            "ihd,jd->hij", query[..., NOPE:], key_rope, preferred_element_type=jnp.float32
        )
        return jnp.where(allowed[None], raw * score_scale, -1e30)

    scores = score_block()
    peak = jnp.max(scores, axis=-1, keepdims=True)
    weights = jnp.exp(scores - peak)
    total = jnp.sum(weights, axis=-1, keepdims=True)
    log_total = peak + jnp.log(total)
    mixed = jnp.einsum(
        "hij,jhd->ihd",
        (weights / total).astype(jnp.bfloat16),
        values,
        preferred_element_type=jnp.float32,
    )
    mixed = mixed.astype(jnp.bfloat16).reshape(group_rows, heads_here * VDIM)
    attended = lax.psum_scatter(
        matmul(mixed, output_weight), "weight", scatter_dimension=0, tiled=True
    )
    hidden_one = activations + attended
    second_scale = inv_rms(hidden_one)
    normed_two = (hidden_one * second_scale * second_gain).astype(jnp.bfloat16)
    gates = jax.nn.sigmoid(matmul(normed_two, router_weight))
    choose = (
        routes[:, :, None] == jnp.arange(expert_count, dtype=jnp.int32)[None, None, :]
    ).astype(jnp.float32)
    chosen = jnp.sum(choose * gates[:, None, :], axis=-1)
    chosen_total = jnp.sum(chosen, axis=1, keepdims=True)
    mixing = route_scale * chosen / chosen_total
    flat_ids = routes.reshape(-1)
    hits = (flat_ids[:, None] == jnp.arange(expert_count, dtype=jnp.int32)[None, :]).astype(
        jnp.int32
    )
    place = jnp.sum(jnp.cumsum(hits, axis=0) * hits, axis=1) - 1
    slot_of = flat_ids * CAP + place
    slot_token = (
        jnp.zeros((expert_count * CAP,), jnp.int32)
        .at[slot_of]
        .set(jnp.arange(token_rows * TOPK, dtype=jnp.int32) // TOPK)
    )
    slot_mix = jnp.zeros((expert_count * CAP,), jnp.float32).at[slot_of].set(mixing.reshape(-1))
    slot_used = jnp.zeros((expert_count * CAP,), jnp.bool_).at[slot_of].set(True)
    upstream = cotangent.astype(jnp.float32)
    send_rows = jnp.where(
        slot_used[:, None], normed_two[slot_token], jnp.zeros((), jnp.bfloat16)
    ).reshape(expert_count, CAP, width)
    send_grads = (
        (slot_mix[:, None] * upstream[slot_token])
        .astype(jnp.bfloat16)
        .reshape(expert_count, CAP, width)
    )
    got_rows, got_grads = (
        lax.all_to_all(send_rows, "expert", split_axis=0, concat_axis=0, tiled=True),
        lax.all_to_all(send_grads, "expert", split_axis=0, concat_axis=0, tiled=True),
    )
    normed_group, upstream_group, rows_group, grads_group = (
        lax.all_gather(normed_two, "weight", axis=0, tiled=True),
        lax.all_gather(cotangent, "weight", axis=0, tiled=True),
        lax.all_gather(got_rows, "weight", axis=0, tiled=True),
        lax.all_gather(got_grads, "weight", axis=0, tiled=True),
    )
    shared_act, shared_gate_grad, shared_lift_grad, shared_grads = shared_pass(
        normed_group, upstream_group, shared_gate, shared_up, shared_down
    )
    routed_in = rows_group.reshape(-1, local_experts, CAP, width)
    routed_grad = grads_group.reshape(-1, local_experts, CAP, width)
    routed_act, routed_gate_grad, routed_lift_grad, expert_grads = expert_pass(
        routed_in, routed_grad, expert_gate, expert_up, expert_down
    )
    per_block = token_rows + expert_count * CAP
    blocks = per_block * lax.axis_size("weight") // per_block
    shared_part, shared_in = shared_rows(
        shared_act, shared_gate_grad, shared_lift_grad, shared_gate, shared_up, shared_down
    )
    routed_part, routed_in_back = expert_rows(
        routed_act, routed_gate_grad, routed_lift_grad, expert_gate, expert_up, expert_down
    )
    forward_part = jnp.concatenate(
        [shared_part.reshape(blocks, token_rows, width), routed_part.reshape(blocks, -1, width)],
        axis=1,
    )
    backward_part = jnp.concatenate(
        [shared_in.reshape(blocks, token_rows, width), routed_in_back.reshape(blocks, -1, width)],
        axis=1,
    )
    summed = lax.psum_scatter(
        jnp.concatenate([forward_part, backward_part], axis=2)
        .reshape(per_block * lax.axis_size("weight"), 2 * width)
        .astype(jnp.bfloat16),
        "weight",
        scatter_dimension=0,
        tiled=True,
    ).astype(jnp.float32)
    shared_out = summed[:token_rows, :width]
    shared_back = summed[:token_rows, width:]
    routed_out = summed[token_rows:, :width]
    routed_back = summed[token_rows:, width:]
    back_out, back_in = (
        lax.all_to_all(
            routed_out.astype(jnp.bfloat16).reshape(expert_count, CAP, width),
            "expert",
            split_axis=0,
            concat_axis=0,
            tiled=True,
        ),
        lax.all_to_all(
            routed_back.astype(jnp.bfloat16).reshape(expert_count, CAP, width),
            "expert",
            split_axis=0,
            concat_axis=0,
            tiled=True,
        ),
    )
    picked = (
        back_out.reshape(-1, width)[slot_of].reshape(token_rows, TOPK, width).astype(jnp.float32)
    )
    layer_out = (hidden_one + shared_out + jnp.sum(mixing[:, :, None] * picked, axis=1)).astype(
        jnp.bfloat16
    )
    mix_grad = jnp.sum(upstream[:, None, :] * picked, axis=-1)
    chosen_grad = route_scale * (
        mix_grad / chosen_total
        - jnp.sum(mix_grad * chosen, axis=1, keepdims=True) / chosen_total**2
    )
    logit_grad = jnp.sum(choose * chosen_grad[:, :, None], axis=1) * gates * (1.0 - gates)
    routed_sum = jnp.sum(
        back_in.reshape(-1, width)[slot_of].reshape(token_rows, TOPK, width).astype(jnp.float32),
        axis=1,
    )
    normed_two_grad = (
        shared_back
        + routed_sum
        + jnp.dot(logit_grad, router_weight.astype(jnp.float32).T, precision=highest)
    )
    router_gradient = jnp.dot(normed_two.astype(jnp.float32).T, logit_grad, precision=highest)
    back_two, second_gain_gradient = norm_back(
        normed_two_grad, hidden_one, second_scale, second_gain
    )
    hidden_grad = upstream + back_two
    hidden_group = lax.all_gather(hidden_grad.astype(jnp.bfloat16), "weight", axis=0, tiled=True)
    output_gradient = trans_times(mixed, hidden_group)
    mixed_grad = (
        times_trans(hidden_group, output_weight)
        .astype(jnp.bfloat16)
        .reshape(group_rows, heads_here, VDIM)
    )
    probs = jnp.exp(score_block() - log_total)
    prob_grad = jnp.einsum("ihd,jhd->hij", mixed_grad, values, preferred_element_type=jnp.float32)
    centre = jnp.sum(probs * prob_grad, axis=-1, keepdims=True)
    score_grad = (probs * (prob_grad - centre)).astype(jnp.bfloat16)
    value_grad = jnp.einsum(
        "hij,ihd->jhd", probs.astype(jnp.bfloat16), mixed_grad, preferred_element_type=jnp.float32
    )
    query_nope_grad = (
        jnp.einsum("hij,jhd->ihd", score_grad, key_nope, preferred_element_type=jnp.float32)
        * score_scale
    )
    query_rope_grad = (
        jnp.einsum("hij,jd->ihd", score_grad, key_rope, preferred_element_type=jnp.float32)
        * score_scale
    )
    key_nope_grad = (
        jnp.einsum(
            "hij,ihd->jhd", score_grad, query[..., :NOPE], preferred_element_type=jnp.float32
        )
        * score_scale
    )
    key_rope_grad = (
        jnp.einsum("hij,ihd->jd", score_grad, query[..., NOPE:], preferred_element_type=jnp.float32)
        * score_scale
    )
    query_grad = jnp.concatenate(
        [query_nope_grad, unrotate(query_rope_grad, cosine[:, None, :], sine[:, None, :])], axis=-1
    )
    query_grad = query_grad.astype(jnp.bfloat16).reshape(group_rows, heads_here * query_width)
    expand_grad = (
        jnp.concatenate([key_nope_grad, value_grad], axis=-1)
        .astype(jnp.bfloat16)
        .reshape(group_rows, heads_here * (NOPE + VDIM))
    )
    query_gradient = trans_times(normed_all, query_grad)
    expand_gradient = trans_times(latent_normed, expand_grad)
    latent_normed_grad = times_trans(expand_grad, expand_weight)
    latent_back, latent_gain_gradient = norm_back(
        latent_normed_grad, latent, latent_scale, latent_gain
    )
    compressed_grad = jnp.concatenate([latent_back, unrotate(key_rope_grad, cosine, sine)], axis=-1)
    latent_weight_gradient = jnp.dot(
        normed_all.astype(jnp.float32).T, compressed_grad, precision=highest
    )
    latent_float = latent_weight.astype(jnp.float32)
    normed_grad = lax.psum_scatter(
        (
            times_trans(query_grad, query_weight)
            + jnp.dot(compressed_grad, latent_float.T, precision=highest)
        ).astype(jnp.bfloat16),
        "weight",
        scatter_dimension=0,
        tiled=True,
    ).astype(jnp.float32)
    back_one, first_gain_gradient = norm_back(normed_grad, activations, first_scale, first_gain)
    token_gradient = hidden_grad + back_one
    shards = (
        lax.psum_scatter(
            query_gradient.astype(jnp.bfloat16), "expert", scatter_dimension=0, tiled=True
        ).astype(jnp.float32),
        lax.psum_scatter(
            expand_gradient.astype(jnp.bfloat16), "expert", scatter_dimension=0, tiled=True
        ).astype(jnp.float32),
        lax.psum_scatter(
            output_gradient.astype(jnp.bfloat16), "expert", scatter_dimension=1, tiled=True
        ).astype(jnp.float32),
        lax.psum_scatter(
            shared_grads[0].astype(jnp.bfloat16), "expert", scatter_dimension=0, tiled=True
        ).astype(jnp.float32),
        lax.psum_scatter(
            shared_grads[1].astype(jnp.bfloat16), "expert", scatter_dimension=0, tiled=True
        ).astype(jnp.float32),
        lax.psum_scatter(
            shared_grads[2].astype(jnp.bfloat16), "expert", scatter_dimension=1, tiled=True
        ).astype(jnp.float32),
    )
    totals = lax.psum(
        (
            latent_weight_gradient,
            latent_gain_gradient,
            router_gradient,
            first_gain_gradient,
            second_gain_gradient,
        ),
        ("expert", "weight"),
    )
    return (
        layer_out,
        token_gradient,
        totals[3],
        shards[0],
        totals[0],
        totals[1],
        shards[1],
        shards[2],
        totals[4],
        totals[2],
        shards[3],
        shards[4],
        shards[5],
        expert_grads[0],
        expert_grads[1],
        expert_grads[2],
    )


def solution(mesh):
    return jax.shard_map(
        per_device,
        mesh=mesh,
        in_specs=(
            P(("expert", "weight"), None),
            P(("expert", "weight"), None),
            P("expert", None),
            P(("expert", "weight"), None),
            P(),
            P(None, "weight"),
            P(),
            P(),
            P(None, "weight"),
            P("weight", None),
            P(),
            P(),
            P(None, "weight"),
            P(None, "weight"),
            P("weight", None),
            P("expert", None, "weight"),
            P("expert", None, "weight"),
            P("expert", "weight", None),
        ),
        out_specs=(
            P(("expert", "weight"), None),
            P(("expert", "weight"), None),
            P(),
            P("expert", "weight"),
            P(),
            P(),
            P("expert", "weight"),
            P("weight", "expert"),
            P(),
            P(),
            P("expert", "weight"),
            P("expert", "weight"),
            P("weight", "expert"),
            P("expert", None, "weight"),
            P("expert", None, "weight"),
            P("expert", "weight", None),
        ),
        check_vma=False,
    )
```

profile of v0, /device:TPU:0, one launch (start us, length us, event | category | flops | bytes accessed | tf_op | source)
XLA Modules:
  0.0 2270.9 jit_solution(17516090737797783811)
XLA Ops:
  17.0 23.4 %all-gather.7.cloned.1.call-done = bf16[640,2048]{1,0:T(8,128)(2,1)} async-done(((bf16[160,2048]{1,0:T(8,128)(2,1)}), bf16[640,2048]{1,0:T(8,128)(2,1)}) %all-gather.7.cloned.1.call-update) | async-done | bytes 2621456 | tf_op jit(solution)/shard_map/all_gather | solution.py:168
  77.6 31.2 %reduce-window.19 = s32[64,8,128]{2,1,0:T(8,128)S(1)} reduce-window(s32[64,8,128]{2,1,0:T(8,128)} %bitcast.203, s32[]{:T(128)} %constant.30.clone.1), window={size=1x1x128 pad=0_0x0_0x127_0}, to_apply=%region_8.9 | reduce-window | flops 8323072 | bytes 524292 | tf_op jit(solution)/shard_map/reduce-window.2
  119.3 12.1 gather_fusion.1
  131.3 12.4 gather.19
  155.3 8.0 multiply_convert_fusion
  170.2 137.3 %all-to-all-done.1 = bf16[64,20,2048]{2,1,0:T(8,128)(2,1)} async-done(((bf16[64,20,2048]{2,1,0:T(8,128)(2,1)}), bf16[64,20,2048]{2,1,0:T(8,128)(2,1)}, u32[]{:S(2)}, u32[]{:S(2)}) %all-to-all-start.1) | async-done | bytes 5242912 | tf_op jit(solution)/shard_map/all_to_all | solution.py:250
  307.6 8.0 copy.187
  320.3 12.1 gather_fusion
  332.4 9.0 gather.17
  344.7 141.8 %all_to_all.20 = bf16[64,20,2048]{2,1,0:T(8,128)(2,1)S(1)} all-to-all(bf16[64,20,2048]{2,1,0:T(8,128)(2,1)S(1)} %broadcast_select_fusion), channel_id=1, replica_groups=mesh['expert'=8,'weight'=4] {'expert'}, dimensions={0} | all-to-all | bytes 10485760 | tf_op jit(solution)/shard_map/all_to_all | solution.py:249
  519.1 40.6 %fusion.3 = f32[8,32,20,352]{3,1,2,0:T(8,128)} fusion(bf16[32,8,20,2048]{3,1,0,2:T(8,128)(2,1)} %bitcast.192, bf16[8,352,2048]{2,1,0:T(8,128)(2,1)} %param.35), kind=kOutput, calls=%fused_computation.13 | convolution fusion | flops 7381975040 | bytes 39714816 | tf_op jit(solution)/shard_map/sjcd,jfd->sjcf/dot_general | solution.py:114
  559.7 62.0 %all-gather.11.cloned.1.call-done = bf16[256,20,2048]{2,0,1:T(8,128)(2,1)} async-done(((bf16[64,20,2048]{2,0,1:T(8,128)(2,1)}), bf16[256,20,2048]{2,0,1:T(8,128)(2,1)}) %all-gather.11.cloned.1.call-update) | async-done | bytes 20971536 | tf_op jit(solution)/shard_map/all_gather | solution.py:255
  621.7 40.8 %fusion.11 = f32[8,32,20,352]{3,1,2,0:T(8,128)} fusion(bf16[32,8,20,2048]{3,1,0,2:T(8,128)(2,1)} %bitcast.188, bf16[8,2048,352]{1,2,0:T(8,128)(2,1)} %param.33), kind=kOutput, calls=%fused_computation.21 | convolution fusion | flops 7381975040 | bytes 39714816 | tf_op jit(solution)/shard_map/sjcd,jdf->sjcf/dot_general | solution.py:109
  662.5 43.9 %fusion.33 = (bf16[32,8,20,352]{3,0,2,1:T(8,128)(2,1)}, bf16[32,8,20,352]{3,0,2,1:T(8,128)(2,1)}, bf16[32,8,20,352]{3,0,2,1:T(8,128)(2,1)}) fusion(f32[8,32,20,352]{3,1,2,0:T(8,128)} %fusion.11, f32[8,32,20,352]{3,1,2,0:T(8,128)} %fusion.3, bf16[8,2048,352]{1,2,0:T(8,128)(2,1)} %param.34, bf16[32,8,20,2048]{3,1,0,2:T(8,128)(2,1)} %bitcast.189), kind=kOutput, calls=%fused_computation.43 | convolution fusion | flops 7409008640 | bytes 57737216 | tf_op jit(solution)/shard_map/sjcd,jdf->sjcf/dot_general | solution.py:110
  706.4 23.7 %fusion.15 = f32[8,32,20,2048]{3,1,2,0:T(8,128)} fusion(bf16[32,8,20,352]{3,0,2,1:T(8,128)(2,1)} %get-tuple-element.36, bf16[8,2048,352]{1,2,0:T(8,128)(2,1)} %param.33), kind=kOutput, calls=%fused_computation.26 | convolution fusion | flops 7381975040 | bytes 57081856 | tf_op jit(solution)/shard_map/sjcf,jdf->sjcd/dot_general | solution.py:127
  730.1 27.5 %fusion = bf16[32,8,20,2048]{3,0,2,1:T(8,128)(2,1)} fusion(f32[8,32,20,2048]{3,1,2,0:T(8,128)} %fusion.15, bf16[32,8,20,352]{3,0,2,1:T(8,128)(2,1)} %get-tuple-element.37, bf16[8,2048,352]{1,2,0:T(8,128)(2,1)} %param.34), kind=kOutput, calls=%fused_computation.9 | convolution fusion | flops 7402946560 | bytes 78053376 | tf_op jit(solution)/shard_map/sjcf,jdf->sjcd/dot_general | solution.py:130
  757.6 25.9 %copy.189 = bf16[32,8,20,2048]{3,2,1,0:T(8,128)(2,1)} copy(bf16[32,8,20,2048]{3,0,2,1:T(8,128)(2,1)} %fusion) | data formatting | bytes 41943040 | tf_op jit(solution)/shard_map/add | solution.py:130
  783.5 31.5 %reshape.442 = bf16[4,1280,2048]{2,1,0:T(8,128)(2,1)} reshape(bf16[32,8,20,2048]{3,2,1,0:T(8,128)(2,1)} %copy.189) | data formatting | bytes 41943040 | tf_op jit(solution)/shard_map/reshape | solution.py:279
  815.0 20.2 convert_bitcast_fusion
  835.2 25.9 %copy.185 = bf16[32,8,20,2048]{3,2,1,0:T(8,128)(2,1)} copy(bf16[32,8,20,2048]{3,0,2,1:T(8,128)(2,1)} %convert_bitcast_fusion) | data formatting | bytes 41943040 | tf_op jit(solution)/shard_map/sjcf,jfd->sjcd/transpose | solution.py:126
  861.1 31.5 %reshape.439 = bf16[4,1280,2048]{2,1,0:T(8,128)(2,1)} reshape(bf16[32,8,20,2048]{3,2,1,0:T(8,128)(2,1)} %copy.185) | data formatting | bytes 41943040 | tf_op jit(solution)/shard_map/reshape | solution.py:275
  892.6 32.3 %maximum_maximum_fusion = bf16[4,1440,4096]{2,1,0:T(8,128)(2,1)} fusion(bf16[4,1280,2048]{2,1,0:T(8,128)(2,1)} %reshape.442, bf16[4,160,2048]{2,1,0:T(8,128)(2,1)} %bitcast.198, bf16[4,1280,2048]{2,1,0:T(8,128)(2,1)} %reshape.439, bf16[4,160,2048]{2,1,0:T(8,128)(2,1)} %bitcast.197), kind=kLoop, calls=%fused_computation.7 | loop fusion | flops 188743680 | bytes 94371840 | tf_op jit(solution)/shard_map/concatenate | solution.py:283
  924.9 324.3 %reduce-scatter.12.cloned.1.call-done = bf16[1440,4096]{1,0:T(8,128)(2,1)} async-done(((bf16[5760,4096]{1,0:T(8,128)(2,1)}), bf16[1440,4096]{1,0:T(8,128)(2,1)}) %reduce-scatter.12.cloned.1.call-update) | async-done | bytes 11796496 | tf_op jit(solution)/shard_map/reduce_scatter | solution.py:282
  1249.2 10.3 fusion.114
  1259.4 8.9 reshape.445
  1273.9 8.9 reshape.443
  1282.8 129.1 %all-to-all-done.3 = bf16[64,20,2048]{2,1,0:T(8,128)(2,1)} async-done(((bf16[64,20,2048]{2,1,0:T(8,128)(2,1)}), bf16[64,20,2048]{2,1,0:T(8,128)(2,1)}, u32[]{:S(2)}, u32[]{:S(2)}) %all-to-all-start.3) | async-done | bytes 5242912 | tf_op jit(solution)/shard_map/all_to_all | solution.py:302
  1416.8 13.8 convert_element_type.175
  1430.6 9.0 reshape.446
  1439.6 11.9 gather_fusion.3
  1451.5 7.8 reshape.450
  1459.2 8.4 reduce_sum.179
  1467.6 86.4 %all-to-all-done.2 = bf16[64,20,2048]{2,1,0:T(8,128)(2,1)} async-done(((bf16[64,20,2048]{2,1,0:T(8,128)(2,1)}), bf16[64,20,2048]{2,1,0:T(8,128)(2,1)}, u32[]{:S(2)}, u32[]{:S(2)}) %all-to-all-start.2) | async-done | bytes 5242912 | tf_op jit(solution)/shard_map/all_to_all | solution.py:295
  1554.0 9.0 reshape.444
  1563.0 11.9 gather_fusion.2
  1574.9 7.8 reshape.449
  1582.7 8.7 multiply_reduce_fusion
  1674.3 25.2 %reduce-scatter.22.cloned.1.call-done = bf16[256,704]{0,1:T(8,128)(2,1)} async-done(((bf16[2048,704]{0,1:T(8,128)(2,1)}), bf16[256,704]{0,1:T(8,128)(2,1)}) %reduce-scatter.22.cloned.1.call-update) | async-done | bytes 360464 | tf_op jit(solution)/shard_map/reduce_scatter | solution.py:409
  1701.4 73.7 %reduce-scatter.24.cloned.1.call-done = bf16[256,704]{0,1:T(8,128)(2,1)} async-done(((bf16[2048,704]{0,1:T(8,128)(2,1)}), bf16[256,704]{0,1:T(8,128)(2,1)}) %reduce-scatter.24.cloned.1.call-update) | async-done | bytes 360464 | tf_op jit(solution)/shard_map/reduce_scatter | solution.py:412
  1776.9 73.9 %reduce-scatter.26.cloned.1.call-done = bf16[704,256]{1,0:T(8,128)(2,1)} async-done(((bf16[704,2048]{1,0:T(8,128)(2,1)}), bf16[704,256]{1,0:T(8,128)(2,1)}) %reduce-scatter.26.cloned.1.call-update) | async-done | bytes 360464 | tf_op jit(solution)/shard_map/reduce_scatter | solution.py:415
  1852.7 30.1 %fusion.23 = f32[8,2048,352]{1,2,0:T(8,128)} fusion(bf16[32,8,20,352]{3,0,2,1:T(8,128)(2,1)} %get-tuple-element.36, bf16[32,8,20,2048]{3,1,0,2:T(8,128)(2,1)} %bitcast.190), kind=kOutput, calls=%fused_computation.34 | convolution fusion | flops 7381975040 | bytes 47644672 | tf_op jit(solution)/shard_map/sjcd,sjcf->jdf/dot_general | solution.py:118
  1882.8 27.9 %fusion.20 = f32[8,352,2048]{2,1,0:T(8,128)} fusion(bf16[32,8,20,352]{3,0,2,1:T(8,128)(2,1)S(1)} %copy-done.16, bf16[32,8,20,2048]{3,1,0,2:T(8,128)(2,1)} %bitcast.193), kind=kOutput, calls=%fused_computation.33 | convolution fusion | flops 7381975040 | bytes 47644672 | tf_op jit(solution)/shard_map/sjcf,sjcd->jfd/dot_general | solution.py:120
  1919.5 29.7 %fusion.26 = f32[8,2048,352]{1,2,0:T(8,128)} fusion(bf16[32,8,20,352]{3,0,2,1:T(8,128)(2,1)} %get-tuple-element.37, bf16[32,8,20,2048]{3,1,0,2:T(8,128)(2,1)} %bitcast.191), kind=kOutput, calls=%fused_computation.35 | convolution fusion | flops 7381975040 | bytes 47644672 | tf_op jit(solution)/shard_map/sjcd,sjcf->jdf/dot_general | solution.py:119
  1950.9 38.3 %reduce-scatter.20.cloned.1.call-done = bf16[512,256]{1,0:T(8,128)(2,1)} async-done(((bf16[512,2048]{1,0:T(8,128)(2,1)}), bf16[512,256]{1,0:T(8,128)(2,1)}) %reduce-scatter.20.cloned.1.call-update) | async-done | bytes 262160 | tf_op jit(solution)/shard_map/reduce_scatter | solution.py:406
  1990.9 34.2 %reduce-scatter.14.cloned.1.call-done = bf16[160,2048]{1,0:T(8,128)(2,1)} async-done(((bf16[640,2048]{1,0:T(8,128)(2,1)}), bf16[160,2048]{1,0:T(8,128)(2,1)}) %reduce-scatter.14.cloned.1.call-update) | async-done | bytes 655376 | tf_op jit(solution)/shard_map/reduce_scatter | solution.py:388
  2026.9 41.5 %all-reduce.1 = (f32[2048]{0:T(1024)}, f32[512]{0:T(512)}, f32[2048]{0:T(1024)}) all-reduce(f32[2048]{0:T(1024)S(1)} %get-tuple-element.22, f32[512]{0:T(512)S(1)} %get-tuple-element.18, f32[2048]{0:T(1024)S(1)} %get-tuple-element.20), channel_id=1, replica_groups=mesh['expert'=8,'weight'=4] {'expert','weight'}, use_global_device_ids=true, to_apply=%region_28.29 | all-reduce | flops 4608 | bytes 36864 | tf_op jit(solution)/shard_map/psum | solution.py:419
  2071.5 32.7 %reduce-scatter.16.cloned.1.call-done = bf16[256,768]{1,0:T(8,128)(2,1)} async-done(((bf16[2048,768]{1,0:T(8,128)(2,1)}), bf16[256,768]{1,0:T(8,128)(2,1)}) %reduce-scatter.16.cloned.1.call-update) | async-done | bytes 393232 | tf_op jit(solution)/shard_map/reduce_scatter | solution.py:400
  2106.2 151.8 %all-reduce.5.cloned.1.call-done = (f32[2048,576]{0,1:T(8,128)}, f32[2048,64]{0,1:T(8,128)}) async-done(((f32[2048,576]{0,1:T(8,128)}, f32[2048,64]{0,1:T(8,128)}), (f32[2048,576]{0,1:T(8,128)}, f32[2048,64]{0,1:T(8,128)})) %all-reduce.5.cloned.1.call-update) | async-done | bytes 5242896 | tf_op jit(solution)/shard_map/psum | solution.py:419
  (332 shorter events, 239.0 us)
Async XLA Ops:
  7.2 51.6 %copy-start = (bf16[2048,768]{1,0:T(8,128)(2,1)S(1)}, bf16[2048,768]{1,0:T(8,128)(2,1)}, u32[]{:S(2)}) copy-start(bf16[2048,768]{1,0:T(8,128)(2,1)} %param.23) | copy-start | bytes 9437188
  7.2 33.2 %all-gather.7.cloned.1.call-start = ((), (), s32[]{:S(2)}) async-start(), calls=%async_computation.13 | async-start | bytes 3276800 | tf_op jit(solution)/shard_map/all_gather | solution.py:168
  11.9 131.8 %reduce-scatter.10.cloned.1.call-start = ((), (), s32[]{:S(2)}) async-start(), calls=%async_computation.14 | async-start | bytes 6553600 | tf_op jit(solution)/shard_map/reduce_scatter | solution.py:213
  40.4 6.1 copy-start.71
  40.4 6.1 copy-start.79
  113.7 201.9 %copy-start.60 = (s32[960,1]{0,1:T(1,128)}, s32[960,1]{0,1:T(1,128)S(1)}, u32[]{:S(2)}) copy-start(s32[960,1]{0,1:T(1,128)S(1)} %compare_select_fusion) | copy-start | bytes 11524
  146.2 17.2 copy-start.58
  149.2 14.2 copy-start.50
  149.2 14.2 copy-start.62
  149.8 13.5 copy-start.32
  163.4 144.2 %all-to-all-start.1 = ((bf16[64,20,2048]{2,1,0:T(8,128)(2,1)}), bf16[64,20,2048]{2,1,0:T(8,128)(2,1)}, u32[]{:S(2)}, u32[]{:S(2)}) async-start(bf16[64,20,2048]{2,1,0:T(8,128)(2,1)} %multiply_convert_fusion), calls=%async_computation.2 | async-start | bytes 12582912 | tf_op jit(solution)/shard_map/all_to_all | solution.py:250
  168.9 323.1 %all-gather.13.cloned.1.call-start = ((), (), s32[]{:S(2)}) async-start(), calls=%async_computation.17 | async-start | bytes 3276800 | tf_op jit(solution)/shard_map/all_gather | solution.py:254
  169.6 328.7 %all-gather.9.cloned.1.call-start = ((), (), s32[]{:S(2)}) async-start(), calls=%async_computation.15 | async-start | bytes 3276800 | tf_op jit(solution)/shard_map/all_gather | solution.py:253
  170.2 348.9 %all-gather.15.cloned.1.call-start = ((), (), s32[]{:S(2)}) async-start(), calls=%async_computation.18 | async-start | bytes 26214400 | tf_op jit(solution)/shard_map/all_gather | solution.py:256
  315.5 306.1 %all-gather.11.cloned.1.call-start = ((), (), s32[]{:S(2)}) async-start(), calls=%async_computation.16 | async-start | bytes 26214400 | tf_op jit(solution)/shard_map/all_gather | solution.py:255
  491.8 757.4 %reduce-scatter.12.cloned.1.call-start = ((), (), s32[]{:S(2)}) async-start(), calls=%async_computation.19 | async-start | bytes 58982400 | tf_op jit(solution)/shard_map/reduce_scatter | solution.py:282
  498.3 6.5 copy-start.75
  498.3 6.5 copy-start.77
  498.3 7.1 copy-start.82
  508.4 6.8 copy-start.83
  1268.3 143.6 %all-to-all-start.3 = ((bf16[64,20,2048]{2,1,0:T(8,128)(2,1)}), bf16[64,20,2048]{2,1,0:T(8,128)(2,1)}, u32[]{:S(2)}, u32[]{:S(2)}) async-start(bf16[64,20,2048]{2,1,0:T(8,128)(2,1)} %reshape.445), calls=%async_computation.5 | async-start | bytes 12582912 | tf_op jit(solution)/shard_map/all_to_all | solution.py:302
  1282.8 133.9 %copy-start.61 = (s32[960,1]{0,1:T(1,128)S(1)}, s32[960,1]{0,1:T(1,128)}, u32[]{:S(2)}) copy-start(s32[960,1]{0,1:T(1,128)} %copy-done.60) | copy-start | bytes 11524
  1411.9 142.1 %all-to-all-start.2 = ((bf16[64,20,2048]{2,1,0:T(8,128)(2,1)}), bf16[64,20,2048]{2,1,0:T(8,128)(2,1)}, u32[]{:S(2)}, u32[]{:S(2)}) async-start(bf16[64,20,2048]{2,1,0:T(8,128)(2,1)} %reshape.443), calls=%async_computation.4 | async-start | bytes 12582912 | tf_op jit(solution)/shard_map/all_to_all | solution.py:295
  1416.7 205.8 %all-gather.17.cloned.1.call-start = ((), (), s32[]{:S(2)}) async-start(), calls=%async_computation.20 | async-start | bytes 3276800 | tf_op jit(solution)/shard_map/all_gather | solution.py:336
  1574.9 7.8 copy-start.33
  1582.7 8.9 copy-start.51
  1582.7 8.9 copy-start.63
  1582.7 9.0 copy-start.47
  1582.7 9.0 copy-start.39
  1582.7 9.0 copy-start.54
  1582.7 9.0 copy-start.59
  1598.7 100.8 %reduce-scatter.22.cloned.1.call-start = ((), (), s32[]{:S(2)}) async-start(), calls=%async_computation.25 | async-start | bytes 3244032 | tf_op jit(solution)/shard_map/reduce_scatter | solution.py:409
  1605.1 169.9 %reduce-scatter.24.cloned.1.call-start = ((), (), s32[]{:S(2)}) async-start(), calls=%async_computation.26 | async-start | bytes 3244032 | tf_op jit(solution)/shard_map/reduce_scatter | solution.py:412
  1611.2 239.6 %reduce-scatter.26.cloned.1.call-start = ((), (), s32[]{:S(2)}) async-start(), calls=%async_computation.27 | async-start | bytes 3244032 | tf_op jit(solution)/shard_map/reduce_scatter | solution.py:415
  1617.4 331.8 %reduce-scatter.18.cloned.1.call-start = ((), (), s32[]{:S(2)}) async-start(), calls=%async_computation.23 | async-start | bytes 1179648 | tf_op jit(solution)/shard_map/reduce_scatter | solution.py:403
  1626.8 7.2 slice-start
  1626.8 7.1 slice-start.1
  1643.8 345.3 %reduce-scatter.20.cloned.1.call-start = ((), (), s32[]{:S(2)}) async-start(), calls=%async_computation.24 | async-start | bytes 2359296 | tf_op jit(solution)/shard_map/reduce_scatter | solution.py:406
  1649.2 375.9 %reduce-scatter.14.cloned.1.call-start = ((), (), s32[]{:S(2)}) async-start(), calls=%async_computation.21 | async-start | bytes 3276800 | tf_op jit(solution)/shard_map/reduce_scatter | solution.py:388
  1667.8 436.5 %reduce-scatter.16.cloned.1.call-start = ((), (), s32[]{:S(2)}) async-start(), calls=%async_computation.22 | async-start | bytes 3538944 | tf_op jit(solution)/shard_map/reduce_scatter | solution.py:400
  1674.2 583.7 %all-reduce.5.cloned.1.call-start = ((), (), s32[]{:S(2)}) async-start(), calls=%async_computation.28 | async-start | bytes 10485760 | tf_op jit(solution)/shard_map/psum | solution.py:419
  1852.7 30.1 %copy-start.16 = (bf16[32,8,20,352]{3,0,2,1:T(8,128)(2,1)S(1)}, bf16[32,8,20,352]{3,0,2,1:T(8,128)(2,1)}, u32[]{:S(2)}) copy-start(bf16[32,8,20,352]{3,0,2,1:T(8,128)(2,1)} %get-tuple-element.35) | copy-start | bytes 10813444
  1882.8 28.0 %copy-start.1 = (bf16[160,2048]{1,0:T(8,128)(2,1)S(1)}, bf16[160,2048]{1,0:T(8,128)(2,1)}, u32[]{:S(2)}) copy-start(bf16[160,2048]{1,0:T(8,128)(2,1)} %multiply_convert_fusion.5) | copy-start | bytes 1966084
  1882.8 29.2 %copy-start.26 = (f32[640,512]{0,1:T(8,128)S(1)}, f32[640,512]{0,1:T(8,128)}, u32[]{:S(2)}) copy-start(f32[640,512]{0,1:T(8,128)} %copy-done.25) | copy-start | bytes 3932164
  1882.8 29.2 %copy-start.76 = (bf16[640,2048]{1,0:T(8,128)(2,1)S(1)}, bf16[640,2048]{1,0:T(8,128)(2,1)}, u32[]{:S(2)}) copy-start(bf16[640,2048]{1,0:T(8,128)(2,1)} %all-gather.7.cloned.1.call-done) | copy-start | bytes 7864324
  1919.4 105.7 %copy-start.52 = (f32[2048]{0:T(1024)S(1)}, f32[2048]{0:T(1024)}, u32[]{:S(2)}) copy-start(f32[2048]{0:T(1024)} %param.22) | copy-start | bytes 24580
  1919.5 105.7 %copy-start.68 = (f32[160]{0:T(256)S(1)}, f32[160]{0:T(256)}, u32[]{:S(2)}) copy-start(f32[160]{0:T(256)} %copy-done.67) | copy-start | bytes 1924
  1919.5 148.9 %copy-start.70 = (f32[160]{0:T(256)S(1)}, f32[160]{0:T(256)}, u32[]{:S(2)}) copy-start(f32[160]{0:T(256)} %get-tuple-element.58) | copy-start | bytes 1924
  (57 other events, 142.2 us)
Sparse Core Ops, SparseCore 0:
  12.1 28.2 all-gather.6
  76.0 51.3 reduce-scatter.9
  171.3 25.9 all-gather.12
  199.3 25.5 all-gather.8
  315.7 129.7 all-gather.14
  491.9 129.7 all-gather.10
  925.0 324.0 reduce-scatter.11
  1598.8 23.6 all-gather.16
  1626.6 72.7 reduce-scatter.21
  1702.9 72.0 reduce-scatter.23
  1778.6 72.1 reduce-scatter.25
  1854.1 63.5 reduce-scatter.17
  1921.2 67.8 reduce-scatter.19
  1991.5 33.5 reduce-scatter.13
  2028.6 75.6 reduce-scatter.15
  2110.9 147.0 all-reduce.4
where the time goes:
time: 2280 us; the launch traced here: 2270 us
  waiting for transfers between devices  1200 us (53%)
  matrix products  404 us (18%)
  local copies, waits for them, and re-layouts  304 us (13%)
  blocking collectives  183 us (8%)
  other arithmetic  148 us (6%)
    reduce_scatter x1, waiting for transfers between devices, per_device(): lax.psum_scatter(jnp.concatenate([forward_part, backward_part], axis=2).r...  324 us
    psum x1, waiting for transfers between devices, per_device(): lax.psum((latent_weight_gradient, latent_gain_gradient, router_gradient,...  152 us
    all_to_all x1, blocking collectives, per_device(): lax.all_to_all(send_rows, 'expert', split_axis=0, concat_axis=0, tiled=True)  142 us
    all_to_all x1, waiting for transfers between devices, per_device(): lax.all_to_all(send_grads, 'expert', split_axis=0, concat_axis=0, tiled=T...  137 us
    all_to_all x1, waiting for transfers between devices, per_device(): lax.all_to_all(routed_back.astype(jnp.bfloat16).reshape(expert_count, CAP...  129 us
    all_to_all x1, waiting for transfers between devices, per_device(): lax.all_to_all(routed_out.astype(jnp.bfloat16).reshape(expert_count, CAP,...  86.4 us
    reduce_scatter x1, waiting for transfers between devices, per_device(): lax.psum_scatter(shared_grads[2].astype(jnp.bfloat16), 'expert', scatter_...  73.9 us
    reduce_scatter x1, waiting for transfers between devices, per_device(): lax.psum_scatter(shared_grads[1].astype(jnp.bfloat16), 'expert', scatter_...  73.7 us
  transfers between devices with their start and end apart: 19, of which 14 were waited for; matrix products, arithmetic and copies ran while one was open for 18% of the time, Pallas kernels for 0%

commit v1 on v0

v1 whole, which is shorter than its diff:
```python
import functools

import jax
import jax.numpy as jnp
from jax import lax
from jax.experimental import pallas as pl
from jax.experimental.pallas import tpu as pltpu
from jax.sharding import PartitionSpec as P

NOPE = 128
ROPE = 64
VDIM = 128
LATENT = 512
TOPK = 6
CAP = 20


eps = 1e-06
route_scale = 2.446
rope_base = 50000.0
highest = lax.Precision.HIGHEST


def matmul(left, right):
    return jnp.dot(left, right, preferred_element_type=jnp.float32)


def trans_times(left, right):
    return lax.dot_general(
        left, right, (((0,), (0,)), ((), ())), preferred_element_type=jnp.float32
    )


def times_trans(left, right):
    return lax.dot_general(
        left, right, (((1,), (1,)), ((), ())), preferred_element_type=jnp.float32
    )


def inv_rms(value):
    return lax.rsqrt(jnp.mean(value * value, axis=-1, keepdims=True) + eps)


def norm_back(grad_out, value, scale, gain):
    scaled = grad_out * gain
    grad_in = scale * scaled - value * scale**3 * jnp.mean(scaled * value, axis=-1, keepdims=True)
    gain_grad = jnp.sum(grad_out * value * scale, axis=0)
    return (grad_in, gain_grad)


def rope_tables(seg):
    size = seg.shape[0]
    index = jnp.arange(size, dtype=jnp.int32)
    fresh = jnp.concatenate([jnp.ones((1,), dtype=bool), seg[1:] != seg[:-1]])
    first = lax.cummax(jnp.where(fresh, index, jnp.zeros_like(index)), axis=0)
    place = (index - first).astype(jnp.float32)
    half = ROPE // 2
    freqs = rope_base ** (-(jnp.arange(half, dtype=jnp.float32) * 2.0 / ROPE))
    angle = place[:, None] * freqs[None, :]
    return (jnp.cos(angle), jnp.sin(angle))


def attention_mask(seg):
    index = jnp.arange(seg.shape[0], dtype=jnp.int32)
    return (seg[:, None] == seg[None, :]) & (index[None, :] <= index[:, None])


def rotate(value, cosine, sine):
    half = value.shape[-1] // 2
    first, second = (value[..., :half], value[..., half:])
    return jnp.concatenate(
        [first * cosine - second * sine, second * cosine + first * sine], axis=-1
    )


def unrotate(value, cosine, sine):
    half = value.shape[-1] // 2
    first, second = (value[..., :half], value[..., half:])
    return jnp.concatenate(
        [first * cosine + second * sine, second * cosine - first * sine], axis=-1
    )


lanes = 128
vmem_limit = 64 * 1024 * 1024 - 131072


def token_slots(marks, here, local_experts, half):
    codes = times_trans(here, marks)
    count = codes.shape[1]
    rank = jnp.floor(codes * (1.0 / 32.0))
    place = codes - 32.0 * rank
    token = lax.broadcasted_iota(jnp.int32, codes.shape, 1)
    slot = jnp.where(codes >= 0, place + jnp.where(token >= half, float(CAP), 0.0), -1.0)
    row = lax.broadcasted_iota(jnp.int32, (2 * CAP, count), 0).astype(jnp.float32)
    picks = [jnp.where(row == slot[e : e + 1], 1.0, 0.0) for e in range(local_experts)]
    return picks, rank


def gather_rows(picks, values, out_ref):
    rows = jnp.dot(
        jnp.concatenate(picks, axis=0).astype(jnp.bfloat16),
        values,
        preferred_element_type=jnp.float32,
    )
    for e in range(len(picks)):
        out_ref[e] = rows[e * 2 * CAP : (e + 1) * 2 * CAP].astype(jnp.bfloat16)


def grads_kernel(here_ref, value_ref, down_ref, rows_ref, back_ref):
    width = rows_ref.shape[2]
    local_experts, half = rows_ref.shape[0], value_ref.shape[0] // 2
    picks, _ = token_slots(value_ref[:, width:], here_ref[...], local_experts, half)
    values = value_ref[:, :width]
    gather_rows(picks, values, rows_ref)
    back_ref[...] = times_trans(values, down_ref[...])


def rows_kernel(
    here_ref,
    twice_ref,
    marks_ref,
    value_ref,
    back_ref,
    gate_ref,
    up_ref,
    rows_ref,
    mix_ref,
    hidden_ref,
    gate_grad_ref,
    lift_grad_ref,
):
    width = rows_ref.shape[2]
    local_experts, half = rows_ref.shape[0], value_ref.shape[0] // 2
    picks, _ = token_slots(marks_ref[...], here_ref[...], local_experts, half)
    values = value_ref[:, :width]
    gather_rows(picks, values, rows_ref)
    mixing = times_trans(twice_ref[...], value_ref[:, width:])
    for e in range(local_experts):
        column = jnp.sum(picks[e] * mixing[e : e + 1], axis=1, keepdims=True)
        mix_ref[e] = jnp.broadcast_to(column, mix_ref.shape[1:])
    gate = times_trans(values, gate_ref[...])
    lift = times_trans(values, up_ref[...])
    back = back_ref[...]
    sigma = jax.nn.sigmoid(gate)
    active = gate * sigma
    hidden_ref[...] = (active * lift).astype(jnp.bfloat16)
    gate_grad_ref[...] = (back * lift * sigma * (1.0 + gate * (1.0 - sigma))).astype(jnp.bfloat16)
    lift_grad_ref[...] = (back * active).astype(jnp.bfloat16)


def experts_kernel(
    rows_ref,
    grads_ref,
    mix_ref,
    gate_ref,
    up_ref,
    down_ref,
    hidden_ref,
    gate_grad_ref,
    lift_grad_ref,
    returned_ref,
    mix_grad_ref,
):
    rows, gate_matrix, up_matrix = rows_ref[0], gate_ref[0], up_ref[0]
    gate = times_trans(rows, gate_matrix)
    lift = times_trans(rows, up_matrix)
    back = times_trans(grads_ref[0], down_ref[0])
    mix = mix_ref[0][:, :1]
    sigma = jax.nn.sigmoid(gate)
    active = gate * sigma
    hidden = active * lift
    mix_grad = jnp.sum(hidden * back, axis=1, keepdims=True)
    mix_grad_ref[0] = jnp.broadcast_to(mix_grad, mix_grad_ref.shape[1:])
    hidden_ref[0] = (mix * hidden).astype(jnp.bfloat16)
    back = back * mix
    gate_grad = (back * lift * sigma * (1.0 + gate * (1.0 - sigma))).astype(jnp.bfloat16)
    lift_grad = (back * active).astype(jnp.bfloat16)
    gate_grad_ref[0] = gate_grad
    lift_grad_ref[0] = lift_grad
    returned = matmul(gate_grad, gate_matrix) + matmul(lift_grad, up_matrix)
    returned_ref[0] = returned.astype(jnp.bfloat16)


def produce_kernel(hidden_ref, down_ref, out_ref):
    out_ref[0] = matmul(hidden_ref[0], down_ref[0]).astype(jnp.bfloat16)


def spread_rows(picks, rows_ref):
    rows = jnp.concatenate([rows_ref[e].astype(jnp.float32) for e in range(len(picks))], axis=0)
    pick = jnp.concatenate(picks, axis=0).astype(jnp.bfloat16)
    return trans_times(pick, rows.astype(jnp.bfloat16))


def back_kernel(
    here_ref,
    high_ref,
    low_ref,
    marks_ref,
    rows_ref,
    mix_grad_ref,
    gate_grad_ref,
    lift_grad_ref,
    gate_ref,
    up_ref,
    out_ref,
):
    width = rows_ref.shape[2]
    local_experts, half = rows_ref.shape[0], out_ref.shape[0] // 2
    picks, rank = token_slots(marks_ref[...], here_ref[...], local_experts, half)
    total = spread_rows(picks, rows_ref)
    total = total + matmul(gate_grad_ref[...], gate_ref[...])
    total = total + matmul(lift_grad_ref[...], up_ref[...])
    out_ref[:, :width] = total.astype(jnp.bfloat16)
    choice = lax.broadcasted_iota(jnp.int32, rank.shape, 0).astype(jnp.float32)
    mix_grad = jnp.zeros(rank.shape, jnp.float32)
    for e in range(local_experts):
        row = jnp.sum(picks[e] * mix_grad_ref[e][:, :1], axis=0, keepdims=True)
        mix_grad = mix_grad + jnp.where(choice == rank[e : e + 1], row, 0.0)
    high = mix_grad.astype(jnp.bfloat16)
    low = (mix_grad - high.astype(jnp.float32)).astype(jnp.bfloat16)
    sent = trans_times(high, high_ref[...]) + trans_times(low, low_ref[...])
    out_ref[:, width:] = sent.astype(jnp.bfloat16)


def out_kernel(here_ref, marks_ref, rows_ref, hidden_ref, down_ref, out_ref):
    local_experts, half = rows_ref.shape[0], out_ref.shape[0] // 2
    picks, _ = token_slots(marks_ref[...], here_ref[...], local_experts, half)
    total = spread_rows(picks, rows_ref)
    total = total + matmul(hidden_ref[...], down_ref[...])
    out_ref[...] = total.astype(jnp.bfloat16)


def whole_spec(array):
    zeros = (0,) * array.ndim
    return pl.BlockSpec(array.shape, lambda i: zeros)


def pair_spec(array, pairs):
    block = (array.shape[0] // pairs,) + array.shape[1:]
    zeros = (0,) * (array.ndim - 1)
    return pl.BlockSpec(block, lambda i: (i,) + zeros)


def slots_spec(array, pairs):
    block = (array.shape[0], array.shape[1] // pairs) + array.shape[2:]
    return pl.BlockSpec(block, lambda i: (0, i, 0))


def cost(flops, *arrays):
    moved = sum(a.size * a.dtype.itemsize for a in arrays)
    return pl.CostEstimate(flops=int(flops), bytes_accessed=int(moved), transcendentals=0)


def call(kernel, grid, ins, outs, flops):
    arrays = [a for a, _ in ins]
    shapes = [s for s, _ in outs]
    return pl.pallas_call(
        kernel,
        grid=(grid,),
        in_specs=[s for _, s in ins],
        out_specs=[s for _, s in outs],
        out_shape=shapes,
        cost_estimate=cost(flops, *arrays, *shapes),
        compiler_params=pltpu.CompilerParams(vmem_limit_bytes=vmem_limit),
    )(*arrays)


MESH = pl.DeviceIdType.MESH


def places():
    expert, weight = lax.axis_index("expert"), lax.axis_index("weight")
    return lax.div(expert, 2), lax.rem(expert, 2), lax.div(weight, 2), lax.rem(weight, 2)


def device(z, x, y, c):
    return (z * 2 + x, y * 2 + c)


def shard(z, x, y, c):
    return z * 8 + x * 4 + y * 2 + c


def push(source, target, send, receive, to):
    return pltpu.make_async_remote_copy(
        src_ref=source,
        dst_ref=target,
        send_sem=send,
        recv_sem=receive,
        device_id=to,
        device_id_type=MESH,
    )


class Sends:
    def __init__(self, semaphores):
        self.semaphores = semaphores
        self.started = []

    def start(self, source, target, receive, to, when=None):
        copy = push(source, target, self.semaphores.at[len(self.started)], receive, to)
        self.started.append((copy, when))
        if when is None:
            copy.start()
        else:
            pl.when(when)(copy.start)

    def finish(self):
        for copy, when in self.started:
            if when is None:
                copy.wait_send()
            else:
                pl.when(when)(copy.wait_send)


def landed(target, receive, to):
    push(target, target, receive, receive, to).wait_recv()


def greet(devices):
    barrier = pltpu.get_barrier_semaphore()
    count = 0
    for to, when in devices:
        signal = functools.partial(
            pl.semaphore_signal, barrier, inc=1, device_id=to, device_id_type=MESH
        )
        if when is None:
            signal()
            count = count + 1
        else:
            pl.when(when)(signal)
            count = count + when.astype(jnp.int32)
    pl.semaphore_wait(barrier, count)


def add_rows(target, sources, start, rows):
    step = 16

    def body(i, carry):
        part = pl.ds(pl.multiple_of(start + i * step, step), step)
        total = target[part].astype(jnp.float32)
        for source, offset in sources:
            there = pl.ds(pl.multiple_of(start - offset + i * step, step), step)
            total = total + source[there].astype(jnp.float32)
        target[part] = total.astype(target.dtype)
        return carry

    lax.fori_loop(0, rows // step, body, 0)


def ordered(z, first, second):
    upper = lax.div(z, 2)
    inner = z + upper * (3 - 2 * z)
    value = first + inner * (second - first)
    return value + upper * (3 - 2 * value)


def gather_all_kernel(x_ref, out_ref, send_sems, recv_sems, local_sem):
    z, x, y, c = places()
    half = x_ref.shape[0] // 2
    over, side, mate = device(z, 1 - x, y, c), device(z, x, 1 - y, c), device(z, x, y, 1 - c)
    up, down = device(z + 1, x, y, c), device(z - 1, x, y, c)
    greet([(over, None), (side, None), (mate, None), (up, z < 3), (down, z > 0)])
    sends = Sends(send_sems)
    own = shard(z, x, y, c)
    keep = pltpu.make_async_copy(x_ref, out_ref.at[own], local_sem)
    keep.start()

    def halves(i, h):
        return out_ref.at[i, pl.ds(h * half, half)]

    def whole(step):
        zz = ordered(z, (0, 1, 2, 3)[step], (1, 0, 2, 3)[step])
        i = shard(zz, x, y, c)
        source, receive = out_ref.at[i], recv_sems.at[i, 0]
        if step == 0:
            source = x_ref
        else:
            landed(out_ref.at[i], receive, mate)
        sends.start(source, out_ref.at[i], receive, up, (zz <= z) & (z < 3))
        sends.start(source, out_ref.at[i], receive, down, (zz >= z) & (z > 0))
        sends.start(source, out_ref.at[i], receive, over)
        sends.start(source, out_ref.at[i], receive, side)
        sends.start(source, out_ref.at[i], receive, mate)

    def relay(step):
        zz = ordered(z, (0, 1, 2, 3)[step], (1, 0, 2, 3)[step])
        i = shard(zz, 1 - x, y, c)
        landed(out_ref.at[i], recv_sems.at[i, 0], mate)
        sends.start(halves(i, 0), halves(i, 0), recv_sems.at[i, 0], side)
        sends.start(out_ref.at[i], out_ref.at[i], recv_sems.at[i, 0], mate)
        i = shard(zz, x, 1 - y, c)
        landed(out_ref.at[i], recv_sems.at[i, 0], mate)
        sends.start(halves(i, 1), halves(i, 1), recv_sems.at[i, 1], over)
        sends.start(out_ref.at[i], out_ref.at[i], recv_sems.at[i, 0], mate)

    def corner(step):
        zz = ordered(z, (0, 1, 2, 3)[step], (1, 0, 2, 3)[step])
        i = shard(zz, 1 - x, 1 - y, c)
        for h in range(2):
            landed(halves(i, h), recv_sems.at[i, h], mate)
            sends.start(halves(i, h), halves(i, h), recv_sems.at[i, h], mate)

    whole(0)
    whole(1)
    relay(0)
    whole(2)
    relay(1)
    corner(0)
    whole(3)
    relay(2)
    corner(1)
    relay(3)
    corner(2)
    corner(3)
    for step in range(4):
        zz = ordered(z, (0, 1, 2, 3)[step], (1, 0, 2, 3)[step])
        for i in (shard(zz, x, y, 1 - c), shard(zz, 1 - x, y, 1 - c), shard(zz, x, 1 - y, 1 - c)):
            landed(out_ref.at[i], recv_sems.at[i, 0], mate)
        i = shard(zz, 1 - x, 1 - y, 1 - c)
        for h in range(2):
            landed(halves(i, h), recv_sems.at[i, h], mate)
    sends.finish()
    keep.wait()


def gather_all(value, number):
    if lax.axis_size("expert") != 8 or lax.axis_size("weight") != 4:
        return lax.all_gather(value, ("expert", "weight"), axis=0)
    out = jax.ShapeDtypeStruct((32,) + value.shape, value.dtype)
    return pl.pallas_call(
        gather_all_kernel,
        out_shape=out,
        in_specs=[pl.BlockSpec(memory_space=pltpu.VMEM)],
        out_specs=pl.BlockSpec(memory_space=pl.ANY),
        scratch_shapes=[
            pltpu.SemaphoreType.DMA((44,)),
            pltpu.SemaphoreType.DMA((32, 2)),
            pltpu.SemaphoreType.DMA,
        ],
        compiler_params=pltpu.CompilerParams(collective_id=number, has_side_effects=True),
        cost_estimate=cost(0, value, out),
    )(value)


def sum_all_kernel(
    p_ref,
    out_ref,
    own,
    mates,
    over_half,
    side_half,
    over_full,
    side_full,
    below,
    above,
    send_sems,
    mate_sems,
    half_sems,
    full_sems,
    line_sems,
    local_sems,
):
    z, x, y, c = places()
    rows = out_ref.shape[0]
    half = rows // 2
    over, side, mate = device(z, 1 - x, y, c), device(z, x, 1 - y, c), device(z, x, y, 1 - c)
    up, down = device(z + 1, x, y, c), device(z - 1, x, y, c)
    greet([(over, None), (side, None), (mate, None), (up, z < 3), (down, z > 0)])
    sends = Sends(send_sems)
    targets = [ordered(z, (3, 2, 1, 0)[step], (3, 0, 2, 1)[step]) for step in range(4)]
    spots = [(1 - x, 1 - y), (1 - x, y), (x, 1 - y), (x, y)]
    loads = []
    for step in range(4):
        zz = targets[step]
        for j, (xx, yy) in enumerate(spots):
            slot = step * 4 + j
            sends.start(
                p_ref.at[shard(zz, xx, yy, 1 - c)], mates.at[slot], mate_sems.at[slot], mate
            )
            load = pltpu.make_async_copy(
                p_ref.at[shard(zz, xx, yy, c)], own.at[slot], local_sems.at[slot]
            )
            load.start()
            loads.append(load)

    def join(slot):
        loads[slot].wait()
        landed(mates.at[slot], mate_sems.at[slot], mate)

    def corner(step):
        slot = step * 4
        join(slot)
        add_rows(own.at[slot], [(mates.at[slot], 0)], 0, rows)
        sends.start(
            own.at[slot, pl.ds(half, half)], over_half.at[step], half_sems.at[step, 0], over
        )
        sends.start(own.at[slot, pl.ds(0, half)], side_half.at[step], half_sems.at[step, 1], side)

    def relay(step):
        slot = step * 4 + 1
        join(slot)
        add_rows(own.at[slot], [(mates.at[slot], 0)], half, half)
        landed(side_half.at[step], half_sems.at[step, 1], mate)
        add_rows(own.at[slot], [(mates.at[slot], 0), (side_half.at[step], 0)], 0, half)
        sends.start(own.at[slot], over_full.at[step], full_sems.at[step, 0], over)
        slot = step * 4 + 2
        join(slot)
        add_rows(own.at[slot], [(mates.at[slot], 0)], 0, half)
        landed(over_half.at[step], half_sems.at[step, 0], mate)
        add_rows(own.at[slot], [(mates.at[slot], 0), (over_half.at[step], half)], half, half)
        sends.start(own.at[slot], side_full.at[step], full_sems.at[step, 1], side)

    def whole(step):
        zz = targets[step]
        slot = step * 4 + 3
        join(slot)
        landed(over_full.at[step], full_sems.at[step, 0], mate)
        landed(side_full.at[step], full_sems.at[step, 1], mate)
        add_rows(
            own.at[slot],
            [(mates.at[slot], 0), (over_full.at[step], 0), (side_full.at[step], 0)],
            0,
            rows,
        )

        @pl.when((zz >= z) & (z > 0))
        def _():
            landed(below.at[zz], line_sems.at[zz, 0], mate)
            add_rows(own.at[slot], [(below.at[zz], 0)], 0, rows)

        @pl.when((zz <= z) & (z < 3))
        def _():
            landed(above.at[zz], line_sems.at[zz, 1], mate)
            add_rows(own.at[slot], [(above.at[zz], 0)], 0, rows)

        if step < 3:
            sends.start(own.at[slot], below.at[zz], line_sems.at[zz, 0], up, zz > z)
            sends.start(own.at[slot], above.at[zz], line_sems.at[zz, 1], down, zz < z)

    corner(0)
    corner(1)
    relay(0)
    corner(2)
    relay(1)
    whole(0)
    corner(3)
    relay(2)
    whole(1)
    relay(3)
    whole(2)
    whole(3)
    out_ref[...] = own[15].astype(out_ref.dtype)
    sends.finish()


def sum_all(value, number):
    if lax.axis_size("expert") != 8 or lax.axis_size("weight") != 4:
        summed = lax.psum_scatter(
            value.reshape(-1, value.shape[2]), ("expert", "weight"), scatter_dimension=0, tiled=True
        )
        return summed.astype(jnp.float32)
    _, rows, width = value.shape
    out = jax.ShapeDtypeStruct((rows, width), jnp.float32)
    buffer = lambda n, r: pltpu.VMEM((n, r, width), value.dtype)
    return pl.pallas_call(
        sum_all_kernel,
        out_shape=out,
        in_specs=[pl.BlockSpec(memory_space=pl.ANY)],
        out_specs=pl.BlockSpec(memory_space=pltpu.VMEM),
        scratch_shapes=[
            buffer(16, rows),
            buffer(16, rows),
            buffer(4, rows // 2),
            buffer(4, rows // 2),
            buffer(4, rows),
            buffer(4, rows),
            buffer(4, rows),
            buffer(4, rows),
            pltpu.SemaphoreType.DMA((40,)),
            pltpu.SemaphoreType.DMA((16,)),
            pltpu.SemaphoreType.DMA((4, 2)),
            pltpu.SemaphoreType.DMA((4, 2)),
            pltpu.SemaphoreType.DMA((4, 2)),
            pltpu.SemaphoreType.DMA((16,)),
        ],
        compiler_params=pltpu.CompilerParams(
            collective_id=number, has_side_effects=True, vmem_limit_bytes=vmem_limit
        ),
        cost_estimate=cost(0, value, out),
    )(value)


def gather_group_kernel(x_ref, out_ref, send_sems, recv_sems, local_sem):
    z, x, y, c = places()
    half = x_ref.shape[0] // 2
    side, mate = device(z, x, 1 - y, c), device(z, x, y, 1 - c)
    greet([(side, None), (mate, None)])
    sends = Sends(send_sems)
    own, across = y * 2 + c, (1 - y) * 2 + c
    keep = pltpu.make_async_copy(x_ref, out_ref.at[own], local_sem)
    keep.start()

    def part(i, h):
        return out_ref.at[i, pl.ds(h * half, half)]

    for h in range(2):
        piece = x_ref.at[pl.ds(h * half, half)]
        sends.start(piece, part(own, h), recv_sems.at[own, h], side)
    for h in range(2):
        piece = x_ref.at[pl.ds(h * half, half)]
        sends.start(piece, part(own, h), recv_sems.at[own, h], mate)
    for h in range(2):
        landed(part(across, h), recv_sems.at[across, h], mate)
        sends.start(part(across, h), part(across, h), recv_sems.at[across, h], mate)
    for i in (y * 2 + 1 - c, (1 - y) * 2 + 1 - c):
        for h in range(2):
            landed(part(i, h), recv_sems.at[i, h], mate)
    sends.finish()
    keep.wait()


def gather_group(value, number):
    if lax.axis_size("expert") != 8 or lax.axis_size("weight") != 4:
        return lax.all_gather(value, "weight", axis=0, tiled=True)
    out = jax.ShapeDtypeStruct((4,) + value.shape, value.dtype)
    return pl.pallas_call(
        gather_group_kernel,
        out_shape=out,
        in_specs=[pl.BlockSpec(memory_space=pltpu.VMEM)],
        out_specs=pl.BlockSpec(memory_space=pltpu.VMEM),
        scratch_shapes=[
            pltpu.SemaphoreType.DMA((6,)),
            pltpu.SemaphoreType.DMA((4, 2)),
            pltpu.SemaphoreType.DMA,
        ],
        compiler_params=pltpu.CompilerParams(collective_id=number, has_side_effects=True),
        cost_estimate=cost(0, value, out),
    )(value).reshape(-1, value.shape[1])


def sum_group_kernel(p_ref, out_ref, mates, sides, carried, send_sems, mate_sems, side_sems):
    z, x, y, c = places()
    rows = out_ref.shape[0]
    half = rows // 2
    side, mate = device(z, x, 1 - y, c), device(z, x, y, 1 - c)
    greet([(side, None), (mate, None)])
    sends = Sends(send_sems)

    for j, yy in enumerate((1 - y, y)):
        for h in range(2):
            part = pl.ds(h * half, half)
            sends.start(
                p_ref.at[yy * 2 + 1 - c, part], mates.at[j, part], mate_sems.at[j, h], mate
            )

    def add(target, sources, h):
        step = 16

        def body(i, carry):
            part = pl.ds(pl.multiple_of(h * half + i * step, step), step)
            total = sources[0][part].astype(jnp.float32)
            for source in sources[1:]:
                total = total + source[part].astype(jnp.float32)
            target[part] = total.astype(target.dtype)
            return carry

        lax.fori_loop(0, half // step, body, 0)

    for h in range(2):
        part = pl.ds(h * half, half)
        landed(mates.at[0, part], mate_sems.at[0, h], mate)
        add(carried, [p_ref.at[(1 - y) * 2 + c], mates.at[0]], h)
        sends.start(carried.at[part], sides.at[part], side_sems.at[h], side)
    for h in range(2):
        part = pl.ds(h * half, half)
        landed(mates.at[1, part], mate_sems.at[1, h], mate)
        landed(sides.at[part], side_sems.at[h], mate)
        add(out_ref, [p_ref.at[y * 2 + c], mates.at[1], sides], h)
    sends.finish()


def sum_group(value, number):
    if lax.axis_size("expert") != 8 or lax.axis_size("weight") != 4:
        summed = lax.psum_scatter(value, "weight", scatter_dimension=0, tiled=True)
        return summed.astype(jnp.float32)
    rows, width = value.shape[0] // 4, value.shape[1]
    value = value.reshape(4, rows, width)
    out = jax.ShapeDtypeStruct((rows, width), jnp.float32)
    return pl.pallas_call(
        sum_group_kernel,
        out_shape=out,
        in_specs=[pl.BlockSpec(memory_space=pltpu.VMEM)],
        out_specs=pl.BlockSpec(memory_space=pltpu.VMEM),
        scratch_shapes=[
            pltpu.VMEM((2, rows, width), value.dtype),
            pltpu.VMEM((rows, width), value.dtype),
            pltpu.VMEM((rows, width), value.dtype),
            pltpu.SemaphoreType.DMA((6,)),
            pltpu.SemaphoreType.DMA((2, 2)),
            pltpu.SemaphoreType.DMA((2,)),
        ],
        compiler_params=pltpu.CompilerParams(collective_id=number, has_side_effects=True),
        cost_estimate=cost(0, value, out),
    )(value)


def per_device(
    tokens,
    cotangent,
    segments,
    routes,
    first_gain,
    query_weight,
    latent_weight,
    latent_gain,
    expand_weight,
    output_weight,
    second_gain,
    router_weight,
    shared_gate,
    shared_up,
    shared_down,
    expert_gate,
    expert_up,
    expert_down,
):
    weight_count = lax.axis_size("weight")
    token_rows = tokens.shape[0]
    width = tokens.shape[1]
    group_rows = token_rows * weight_count
    query_width = NOPE + ROPE
    heads_here = query_weight.shape[1] // query_width
    expert_count = router_weight.shape[1]
    local_experts = expert_gate.shape[0]
    score_scale = query_width ** (-0.5)
    activations = tokens.astype(jnp.float32)
    first_scale = inv_rms(activations)
    normed = (activations * first_scale * first_gain).astype(jnp.bfloat16)
    normed_all = gather_group(normed, 0)
    both = ("expert", "weight")
    expert_index = lax.axis_index("expert")
    expert_lanes = lax.axis_size("expert")
    blocks = expert_lanes * weight_count
    pairs = blocks // 2
    pair_rows = 2 * token_rows
    all_rows = blocks * token_rows
    slot_rows = blocks * CAP
    choose = (
        routes[:, :, None] == jnp.arange(expert_count, dtype=jnp.int32)[None, None, :]
    ).astype(jnp.float32)
    hit = jnp.sum(choose, axis=1)
    order = jnp.arange(token_rows, dtype=jnp.int32)
    before = (order[None, :] < order[:, None]).astype(jnp.bfloat16)
    place = matmul(before, hit.astype(jnp.bfloat16))
    rank = jnp.sum(choose * jnp.arange(routes.shape[1], dtype=jnp.float32)[None, :, None], axis=1)
    code = jnp.where(hit > 0, 32.0 * rank + place, -1.0)
    extra = jnp.pad(code, ((0, 0), (0, lanes - expert_count)), constant_values=-1.0)
    cotangent_wide = jnp.concatenate([cotangent, extra.astype(jnp.bfloat16)], axis=1)
    column = jnp.arange(lanes, dtype=jnp.int32)[None, :]
    row = jnp.arange(8, dtype=jnp.int32)[:, None]
    first_here = expert_index * local_experts
    here = (row < local_experts) & (column == first_here + row)
    twice = here | ((row < local_experts) & (column == first_here + row + expert_count))
    here, twice = here.astype(jnp.bfloat16), twice.astype(jnp.bfloat16)
    weight_index = lax.axis_index("weight")
    high_column = 2 * (row * weight_count + weight_index)
    known = row < routes.shape[1]
    high_at = (known & (column == high_column)).astype(jnp.bfloat16)
    low_at = (known & (column == high_column + 1)).astype(jnp.bfloat16)
    shared_here = shared_gate.shape[1] // expert_lanes
    shared_wide = -(-shared_here // lanes) * lanes
    start = expert_index * shared_here

    def shared_part(matrix):
        part = lax.dynamic_slice_in_dim(matrix, start, shared_here, axis=0)
        return jnp.pad(part, ((0, shared_wide - shared_here), (0, 0)))

    gate_part = shared_part(shared_gate.T)
    up_part = shared_part(shared_up.T)
    down_part = shared_part(shared_down)
    shape = jax.ShapeDtypeStruct
    whole = lambda array: (array, whole_spec(array))
    slots = shape((local_experts, slot_rows, width), jnp.bfloat16)
    slots_one = shape((local_experts, slot_rows, lanes), jnp.float32)
    gather_flops = 2 * all_rows * width * (2 * CAP * local_experts + shared_wide)
    cotangent_all = lax.all_gather(cotangent_wide, both, axis=0, tiled=True)
    marks = (cotangent_all, pl.BlockSpec((pair_rows, lanes), lambda i: (i, width // lanes)))
    grads_slots, shared_raw = call(
        grads_kernel,
        pairs,
        [whole(here), (cotangent_all, pair_spec(cotangent_all, pairs)), whole(down_part)],
        [
            (slots, slots_spec(slots, pairs)),
            (shape((all_rows, shared_wide), jnp.float32), pl.BlockSpec((pair_rows, shared_wide), lambda i: (i, 0))),
        ],
        gather_flops,
    )
    cosine, sine = rope_tables(segments[0])
    allowed = attention_mask(segments[0])
    query_full = matmul(normed_all, query_weight).reshape(group_rows, heads_here, query_width)
    query = jnp.concatenate(
        [
            query_full[..., :NOPE],
            rotate(query_full[..., NOPE:], cosine[:, None, :], sine[:, None, :]),
        ],
        axis=-1,
    ).astype(jnp.bfloat16)
    compressed = matmul(normed_all, latent_weight)
    latent = compressed[:, :LATENT]
    latent_scale = inv_rms(latent)
    latent_normed = (latent * latent_scale * latent_gain).astype(jnp.bfloat16)
    key_rope = rotate(compressed[:, LATENT:], cosine, sine).astype(jnp.bfloat16)
    expanded = (
        matmul(latent_normed, expand_weight)
        .astype(jnp.bfloat16)
        .reshape(group_rows, heads_here, NOPE + VDIM)
    )
    key_nope = expanded[..., :NOPE]
    values = expanded[..., NOPE:]

    def score_block():
        raw = jnp.einsum(
            "ihd,jhd->hij", query[..., :NOPE], key_nope, preferred_element_type=jnp.float32
        )
        raw = raw + jnp.einsum(
            "ihd,jd->hij", query[..., NOPE:], key_rope, preferred_element_type=jnp.float32
        )
        return jnp.where(allowed[None], raw * score_scale, -1e30)

    scores = score_block()
    peak = jnp.max(scores, axis=-1, keepdims=True)
    weights = jnp.exp(scores - peak)
    total = jnp.sum(weights, axis=-1, keepdims=True)
    log_total = peak + jnp.log(total)
    mixed = jnp.einsum(
        "hij,jhd->ihd",
        (weights / total).astype(jnp.bfloat16),
        values,
        preferred_element_type=jnp.float32,
    )
    mixed = mixed.astype(jnp.bfloat16).reshape(group_rows, heads_here * VDIM)
    attended = sum_group(matmul(mixed, output_weight).astype(jnp.bfloat16), 1)
    hidden_one = activations + attended
    second_scale = inv_rms(hidden_one)
    normed_two = (hidden_one * second_scale * second_gain).astype(jnp.bfloat16)
    gates = jax.nn.sigmoid(matmul(normed_two, router_weight))
    chosen = jnp.sum(choose * gates[:, None, :], axis=-1)
    chosen_total = jnp.sum(chosen, axis=1, keepdims=True)
    mixing = route_scale * chosen / chosen_total
    upstream = cotangent.astype(jnp.float32)
    mixing_at = jnp.sum(choose * mixing[:, :, None], axis=1)
    mixing_high = mixing_at.astype(jnp.bfloat16)
    mixing_low = (mixing_at - mixing_high.astype(jnp.float32)).astype(jnp.bfloat16)
    normed_wide = jnp.concatenate([normed_two, mixing_high, mixing_low], axis=1)
    normed_tokens = gather_all(normed_wide, 2).reshape(all_rows, -1)
    token_spec = pl.BlockSpec((pair_rows, shared_wide), lambda i: (i, 0))
    token_shape = shape((all_rows, shared_wide), jnp.bfloat16)
    rows_slots, mix_slots, shared_hidden, shared_gate_grad, shared_lift_grad = call(
        rows_kernel,
        pairs,
        [
            whole(here),
            whole(twice),
            marks,
            (normed_tokens, pair_spec(normed_tokens, pairs)),
            (shared_raw, token_spec),
            whole(gate_part),
            whole(up_part),
        ],
        [
            (slots, slots_spec(slots, pairs)),
            (slots_one, slots_spec(slots_one, pairs)),
            (token_shape, token_spec),
            (token_shape, token_spec),
            (token_shape, token_spec),
        ],
        gather_flops + 2 * all_rows * width * shared_wide,
    )
    hidden_here = expert_gate.shape[2]
    gate_rows, up_rows = expert_gate.transpose(0, 2, 1), expert_up.transpose(0, 2, 1)
    tile = slot_rows // 2
    tile_spec = lambda n: pl.BlockSpec((1, tile, n), lambda i: (i // 2, i % 2, 0))
    expert_spec = lambda m: pl.BlockSpec((1,) + m.shape[1:], lambda i: (i // 2, 0, 0))
    narrow = shape((local_experts, slot_rows, hidden_here), jnp.bfloat16)
    one_matmul = 2 * local_experts * slot_rows * width * hidden_here
    routed_hidden, gate_grad, lift_grad, returned, mix_grad_slots = call(
        experts_kernel,
        2 * local_experts,
        [
            (rows_slots, tile_spec(width)),
            (grads_slots, tile_spec(width)),
            (mix_slots, tile_spec(lanes)),
            (gate_rows, expert_spec(gate_rows)),
            (up_rows, expert_spec(up_rows)),
            (expert_down, expert_spec(expert_down)),
        ],
        [
            (narrow, tile_spec(hidden_here)),
            (narrow, tile_spec(hidden_here)),
            (narrow, tile_spec(hidden_here)),
            (slots, tile_spec(width)),
            (slots_one, tile_spec(lanes)),
        ],
        5 * one_matmul,
    )
    dense = shape((all_rows, width), jnp.bfloat16)
    dense_spec = pl.BlockSpec((pair_rows, width), lambda i: (i, 0))
    dense_wide = shape((all_rows, width + lanes), jnp.bfloat16)
    (back_dense,) = call(
        back_kernel,
        pairs,
        [
            whole(here),
            whole(high_at),
            whole(low_at),
            marks,
            (returned, slots_spec(slots, pairs)),
            (mix_grad_slots, slots_spec(slots_one, pairs)),
            (shared_gate_grad, token_spec),
            (shared_lift_grad, token_spec),
            whole(gate_part),
            whole(up_part),
        ],
        [(dense_wide, pair_spec(dense_wide, pairs))],
        gather_flops + 2 * all_rows * width * shared_wide,
    )
    back_here = sum_all(back_dense.reshape(blocks, token_rows, -1), 3)
    routed_back = back_here[:, :width]
    mix_grad = back_here[:, width : width + 2 * weight_count * routes.shape[1]]
    mix_grad = jnp.sum(mix_grad.reshape(token_rows, routes.shape[1], -1), axis=2)
    (produced,) = call(
        produce_kernel,
        2 * local_experts,
        [(routed_hidden, tile_spec(hidden_here)), (expert_down, expert_spec(expert_down))],
        [(slots, tile_spec(width))],
        one_matmul,
    )
    (out_dense,) = call(
        out_kernel,
        pairs,
        [
            whole(here),
            marks,
            (produced, slots_spec(slots, pairs)),
            (shared_hidden, token_spec),
            whole(down_part),
        ],
        [(dense, dense_spec)],
        gather_flops,
    )
    routed_out = lax.psum_scatter(out_dense, both, scatter_dimension=0, tiled=True).astype(jnp.float32)
    expert_grads = (
        jnp.einsum("jsf,jsd->jfd", gate_grad, rows_slots, preferred_element_type=jnp.float32).transpose(0, 2, 1),
        jnp.einsum("jsf,jsd->jfd", lift_grad, rows_slots, preferred_element_type=jnp.float32).transpose(0, 2, 1),
        jnp.einsum("jsf,jsd->jfd", routed_hidden, grads_slots, preferred_element_type=jnp.float32),
    )
    normed_plain, cotangent_plain = normed_tokens[:, :width], cotangent_all[:, :width]
    shared_grads = jnp.concatenate(
        [
            trans_times(shared_gate_grad, normed_plain)[:shared_here],
            trans_times(shared_lift_grad, normed_plain)[:shared_here],
            trans_times(shared_hidden, cotangent_plain)[:shared_here],
        ],
        axis=0,
    ).astype(jnp.bfloat16)
    swapped = lax.all_to_all(shared_grads, "expert", split_axis=1, concat_axis=0, tiled=True)
    swapped = swapped.reshape(expert_lanes, 3, shared_here, -1).astype(jnp.float32)
    shared_gradients = [swapped[:, i].reshape(expert_lanes * shared_here, -1) for i in range(3)]
    layer_out = (hidden_one + routed_out).astype(jnp.bfloat16)
    chosen_grad = route_scale * (
        mix_grad / chosen_total
        - jnp.sum(mix_grad * chosen, axis=1, keepdims=True) / chosen_total**2
    )
    logit_grad = jnp.sum(choose * chosen_grad[:, :, None], axis=1) * gates * (1.0 - gates)
    normed_two_grad = (
        routed_back
        + jnp.dot(logit_grad, router_weight.astype(jnp.float32).T, precision=highest)
    )
    router_gradient = jnp.dot(normed_two.astype(jnp.float32).T, logit_grad, precision=highest)
    back_two, second_gain_gradient = norm_back(
        normed_two_grad, hidden_one, second_scale, second_gain
    )
    hidden_grad = upstream + back_two
    hidden_group = gather_group(hidden_grad.astype(jnp.bfloat16), 4)
    output_gradient = trans_times(mixed, hidden_group)
    mixed_grad = (
        times_trans(hidden_group, output_weight)
        .astype(jnp.bfloat16)
        .reshape(group_rows, heads_here, VDIM)
    )
    probs = jnp.exp(score_block() - log_total)
    prob_grad = jnp.einsum("ihd,jhd->hij", mixed_grad, values, preferred_element_type=jnp.float32)
    centre = jnp.sum(probs * prob_grad, axis=-1, keepdims=True)
    score_grad = (probs * (prob_grad - centre)).astype(jnp.bfloat16)
    value_grad = jnp.einsum(
        "hij,ihd->jhd", probs.astype(jnp.bfloat16), mixed_grad, preferred_element_type=jnp.float32
    )
    query_nope_grad = (
        jnp.einsum("hij,jhd->ihd", score_grad, key_nope, preferred_element_type=jnp.float32)
        * score_scale
    )
    query_rope_grad = (
        jnp.einsum("hij,jd->ihd", score_grad, key_rope, preferred_element_type=jnp.float32)
        * score_scale
    )
    key_nope_grad = (
        jnp.einsum(
            "hij,ihd->jhd", score_grad, query[..., :NOPE], preferred_element_type=jnp.float32
        )
        * score_scale
    )
    key_rope_grad = (
        jnp.einsum("hij,ihd->jd", score_grad, query[..., NOPE:], preferred_element_type=jnp.float32)
        * score_scale
    )
    query_grad = jnp.concatenate(
        [query_nope_grad, unrotate(query_rope_grad, cosine[:, None, :], sine[:, None, :])], axis=-1
    )
    query_grad = query_grad.astype(jnp.bfloat16).reshape(group_rows, heads_here * query_width)
    expand_grad = (
        jnp.concatenate([key_nope_grad, value_grad], axis=-1)
        .astype(jnp.bfloat16)
        .reshape(group_rows, heads_here * (NOPE + VDIM))
    )
    query_gradient = trans_times(normed_all, query_grad)
    expand_gradient = trans_times(latent_normed, expand_grad)
    latent_normed_grad = times_trans(expand_grad, expand_weight)
    latent_back, latent_gain_gradient = norm_back(
        latent_normed_grad, latent, latent_scale, latent_gain
    )
    compressed_grad = jnp.concatenate([latent_back, unrotate(key_rope_grad, cosine, sine)], axis=-1)
    compressed_grad = compressed_grad.astype(jnp.bfloat16)
    latent_weight_gradient = trans_times(normed_all, compressed_grad)
    normed_grad = sum_group(
        (
            times_trans(query_grad, query_weight) + times_trans(compressed_grad, latent_weight)
        ).astype(jnp.bfloat16),
        5,
    )
    back_one, first_gain_gradient = norm_back(normed_grad, activations, first_scale, first_gain)
    token_gradient = hidden_grad + back_one
    shards = (
        lax.psum_scatter(
            query_gradient.astype(jnp.bfloat16), "expert", scatter_dimension=0, tiled=True
        ).astype(jnp.float32),
        lax.psum_scatter(
            expand_gradient.astype(jnp.bfloat16), "expert", scatter_dimension=0, tiled=True
        ).astype(jnp.float32),
        lax.psum_scatter(
            output_gradient.astype(jnp.bfloat16), "expert", scatter_dimension=1, tiled=True
        ).astype(jnp.float32),
    )
    totals = lax.psum(
        (
            latent_weight_gradient,
            latent_gain_gradient,
            router_gradient,
            first_gain_gradient,
            second_gain_gradient,
        ),
        ("expert", "weight"),
    )
    return (
        layer_out,
        token_gradient,
        totals[3],
        shards[0],
        totals[0],
        totals[1],
        shards[1],
        shards[2],
        totals[4],
        totals[2],
        shared_gradients[0].T,
        shared_gradients[1].T,
        shared_gradients[2],
        expert_grads[0],
        expert_grads[1],
        expert_grads[2],
    )


def solution(mesh):
    return jax.shard_map(
        per_device,
        mesh=mesh,
        in_specs=(
            P(("expert", "weight"), None),
            P(("expert", "weight"), None),
            P("expert", None),
            P(("expert", "weight"), None),
            P(),
            P(None, "weight"),
            P(),
            P(),
            P(None, "weight"),
            P("weight", None),
            P(),
            P(),
            P(None, "weight"),
            P(None, "weight"),
            P("weight", None),
            P("expert", None, "weight"),
            P("expert", None, "weight"),
            P("expert", "weight", None),
        ),
        out_specs=(
            P(("expert", "weight"), None),
            P(("expert", "weight"), None),
            P(),
            P("expert", "weight"),
            P(),
            P(),
            P("expert", "weight"),
            P("weight", "expert"),
            P(),
            P(),
            P("expert", "weight"),
            P("expert", "weight"),
            P("weight", "expert"),
            P("expert", None, "weight"),
            P("expert", None, "weight"),
            P("expert", "weight", None),
        ),
        check_vma=False,
    )
```

time: 2280 us -> 1240 us (0.54)
  waiting for transfers between devices: 1200 us -> 290 us
  Pallas kernels: 0 us -> 655 us
  local copies, waits for them, and re-layouts: 304 us -> 38.8 us
  matrix products: 404 us -> 148 us
  blocking collectives: 183 us -> 41.3 us
  other arithmetic: 148 us -> 31.9 us
    pallas_call x0 -> x12, Pallas kernels: none -> 655 us  [the longest x6 211 us: call(): pl.pallas_call(kernel, grid=(grid,), in_specs=[s for _, s in ins], out_sp...]
    reduce_scatter x6 -> x1, waiting for transfers between devices: 531 us -> 88.7 us  [per_device(): lax.psum_scatter(out_dense, both, scatter_dimension=0, tiled=True)]
    all_to_all x3 -> x1, waiting for transfers between devices: 353 us -> 0.01 us  [per_device(): lax.all_to_all(shared_grads, 'expert', split_axis=1, concat_axis=0, tiled...]
    dot_general x11 -> x3, matrix products: 300 us -> 59.5 us  [the longest x1 20.3 us: per_device(): jnp.einsum('jsf,jsd->jfd', lift_grad, rows_slots, preferred_element_type=...]
    all_to_all x1 -> x0, blocking collectives: 142 us -> none  [per_device(): lax.all_to_all(send_rows, 'expert', split_axis=0, concat_axis=0, tiled=True)]
    reshape x6 -> x0, local copies, waits for them, and re-layouts: 98.8 us -> none  [the longest x1 31.5 us: per_device(): routed_in_back.reshape(blocks, -1, width)]
    gather x6 -> x0, local copies, waits for them, and re-layouts: 69.4 us -> none  [the longest x2 24.5 us: per_device(): upstream[slot_token]]
    all_gather x6 -> x1, waiting for transfers between devices: 89.7 us -> 29.2 us  [per_device(): cotangent_all = lax.all_gather(cotangent_wide, both, axis=0, tiled=True)]
  transfers between devices with their start and end apart: 19 -> 7, of which waited for: 14 -> 4; matrix products, arithmetic and copies ran while one was open for 18% -> 11% of each run, Pallas kernels for 0% -> 33%
where the time goes in v1:
time: 1240 us; the launch traced here: 1230 us
  Pallas kernels  655 us (53%)
  waiting for transfers between devices  290 us (23%)
  matrix products  148 us (12%)
  blocking collectives  41.3 us (3%)
  local copies, waits for them, and re-layouts  38.8 us (3%)
  other arithmetic  31.9 us (3%)
  between operations  15.6 us (1%)
    pallas_call x6, Pallas kernels, call(): pl.pallas_call(kernel, grid=(grid,), in_specs=[s for _, s in ins], out_sp...  211 us
    pallas_call x1, Pallas kernels, sum_all(): pl.pallas_call(sum_all_kernel, out_shape=out, in_specs=[pl.BlockSpec(memo...  194 us
    pallas_call x1, Pallas kernels, gather_all(): pl.pallas_call(gather_all_kernel, out_shape=out, in_specs=[pl.BlockSpec(m...  162 us
    psum x1, waiting for transfers between devices, per_device(): lax.psum((latent_weight_gradient, latent_gain_gradient, router_gradient,...  152 us
    reduce_scatter x1, waiting for transfers between devices, per_device(): lax.psum_scatter(out_dense, both, scatter_dimension=0, tiled=True)  88.7 us
    pallas_call x2, Pallas kernels, gather_group(): pl.pallas_call(gather_group_kernel, out_shape=out, in_specs=[pl.BlockSpec...  44.7 us
    pallas_call x2, Pallas kernels, sum_group(): pl.pallas_call(sum_group_kernel, out_shape=out, in_specs=[pl.BlockSpec(me...  43.5 us
    dot_general x7, matrix products, trans_times(): lax.dot_general(left, right, (((0,), (0,)), ((), ())), preferred_element_...  41.6 us
  transfers between devices with their start and end apart: 7, of which 4 were waited for; matrix products, arithmetic and copies ran while one was open for 11% of the time, Pallas kernels for 33%

profile of v1, /device:TPU:0, one launch (start us, length us, event | category | flops | bytes accessed | tf_op | source)
XLA Modules:
  0.0 1226.7 jit_solution(7322600460645605690)
XLA Ops:
  12.4 2.1 fusion.24.x_ref
  14.5 22.5 %shard_map.297 = bf16[4,160,2048]{2,1,0:T(8,128)(2,1)} custom-call(bf16[160,2048]{1,0:T(8,128)(2,1)} %fusion.24.x_ref), custom_call_target="tpu_custom_call" | custom-call | bytes 3276800 | tf_op jit(solution)/shard_map/pallas_call | solution.py:628
  37.1 4.6 fusion.86
  43.2 2.0 convolution_convert_fusion.3
  45.2 2.9 reshape.378
  49.4 1.8 copy.169
  51.2 5.0 copy.130
  56.7 5.4 fusion.87
  63.6 1.8 fusion.85
  66.3 1.9 copy-done
  69.7 3.1 convolution_convert_fusion.1
  72.8 21.8 %shard_map.298 = f32[160,2048]{1,0:T(8,128)} custom-call(bf16[4,160,2048]{2,1,0:T(8,128)(2,1)} %bitcast.135), custom_call_target="tpu_custom_call" | custom-call | bytes 3932160 | tf_op jit(solution)/shard_map/pallas_call | solution.py:691
  106.0 162.0 %shard_map.299 = bf16[32,160,2176]{2,1,0:T(8,128)(2,1)} custom-call(bf16[160,2176]{1,0:T(8,128)(2,1)} %concatenate.47.x_ref), custom_call_target="tpu_custom_call" | custom-call | bytes 22978560 | tf_op jit(solution)/shard_map/pallas_call | solution.py:432
  268.7 29.2 %all-gather.2.cloned.1.call-done.value_ref.marks_ref = bf16[5120,2176]{1,0:T(8,128)(2,1)} async-done(((bf16[160,2176]{1,0:T(8,128)(2,1)}), bf16[5120,2176]{1,0:T(8,128)(2,1)}) %all-gather.2.cloned.1.call-update) | async-done | bytes 22282256 | tf_op jit(solution)/shard_map/all_gather | solution.py:788
  298.0 28.5 %shard_map.300 = (bf16[8,640,2048]{2,1,0:T(8,128)(2,1)}, f32[5120,128]{1,0:T(8,128)}) custom-call(bf16[8,128]{1,0:T(8,128)(2,1)} %get-tuple-element.83.here_ref, bf16[5120,2176]{1,0:T(8,128)(2,1)} %all-gather.2.cloned.1.call-done.value_ref.marks_ref, bf16[128,2048]{1,0:T(8,128)(2,1)} %pad.16.down_ref), custom_call_target="tpu_custom_call" | custom-call | flops 9395240960 | bytes 46401536 | tf_op jit(solution)/shard_map/pallas_call | solution.py:258
  326.4 33.4 %shard_map.301 = (bf16[8,640,2048]{2,1,0:T(8,128)(2,1)}, f32[8,640,128]{2,1,0:T(8,128)}, bf16[5120,128]{1,0:T(8,128)(2,1)}, bf16[5120,128]{1,0:T(8,128)(2,1)}, bf16[5120,128]{1,0:T(8,128)(2,1)}) custom-call(bf16[8,128]{1,0:T(8,128)(2,1)} %get-tuple-element.83.here_ref, bf16[8,128]{1,0:T(8,128)(2,1)} %get-tuple-element.82.twice_ref, ...), custom_call_target="tpu_custom_call" | custom-call | flops 12079595520 | bytes 75763712 | tf_op jit(solution)/shard_map/pallas_call | solution.py:258
  359.8 64.9 %shard_map.302 = (bf16[8,640,352]{2,1,0:T(8,128)(2,1)}, bf16[8,640,352]{2,1,0:T(8,128)(2,1)}, bf16[8,640,352]{2,1,0:T(8,128)(2,1)}, bf16[8,640,2048]{2,1,0:T(8,128)(2,1)}, f32[8,640,128]{2,1,0:T(8,128)}) custom-call(bf16[8,640,2048]{2,1,0:T(8,128)(2,1)} %get-tuple-element.29.rows_ref, bf16[8,640,2048]{2,1,0:T(8,128)(2,1)} %get-tuple-element.30.grads_ref, ...), custom_call_target="tpu_custom_call" | custom-call | flops 36909875200 | bytes 113573888 | tf_op jit(solution)/shard_map/pallas_call | solution.py:258
  424.7 26.6 %shard_map.303.rows_ref = bf16[8,640,2048]{2,1,0:T(8,128)(2,1)} custom-call(bf16[8,640,352]{2,1,0:T(8,128)(2,1)} %get-tuple-element.32.hidden_ref, bf16[8,352,2048]{2,1,0:T(8,128)(2,1)} %down_ref.3), custom_call_target="tpu_custom_call" | custom-call | flops 7381975040 | bytes 36110336 | tf_op jit(solution)/shard_map/pallas_call | solution.py:258
  451.4 26.9 %shard_map.304 = bf16[5120,2048]{1,0:T(8,128)(2,1)} custom-call(bf16[8,128]{1,0:T(8,128)(2,1)} %get-tuple-element.83.here_ref, bf16[5120,2176]{1,0:T(8,128)(2,1)} %all-gather.2.cloned.1.call-done.value_ref.marks_ref, bf16[8,640,2048]{2,1,0:T(8,128)(2,1)} %shard_map.303.rows_ref, bf16[5120,128]{1,0:T(8,128)(2,1)} %get-tuple-element.33.hidden_ref, ...), custom_call_target="tpu_custom_call" | custom-call | flops 9395240960 | bytes 66062336 | tf_op jit(solution)/shard_map/pallas_call | solution.py:258
  479.0 31.2 %shard_map.305 = bf16[5120,2176]{1,0:T(8,128)(2,1)} custom-call(bf16[8,128]{1,0:T(8,128)(2,1)} %get-tuple-element.83.here_ref, bf16[8,128]{1,0:T(8,128)(2,1)} %get-tuple-element.85.high_ref, bf16[8,128]{1,0:T(8,128)(2,1)} %get-tuple-element.84.low_ref, bf16[5120,2176]{1,0:T(8,128)(2,1)} %all-gather.2.cloned.1.call-done.value_ref.marks_ref, ...), custom_call_target="tpu_custom_call" | custom-call | flops 12079595520 | bytes 71833600 | tf_op jit(solution)/shard_map/pallas_call | solution.py:258
  510.1 193.6 %shard_map.306 = f32[160,2176]{1,0:T(8,128)} custom-call(bf16[32,160,2176]{2,1,0:T(8,128)(2,1)} %bitcast.123), custom_call_target="tpu_custom_call" | custom-call | bytes 23674880 | tf_op jit(solution)/shard_map/pallas_call | solution.py:567
  704.9 4.0 multiply_reduce_fusion.1
  708.9 88.7 %reduce-scatter.5.cloned.1.call-done = bf16[160,2048]{1,0:T(8,128)(2,1)} async-done(((bf16[5120,2048]{1,0:T(8,128)(2,1)}), bf16[160,2048]{1,0:T(8,128)(2,1)}) %reduce-scatter.5.cloned.1.call-update) | async-done | bytes 655376 | tf_op jit(solution)/shard_map/reduce_scatter | solution.py:953
  797.6 4.0 fusion.82
  801.6 22.1 %shard_map.307 = bf16[4,160,2048]{2,1,0:T(8,128)(2,1)} custom-call(bf16[160,2048]{1,0:T(8,128)(2,1)} %get-tuple-element.56.x_ref), custom_call_target="tpu_custom_call" | custom-call | bytes 3276800 | tf_op jit(solution)/shard_map/pallas_call | solution.py:628
  823.7 4.4 convolution_convert_fusion.5
  832.4 3.4 fusion.34
  837.7 2.0 convolution_convert_fusion.4
  839.8 10.4 fusion
  851.0 3.1 convolution_convert_fusion.2
  855.5 9.0 fusion.2
  864.5 8.7 fusion.4
  875.3 5.8 all-to-all-start
  884.8 4.1 convolution_convert_fusion
  889.7 2.3 fusion.64
  892.0 19.2 %fusion.91 = f32[8,352,2048]{2,1,0:T(8,128)} fusion(bf16[8,640,352]{2,1,0:T(8,128)(2,1)} %get-tuple-element.32.hidden_ref, bf16[8,640,2048]{2,1,0:T(8,128)(2,1)} %get-tuple-element.30.grads_ref), kind=kOutput, calls=%fused_computation.188 | convolution fusion | flops 7381975040 | bytes 47644672 | tf_op jit(solution)/shard_map/jsf,jsd->jfd/dot_general | solution.py:957
  911.2 20.0 %fusion.89 = f32[8,2048,352]{1,2,0:T(8,128)} fusion(bf16[8,640,2048]{2,1,0:T(8,128)(2,1)} %get-tuple-element.29.rows_ref, bf16[8,640,352]{2,1,0:T(8,128)(2,1)} %get-tuple-element.38), kind=kOutput, calls=%fused_computation.186 | convolution fusion | flops 7381975040 | bytes 47644672 | tf_op jit(solution)/shard_map/jsf,jsd->jfd/dot_general | solution.py:955
  935.4 4.2 fusion.45
  939.6 20.3 %fusion.90 = f32[8,2048,352]{1,2,0:T(8,128)} fusion(bf16[8,640,2048]{2,1,0:T(8,128)(2,1)} %get-tuple-element.29.rows_ref, bf16[8,640,352]{2,1,0:T(8,128)(2,1)} %get-tuple-element.39), kind=kOutput, calls=%fused_computation.187 | convolution fusion | flops 7381975040 | bytes 47644672 | tf_op jit(solution)/shard_map/jsf,jsd->jfd/dot_general | solution.py:956
  964.2 2.3 fusion.88
  966.5 3.8 add_convert_fusion
  970.3 21.8 %shard_map.308 = f32[160,2048]{1,0:T(8,128)} custom-call(bf16[4,160,2048]{2,1,0:T(8,128)(2,1)} %bitcast.134), custom_call_target="tpu_custom_call" | custom-call | bytes 3932160 | tf_op jit(solution)/shard_map/pallas_call | solution.py:691
  993.9 41.3 %all-reduce.4 = (f32[2048]{0:T(1024)}, f32[512]{0:T(512)}, f32[2048]{0:T(1024)}) all-reduce(f32[2048]{0:T(1024)S(1)} %get-tuple-element.44, f32[512]{0:T(512)S(1)} %get-tuple-element.40, f32[2048]{0:T(1024)S(1)} %get-tuple-element.42), channel_id=1, replica_groups=mesh['expert'=8,'weight'=4] {'expert','weight'}, use_global_device_ids=true, to_apply=%region_21.22 | all-reduce | flops 4608 | bytes 36864 | tf_op jit(solution)/shard_map/psum | solution.py:1055
  1038.3 1.8 convert_element_type.179
  1040.0 19.9 %reduce-scatter.7.cloned.1.call-done = bf16[256,768]{1,0:T(8,128)(2,1)} async-done(((bf16[2048,768]{1,0:T(8,128)(2,1)}), bf16[256,768]{1,0:T(8,128)(2,1)}) %reduce-scatter.7.cloned.1.call-update) | async-done | bytes 393232 | tf_op jit(solution)/shard_map/reduce_scatter | solution.py:1045
  1059.9 1.9 convert_element_type.175
  1061.9 151.8 %all-reduce.8.cloned.1.call-done = (f32[2048,576]{0,1:T(8,128)}, f32[2048,64]{0,1:T(8,128)}) async-done(((f32[2048,576]{0,1:T(8,128)}, f32[2048,64]{0,1:T(8,128)}), (f32[2048,576]{0,1:T(8,128)}, f32[2048,64]{0,1:T(8,128)})) %all-reduce.8.cloned.1.call-update) | async-done | bytes 5242896 | tf_op jit(solution)/shard_map/psum | solution.py:1055
  1213.6 5.2 copy.188
  (250 shorter events, 54.7 us)
Async XLA Ops:
  7.2 290.8 %all-gather.2.cloned.1.call-start = ((), (), s32[]{:S(2)}) async-start(), calls=%async_computation.5 | async-start | bytes 22978560 | tf_op jit(solution)/shard_map/all_gather | solution.py:788
  7.2 49.0 %copy-start.63 = (f32[32]{0:T(128)}, f32[32]{0:T(128)S(1)}, u32[]{:S(2)}) copy-start(f32[32]{0:T(128)S(1)} %negate_power_fusion) | copy-start | bytes 388
  10.0 27.1 %copy-start.57 = (f32[160]{0:T(256)}, f32[160]{0:T(256)S(1)}, u32[]{:S(2)}) copy-start(f32[160]{0:T(256)S(1)} %get-tuple-element.79) | copy-start | bytes 1924
  10.7 45.6 %copy-start.49 = (f32[640]{0:T(1024)}, f32[640]{0:T(1024)S(1)}, u32[]{:S(2)}) copy-start(f32[640]{0:T(1024)S(1)} %fusion.65) | copy-start | bytes 7684
  37.1 6.1 copy-start.65
  37.1 6.1 copy-start.70
  41.7 14.6 %copy-start.11 = (f32[640,576]{0,1:T(8,128)}, f32[640,576]{0,1:T(8,128)S(1)}, u32[]{:S(2)}) copy-start(f32[640,576]{0,1:T(8,128)S(1)} %fusion.86) | copy-start | bytes 4423684
  49.4 13.9 %copy-start.7 = (bf16[640,4,128]{2,1,0:T(4,128)(2,1)}, bf16[640,4,128]{2,1,0:T(4,128)(2,1)S(1)}, u32[]{:S(2)}) copy-start(bf16[640,4,128]{2,1,0:T(4,128)(2,1)S(1)} %get-tuple-element.68) | copy-start | bytes 1966084
  51.2 15.0 %copy-start.16 = (bf16[640,4,128]{0,2,1:T(8,128)(2,1)}, bf16[640,4,128]{0,2,1:T(8,128)(2,1)S(1)}, u32[]{:S(2)}) copy-start(bf16[640,4,128]{0,2,1:T(8,128)(2,1)S(1)} %copy.169) | copy-start | bytes 1966084
  56.7 5.4 copy-start.35
  56.7 5.4 copy-start.37
  56.7 5.6 copy-start.42
  56.7 5.6 copy-start.44
  69.6 3.2 copy-start.72
  72.8 21.8 %copy-start.4 = (bf16[160,2048]{1,0:T(8,128)(2,1)S(1)}, bf16[160,2048]{1,0:T(8,128)(2,1)}, u32[]{:S(2)}) copy-start(bf16[160,2048]{1,0:T(8,128)(2,1)} %param.18) | copy-start | bytes 1966084
  97.5 7.5 copy-start.9
  98.6 3.5 copy-start.55
  100.0 697.5 %reduce-scatter.5.cloned.1.call-start = ((), (), s32[]{:S(2)}) async-start(), calls=%async_computation.6 | async-start | bytes 21626880 | tf_op jit(solution)/shard_map/reduce_scatter | solution.py:953
  478.2 558.4 %reduce-scatter.9.cloned.1.call-start = ((), (), s32[]{:S(2)}) async-start(), calls=%async_computation.8 | async-start | bytes 1179648 | tf_op jit(solution)/shard_map/reduce_scatter | solution.py:1048
  510.1 194.6 %copy-start.56 = (f32[160]{0:T(256)S(1)}, f32[160]{0:T(256)}, u32[]{:S(2)}) copy-start(f32[160]{0:T(256)} %copy-done.55) | copy-start | bytes 1924
  510.1 194.7 %copy-start.60 = (f32[160]{0:T(256)S(1)}, f32[160]{0:T(256)}, u32[]{:S(2)}) copy-start(f32[160]{0:T(256)} %copy-done.59) | copy-start | bytes 1924
  704.9 92.7 %copy-start.19 = (bf16[160,2048]{1,0:T(8,128)(2,1)S(1)}, bf16[160,2048]{1,0:T(8,128)(2,1)}, u32[]{:S(2)}) copy-start(bf16[160,2048]{1,0:T(8,128)(2,1)} %param.19) | copy-start | bytes 1966084
  704.9 92.7 %copy-start.62 = (f32[160]{0:T(256)S(1)}, f32[160]{0:T(256)}, u32[]{:S(2)}) copy-start(f32[160]{0:T(256)} %get-tuple-element.80) | copy-start | bytes 1924
  797.6 30.6 %slice-start = ((s8[6553600]{0:T(1024)(128)(4,1)}), s8[2359296]{0:T(1024)(128)(4,1)S(1)}, s32[]{:S(2)}) async-start(s8[6553600]{0:T(1024)(128)(4,1)} %bitcast.118), calls=%async_computation.11 | async-start | bytes 4718592
  823.7 4.4 slice-start.1
  832.4 3.4 copy-start.1
  839.7 11.3 copy-start.22
  839.7 198.5 %reduce-scatter.11.cloned.1.call-start = ((), (), s32[]{:S(2)}) async-start(), calls=%async_computation.9 | async-start | bytes 2359296 | tf_op jit(solution)/shard_map/reduce_scatter | solution.py:1051
  839.8 11.2 copy-start.73
  855.5 9.0 copy-start.31
  874.3 6.9 copy-start.2
  874.3 6.9 copy-start.43
  875.3 84.6 %all-to-all-start = ((bf16[264,8,256]{2,0,1:T(8,128)(2,1)}), bf16[264,8,256]{2,0,1:T(8,128)(2,1)}, u32[]{:S(2)}, u32[]{:S(2)}) async-start(bf16[264,8,256]{2,0,1:T(8,128)(2,1)} %pad_maximum_fusion.1), calls=%async_computation.4 | async-start | bytes 2162688 | tf_op jit(solution)/shard_map/all_to_all | solution.py:968
  881.1 178.8 %reduce-scatter.7.cloned.1.call-start = ((), (), s32[]{:S(2)}) async-start(), calls=%async_computation.7 | async-start | bytes 3538944 | tf_op jit(solution)/shard_map/reduce_scatter | solution.py:1045
  888.9 324.8 %all-reduce.8.cloned.1.call-start = ((), (), s32[]{:S(2)}) async-start(), calls=%async_computation.10 | async-start | bytes 10485760 | tf_op jit(solution)/shard_map/psum | solution.py:1055
  911.2 20.1 %copy-start.13 = (f32[640,576]{0,1:T(8,128)S(1)}, f32[640,576]{0,1:T(8,128)}, u32[]{:S(2)}) copy-start(f32[640,576]{0,1:T(8,128)} %copy-done.11) | copy-start | bytes 4423684
  911.2 20.1 %copy-start.30 = (bf16[640,4,256]{0,2,1:T(8,128)(2,1)S(1)}, bf16[640,4,256]{0,2,1:T(8,128)(2,1)}, u32[]{:S(2)}) copy-start(bf16[640,4,256]{0,2,1:T(8,128)(2,1)} %copy-done.29) | copy-start | bytes 3932164
  911.2 20.1 %copy-start.54 = (f32[640]{0:T(1024)S(1)}, f32[640]{0:T(1024)}, u32[]{:S(2)}) copy-start(f32[640]{0:T(1024)} %copy-done.52) | copy-start | bytes 7684
  911.2 20.1 %copy-start.67 = (f32[512]{0:T(512)S(1)}, f32[512]{0:T(512)}, u32[]{:S(2)}) copy-start(f32[512]{0:T(512)} %param.25) | copy-start | bytes 6148
  911.2 20.1 %copy-start.71 = (bf16[512,1024]{1,0:T(8,128)(2,1)S(1)}, bf16[512,1024]{1,0:T(8,128)(2,1)}, u32[]{:S(2)}) copy-start(bf16[512,1024]{1,0:T(8,128)(2,1)} %param.26) | copy-start | bytes 3145732
  961.3 2.9 copy-start.34
  970.3 21.8 %copy-start.5 = (bf16[160,2048]{1,0:T(8,128)(2,1)S(1)}, bf16[160,2048]{1,0:T(8,128)(2,1)}, u32[]{:S(2)}) copy-start(bf16[160,2048]{1,0:T(8,128)(2,1)} %param.18) | copy-start | bytes 1966084
  970.3 21.8 %copy-start.47 = (f32[2048]{0:T(1024)S(1)}, f32[2048]{0:T(1024)}, u32[]{:S(2)}) copy-start(f32[2048]{0:T(1024)} %param.22) | copy-start | bytes 24580
  970.3 21.8 %copy-start.58 = (f32[160]{0:T(256)S(1)}, f32[160]{0:T(256)}, u32[]{:S(2)}) copy-start(f32[160]{0:T(256)} %copy-done.57) | copy-start | bytes 1924
  970.3 64.9 %copy-start.14 = (f32[160,2048]{1,0:T(8,128)S(1)}, f32[160,2048]{1,0:T(8,128)}, u32[]{:S(2)}) copy-start(f32[160,2048]{1,0:T(8,128)} %get-tuple-element.57) | copy-start | bytes 3932164
  970.3 64.9 %copy-start.61 = (f32[160]{0:T(256)S(1)}, f32[160]{0:T(256)}, u32[]{:S(2)}) copy-start(f32[160]{0:T(256)} %get-tuple-element.78) | copy-start | bytes 1924
  992.1 43.1 %copy-start.6 = (f32[160,2048]{1,0:T(8,128)S(1)}, f32[160,2048]{1,0:T(8,128)}, u32[]{:S(2)}) copy-start(f32[160,2048]{1,0:T(8,128)} %shard_map.308) | copy-start | bytes 3932164
  1213.6 5.2 copy-start.41
  (35 other events, 54.4 us)
Sparse Core Ops, SparseCore 0:
  100.1 197.8 all-gather.1
  478.3 319.1 reduce-scatter.4
  839.9 70.2 reduce-scatter.8
  913.5 68.2 reduce-scatter.10
  985.2 74.6 reduce-scatter.6
  1066.5 147.0 all-reduce.7

commit v2 on v1

--- a/solution.py
+++ b/solution.py
@@ -298,9 +298,13 @@
         self.semaphores = semaphores
         self.started = []
 
-    def start(self, source, target, receive, to, when=None):
+    def plan(self, source, target, receive, to, when=None):
         copy = push(source, target, self.semaphores.at[len(self.started)], receive, to)
         self.started.append((copy, when))
+        return copy
+
+    def start(self, source, target, receive, to, when=None):
+        copy = self.plan(source, target, receive, to, when)
         if when is None:
             copy.start()
         else:
@@ -444,46 +448,73 @@
     )(value)
 
 
-def sum_all_kernel(
-    p_ref,
-    out_ref,
-    own,
-    mates,
-    over_half,
-    side_half,
-    over_full,
-    side_full,
-    below,
-    above,
-    send_sems,
-    mate_sems,
-    half_sems,
-    full_sems,
-    line_sems,
-    local_sems,
-):
+def sum_all_kernel(inner, cover_ins, cover_outs, p_ref, *refs):
+    ins, refs = refs[:cover_ins], refs[cover_ins:]
+    out_ref, refs = refs[0], refs[1:]
+    outs, refs = refs[:cover_outs], refs[cover_outs:]
+    own, mates, over_half, side_half, over_full, side_full, below, above = refs[:8]
+    send_sems, mate_sems, half_sems, full_sems, line_sems, local_sems = refs[8:]
     z, x, y, c = places()
+    turn, turns = pl.program_id(0), pl.num_programs(0)
     rows = out_ref.shape[0]
     half = rows // 2
     over, side, mate = device(z, 1 - x, y, c), device(z, x, 1 - y, c), device(z, x, y, 1 - c)
     up, down = device(z + 1, x, y, c), device(z - 1, x, y, c)
-    greet([(over, None), (side, None), (mate, None), (up, z < 3), (down, z > 0)])
     sends = Sends(send_sems)
     targets = [ordered(z, (3, 2, 1, 0)[step], (3, 0, 2, 1)[step]) for step in range(4)]
     spots = [(1 - x, 1 - y), (1 - x, y), (x, 1 - y), (x, y)]
-    loads = []
+    shards = [[shard(zz, xx, yy, 1 - c) for xx, yy in spots] for zz in targets]
+    mine = [[shard(zz, xx, yy, c) for xx, yy in spots] for zz in targets]
+    higher = [zz > z for zz in targets]
+    lower = [zz < z for zz in targets]
+    loads = [
+        pltpu.make_async_copy(p_ref.at[mine[slot // 4][slot % 4]], own.at[slot], local_sems.at[slot])
+        for slot in range(16)
+    ]
+
+    mate_copies = [
+        sends.plan(p_ref.at[shards[slot // 4][slot % 4]], mates.at[slot], mate_sems.at[slot], mate)
+        for slot in range(16)
+    ]
+    corner_copies, relay_copies, line_copies = [], [], []
     for step in range(4):
-        zz = targets[step]
-        for j, (xx, yy) in enumerate(spots):
-            slot = step * 4 + j
-            sends.start(
-                p_ref.at[shard(zz, xx, yy, 1 - c)], mates.at[slot], mate_sems.at[slot], mate
+        corner_copies.append(
+            (
+                sends.plan(
+                    own.at[step * 4, pl.ds(half, half)],
+                    over_half.at[step],
+                    half_sems.at[step, 0],
+                    over,
+                ),
+                sends.plan(
+                    own.at[step * 4, pl.ds(0, half)], side_half.at[step], half_sems.at[step, 1], side
+                ),
             )
-            load = pltpu.make_async_copy(
-                p_ref.at[shard(zz, xx, yy, c)], own.at[slot], local_sems.at[slot]
+        )
+        relay_copies.append(
+            (
+                sends.plan(
+                    own.at[step * 4 + 1], over_full.at[step], full_sems.at[step, 0], over
+                ),
+                sends.plan(
+                    own.at[step * 4 + 2], side_full.at[step], full_sems.at[step, 1], side
+                ),
             )
-            load.start()
-            loads.append(load)
+        )
+    for step in range(3):
+        zz, slot = targets[step], step * 4 + 3
+        line_copies.append(
+            (
+                sends.plan(own.at[slot], below.at[zz], line_sems.at[zz, 0], up, higher[step]),
+                sends.plan(own.at[slot], above.at[zz], line_sems.at[zz, 1], down, lower[step]),
+            )
+        )
+
+    def begin():
+        greet([(over, None), (side, None), (mate, None), (up, z < 3), (down, z > 0)])
+        for slot in range(16):
+            mate_copies[slot].start()
+            loads[slot].start()
 
     def join(slot):
         loads[slot].wait()
@@ -493,10 +524,8 @@
         slot = step * 4
         join(slot)
         add_rows(own.at[slot], [(mates.at[slot], 0)], 0, rows)
-        sends.start(
-            own.at[slot, pl.ds(half, half)], over_half.at[step], half_sems.at[step, 0], over
-        )
-        sends.start(own.at[slot, pl.ds(0, half)], side_half.at[step], half_sems.at[step, 1], side)
+        for copy in corner_copies[step]:
+            copy.start()
 
     def relay(step):
         slot = step * 4 + 1
@@ -504,13 +533,13 @@
         add_rows(own.at[slot], [(mates.at[slot], 0)], half, half)
         landed(side_half.at[step], half_sems.at[step, 1], mate)
         add_rows(own.at[slot], [(mates.at[slot], 0), (side_half.at[step], 0)], 0, half)
-        sends.start(own.at[slot], over_full.at[step], full_sems.at[step, 0], over)
+        relay_copies[step][0].start()
         slot = step * 4 + 2
         join(slot)
         add_rows(own.at[slot], [(mates.at[slot], 0)], 0, half)
         landed(over_half.at[step], half_sems.at[step, 0], mate)
         add_rows(own.at[slot], [(mates.at[slot], 0), (over_half.at[step], half)], half, half)
-        sends.start(own.at[slot], side_full.at[step], full_sems.at[step, 1], side)
+        relay_copies[step][1].start()
 
     def whole(step):
         zz = targets[step]
@@ -536,39 +565,54 @@
             add_rows(own.at[slot], [(above.at[zz], 0)], 0, rows)
 
         if step < 3:
-            sends.start(own.at[slot], below.at[zz], line_sems.at[zz, 0], up, zz > z)
-            sends.start(own.at[slot], above.at[zz], line_sems.at[zz, 1], down, zz < z)
-
-    corner(0)
-    corner(1)
-    relay(0)
-    corner(2)
-    relay(1)
-    whole(0)
-    corner(3)
-    relay(2)
-    whole(1)
-    relay(3)
-    whole(2)
-    whole(3)
-    out_ref[...] = own[15].astype(out_ref.dtype)
-    sends.finish()
-
-
-def sum_all(value, number):
+            pl.when(higher[step])(line_copies[step][0].start)
+            pl.when(lower[step])(line_copies[step][1].start)
+
+    def end():
+        whole(3)
+        out_ref[...] = own[15].astype(out_ref.dtype)
+        sends.finish()
+
+    pieces = [
+        begin,
+        functools.partial(corner, 0),
+        functools.partial(corner, 1),
+        functools.partial(relay, 0),
+        functools.partial(corner, 2),
+        functools.partial(relay, 1),
+        functools.partial(whole, 0),
+        functools.partial(corner, 3),
+        functools.partial(relay, 2),
+        functools.partial(whole, 1),
+        functools.partial(relay, 3),
+        functools.partial(whole, 2),
+    ]
+    for number, piece in enumerate(pieces):
+        pl.when(turn == number)(piece)
+    inner(turn, ins, outs)
+    pl.when(turn == turns - 1)(end)
+
+
+def sum_all(value, number, inner, turns, ins, outs, flops):
     if lax.axis_size("expert") != 8 or lax.axis_size("weight") != 4:
         summed = lax.psum_scatter(
             value.reshape(-1, value.shape[2]), ("expert", "weight"), scatter_dimension=0, tiled=True
         )
-        return summed.astype(jnp.float32)
+
+        def alone(*refs):
+            inner(pl.program_id(0), refs[: len(ins)], refs[len(ins) :])
+
+        return summed.astype(jnp.float32), call(alone, turns, ins, outs, flops)
     _, rows, width = value.shape
     out = jax.ShapeDtypeStruct((rows, width), jnp.float32)
     buffer = lambda n, r: pltpu.VMEM((n, r, width), value.dtype)
-    return pl.pallas_call(
-        sum_all_kernel,
-        out_shape=out,
-        in_specs=[pl.BlockSpec(memory_space=pl.ANY)],
-        out_specs=pl.BlockSpec(memory_space=pltpu.VMEM),
+    arrays, shapes = [a for a, _ in ins], [o for o, _ in outs]
+    results = pl.pallas_call(
+        functools.partial(sum_all_kernel, inner, len(ins), len(outs)),
+        grid=(turns,),
+        out_shape=[out] + shapes,
+        in_specs=[pl.BlockSpec(memory_space=pl.ANY)] + [spec for _, spec in ins],
+        out_specs=[pl.BlockSpec((rows, width), lambda i: (0, 0))] + [spec for _, spec in outs],
         scratch_shapes=[
             buffer(16, rows),
             buffer(16, rows),
@@ -588,8 +632,9 @@
         compiler_params=pltpu.CompilerParams(
             collective_id=number, has_side_effects=True, vmem_limit_bytes=vmem_limit
         ),
-        cost_estimate=cost(0, value, out),
-    )(value)
+        cost_estimate=cost(flops, value, out, *arrays, *shapes),
+    )(value, *arrays)
+    return results[0], results[1:]
 
 
 def gather_group_kernel(x_ref, out_ref, send_sems, recv_sems, local_sem):
@@ -704,6 +749,181 @@
         compiler_params=pltpu.CompilerParams(collective_id=number, has_side_effects=True),
         cost_estimate=cost(0, value, out),
     )(value)
+
+
+def columns(start, size):
+    return pl.ds(pl.multiple_of(start, lanes), size)
+
+
+def add_block(target, sources, rows, row_start=0):
+    step = 16
+
+    def body(i, carry):
+        part = pl.ds(pl.multiple_of(row_start + i * step, step), step)
+        total = target[part].astype(jnp.float32)
+        for source in sources:
+            there = pl.ds(pl.multiple_of(i * step, step), step)
+            total = total + source[there].astype(jnp.float32)
+        target[part] = total.astype(target.dtype)
+        return carry
+
+    lax.fori_loop(0, rows // step, body, 0)
+
+
+def total_kernel(
+    p_ref, out_ref, acc, mates, first_over, first_side, next_side, next_over, line, send_sems, sems
+):
+    z, x, y, c = places()
+    rows, width = p_ref.shape
+    half, quarter, eighth, sixteenth = width // 2, width // 4, width // 8, width // 16
+    strip = rows // 4
+    over, side, mate = device(z, 1 - x, y, c), device(z, x, 1 - y, c), device(z, x, y, 1 - c)
+    others = [lax.rem(z + d, 4) for d in (1, 2, 3)]
+    greet(
+        [(over, None), (side, None), (mate, None)] + [(device(zz, x, y, c), None) for zz in others]
+    )
+    sends = Sends(send_sems)
+    base = c * half
+    for j in range(2):
+        sends.start(
+            p_ref.at[:, columns((1 - c) * half + j * quarter, quarter)],
+            mates.at[:, columns(j * quarter, quarter)],
+            sems.at[j],
+            mate,
+        )
+    kept = (x * eighth + y * sixteenth, quarter + y * eighth + x * sixteenth)
+    firsts, nexts = (first_over, first_side), (next_side, next_over)
+    for j in range(2):
+        part = columns(j * quarter, quarter)
+        landed(mates.at[:, part], sems.at[j], mate)
+        wide = 16
+
+        def join(i, carry, j=j):
+            some = pl.ds(pl.multiple_of(i * wide, wide), wide)
+            mine = p_ref[some, columns(base + j * quarter, quarter)].astype(jnp.float32)
+            total = mine + mates[some, columns(j * quarter, quarter)].astype(jnp.float32)
+            acc[some, columns(j * quarter, quarter)] = total.astype(acc.dtype)
+            return carry
+
+        lax.fori_loop(0, rows // wide, join, 0)
+        away = (1 - x) * eighth if j == 0 else quarter + (1 - y) * eighth
+        sends.start(
+            acc.at[:, columns(away, eighth)], firsts[j], sems.at[2 + j], (over, side)[j]
+        )
+    for j in range(2):
+        landed(firsts[j], sems.at[2 + j], mate)
+        near = x * eighth if j == 0 else quarter + y * eighth
+        add_block(acc.at[:, columns(near, eighth)], [firsts[j]], rows)
+        away = near + ((1 - y) if j == 0 else (1 - x)) * sixteenth
+        sends.start(
+            acc.at[:, columns(away, sixteenth)], nexts[j], sems.at[4 + j], (side, over)[j]
+        )
+    for j in range(2):
+        landed(nexts[j], sems.at[4 + j], mate)
+        add_block(acc.at[:, columns(kept[j], sixteenth)], [nexts[j]], rows)
+        for d, zz in enumerate(others):
+            sends.start(
+                acc.at[pl.ds(pl.multiple_of(zz * strip, 16), strip), columns(kept[j], sixteenth)],
+                line.at[j, d],
+                sems.at[6 + j * 3 + d],
+                device(zz, x, y, c),
+            )
+    strip_here = pl.multiple_of(z * strip, 16)
+    for j in range(2):
+        for d in range(3):
+            landed(line.at[j, d], sems.at[6 + j * 3 + d], mate)
+        block = acc.at[:, columns(kept[j], sixteenth)]
+        add_block(block, [line.at[j, d] for d in range(3)], strip, strip_here)
+
+        def place(i, carry, j=j):
+            some = pl.ds(pl.multiple_of(strip_here + i * 16, 16), 16)
+            out_ref[some, columns(base + kept[j], sixteenth)] = acc[
+                some, columns(kept[j], sixteenth)
+            ]
+            return carry
+
+        lax.fori_loop(0, strip // 16, place, 0)
+        done = out_ref.at[pl.ds(strip_here, strip), columns(base + kept[j], sixteenth)]
+        for d, zz in enumerate(others):
+            sends.start(done, done, sems.at[12 + j * 3 + d], device(zz, x, y, c))
+    for j in range(2):
+        for d in range(3):
+            source = pl.multiple_of(lax.rem(z + 3 - d, 4) * strip, 16)
+            landed(
+                out_ref.at[pl.ds(source, strip), columns(base + kept[j], sixteenth)],
+                sems.at[12 + j * 3 + d],
+                mate,
+            )
+        part = out_ref.at[:, columns(base + kept[j], sixteenth)]
+        sends.start(part, part, sems.at[18 + j], (side, over)[j])
+    others_kept = (
+        x * eighth + (1 - y) * sixteenth,
+        quarter + y * eighth + (1 - x) * sixteenth,
+    )
+    for j in range(2):
+        landed(out_ref.at[:, columns(base + others_kept[j], sixteenth)], sems.at[18 + j], mate)
+        near = x * eighth if j == 0 else quarter + y * eighth
+        part = out_ref.at[:, columns(base + near, eighth)]
+        sends.start(part, part, sems.at[20 + j], (over, side)[j])
+    for j in range(2):
+        away = (1 - x) * eighth if j == 0 else quarter + (1 - y) * eighth
+        landed(out_ref.at[:, columns(base + away, eighth)], sems.at[20 + j], mate)
+        part = out_ref.at[:, columns(base + j * quarter, quarter)]
+        sends.start(part, part, sems.at[22 + j], mate)
+    for j in range(2):
+        landed(
+            out_ref.at[:, columns((1 - c) * half + j * quarter, quarter)], sems.at[22 + j], mate
+        )
+    sends.finish()
+
+
+def total_over_all(value, number):
+    if lax.axis_size("expert") != 8 or lax.axis_size("weight") != 4:
+        return lax.psum(value.astype(jnp.float32), ("expert", "weight"))
+    rows, width = value.shape
+    out = jax.ShapeDtypeStruct(value.shape, value.dtype)
+    buffer = lambda n: pltpu.VMEM((rows, n), value.dtype)
+    return pl.pallas_call(
+        total_kernel,
+        out_shape=out,
+        in_specs=[pl.BlockSpec(memory_space=pltpu.VMEM)],
+        out_specs=pl.BlockSpec(memory_space=pltpu.VMEM),
+        scratch_shapes=[
+            buffer(width // 2),
+            buffer(width // 2),
+            buffer(width // 8),
+            buffer(width // 8),
+            buffer(width // 16),
+            buffer(width // 16),
+            pltpu.VMEM((2, 3, rows // 4, width // 16), value.dtype),
+            pltpu.SemaphoreType.DMA((24,)),
+            pltpu.SemaphoreType.DMA((24,)),
+        ],
+        compiler_params=pltpu.CompilerParams(collective_id=number, has_side_effects=True),
+        cost_estimate=cost(0, value, out),
+    )(value).astype(jnp.float32)
+
+
+def shared_kernel(turn, ins, outs):
+    normed_ref, cotangent_ref, gate_grad_ref, lift_grad_ref, hidden_ref = ins
+
+    @pl.when(turn == 0)
+    def _():
+        for out_ref in outs:
+            out_ref[...] = jnp.zeros_like(out_ref)
+
+    normed, cotangent = normed_ref[...], cotangent_ref[...]
+    outs[0][...] += trans_times(gate_grad_ref[...], normed)
+    outs[1][...] += trans_times(lift_grad_ref[...], normed)
+    outs[2][...] += trans_times(hidden_ref[...], cotangent)
+
+
+def weight_kernel(turn, ins, outs):
+    rows_ref, grads_ref, gate_grad_ref, lift_grad_ref, hidden_ref = ins
+    rows = rows_ref[0]
+    outs[0][0] = trans_times(gate_grad_ref[0], rows)
+    outs[1][0] = trans_times(lift_grad_ref[0], rows)
+    outs[2][0] = trans_times(hidden_ref[0], grads_ref[0])
 
 
 def per_device(
@@ -926,10 +1146,87 @@
         [(dense_wide, pair_spec(dense_wide, pairs))],
         gather_flops + 2 * all_rows * width * shared_wide,
     )
-    back_here = sum_all(back_dense.reshape(blocks, token_rows, -1), 3)
+    shared_sum = shape((shared_wide, width), jnp.float32)
+    shared_out = (shared_sum, whole_spec(shared_sum))
+    plain_spec = pl.BlockSpec((pair_rows, width), lambda i: (i, 0))
+    back_here, shared_sums = sum_all(
+        back_dense.reshape(blocks, token_rows, -1),
+        3,
+        shared_kernel,
+        pairs,
+        [
+            (normed_tokens, plain_spec),
+            (cotangent_all, plain_spec),
+            (shared_gate_grad, token_spec),
+            (shared_lift_grad, token_spec),
+            (shared_hidden, token_spec),
+        ],
+        [shared_out] * 3,
+        6 * all_rows * width * shared_wide,
+    )
     routed_back = back_here[:, :width]
     mix_grad = back_here[:, width : width + 2 * weight_count * routes.shape[1]]
     mix_grad = jnp.sum(mix_grad.reshape(token_rows, routes.shape[1], -1), axis=2)
+    shared_grads = jnp.concatenate([total[:shared_here] for total in shared_sums], axis=0)
+    shared_grads = shared_grads.astype(jnp.bfloat16)
+    swapped = lax.all_to_all(shared_grads, "expert", split_axis=1, concat_axis=0, tiled=True)
+    swapped = swapped.reshape(expert_lanes, 3, shared_here, -1).astype(jnp.float32)
+    shared_gradients = [swapped[:, i].reshape(expert_lanes * shared_here, -1) for i in range(3)]
+    chosen_grad = route_scale * (
+        mix_grad / chosen_total
+        - jnp.sum(mix_grad * chosen, axis=1, keepdims=True) / chosen_total**2
+    )
+    logit_grad = jnp.sum(choose * chosen_grad[:, :, None], axis=1) * gates * (1.0 - gates)
+    normed_two_grad = (
+        routed_back
+        + jnp.dot(logit_grad, router_weight.astype(jnp.float32).T, precision=highest)
+    )
+    router_gradient = jnp.dot(normed_two.astype(jnp.float32).T, logit_grad, precision=highest)
+    back_two, second_gain_gradient = norm_back(
+        normed_two_grad, hidden_one, second_scale, second_gain
+    )
+    hidden_grad = upstream + back_two
+    hidden_group = gather_group(hidden_grad.astype(jnp.bfloat16), 4)
+    output_gradient = trans_times(mixed, hidden_group)
+    mixed_grad = (
+        times_trans(hidden_group, output_weight)
+        .astype(jnp.bfloat16)
+        .reshape(group_rows, heads_here, VDIM)
+    )
+    probs = jnp.exp(score_block() - log_total)
+    prob_grad = jnp.einsum("ihd,jhd->hij", mixed_grad, values, preferred_element_type=jnp.float32)
+    centre = jnp.sum(probs * prob_grad, axis=-1, keepdims=True)
+    score_grad = (probs * (prob_grad - centre)).astype(jnp.bfloat16)
+    value_grad = jnp.einsum(
+        "hij,ihd->jhd", probs.astype(jnp.bfloat16), mixed_grad, preferred_element_type=jnp.float32
+    )
+    query_nope_grad = (
+        jnp.einsum("hij,jhd->ihd", score_grad, key_nope, preferred_element_type=jnp.float32)
+        * score_scale
+    )
+    query_rope_grad = (
+        jnp.einsum("hij,jd->ihd", score_grad, key_rope, preferred_element_type=jnp.float32)
+        * score_scale
+    )
+    key_nope_grad = (
+        jnp.einsum(
+            "hij,ihd->jhd", score_grad, query[..., :NOPE], preferred_element_type=jnp.float32
+        )
+        * score_scale
+    )
+    key_rope_grad = (
+        jnp.einsum("hij,ihd->jd", score_grad, query[..., NOPE:], preferred_element_type=jnp.float32)
+        * score_scale
+    )
+    query_grad = jnp.concatenate(
+        [query_nope_grad, unrotate(query_rope_grad, cosine[:, None, :], sine[:, None, :])], axis=-1
+    )
+    query_grad = query_grad.astype(jnp.bfloat16).reshape(group_rows, heads_here * query_width)
+    expand_grad = (
+        jnp.concatenate([key_nope_grad, value_grad], axis=-1)
+        .astype(jnp.bfloat16)
+        .reshape(group_rows, heads_here * (NOPE + VDIM))
+    )
     (produced,) = call(
         produce_kernel,
         2 * local_experts,
@@ -950,80 +1247,28 @@
         [(dense, dense_spec)],
         gather_flops,
     )
-    routed_out = lax.psum_scatter(out_dense, both, scatter_dimension=0, tiled=True).astype(jnp.float32)
-    expert_grads = (
-        jnp.einsum("jsf,jsd->jfd", gate_grad, rows_slots, preferred_element_type=jnp.float32).transpose(0, 2, 1),
-        jnp.einsum("jsf,jsd->jfd", lift_grad, rows_slots, preferred_element_type=jnp.float32).transpose(0, 2, 1),
-        jnp.einsum("jsf,jsd->jfd", routed_hidden, grads_slots, preferred_element_type=jnp.float32),
-    )
-    normed_plain, cotangent_plain = normed_tokens[:, :width], cotangent_all[:, :width]
-    shared_grads = jnp.concatenate(
+    column_half = width // 2
+    half_spec = lambda m: pl.BlockSpec((1, m, column_half), lambda i: (i // 2, 0, i % 2))
+    narrow_spec = pl.BlockSpec((1, slot_rows, hidden_here), lambda i: (i // 2, 0, 0))
+    weight_shape = shape((local_experts, hidden_here, width), jnp.float32)
+    out_dense, query_grad = lax.optimization_barrier((out_dense, query_grad))
+    routed_out, weight_grads = sum_all(
+        out_dense.reshape(blocks, token_rows, width),
+        6,
+        weight_kernel,
+        2 * local_experts,
         [
-            trans_times(shared_gate_grad, normed_plain)[:shared_here],
-            trans_times(shared_lift_grad, normed_plain)[:shared_here],
-            trans_times(shared_hidden, cotangent_plain)[:shared_here],
-        ],
-        axis=0,
-    ).astype(jnp.bfloat16)
-    swapped = lax.all_to_all(shared_grads, "expert", split_axis=1, concat_axis=0, tiled=True)
-    swapped = swapped.reshape(expert_lanes, 3, shared_here, -1).astype(jnp.float32)
-    shared_gradients = [swapped[:, i].reshape(expert_lanes * shared_here, -1) for i in range(3)]
+            (rows_slots, half_spec(slot_rows)),
+            (grads_slots, half_spec(slot_rows)),
+            (gate_grad, narrow_spec),
+            (lift_grad, narrow_spec),
+            (routed_hidden, narrow_spec),
+        ],
+        [(weight_shape, half_spec(hidden_here))] * 3,
+        3 * one_matmul,
+    )
+    expert_grads = (weight_grads[0].transpose(0, 2, 1), weight_grads[1].transpose(0, 2, 1), weight_grads[2])
     layer_out = (hidden_one + routed_out).astype(jnp.bfloat16)
-    chosen_grad = route_scale * (
-        mix_grad / chosen_total
-        - jnp.sum(mix_grad * chosen, axis=1, keepdims=True) / chosen_total**2
-    )
-    logit_grad = jnp.sum(choose * chosen_grad[:, :, None], axis=1) * gates * (1.0 - gates)
-    normed_two_grad = (
-        routed_back
-        + jnp.dot(logit_grad, router_weight.astype(jnp.float32).T, precision=highest)
-    )
-    router_gradient = jnp.dot(normed_two.astype(jnp.float32).T, logit_grad, precision=highest)
-    back_two, second_gain_gradient = norm_back(
-        normed_two_grad, hidden_one, second_scale, second_gain
-    )
-    hidden_grad = upstream + back_two
-    hidden_group = gather_group(hidden_grad.astype(jnp.bfloat16), 4)
-    output_gradient = trans_times(mixed, hidden_group)
-    mixed_grad = (
-        times_trans(hidden_group, output_weight)
-        .astype(jnp.bfloat16)
-        .reshape(group_rows, heads_here, VDIM)
-    )
-    probs = jnp.exp(score_block() - log_total)
-    prob_grad = jnp.einsum("ihd,jhd->hij", mixed_grad, values, preferred_element_type=jnp.float32)
-    centre = jnp.sum(probs * prob_grad, axis=-1, keepdims=True)
-    score_grad = (probs * (prob_grad - centre)).astype(jnp.bfloat16)
-    value_grad = jnp.einsum(
-        "hij,ihd->jhd", probs.astype(jnp.bfloat16), mixed_grad, preferred_element_type=jnp.float32
-    )
-    query_nope_grad = (
-        jnp.einsum("hij,jhd->ihd", score_grad, key_nope, preferred_element_type=jnp.float32)
-        * score_scale
-    )
-    query_rope_grad = (
-        jnp.einsum("hij,jd->ihd", score_grad, key_rope, preferred_element_type=jnp.float32)
-        * score_scale
-    )
-    key_nope_grad = (
-        jnp.einsum(
-            "hij,ihd->jhd", score_grad, query[..., :NOPE], preferred_element_type=jnp.float32
-        )
-        * score_scale
-    )
-    key_rope_grad = (
-        jnp.einsum("hij,ihd->jd", score_grad, query[..., NOPE:], preferred_element_type=jnp.float32)
-        * score_scale
-    )
-    query_grad = jnp.concatenate(
-        [query_nope_grad, unrotate(query_rope_grad, cosine[:, None, :], sine[:, None, :])], axis=-1
-    )
-    query_grad = query_grad.astype(jnp.bfloat16).reshape(group_rows, heads_here * query_width)
-    expand_grad = (
-        jnp.concatenate([key_nope_grad, value_grad], axis=-1)
-        .astype(jnp.bfloat16)
-        .reshape(group_rows, heads_here * (NOPE + VDIM))
-    )
     query_gradient = trans_times(normed_all, query_grad)
     expand_gradient = trans_times(latent_normed, expand_grad)
     latent_normed_grad = times_trans(expand_grad, expand_weight)
@@ -1032,7 +1277,7 @@
     )
     compressed_grad = jnp.concatenate([latent_back, unrotate(key_rope_grad, cosine, sine)], axis=-1)
     compressed_grad = compressed_grad.astype(jnp.bfloat16)
-    latent_weight_gradient = trans_times(normed_all, compressed_grad)
+    latent_weight_gradient = trans_times(compressed_grad, normed_all)
     normed_grad = sum_group(
         (
             times_trans(query_grad, query_weight) + times_trans(compressed_grad, latent_weight)
@@ -1052,15 +1297,27 @@
             output_gradient.astype(jnp.bfloat16), "expert", scatter_dimension=1, tiled=True
         ).astype(jnp.float32),
     )
-    totals = lax.psum(
-        (
+    latent_columns = latent_weight.shape[1]
+    filled = jnp.concatenate(
+        [
             latent_weight_gradient,
-            latent_gain_gradient,
-            router_gradient,
-            first_gain_gradient,
-            second_gain_gradient,
-        ),
-        ("expert", "weight"),
+            router_gradient.T,
+            first_gain_gradient[None],
+            second_gain_gradient[None],
+            jnp.pad(latent_gain_gradient, (0, width - LATENT))[None],
+        ],
+        axis=0,
+    ).astype(jnp.bfloat16)
+    wanted = -(-filled.shape[0] // 64) * 64
+    filled = jnp.pad(filled, ((0, wanted - filled.shape[0]), (0, 0)))
+    total = total_over_all(filled, 7)
+    gains_at = latent_columns + expert_count
+    totals = (
+        total[:latent_columns].T,
+        total[gains_at + 2, :LATENT],
+        total[latent_columns:gains_at].T,
+        total[gains_at],
+        total[gains_at + 1],
     )
     return (
         layer_out,

time: 1240 us -> 1010 us (0.81)
  waiting for transfers between devices: 290 us -> 28 us
  Pallas kernels: 655 us -> 744 us
  matrix products: 148 us -> 67.1 us
  local copies, waits for them, and re-layouts: 38.8 us -> 97.8 us
  blocking collectives: 41.3 us -> 0 us
    psum x1 -> x0, waiting for transfers between devices: 152 us -> none  [per_device(): lax.psum((latent_weight_gradient, latent_gain_gradient, router_gradient,...]
    pallas_call x1 -> x3, Pallas kernels: 194 us -> 283 us  [the longest x2 207 us: sum_all(): pl.pallas_call(functools.partial(sum_all_kernel, inner, len(ins), len(out...]
    reduce_scatter x1 -> x0, waiting for transfers between devices: 88.7 us -> none  [per_device(): lax.psum_scatter(out_dense, both, scatter_dimension=0, tiled=True)]
    dot_general x3 -> x0, matrix products: 59.5 us -> none  [the longest x1 20.3 us: per_device(): jnp.einsum('jsf,jsd->jfd', lift_grad, rows_slots, preferred_element_type=...]
    psum x1 -> x0, blocking collectives: 41.3 us -> none  [per_device(): lax.psum((latent_weight_gradient, latent_gain_gradient, router_gradient,...]
    unnamed x156 -> x193, local copies, waits for them, and re-layouts: 25.1 us -> 62 us
    dot_general x7 -> x4, matrix products: 41.6 us -> 12.7 us  [trans_times(): lax.dot_general(left, right, (((0,), (0,)), ((), ())), preferred_element_...]
    reduce_scatter x1, waiting for transfers between devices: 19.9 us -> 0.01 us  [per_device(): lax.psum_scatter(query_gradient.astype(jnp.bfloat16), 'expert', scatter_d...]
  transfers between devices with their start and end apart: 7 -> 5, of which waited for: 4 -> 1; matrix products, arithmetic and copies ran while one was open for 11% -> 8% of each run, Pallas kernels for 33% -> 42%
where the time goes in v2:
time: 1010 us; the launch traced here: 1000 us
  Pallas kernels  744 us (74%)
  local copies, waits for them, and re-layouts  97.8 us (10%)
  matrix products  67.1 us (7%)
  other arithmetic  41.8 us (4%)
  waiting for transfers between devices  28 us (3%)
  between operations  15.3 us (2%)
    pallas_call x6, Pallas kernels, call(): pl.pallas_call(kernel, grid=(grid,), in_specs=[s for _, s in ins], out_sp...  212 us
    pallas_call x2, Pallas kernels, sum_all(): pl.pallas_call(functools.partial(sum_all_kernel, inner, len(ins), len(out...  207 us
    pallas_call x1, Pallas kernels, gather_all(): pl.pallas_call(gather_all_kernel, out_shape=out, in_specs=[pl.BlockSpec(m...  162 us
    pallas_call x1, Pallas kernels, total_over_all(): pl.pallas_call(total_kernel, out_shape=out, in_specs=[pl.BlockSpec(memory...  76.2 us
    unnamed x193, local copies, waits for them, and re-layouts  62 us
    pallas_call x2, Pallas kernels, sum_group(): pl.pallas_call(sum_group_kernel, out_shape=out, in_specs=[pl.BlockSpec(me...  43.6 us
    pallas_call x2, Pallas kernels, gather_group(): pl.pallas_call(gather_group_kernel, out_shape=out, in_specs=[pl.BlockSpec...  43.5 us
    all_gather x1, waiting for transfers between devices, per_device(): cotangent_all = lax.all_gather(cotangent_wide, both, axis=0, tiled=True)  28 us
  transfers between devices with their start and end apart: 5, of which 1 were waited for; matrix products, arithmetic and copies ran while one was open for 8% of the time, Pallas kernels for 42%

profile of v2, /device:TPU:0, one launch (start us, length us, event | category | flops | bytes accessed | tf_op | source)
XLA Modules:
  0.0 1000.2 jit_solution(9803071209061187506)
XLA Ops:
  12.4 2.1 fusion.18.x_ref
  14.5 22.5 %shard_map.297 = bf16[4,160,2048]{2,1,0:T(8,128)(2,1)} custom-call(bf16[160,2048]{1,0:T(8,128)(2,1)} %fusion.18.x_ref), custom_call_target="tpu_custom_call" | custom-call | bytes 3276800 | tf_op jit(solution)/shard_map/pallas_call | solution.py:673
  37.1 4.6 fusion.80
  43.2 2.0 convolution_convert_fusion.5
  45.2 2.9 reshape.374
  49.4 1.8 copy.151
  51.2 5.4 copy.118
  57.0 5.4 fusion.81
  66.6 1.9 copy-done
  70.0 3.1 convolution_convert_fusion.1
  73.1 21.8 %shard_map.298 = f32[160,2048]{1,0:T(8,128)} custom-call(bf16[4,160,2048]{2,1,0:T(8,128)(2,1)} %bitcast.140), custom_call_target="tpu_custom_call" | custom-call | bytes 3932160 | tf_op jit(solution)/shard_map/pallas_call | solution.py:736
  106.3 162.0 %shard_map.299 = bf16[32,160,2176]{2,1,0:T(8,128)(2,1)} custom-call(bf16[160,2176]{1,0:T(8,128)(2,1)} %concatenate.52.x_ref), custom_call_target="tpu_custom_call" | custom-call | bytes 22978560 | tf_op jit(solution)/shard_map/pallas_call | solution.py:436
  270.3 28.0 %all-gather.2.cloned.1.call-done.value_ref.marks_ref.refs_1_ = bf16[5120,2176]{1,0:T(8,128)(2,1)} async-done(((bf16[160,2176]{1,0:T(8,128)(2,1)}), bf16[5120,2176]{1,0:T(8,128)(2,1)}) %all-gather.2.cloned.1.call-update) | async-done | bytes 22282256 | tf_op jit(solution)/shard_map/all_gather | solution.py:1008
  298.3 28.4 %shard_map.300 = (bf16[8,640,2048]{2,1,0:T(8,128)(2,1)}, f32[5120,128]{1,0:T(8,128)}) custom-call(bf16[8,128]{1,0:T(8,128)(2,1)} %get-tuple-element.99.here_ref, bf16[5120,2176]{1,0:T(8,128)(2,1)} %all-gather.2.cloned.1.call-done.value_ref.marks_ref.refs_1_, bf16[128,2048]{1,0:T(8,128)(2,1)} %pad.25.down_ref), custom_call_target="tpu_custom_call" | custom-call | flops 9395240960 | bytes 46401536 | tf_op jit(solution)/shard_map/pallas_call | solution.py:258
  326.7 33.4 %shard_map.301 = (bf16[8,640,2048]{2,1,0:T(8,128)(2,1)}, f32[8,640,128]{2,1,0:T(8,128)}, bf16[5120,128]{1,0:T(8,128)(2,1)}, bf16[5120,128]{1,0:T(8,128)(2,1)}, bf16[5120,128]{1,0:T(8,128)(2,1)}) custom-call(bf16[8,128]{1,0:T(8,128)(2,1)} %get-tuple-element.99.here_ref, bf16[8,128]{1,0:T(8,128)(2,1)} %get-tuple-element.98.twice_ref, ...), custom_call_target="tpu_custom_call" | custom-call | flops 12079595520 | bytes 75763712 | tf_op jit(solution)/shard_map/pallas_call | solution.py:258
  360.0 64.9 %shard_map.302 = (bf16[8,640,352]{2,1,0:T(8,128)(2,1)}, bf16[8,640,352]{2,1,0:T(8,128)(2,1)}, bf16[8,640,352]{2,1,0:T(8,128)(2,1)}, bf16[8,640,2048]{2,1,0:T(8,128)(2,1)}, f32[8,640,128]{2,1,0:T(8,128)}) custom-call(bf16[8,640,2048]{2,1,0:T(8,128)(2,1)} %get-tuple-element.39.rows_ref.refs_0_, bf16[8,640,2048]{2,1,0:T(8,128)(2,1)} %get-tuple-element.40.grads_ref.refs_1_, ...), custom_call_target="tpu_custom_call" | custom-call | flops 36909875200 | bytes 113573888 | tf_op jit(solution)/shard_map/pallas_call | solution.py:258
  424.9 31.0 %shard_map.305 = bf16[5120,2176]{1,0:T(8,128)(2,1)} custom-call(bf16[8,128]{1,0:T(8,128)(2,1)} %get-tuple-element.99.here_ref, bf16[8,128]{1,0:T(8,128)(2,1)} %get-tuple-element.101.high_ref, bf16[8,128]{1,0:T(8,128)(2,1)} %get-tuple-element.100.low_ref, bf16[5120,2176]{1,0:T(8,128)(2,1)} %all-gather.2.cloned.1.call-done.value_ref.marks_ref.refs_1_, ...), custom_call_target="tpu_custom_call" | custom-call | flops 12079595520 | bytes 71833600 | tf_op jit(solution)/shard_map/pallas_call | solution.py:258
  455.9 104.4 %shard_map.306 = (f32[160,2176]{1,0:T(8,128)}, f32[128,2048]{1,0:T(8,128)}, f32[128,2048]{1,0:T(8,128)}, f32[128,2048]{1,0:T(8,128)}) custom-call(bf16[32,160,2176]{2,1,0:T(8,128)(2,1)} %bitcast.123, bf16[5120,2176]{1,0:T(8,128)(2,1)} %bitcast.120, bf16[5120,2176]{1,0:T(8,128)(2,1)} %all-gather.2.cloned.1.call-done.value_ref.marks_ref.refs_1_, ...), custom_call_target="tpu_custom_call" | custom-call | flops 8053063680 | bytes 75317248 | tf_op jit(solution)/shard_map/pallas_call | solution.py:610
  564.1 3.6 multiply_reduce_fusion.2
  569.6 21.0 %shard_map.307 = bf16[4,160,2048]{2,1,0:T(8,128)(2,1)} custom-call(bf16[160,2048]{1,0:T(8,128)(2,1)} %get-tuple-element.71.x_ref), custom_call_target="tpu_custom_call" | custom-call | bytes 3276800 | tf_op jit(solution)/shard_map/pallas_call | solution.py:673
  590.6 4.4 convolution_convert_fusion.7
  599.3 3.4 fusion.28
  604.6 2.0 convolution_convert_fusion.6
  611.3 6.0 all-to-all-start
  619.4 3.1 convolution_convert_fusion.3
  622.6 2.0 fusion.29
  625.7 27.3 %shard_map.303.rows_ref = bf16[8,640,2048]{2,1,0:T(8,128)(2,1)} custom-call(bf16[8,640,352]{2,1,0:T(8,128)(2,1)} %get-tuple-element.42.hidden_ref.refs_4_, bf16[8,352,2048]{2,1,0:T(8,128)(2,1)} %down_ref.3), custom_call_target="tpu_custom_call" | custom-call | flops 7381975040 | bytes 36110336 | tf_op jit(solution)/shard_map/pallas_call | solution.py:258
  652.9 26.8 %shard_map.304 = bf16[5120,2048]{1,0:T(8,128)(2,1)} custom-call(bf16[8,128]{1,0:T(8,128)(2,1)} %get-tuple-element.99.here_ref, bf16[5120,2176]{1,0:T(8,128)(2,1)} %all-gather.2.cloned.1.call-done.value_ref.marks_ref.refs_1_, bf16[8,640,2048]{2,1,0:T(8,128)(2,1)} %shard_map.303.rows_ref, bf16[5120,128]{1,0:T(8,128)(2,1)} %get-tuple-element.43.hidden_ref.refs_4_, ...), custom_call_target="tpu_custom_call" | custom-call | flops 9395240960 | bytes 66062336 | tf_op jit(solution)/shard_map/pallas_call | solution.py:258
  679.8 4.3 multiply_reduce_fusion.1
  686.1 4.1 convolution_convert_fusion
  690.1 5.8 fusion.82
  698.5 6.3 add_convert_fusion
  705.4 21.9 %shard_map.309 = f32[160,2048]{1,0:T(8,128)} custom-call(bf16[4,160,2048]{2,1,0:T(8,128)(2,1)} %bitcast.139), custom_call_target="tpu_custom_call" | custom-call | bytes 3932160 | tf_op jit(solution)/shard_map/pallas_call | solution.py:736
  727.4 2.3 fusion.24
  730.8 3.4 convolution_convert_fusion.2
  734.2 9.5 concatenate.56
  743.7 1.9 pad.29.p_ref
  745.6 76.2 %shard_map.310 = bf16[704,2048]{1,0:T(8,128)(2,1)} custom-call(bf16[704,2048]{1,0:T(8,128)(2,1)} %pad.29.p_ref), custom_call_target="tpu_custom_call" | custom-call | bytes 5767168 | tf_op jit(solution)/shard_map/pallas_call | solution.py:886
  821.8 2.6 convert_element_type.168
  824.4 1.9 fusion.76
  827.8 102.4 %shard_map.308 = (f32[160,2048]{1,0:T(8,128)}, f32[8,352,2048]{2,1,0:T(8,128)}, f32[8,352,2048]{2,1,0:T(8,128)}, f32[8,352,2048]{2,1,0:T(8,128)}) custom-call(bf16[32,160,2048]{2,1,0:T(8,128)(2,1)} %bitcast.128, bf16[8,640,2048]{2,1,0:T(8,128)(2,1)} %get-tuple-element.39.rows_ref.refs_0_, bf16[8,640,2048]{2,1,0:T(8,128)(2,1)} %get-tuple-element.40.grads_ref.refs_1_, ...), custom_call_target="tpu_custom_call" | custom-call | flops 22145925120 | bytes 144244736 | tf_op jit(solution)/shard_map/pallas_call | solution.py:610
  931.6 2.9 add_convert_fusion.1
  934.5 2.8 fusion.21
  937.3 2.8 slice_bitcast_fusion
  946.2 1.9 convert_element_type.170
  948.2 18.5 %copy.171 = f32[8,2048,352]{1,2,0:T(8,128)} copy(f32[8,2048,352]{1,2,0:T(8,128)} %bitcast.127) | data formatting | bytes 46137344
  966.7 18.5 %copy.172 = f32[8,2048,352]{1,2,0:T(8,128)} copy(f32[8,2048,352]{1,2,0:T(8,128)} %bitcast.126) | data formatting | bytes 46137344
  985.2 8.2 copy.173
  (289 shorter events, 61.7 us)
Async XLA Ops:
  7.2 291.1 %all-gather.2.cloned.1.call-start = ((), (), s32[]{:S(2)}) async-start(), calls=%async_computation.4 | async-start | bytes 22978560 | tf_op jit(solution)/shard_map/all_gather | solution.py:1008
  7.2 49.3 %copy-start.77 = (f32[32]{0:T(128)}, f32[32]{0:T(128)S(1)}, u32[]{:S(2)}) copy-start(f32[32]{0:T(128)S(1)} %negate_power_fusion) | copy-start | bytes 388
  10.0 27.1 %copy-start.69 = (f32[160]{0:T(256)}, f32[160]{0:T(256)S(1)}, u32[]{:S(2)}) copy-start(f32[160]{0:T(256)S(1)} %get-tuple-element.95) | copy-start | bytes 1924
  10.6 45.9 %copy-start.62 = (f32[640]{0:T(1024)}, f32[640]{0:T(1024)S(1)}, u32[]{:S(2)}) copy-start(f32[640]{0:T(1024)S(1)} %fusion.58) | copy-start | bytes 7684
  37.1 6.1 copy-start.79
  37.1 6.1 copy-start.83
  41.7 14.9 %copy-start.16 = (f32[640,576]{0,1:T(8,128)}, f32[640,576]{0,1:T(8,128)S(1)}, u32[]{:S(2)}) copy-start(f32[640,576]{0,1:T(8,128)S(1)} %fusion.80) | copy-start | bytes 4423684
  49.4 14.3 %copy-start.12 = (bf16[640,4,128]{2,1,0:T(4,128)(2,1)}, bf16[640,4,128]{2,1,0:T(4,128)(2,1)S(1)}, u32[]{:S(2)}) copy-start(bf16[640,4,128]{2,1,0:T(4,128)(2,1)S(1)} %get-tuple-element.84) | copy-start | bytes 1966084
  51.2 15.4 %copy-start.20 = (bf16[640,4,128]{0,2,1:T(8,128)(2,1)}, bf16[640,4,128]{0,2,1:T(8,128)(2,1)S(1)}, u32[]{:S(2)}) copy-start(bf16[640,4,128]{0,2,1:T(8,128)(2,1)S(1)} %copy.151) | copy-start | bytes 1966084
  57.0 5.4 copy-start.35
  57.0 5.4 copy-start.37
  57.0 5.5 copy-start.47
  57.0 5.5 copy-start.49
  73.1 21.8 %copy-start.8 = (bf16[160,2048]{1,0:T(8,128)(2,1)S(1)}, bf16[160,2048]{1,0:T(8,128)(2,1)}, u32[]{:S(2)}) copy-start(bf16[160,2048]{1,0:T(8,128)(2,1)} %param.18) | copy-start | bytes 1966084
  97.8 7.5 copy-start.13
  98.2 465.9 %copy-start.45 = (f32[160,64]{0,1:T(8,128)}, f32[160,64]{0,1:T(8,128)S(1)}, u32[]{:S(2)}) copy-start(f32[160,64]{0,1:T(8,128)S(1)} %fusion.35) | copy-start | bytes 122884
  100.3 842.6 %reduce-scatter.6.cloned.1.call-start = ((), (), s32[]{:S(2)}) async-start(), calls=%async_computation.6 | async-start | bytes 1179648 | tf_op jit(solution)/shard_map/reduce_scatter | solution.py:1293
  567.8 27.1 %slice-start = ((s8[6553600]{0:T(1024)(128)(4,1)}), s8[2359296]{0:T(1024)(128)(4,1)S(1)}, s32[]{:S(2)}) async-start(s8[6553600]{0:T(1024)(128)(4,1)} %bitcast.121), calls=%async_computation.8 | async-start | bytes 4718592
  590.5 4.4 slice-start.1
  590.5 4.4 copy-start.52
  610.2 7.2 copy-start.2
  610.2 7.2 copy-start.48
  610.2 7.2 copy-start.50
  611.3 328.7 %all-to-all-start = ((bf16[264,8,256]{2,0,1:T(8,128)(2,1)}), bf16[264,8,256]{2,0,1:T(8,128)(2,1)}, u32[]{:S(2)}, u32[]{:S(2)}) async-start(bf16[264,8,256]{2,0,1:T(8,128)(2,1)} %pad_maximum_fusion.1), calls=%async_computation.3 | async-start | bytes 2162688 | tf_op jit(solution)/shard_map/all_to_all | solution.py:1172
  617.3 327.1 %reduce-scatter.8.cloned.1.call-start = ((), (), s32[]{:S(2)}) async-start(), calls=%async_computation.7 | async-start | bytes 2359296 | tf_op jit(solution)/shard_map/reduce_scatter | solution.py:1296
  622.6 323.7 %reduce-scatter.4.cloned.1.call-start = ((), (), s32[]{:S(2)}) async-start(), calls=%async_computation.5 | async-start | bytes 3538944 | tf_op jit(solution)/shard_map/reduce_scatter | solution.py:1290
  679.8 4.3 copy-start.29
  679.8 4.3 copy-start.31
  686.1 11.9 %copy-start.58 = (bf16[640,32]{0,1:T(8,128)(2,1)}, bf16[640,32]{0,1:T(8,128)(2,1)S(1)}, u32[]{:S(2)}) copy-start(bf16[640,32]{0,1:T(8,128)(2,1)S(1)} %get-tuple-element.88) | copy-start | bytes 122884
  686.1 12.0 %copy-start.60 = (bf16[640,32]{0,1:T(8,128)(2,1)}, bf16[640,32]{0,1:T(8,128)(2,1)S(1)}, u32[]{:S(2)}) copy-start(bf16[640,32]{0,1:T(8,128)(2,1)S(1)} %get-tuple-element.89) | copy-start | bytes 122884
  698.0 6.8 copy-start.39
  698.5 6.3 copy-start.67
  705.4 21.9 %copy-start.9 = (bf16[160,2048]{1,0:T(8,128)(2,1)S(1)}, bf16[160,2048]{1,0:T(8,128)(2,1)}, u32[]{:S(2)}) copy-start(bf16[160,2048]{1,0:T(8,128)(2,1)} %param.18) | copy-start | bytes 1966084
  705.4 21.9 %copy-start.55 = (f32[2048]{0:T(1024)S(1)}, f32[2048]{0:T(1024)}, u32[]{:S(2)}) copy-start(f32[2048]{0:T(1024)} %param.22) | copy-start | bytes 24580
  705.4 21.9 %copy-start.70 = (f32[160]{0:T(256)S(1)}, f32[160]{0:T(256)}, u32[]{:S(2)}) copy-start(f32[160]{0:T(256)} %copy-done.69) | copy-start | bytes 1924
  705.4 25.3 %copy-start.23 = (bf16[4,160,2048]{2,1,0:T(8,128)(2,1)S(1)}, bf16[4,160,2048]{2,1,0:T(8,128)(2,1)}, u32[]{:S(2)}) copy-start(bf16[4,160,2048]{2,1,0:T(8,128)(2,1)} %shard_map.297) | copy-start | bytes 7864324
  827.8 102.4 %copy-start.75 = (f32[160]{0:T(256)S(1)}, f32[160]{0:T(256)}, u32[]{:S(2)}) copy-start(f32[160]{0:T(256)} %get-tuple-element.65) | copy-start | bytes 1924
  930.2 4.3 copy-start.10
  930.2 4.3 copy-start.11
  930.2 4.3 copy-start.71
  930.2 4.3 copy-start.74
  931.6 5.7 copy-start.7
  948.2 37.0 %slice-start.2 = ((s8[23068672]{0:T(1024)(128)(4,1)}), s8[4194304]{0:T(1024)(128)(4,1)S(1)}, s32[]{:S(2)}) async-start(s8[23068672]{0:T(1024)(128)(4,1)} %bitcast.124), calls=%async_computation.10 | async-start | bytes 8388608
  948.2 37.0 %slice-start.3 = ((s8[23068672]{0:T(1024)(128)(4,1)}), s8[4194304]{0:T(1024)(128)(4,1)S(1)}, s32[]{:S(2)}) async-start(s8[23068672]{0:T(1024)(128)(4,1)} %bitcast.124), calls=%async_computation.11 | async-start | bytes 8388608
  948.2 37.0 %slice-start.4 = ((s8[23068672]{0:T(1024)(128)(4,1)}), s8[4194304]{0:T(1024)(128)(4,1)S(1)}, s32[]{:S(2)}) async-start(s8[23068672]{0:T(1024)(128)(4,1)} %bitcast.124), calls=%async_computation.12 | async-start | bytes 8388608
  966.7 18.5 %slice-start.5 = ((s8[23068672]{0:T(1024)(128)(4,1)}), s8[4194304]{0:T(1024)(128)(4,1)S(1)}, s32[]{:S(2)}) async-start(s8[23068672]{0:T(1024)(128)(4,1)} %bitcast.124), calls=%async_computation.13 | async-start | bytes 8388608
  966.7 18.5 %slice-start.6 = ((s8[23068672]{0:T(1024)(128)(4,1)}), s8[4194304]{0:T(1024)(128)(4,1)S(1)}, s32[]{:S(2)}) async-start(s8[23068672]{0:T(1024)(128)(4,1)} %bitcast.124), calls=%async_computation.14 | async-start | bytes 8388608
  966.7 18.5 %slice-start.7 = ((s8[23068672]{0:T(1024)(128)(4,1)}), s8[2097152]{0:T(1024)(128)(4,1)S(1)}, s32[]{:S(2)}) async-start(s8[23068672]{0:T(1024)(128)(4,1)} %bitcast.124), calls=%async_computation.15 | async-start | bytes 4194304
  (51 other events, 112.3 us)
Sparse Core Ops, SparseCore 0:
  100.4 197.8 all-gather.1
  606.8 72.8 reduce-scatter.5
  683.2 67.9 reduce-scatter.7
  754.7 94.3 reduce-scatter.3

commit v3 on v2

--- a/solution.py
+++ b/solution.py
@@ -97,26 +97,53 @@
     return picks, rank
 
 
-def gather_rows(picks, values, out_ref):
-    rows = jnp.dot(
-        jnp.concatenate(picks, axis=0).astype(jnp.bfloat16),
-        values,
-        preferred_element_type=jnp.float32,
-    )
-    for e in range(len(picks)):
-        out_ref[e] = rows[e * 2 * CAP : (e + 1) * 2 * CAP].astype(jnp.bfloat16)
-
-
-def grads_kernel(here_ref, value_ref, down_ref, rows_ref, back_ref):
+def pair_slots(marks_ref, here_ref, local_experts, pair):
+    count = marks_ref.shape[0] // pair
+    return [
+        token_slots(marks_ref[j * pair : (j + 1) * pair], here_ref[...], local_experts, pair // 2)
+        for j in range(count)
+    ]
+
+
+def slot_part(value, e):
+    return value[e * 2 * CAP : (e + 1) * 2 * CAP]
+
+
+def gather_rows(slots, values, pair, out_ref):
+    rows = [
+        jnp.dot(
+            jnp.concatenate(picks, axis=0).astype(jnp.bfloat16),
+            values[j * pair : (j + 1) * pair],
+            preferred_element_type=jnp.float32,
+        )
+        for j, (picks, _) in enumerate(slots)
+    ]
+    for e in range(out_ref.shape[0]):
+        together = jnp.concatenate([slot_part(value, e) for value in rows], axis=0)
+        out_ref[e] = together.astype(jnp.bfloat16)
+
+
+def spread_rows(slots, rows_ref):
+    local_experts = rows_ref.shape[0]
+    rows = [rows_ref[e].astype(jnp.float32) for e in range(local_experts)]
+    totals = []
+    for j, (picks, _) in enumerate(slots):
+        part = jnp.concatenate([slot_part(value, j) for value in rows], axis=0)
+        pick = jnp.concatenate(picks, axis=0).astype(jnp.bfloat16)
+        totals.append(trans_times(pick, part.astype(jnp.bfloat16)))
+    return jnp.concatenate(totals, axis=0)
+
+
+def grads_kernel(pair, here_ref, value_ref, down_ref, rows_ref, back_ref):
     width = rows_ref.shape[2]
-    local_experts, half = rows_ref.shape[0], value_ref.shape[0] // 2
-    picks, _ = token_slots(value_ref[:, width:], here_ref[...], local_experts, half)
+    slots = pair_slots(value_ref.at[:, width:], here_ref, rows_ref.shape[0], pair)
     values = value_ref[:, :width]
-    gather_rows(picks, values, rows_ref)
+    gather_rows(slots, values, pair, rows_ref)
     back_ref[...] = times_trans(values, down_ref[...])
 
 
 def rows_kernel(
+    pair,
     here_ref,
     twice_ref,
     marks_ref,
@@ -131,14 +158,15 @@
     lift_grad_ref,
 ):
     width = rows_ref.shape[2]
-    local_experts, half = rows_ref.shape[0], value_ref.shape[0] // 2
-    picks, _ = token_slots(marks_ref[...], here_ref[...], local_experts, half)
+    slots = pair_slots(marks_ref, here_ref, rows_ref.shape[0], pair)
     values = value_ref[:, :width]
-    gather_rows(picks, values, rows_ref)
-    mixing = times_trans(twice_ref[...], value_ref[:, width:])
-    for e in range(local_experts):
-        column = jnp.sum(picks[e] * mixing[e : e + 1], axis=1, keepdims=True)
-        mix_ref[e] = jnp.broadcast_to(column, mix_ref.shape[1:])
+    gather_rows(slots, values, pair, rows_ref)
+    for j, (picks, _) in enumerate(slots):
+        mixing = times_trans(twice_ref[...], value_ref[j * pair : (j + 1) * pair, width:])
+        for e, pick in enumerate(picks):
+            column = jnp.sum(pick * mixing[e : e + 1], axis=1, keepdims=True)
+            column = jnp.broadcast_to(column, (2 * CAP, lanes))
+            mix_ref[e, j * 2 * CAP : (j + 1) * 2 * CAP] = column
     gate = times_trans(values, gate_ref[...])
     lift = times_trans(values, up_ref[...])
     back = back_ref[...]
@@ -149,50 +177,49 @@
     lift_grad_ref[...] = (back * active).astype(jnp.bfloat16)
 
 
-def experts_kernel(
+def forward_kernel(
     rows_ref,
-    grads_ref,
     mix_ref,
     gate_ref,
     up_ref,
     down_ref,
     hidden_ref,
-    gate_grad_ref,
-    lift_grad_ref,
-    returned_ref,
-    mix_grad_ref,
+    mixed_ref,
+    slope_ref,
+    active_ref,
+    produced_ref,
 ):
-    rows, gate_matrix, up_matrix = rows_ref[0], gate_ref[0], up_ref[0]
-    gate = times_trans(rows, gate_matrix)
-    lift = times_trans(rows, up_matrix)
-    back = times_trans(grads_ref[0], down_ref[0])
+    rows = rows_ref[0]
+    gate = times_trans(rows, gate_ref[0])
+    lift = times_trans(rows, up_ref[0])
     mix = mix_ref[0][:, :1]
     sigma = jax.nn.sigmoid(gate)
     active = gate * sigma
     hidden = active * lift
-    mix_grad = jnp.sum(hidden * back, axis=1, keepdims=True)
+    mixed_hidden = (mix * hidden).astype(jnp.bfloat16)
+    hidden_ref[0] = hidden.astype(jnp.bfloat16)
+    mixed_ref[0] = mixed_hidden
+    slope_ref[0] = (mix * lift * sigma * (1.0 + gate * (1.0 - sigma))).astype(jnp.bfloat16)
+    active_ref[0] = (mix * active).astype(jnp.bfloat16)
+    produced_ref[0] = matmul(mixed_hidden, down_ref[0]).astype(jnp.bfloat16)
+
+
+def backward_kernel(turn, ins, outs):
+    grads_ref, hidden_ref, slope_ref, active_ref, gate_ref, up_ref, down_ref = ins
+    gate_grad_ref, lift_grad_ref, returned_ref, mix_grad_ref = outs
+    back = times_trans(grads_ref[0], down_ref[0])
+    mix_grad = jnp.sum(hidden_ref[0].astype(jnp.float32) * back, axis=1, keepdims=True)
     mix_grad_ref[0] = jnp.broadcast_to(mix_grad, mix_grad_ref.shape[1:])
-    hidden_ref[0] = (mix * hidden).astype(jnp.bfloat16)
-    back = back * mix
-    gate_grad = (back * lift * sigma * (1.0 + gate * (1.0 - sigma))).astype(jnp.bfloat16)
-    lift_grad = (back * active).astype(jnp.bfloat16)
+    gate_grad = (back * slope_ref[0].astype(jnp.float32)).astype(jnp.bfloat16)
+    lift_grad = (back * active_ref[0].astype(jnp.float32)).astype(jnp.bfloat16)
     gate_grad_ref[0] = gate_grad
     lift_grad_ref[0] = lift_grad
-    returned = matmul(gate_grad, gate_matrix) + matmul(lift_grad, up_matrix)
+    returned = matmul(gate_grad, gate_ref[0]) + matmul(lift_grad, up_ref[0])
     returned_ref[0] = returned.astype(jnp.bfloat16)
 
 
-def produce_kernel(hidden_ref, down_ref, out_ref):
-    out_ref[0] = matmul(hidden_ref[0], down_ref[0]).astype(jnp.bfloat16)
-
-
-def spread_rows(picks, rows_ref):
-    rows = jnp.concatenate([rows_ref[e].astype(jnp.float32) for e in range(len(picks))], axis=0)
-    pick = jnp.concatenate(picks, axis=0).astype(jnp.bfloat16)
-    return trans_times(pick, rows.astype(jnp.bfloat16))
-
-
 def back_kernel(
+    pair,
     here_ref,
     high_ref,
     low_ref,
@@ -206,27 +233,27 @@
     out_ref,
 ):
     width = rows_ref.shape[2]
-    local_experts, half = rows_ref.shape[0], out_ref.shape[0] // 2
-    picks, rank = token_slots(marks_ref[...], here_ref[...], local_experts, half)
-    total = spread_rows(picks, rows_ref)
+    slots = pair_slots(marks_ref, here_ref, rows_ref.shape[0], pair)
+    total = spread_rows(slots, rows_ref)
     total = total + matmul(gate_grad_ref[...], gate_ref[...])
     total = total + matmul(lift_grad_ref[...], up_ref[...])
     out_ref[:, :width] = total.astype(jnp.bfloat16)
-    choice = lax.broadcasted_iota(jnp.int32, rank.shape, 0).astype(jnp.float32)
-    mix_grad = jnp.zeros(rank.shape, jnp.float32)
-    for e in range(local_experts):
-        row = jnp.sum(picks[e] * mix_grad_ref[e][:, :1], axis=0, keepdims=True)
-        mix_grad = mix_grad + jnp.where(choice == rank[e : e + 1], row, 0.0)
-    high = mix_grad.astype(jnp.bfloat16)
-    low = (mix_grad - high.astype(jnp.float32)).astype(jnp.bfloat16)
-    sent = trans_times(high, high_ref[...]) + trans_times(low, low_ref[...])
-    out_ref[:, width:] = sent.astype(jnp.bfloat16)
-
-
-def out_kernel(here_ref, marks_ref, rows_ref, hidden_ref, down_ref, out_ref):
-    local_experts, half = rows_ref.shape[0], out_ref.shape[0] // 2
-    picks, _ = token_slots(marks_ref[...], here_ref[...], local_experts, half)
-    total = spread_rows(picks, rows_ref)
+    for j, (picks, rank) in enumerate(slots):
+        choice = lax.broadcasted_iota(jnp.int32, rank.shape, 0).astype(jnp.float32)
+        mix_grad = jnp.zeros(rank.shape, jnp.float32)
+        for e, pick in enumerate(picks):
+            column = slot_part(mix_grad_ref[e], j)[:, :1]
+            row = jnp.sum(pick * column, axis=0, keepdims=True)
+            mix_grad = mix_grad + jnp.where(choice == rank[e : e + 1], row, 0.0)
+        high = mix_grad.astype(jnp.bfloat16)
+        low = (mix_grad - high.astype(jnp.float32)).astype(jnp.bfloat16)
+        sent = trans_times(high, high_ref[...]) + trans_times(low, low_ref[...])
+        out_ref[j * pair : (j + 1) * pair, width:] = sent.astype(jnp.bfloat16)
+
+
+def out_kernel(pair, here_ref, marks_ref, rows_ref, hidden_ref, down_ref, out_ref):
+    slots = pair_slots(marks_ref, here_ref, rows_ref.shape[0], pair)
+    total = spread_rows(slots, rows_ref)
     total = total + matmul(hidden_ref[...], down_ref[...])
     out_ref[...] = total.astype(jnp.bfloat16)
 
@@ -918,12 +945,13 @@
     outs[2][...] += trans_times(hidden_ref[...], cotangent)
 
 
-def weight_kernel(turn, ins, outs):
-    rows_ref, grads_ref, gate_grad_ref, lift_grad_ref, hidden_ref = ins
+def weight_kernel(
+    rows_ref, grads_ref, gate_grad_ref, lift_grad_ref, hidden_ref, gate_out, up_out, down_out
+):
     rows = rows_ref[0]
-    outs[0][0] = trans_times(gate_grad_ref[0], rows)
-    outs[1][0] = trans_times(lift_grad_ref[0], rows)
-    outs[2][0] = trans_times(hidden_ref[0], grads_ref[0])
+    gate_out[0] = trans_times(gate_grad_ref[0], rows)
+    up_out[0] = trans_times(lift_grad_ref[0], rows)
+    down_out[0] = trans_times(hidden_ref[0], grads_ref[0])
 
 
 def per_device(
@@ -963,8 +991,8 @@
     expert_index = lax.axis_index("expert")
     expert_lanes = lax.axis_size("expert")
     blocks = expert_lanes * weight_count
-    pairs = blocks // 2
-    pair_rows = 2 * token_rows
+    pairs, quads = blocks // 2, blocks // 4
+    pair_rows, quad_rows = 2 * token_rows, 4 * token_rows
     all_rows = blocks * token_rows
     slot_rows = blocks * CAP
     choose = (
@@ -1006,14 +1034,14 @@
     slots_one = shape((local_experts, slot_rows, lanes), jnp.float32)
     gather_flops = 2 * all_rows * width * (2 * CAP * local_experts + shared_wide)
     cotangent_all = lax.all_gather(cotangent_wide, both, axis=0, tiled=True)
-    marks = (cotangent_all, pl.BlockSpec((pair_rows, lanes), lambda i: (i, width // lanes)))
+    marks = (cotangent_all, pl.BlockSpec((quad_rows, lanes), lambda i: (i, width // lanes)))
     grads_slots, shared_raw = call(
-        grads_kernel,
-        pairs,
-        [whole(here), (cotangent_all, pair_spec(cotangent_all, pairs)), whole(down_part)],
+        functools.partial(grads_kernel, pair_rows),
+        quads,
+        [whole(here), (cotangent_all, pair_spec(cotangent_all, quads)), whole(down_part)],
         [
-            (slots, slots_spec(slots, pairs)),
-            (shape((all_rows, shared_wide), jnp.float32), pl.BlockSpec((pair_rows, shared_wide), lambda i: (i, 0))),
+            (slots, slots_spec(slots, quads)),
+            (shape((all_rows, shared_wide), jnp.float32), pl.BlockSpec((quad_rows, shared_wide), lambda i: (i, 0))),
         ],
         gather_flops,
     )
@@ -1075,23 +1103,23 @@
     mixing_low = (mixing_at - mixing_high.astype(jnp.float32)).astype(jnp.bfloat16)
     normed_wide = jnp.concatenate([normed_two, mixing_high, mixing_low], axis=1)
     normed_tokens = gather_all(normed_wide, 2).reshape(all_rows, -1)
-    token_spec = pl.BlockSpec((pair_rows, shared_wide), lambda i: (i, 0))
+    token_spec = pl.BlockSpec((quad_rows, shared_wide), lambda i: (i, 0))
     token_shape = shape((all_rows, shared_wide), jnp.bfloat16)
     rows_slots, mix_slots, shared_hidden, shared_gate_grad, shared_lift_grad = call(
-        rows_kernel,
-        pairs,
+        functools.partial(rows_kernel, pair_rows),
+        quads,
         [
             whole(here),
             whole(twice),
             marks,
-            (normed_tokens, pair_spec(normed_tokens, pairs)),
+            (normed_tokens, pair_spec(normed_tokens, quads)),
             (shared_raw, token_spec),
             whole(gate_part),
             whole(up_part),
         ],
         [
-            (slots, slots_spec(slots, pairs)),
-            (slots_one, slots_spec(slots_one, pairs)),
+            (slots, slots_spec(slots, quads)),
+            (slots_one, slots_spec(slots_one, quads)),
             (token_shape, token_spec),
             (token_shape, token_spec),
             (token_shape, token_spec),
@@ -1100,55 +1128,91 @@
     )
     hidden_here = expert_gate.shape[2]
     gate_rows, up_rows = expert_gate.transpose(0, 2, 1), expert_up.transpose(0, 2, 1)
-    tile = slot_rows // 2
-    tile_spec = lambda n: pl.BlockSpec((1, tile, n), lambda i: (i // 2, i % 2, 0))
-    expert_spec = lambda m: pl.BlockSpec((1,) + m.shape[1:], lambda i: (i // 2, 0, 0))
+
+    def tile_spec(rows, n):
+        per = slot_rows // rows
+        return pl.BlockSpec((1, rows, n), lambda i: (i // per, i % per, 0))
+
+    def expert_spec(rows, matrix):
+        per = slot_rows // rows
+        return pl.BlockSpec((1,) + matrix.shape[1:], lambda i: (i // per, 0, 0))
+
+    large, small = 32 * CAP, 16 * CAP
     narrow = shape((local_experts, slot_rows, hidden_here), jnp.bfloat16)
     one_matmul = 2 * local_experts * slot_rows * width * hidden_here
-    routed_hidden, gate_grad, lift_grad, returned, mix_grad_slots = call(
-        experts_kernel,
-        2 * local_experts,
+    routed_hidden, mixed_hidden, slope, active, produced = call(
+        forward_kernel,
+        local_experts * (slot_rows // large),
         [
-            (rows_slots, tile_spec(width)),
-            (grads_slots, tile_spec(width)),
-            (mix_slots, tile_spec(lanes)),
-            (gate_rows, expert_spec(gate_rows)),
-            (up_rows, expert_spec(up_rows)),
-            (expert_down, expert_spec(expert_down)),
-        ],
+            (rows_slots, tile_spec(large, width)),
+            (mix_slots, tile_spec(large, lanes)),
+            (gate_rows, expert_spec(large, gate_rows)),
+            (up_rows, expert_spec(large, up_rows)),
+            (expert_down, expert_spec(large, expert_down)),
+        ],
+        [(narrow, tile_spec(large, hidden_here))] * 4 + [(slots, tile_spec(large, width))],
+        3 * one_matmul,
+    )
+    dense = shape((all_rows, width), jnp.bfloat16)
+    dense_wide = shape((all_rows, width + lanes), jnp.bfloat16)
+    (out_dense,) = call(
+        functools.partial(out_kernel, pair_rows),
+        quads,
         [
-            (narrow, tile_spec(hidden_here)),
-            (narrow, tile_spec(hidden_here)),
-            (narrow, tile_spec(hidden_here)),
-            (slots, tile_spec(width)),
-            (slots_one, tile_spec(lanes)),
-        ],
-        5 * one_matmul,
-    )
-    dense = shape((all_rows, width), jnp.bfloat16)
-    dense_spec = pl.BlockSpec((pair_rows, width), lambda i: (i, 0))
-    dense_wide = shape((all_rows, width + lanes), jnp.bfloat16)
+            whole(here),
+            marks,
+            (produced, slots_spec(slots, quads)),
+            (shared_hidden, token_spec),
+            whole(down_part),
+        ],
+        [(dense, pair_spec(dense, quads))],
+        gather_flops,
+    )
+    narrow_tile = tile_spec(small, hidden_here)
+    routed_out, (gate_grad, lift_grad, returned, mix_grad_slots) = sum_all(
+        out_dense.reshape(blocks, token_rows, width),
+        6,
+        backward_kernel,
+        local_experts * (slot_rows // small),
+        [
+            (grads_slots, tile_spec(small, width)),
+            (routed_hidden, narrow_tile),
+            (slope, narrow_tile),
+            (active, narrow_tile),
+            (gate_rows, expert_spec(small, gate_rows)),
+            (up_rows, expert_spec(small, up_rows)),
+            (expert_down, expert_spec(small, expert_down)),
+        ],
+        [
+            (narrow, narrow_tile),
+            (narrow, narrow_tile),
+            (slots, tile_spec(small, width)),
+            (slots_one, tile_spec(small, lanes)),
+        ],
+        3 * one_matmul,
+    )
     (back_dense,) = call(
-        back_kernel,
-        pairs,
+        functools.partial(back_kernel, pair_rows),
+        quads,
         [
             whole(here),
             whole(high_at),
             whole(low_at),
             marks,
-            (returned, slots_spec(slots, pairs)),
-            (mix_grad_slots, slots_spec(slots_one, pairs)),
+            (returned, slots_spec(slots, quads)),
+            (mix_grad_slots, slots_spec(slots_one, quads)),
             (shared_gate_grad, token_spec),
             (shared_lift_grad, token_spec),
             whole(gate_part),
             whole(up_part),
         ],
-        [(dense_wide, pair_spec(dense_wide, pairs))],
+        [(dense_wide, pair_spec(dense_wide, quads))],
         gather_flops + 2 * all_rows * width * shared_wide,
     )
     shared_sum = shape((shared_wide, width), jnp.float32)
     shared_out = (shared_sum, whole_spec(shared_sum))
     plain_spec = pl.BlockSpec((pair_rows, width), lambda i: (i, 0))
+    shared_spec = pl.BlockSpec((pair_rows, shared_wide), lambda i: (i, 0))
     back_here, shared_sums = sum_all(
         back_dense.reshape(blocks, token_rows, -1),
         3,
@@ -1157,9 +1221,9 @@
         [
             (normed_tokens, plain_spec),
             (cotangent_all, plain_spec),
-            (shared_gate_grad, token_spec),
-            (shared_lift_grad, token_spec),
-            (shared_hidden, token_spec),
+            (shared_gate_grad, shared_spec),
+            (shared_lift_grad, shared_spec),
+            (shared_hidden, shared_spec),
         ],
         [shared_out] * 3,
         6 * all_rows * width * shared_wide,
@@ -1181,7 +1245,7 @@
         routed_back
         + jnp.dot(logit_grad, router_weight.astype(jnp.float32).T, precision=highest)
     )
-    router_gradient = jnp.dot(normed_two.astype(jnp.float32).T, logit_grad, precision=highest)
+    router_gradient = jnp.dot(logit_grad.T, normed_two.astype(jnp.float32), precision=highest)
     back_two, second_gain_gradient = norm_back(
         normed_two_grad, hidden_one, second_scale, second_gain
     )
@@ -1227,34 +1291,11 @@
         .astype(jnp.bfloat16)
         .reshape(group_rows, heads_here * (NOPE + VDIM))
     )
-    (produced,) = call(
-        produce_kernel,
-        2 * local_experts,
-        [(routed_hidden, tile_spec(hidden_here)), (expert_down, expert_spec(expert_down))],
-        [(slots, tile_spec(width))],
-        one_matmul,
-    )
-    (out_dense,) = call(
-        out_kernel,
-        pairs,
-        [
-            whole(here),
-            marks,
-            (produced, slots_spec(slots, pairs)),
-            (shared_hidden, token_spec),
-            whole(down_part),
-        ],
-        [(dense, dense_spec)],
-        gather_flops,
-    )
     column_half = width // 2
     half_spec = lambda m: pl.BlockSpec((1, m, column_half), lambda i: (i // 2, 0, i % 2))
     narrow_spec = pl.BlockSpec((1, slot_rows, hidden_here), lambda i: (i // 2, 0, 0))
     weight_shape = shape((local_experts, hidden_here, width), jnp.float32)
-    out_dense, query_grad = lax.optimization_barrier((out_dense, query_grad))
-    routed_out, weight_grads = sum_all(
-        out_dense.reshape(blocks, token_rows, width),
-        6,
+    weight_grads = call(
         weight_kernel,
         2 * local_experts,
         [
@@ -1262,7 +1303,7 @@
             (grads_slots, half_spec(slot_rows)),
             (gate_grad, narrow_spec),
             (lift_grad, narrow_spec),
-            (routed_hidden, narrow_spec),
+            (mixed_hidden, narrow_spec),
         ],
         [(weight_shape, half_spec(hidden_here))] * 3,
         3 * one_matmul,
@@ -1301,7 +1342,7 @@
     filled = jnp.concatenate(
         [
             latent_weight_gradient,
-            router_gradient.T,
+            router_gradient,
             first_gain_gradient[None],
             second_gain_gradient[None],
             jnp.pad(latent_gain_gradient, (0, width - LATENT))[None],

time: 1010 us -> 950 us (0.941)
  local copies, waits for them, and re-layouts: 97.8 us -> 52.9 us
  Pallas kernels: 744 us -> 719 us
  waiting for transfers between devices: 28 us -> 44.3 us
    unnamed x193 -> x142, local copies, waits for them, and re-layouts: 62 us -> 15.5 us
    reduce_scatter x1, waiting for transfers between devices: 0.01 us -> 16.5 us  [per_device(): lax.psum_scatter(query_gradient.astype(jnp.bfloat16), 'expert', scatter_d...]
    pallas_call x1, Pallas kernels: 76.2 us -> 63.3 us  [total_over_all(): pl.pallas_call(total_kernel, out_shape=out, in_specs=[pl.BlockSpec(memory...]
  transfers between devices with their start and end apart: 5 -> 5, of which waited for: 1 -> 2; matrix products, arithmetic and copies ran while one was open for 8% -> 9% of each run, Pallas kernels for 42% -> 32%
where the time goes in v3:
time: 950 us; the launch traced here: 943 us
  Pallas kernels  719 us (76%)
  matrix products  67.8 us (7%)
  local copies, waits for them, and re-layouts  52.9 us (6%)
  waiting for transfers between devices  44.3 us (5%)
  other arithmetic  38.3 us (4%)
  between operations  15.5 us (2%)
    pallas_call x6, Pallas kernels, call(): pl.pallas_call(kernel, grid=(grid,), in_specs=[s for _, s in ins], out_sp...  203 us
    pallas_call x2, Pallas kernels, sum_all(): pl.pallas_call(functools.partial(sum_all_kernel, inner, len(ins), len(out...  203 us
    pallas_call x1, Pallas kernels, gather_all(): pl.pallas_call(gather_all_kernel, out_shape=out, in_specs=[pl.BlockSpec(m...  162 us
    pallas_call x1, Pallas kernels, total_over_all(): pl.pallas_call(total_kernel, out_shape=out, in_specs=[pl.BlockSpec(memory...  63.3 us
    pallas_call x2, Pallas kernels, sum_group(): pl.pallas_call(sum_group_kernel, out_shape=out, in_specs=[pl.BlockSpec(me...  43.6 us
    pallas_call x2, Pallas kernels, gather_group(): pl.pallas_call(gather_group_kernel, out_shape=out, in_specs=[pl.BlockSpec...  43.6 us
    all_gather x1, waiting for transfers between devices, per_device(): cotangent_all = lax.all_gather(cotangent_wide, both, axis=0, tiled=True)  27.8 us
    dot_general x4, matrix products, times_trans(): lax.dot_general(left, right, (((1,), (1,)), ((), ())), preferred_element_...  20.3 us
  transfers between devices with their start and end apart: 5, of which 2 were waited for; matrix products, arithmetic and copies ran while one was open for 9% of the time, Pallas kernels for 32%

profile of v3, /device:TPU:0, one launch (start us, length us, event | category | flops | bytes accessed | tf_op | source)
XLA Modules:
  0.0 943.0 jit_solution(3839332297930694404)
XLA Ops:
  12.3 2.1 fusion.18.x_ref
  14.5 22.6 %shard_map.297 = bf16[4,160,2048]{2,1,0:T(8,128)(2,1)} custom-call(bf16[160,2048]{1,0:T(8,128)(2,1)} %fusion.18.x_ref), custom_call_target="tpu_custom_call" | custom-call | bytes 3276800 | tf_op jit(solution)/shard_map/pallas_call | solution.py:700
  37.1 4.6 fusion.79
  43.2 2.0 convolution_convert_fusion.5
  45.2 2.9 reshape.381
  49.4 1.8 copy.151
  51.2 5.1 copy.118
  56.7 5.4 fusion.80
  63.6 1.8 fusion.78
  66.3 1.9 copy-done
  69.8 3.1 convolution_convert_fusion.1
  72.8 21.7 %shard_map.298 = f32[160,2048]{1,0:T(8,128)} custom-call(bf16[4,160,2048]{2,1,0:T(8,128)(2,1)} %bitcast.140), custom_call_target="tpu_custom_call" | custom-call | bytes 3932160 | tf_op jit(solution)/shard_map/pallas_call | solution.py:763
  94.6 1.6 multiply_reduce_fusion.5
  106.0 162.1 %shard_map.299 = bf16[32,160,2176]{2,1,0:T(8,128)(2,1)} custom-call(bf16[160,2176]{1,0:T(8,128)(2,1)} %concatenate.51.x_ref), custom_call_target="tpu_custom_call" | custom-call | bytes 22978560 | tf_op jit(solution)/shard_map/pallas_call | solution.py:463
  270.0 27.8 %all-gather.2.cloned.1.call-done.value_ref.marks_ref.refs_1_ = bf16[5120,2176]{1,0:T(8,128)(2,1)} async-done(((bf16[160,2176]{1,0:T(8,128)(2,1)}), bf16[5120,2176]{1,0:T(8,128)(2,1)}) %all-gather.2.cloned.1.call-update) | async-done | bytes 22282256 | tf_op jit(solution)/shard_map/all_gather | solution.py:1036
  297.8 24.4 %shard_map.300 = (bf16[8,640,2048]{2,1,0:T(8,128)(2,1)}, f32[5120,128]{1,0:T(8,128)}) custom-call(bf16[8,128]{1,0:T(8,128)(2,1)} %get-tuple-element.104.here_ref, bf16[5120,2176]{1,0:T(8,128)(2,1)} %all-gather.2.cloned.1.call-done.value_ref.marks_ref.refs_1_, bf16[128,2048]{1,0:T(8,128)(2,1)} %pad.25.down_ref), custom_call_target="tpu_custom_call" | custom-call | flops 9395240960 | bytes 46401536 | tf_op jit(solution)/shard_map/pallas_call | solution.py:285
  322.2 30.0 %shard_map.301 = (bf16[8,640,2048]{2,1,0:T(8,128)(2,1)}, f32[8,640,128]{2,1,0:T(8,128)}, bf16[5120,128]{1,0:T(8,128)(2,1)}, bf16[5120,128]{1,0:T(8,128)(2,1)}, bf16[5120,128]{1,0:T(8,128)(2,1)}) custom-call(bf16[8,128]{1,0:T(8,128)(2,1)} %get-tuple-element.104.here_ref, bf16[8,128]{1,0:T(8,128)(2,1)} %get-tuple-element.103.twice_ref, ...), custom_call_target="tpu_custom_call" | custom-call | flops 12079595520 | bytes 75763712 | tf_op jit(solution)/shard_map/pallas_call | solution.py:285
  352.2 40.1 %shard_map.302 = (bf16[8,640,352]{2,1,0:T(8,128)(2,1)}, bf16[8,640,352]{2,1,0:T(8,128)(2,1)}, bf16[8,640,352]{2,1,0:T(8,128)(2,1)}, bf16[8,640,352]{2,1,0:T(8,128)(2,1)}, bf16[8,640,2048]{2,1,0:T(8,128)(2,1)}) custom-call(bf16[8,640,2048]{2,1,0:T(8,128)(2,1)} %get-tuple-element.41.rows_ref, f32[8,640,128]{2,1,0:T(8,128)} %get-tuple-element.42.mix_ref, ...), custom_call_target="tpu_custom_call" | custom-call | flops 22145925120 | bytes 93585408 | tf_op jit(solution)/shard_map/pallas_call | solution.py:285
  392.3 24.0 %shard_map.303 = bf16[5120,2048]{1,0:T(8,128)(2,1)} custom-call(bf16[8,128]{1,0:T(8,128)(2,1)} %get-tuple-element.104.here_ref, bf16[5120,2176]{1,0:T(8,128)(2,1)} %all-gather.2.cloned.1.call-done.value_ref.marks_ref.refs_1_, bf16[8,640,2048]{2,1,0:T(8,128)(2,1)} %get-tuple-element.43.rows_ref, bf16[5120,128]{1,0:T(8,128)(2,1)} %get-tuple-element.44.hidden_ref.refs_4_, ...), custom_call_target="tpu_custom_call" | custom-call | flops 9395240960 | bytes 66062336 | tf_op jit(solution)/shard_map/pallas_call | solution.py:285
  416.3 101.3 %shard_map.304 = (f32[160,2048]{1,0:T(8,128)}, bf16[8,640,352]{2,1,0:T(8,128)(2,1)}, bf16[8,640,352]{2,1,0:T(8,128)(2,1)}, bf16[8,640,2048]{2,1,0:T(8,128)(2,1)}, f32[8,640,128]{2,1,0:T(8,128)}) custom-call(bf16[32,160,2048]{2,1,0:T(8,128)(2,1)} %bitcast.124, bf16[8,640,2048]{2,1,0:T(8,128)(2,1)} %get-tuple-element.45.refs_0_.grads_ref, ...), custom_call_target="tpu_custom_call" | custom-call | flops 22145925120 | bytes 119472128 | tf_op jit(solution)/shard_map/pallas_call | solution.py:637
  517.7 30.0 %shard_map.305 = bf16[5120,2176]{1,0:T(8,128)(2,1)} custom-call(bf16[8,128]{1,0:T(8,128)(2,1)} %get-tuple-element.104.here_ref, bf16[8,128]{1,0:T(8,128)(2,1)} %get-tuple-element.106.high_ref, bf16[8,128]{1,0:T(8,128)(2,1)} %get-tuple-element.105.low_ref, bf16[5120,2176]{1,0:T(8,128)(2,1)} %all-gather.2.cloned.1.call-done.value_ref.marks_ref.refs_1_, ...), custom_call_target="tpu_custom_call" | custom-call | flops 12079595520 | bytes 71833600 | tf_op jit(solution)/shard_map/pallas_call | solution.py:285
  547.7 101.8 %shard_map.306 = (f32[160,2176]{1,0:T(8,128)}, f32[128,2048]{1,0:T(8,128)}, f32[128,2048]{1,0:T(8,128)}, f32[128,2048]{1,0:T(8,128)}) custom-call(bf16[32,160,2176]{2,1,0:T(8,128)(2,1)} %bitcast.123, bf16[5120,2176]{1,0:T(8,128)(2,1)} %bitcast.120, bf16[5120,2176]{1,0:T(8,128)(2,1)} %all-gather.2.cloned.1.call-done.value_ref.marks_ref.refs_1_, ...), custom_call_target="tpu_custom_call" | custom-call | flops 8053063680 | bytes 75317248 | tf_op jit(solution)/shard_map/pallas_call | solution.py:637
  653.4 3.1 multiply_reduce_fusion.2
  656.5 2.0 fusion.74
  658.5 21.0 %shard_map.307 = bf16[4,160,2048]{2,1,0:T(8,128)(2,1)} custom-call(bf16[160,2048]{1,0:T(8,128)(2,1)} %get-tuple-element.75.x_ref), custom_call_target="tpu_custom_call" | custom-call | bytes 3276800 | tf_op jit(solution)/shard_map/pallas_call | solution.py:700
  679.6 4.4 convolution_convert_fusion.7
  688.3 3.4 fusion.28
  693.6 2.1 convolution_convert_fusion.6
  695.8 4.9 convolution_convert_fusion.3
  700.7 2.9 multiply_reduce_fusion.1
  708.5 4.3 convolution_convert_fusion
  712.8 6.8 fusion.81
  721.4 6.2 add_convert_fusion
  727.6 21.9 %shard_map.308 = f32[160,2048]{1,0:T(8,128)} custom-call(bf16[4,160,2048]{2,1,0:T(8,128)(2,1)} %bitcast.139), custom_call_target="tpu_custom_call" | custom-call | bytes 3932160 | tf_op jit(solution)/shard_map/pallas_call | solution.py:763
  749.5 1.8 fusion.24
  752.4 3.4 convolution_convert_fusion.2
  755.9 9.5 %concatenate.55 = bf16[643,2048]{1,0:T(8,128)(2,1)S(1)} concatenate(bf16[576,2048]{1,0:T(8,128)(2,1)} %convolution_convert_fusion.2, bf16[64,2048]{1,0:T(8,128)(2,1)} %convolution_convert_fusion.4, bf16[1,2048]{1,0:T(2,128)(2,1)S(1)} %broadcast_in_dim.35, bf16[1,2048]{1,0:T(2,128)(2,1)S(1)} %broadcast_in_dim.36, bf16[1,2048]{1,0:T(2,128)(2,1)S(1)} %broadcast_in_dim.37), dimensions={0} | concatenate | bytes 5267456 | tf_op jit(solution)/shard_map/concatenate | solution.py:1342
  765.4 1.9 pad.29.p_ref
  767.2 63.3 %shard_map.309 = bf16[704,2048]{1,0:T(8,128)(2,1)} custom-call(bf16[704,2048]{1,0:T(8,128)(2,1)} %pad.29.p_ref), custom_call_target="tpu_custom_call" | custom-call | bytes 5767168 | tf_op jit(solution)/shard_map/pallas_call | solution.py:913
  831.8 5.1 convert_element_type.178
  841.6 5.2 all-to-all-start
  848.3 1.9 slice_bitcast_fusion.1
  851.6 5.1 slice_bitcast_fusion
  856.7 54.6 %shard_map.310 = (f32[8,352,2048]{2,1,0:T(8,128)}, f32[8,352,2048]{2,1,0:T(8,128)}, f32[8,352,2048]{2,1,0:T(8,128)}) custom-call(bf16[8,640,2048]{2,1,0:T(8,128)(2,1)} %get-tuple-element.41.rows_ref, bf16[8,640,2048]{2,1,0:T(8,128)(2,1)} %get-tuple-element.45.refs_0_.grads_ref, bf16[8,640,352]{2,1,0:T(8,128)(2,1)} %get-tuple-element.58.gate_grad_ref, ...), custom_call_target="tpu_custom_call" | custom-call | flops 22145925120 | bytes 121962496 | tf_op jit(solution)/shard_map/pallas_call | solution.py:285
  914.1 1.6 convert_element_type.182
  915.7 1.8 convert_element_type.184
  917.5 16.5 %reduce-scatter.4.cloned.1.call-done = bf16[256,768]{1,0:T(8,128)(2,1)} async-done(((bf16[2048,768]{1,0:T(8,128)(2,1)}), bf16[256,768]{1,0:T(8,128)(2,1)}) %reduce-scatter.4.cloned.1.call-update) | async-done | bytes 393232 | tf_op jit(solution)/shard_map/reduce_scatter | solution.py:1331
  934.0 1.9 convert_element_type.180
  (236 shorter events, 52.9 us)
Async XLA Ops:
  7.2 290.6 %all-gather.2.cloned.1.call-start = ((), (), s32[]{:S(2)}) async-start(), calls=%async_computation.4 | async-start | bytes 22978560 | tf_op jit(solution)/shard_map/all_gather | solution.py:1036
  7.2 49.0 %copy-start.59 = (f32[32]{0:T(128)}, f32[32]{0:T(128)S(1)}, u32[]{:S(2)}) copy-start(f32[32]{0:T(128)S(1)} %negate_power_fusion) | copy-start | bytes 388
  10.0 27.1 %copy-start.55 = (f32[160]{0:T(256)}, f32[160]{0:T(256)S(1)}, u32[]{:S(2)}) copy-start(f32[160]{0:T(256)S(1)} %get-tuple-element.100) | copy-start | bytes 1924
  10.6 45.7 %copy-start.47 = (f32[640]{0:T(1024)}, f32[640]{0:T(1024)S(1)}, u32[]{:S(2)}) copy-start(f32[640]{0:T(1024)S(1)} %fusion.57) | copy-start | bytes 7684
  37.1 6.1 copy-start.61
  37.1 6.1 copy-start.65
  41.7 14.6 %copy-start.13 = (f32[640,576]{0,1:T(8,128)}, f32[640,576]{0,1:T(8,128)S(1)}, u32[]{:S(2)}) copy-start(f32[640,576]{0,1:T(8,128)S(1)} %fusion.79) | copy-start | bytes 4423684
  49.4 14.0 %copy-start.8 = (bf16[640,4,128]{2,1,0:T(4,128)(2,1)}, bf16[640,4,128]{2,1,0:T(4,128)(2,1)S(1)}, u32[]{:S(2)}) copy-start(bf16[640,4,128]{2,1,0:T(4,128)(2,1)S(1)} %get-tuple-element.89) | copy-start | bytes 1966084
  51.2 15.1 %copy-start.16 = (bf16[640,4,128]{0,2,1:T(8,128)(2,1)}, bf16[640,4,128]{0,2,1:T(8,128)(2,1)S(1)}, u32[]{:S(2)}) copy-start(bf16[640,4,128]{0,2,1:T(8,128)(2,1)S(1)} %copy.151) | copy-start | bytes 1966084
  56.7 5.4 copy-start.30
  56.7 5.4 copy-start.32
  56.7 5.6 copy-start.36
  56.7 5.6 copy-start.38
  65.4 2.8 copy-start
  69.6 3.2 copy-start.66
  72.8 21.8 %copy-start.5 = (bf16[160,2048]{1,0:T(8,128)(2,1)S(1)}, bf16[160,2048]{1,0:T(8,128)(2,1)}, u32[]{:S(2)}) copy-start(bf16[160,2048]{1,0:T(8,128)(2,1)} %param.18) | copy-start | bytes 1966084
  94.6 2.7 copy-start.42
  94.6 2.9 copy-start.40
  97.5 7.5 copy-start.10
  100.0 814.1 %reduce-scatter.6.cloned.1.call-start = ((), (), s32[]{:S(2)}) async-start(), calls=%async_computation.6 | async-start | bytes 1179648 | tf_op jit(solution)/shard_map/reduce_scatter | solution.py:1334
  653.3 3.1 copy-start.4
  653.3 3.1 copy-start.19
  653.3 3.1 copy-start.27
  653.3 3.1 copy-start.43
  653.3 3.1 copy-start.50
  653.3 3.1 copy-start.58
  656.5 27.4 %slice-start = ((s8[6553600]{0:T(1024)(128)(4,1)}), s8[2359296]{0:T(1024)(128)(4,1)S(1)}, s32[]{:S(2)}) async-start(s8[6553600]{0:T(1024)(128)(4,1)} %bitcast.121), calls=%async_computation.8 | async-start | bytes 4718592
  679.5 4.4 slice-start.1
  679.6 4.4 copy-start.41
  688.3 3.4 copy-start.1
  691.7 1.8 copy-start.14
  693.6 2.2 copy-start.67
  695.7 220.0 %reduce-scatter.8.cloned.1.call-start = ((), (), s32[]{:S(2)}) async-start(), calls=%async_computation.7 | async-start | bytes 2359296 | tf_op jit(solution)/shard_map/reduce_scatter | solution.py:1337
  700.6 233.3 %reduce-scatter.4.cloned.1.call-start = ((), (), s32[]{:S(2)}) async-start(), calls=%async_computation.5 | async-start | bytes 3538944 | tf_op jit(solution)/shard_map/reduce_scatter | solution.py:1331
  700.7 2.9 copy-start.2
  700.7 2.9 copy-start.37
  700.7 2.9 copy-start.39
  705.8 2.5 copy-start.29
  720.6 7.0 copy-start.34
  727.6 21.9 %copy-start.6 = (bf16[160,2048]{1,0:T(8,128)(2,1)S(1)}, bf16[160,2048]{1,0:T(8,128)(2,1)}, u32[]{:S(2)}) copy-start(bf16[160,2048]{1,0:T(8,128)(2,1)} %param.18) | copy-start | bytes 1966084
  727.6 21.9 %copy-start.44 = (f32[2048]{0:T(1024)S(1)}, f32[2048]{0:T(1024)}, u32[]{:S(2)}) copy-start(f32[2048]{0:T(1024)} %param.22) | copy-start | bytes 24580
  727.6 21.9 %copy-start.56 = (f32[160]{0:T(256)S(1)}, f32[160]{0:T(256)}, u32[]{:S(2)}) copy-start(f32[160]{0:T(256)} %copy-done.55) | copy-start | bytes 1924
  727.6 24.8 %copy-start.21 = (bf16[4,160,2048]{2,1,0:T(8,128)(2,1)S(1)}, bf16[4,160,2048]{2,1,0:T(8,128)(2,1)}, u32[]{:S(2)}) copy-start(bf16[4,160,2048]{2,1,0:T(8,128)(2,1)} %shard_map.297) | copy-start | bytes 7864324
  749.5 2.9 copy-start.35
  841.6 8.6 copy-start.7
  841.6 8.6 copy-start.15
  841.6 8.6 copy-start.57
  841.6 69.7 %all-to-all-start = ((bf16[264,8,256]{2,0,1:T(8,128)(2,1)}), bf16[264,8,256]{2,0,1:T(8,128)(2,1)}, u32[]{:S(2)}, u32[]{:S(2)}) async-start(bf16[264,8,256]{2,0,1:T(8,128)(2,1)} %pad_maximum_fusion.1), calls=%async_computation.3 | async-start | bytes 2162688 | tf_op jit(solution)/shard_map/all_to_all | solution.py:1236
  (27 other events, 32.8 us)
Sparse Core Ops, SparseCore 0:
  100.1 197.6 all-gather.1
  695.8 64.8 reduce-scatter.5
  764.2 70.6 reduce-scatter.7
  838.4 95.5 reduce-scatter.3

commit v4 on v3

--- a/solution.py
+++ b/solution.py
@@ -134,7 +134,9 @@
     return jnp.concatenate(totals, axis=0)
 
 
-def grads_kernel(pair, here_ref, value_ref, down_ref, rows_ref, back_ref):
+def grads_kernel(pair, turn, ins, outs):
+    here_ref, value_ref, down_ref = ins
+    rows_ref, back_ref = outs
     width = rows_ref.shape[2]
     slots = pair_slots(value_ref.at[:, width:], here_ref, rows_ref.shape[0], pair)
     values = value_ref[:, :width]
@@ -387,92 +389,421 @@
     return value + upper * (3 - 2 * value)
 
 
-def gather_all_kernel(x_ref, out_ref, send_sems, recv_sems, local_sem):
-    z, x, y, c = places()
-    half = x_ref.shape[0] // 2
-    over, side, mate = device(z, 1 - x, y, c), device(z, x, 1 - y, c), device(z, x, y, 1 - c)
-    up, down = device(z + 1, x, y, c), device(z - 1, x, y, c)
-    greet([(over, None), (side, None), (mate, None), (up, z < 3), (down, z > 0)])
+class Gather:
+    def __init__(self, x_ref, out_ref, sends, recv_sems, local_sem, place):
+        z, x, y, c = place
+        half = x_ref.shape[0] // 2
+        over, side, mate = device(z, 1 - x, y, c), device(z, x, 1 - y, c), device(z, x, y, 1 - c)
+        up, down = device(z + 1, x, y, c), device(z - 1, x, y, c)
+        self.out_ref, self.recv_sems, self.mate, self.half = out_ref, recv_sems, mate, half
+        planes = [ordered(z, (0, 1, 2, 3)[step], (1, 0, 2, 3)[step]) for step in range(4)]
+        self.rising = [(zz <= z) & (z < 3) for zz in planes]
+        self.falling = [(zz >= z) & (z > 0) for zz in planes]
+        self.mine = [shard(zz, x, y, c) for zz in planes]
+        self.overs = [shard(zz, 1 - x, y, c) for zz in planes]
+        self.sides = [shard(zz, x, 1 - y, c) for zz in planes]
+        self.corners = [shard(zz, 1 - x, 1 - y, c) for zz in planes]
+        self.mates = [
+            (shard(zz, x, y, 1 - c), shard(zz, 1 - x, y, 1 - c), shard(zz, x, 1 - y, 1 - c))
+            for zz in planes
+        ]
+        self.mate_corners = [shard(zz, 1 - x, 1 - y, 1 - c) for zz in planes]
+        self.keep = pltpu.make_async_copy(x_ref, out_ref.at[self.mine[0]], local_sem)
+        self.whole_copies, self.relay_copies, self.corner_copies = [], [], []
+
+        def copy(ref, receive, to, when=None, source=None):
+            return sends.plan(ref if source is None else source, ref, receive, to, when)
+
+        for step in range(4):
+            i = self.mine[step]
+            source = x_ref if step == 0 else None
+            there, receive = out_ref.at[i], recv_sems.at[i, 0]
+            self.whole_copies.append(
+                [
+                    (copy(there, receive, up, self.rising[step], source), self.rising[step]),
+                    (copy(there, receive, down, self.falling[step], source), self.falling[step]),
+                    (copy(there, receive, over, None, source), None),
+                    (copy(there, receive, side, None, source), None),
+                    (copy(there, receive, mate, None, source), None),
+                ]
+            )
+            i, j = self.overs[step], self.sides[step]
+            self.relay_copies.append(
+                [
+                    copy(self.halves(i, 0), recv_sems.at[i, 0], side),
+                    copy(out_ref.at[i], recv_sems.at[i, 0], mate),
+                    copy(self.halves(j, 1), recv_sems.at[j, 1], over),
+                    copy(out_ref.at[j], recv_sems.at[j, 0], mate),
+                ]
+            )
+            i = self.corners[step]
+            self.corner_copies.append(
+                [copy(self.halves(i, h), recv_sems.at[i, h], mate) for h in range(2)]
+            )
+
+    def halves(self, i, h):
+        return self.out_ref.at[i, pl.ds(h * self.half, self.half)]
+
+    def full_here(self, i):
+        landed(self.out_ref.at[i], self.recv_sems.at[i, 0], self.mate)
+
+    def half_here(self, i, h):
+        landed(self.halves(i, h), self.recv_sems.at[i, h], self.mate)
+
+    def whole(self, step):
+        if step == 0:
+            self.keep.start()
+        else:
+            self.full_here(self.mine[step])
+        for copy, when in self.whole_copies[step]:
+            if when is None:
+                copy.start()
+            else:
+                pl.when(when)(copy.start)
+
+    def relay(self, step):
+        self.full_here(self.overs[step])
+        self.relay_copies[step][0].start()
+        self.relay_copies[step][1].start()
+        self.full_here(self.sides[step])
+        self.relay_copies[step][2].start()
+        self.relay_copies[step][3].start()
+
+    def corner(self, step):
+        for h in range(2):
+            self.half_here(self.corners[step], h)
+            self.corner_copies[step][h].start()
+
+    def last(self):
+        for step in range(4):
+            for i in self.mates[step]:
+                self.full_here(i)
+            for h in range(2):
+                self.half_here(self.mate_corners[step], h)
+        self.keep.wait()
+
+
+def gather_neighbours(place):
+    z, x, y, c = place
+    return [
+        (device(z, 1 - x, y, c), None),
+        (device(z, x, 1 - y, c), None),
+        (device(z, x, y, 1 - c), None),
+        (device(z + 1, x, y, c), z < 3),
+        (device(z - 1, x, y, c), z > 0),
+    ]
+
+
+def gather_all_kernel(inner, cover_ins, cover_outs, x_ref, *refs):
+    ins, refs = refs[:cover_ins], refs[cover_ins:]
+    out_ref, refs = refs[0], refs[1:]
+    outs, refs = refs[:cover_outs], refs[cover_outs:]
+    send_sems, recv_sems, local_sem = refs
+    turn, turns = pl.program_id(0), pl.num_programs(0)
+    place = places()
     sends = Sends(send_sems)
-    own = shard(z, x, y, c)
-    keep = pltpu.make_async_copy(x_ref, out_ref.at[own], local_sem)
-    keep.start()
-
-    def halves(i, h):
-        return out_ref.at[i, pl.ds(h * half, half)]
-
-    def whole(step):
-        zz = ordered(z, (0, 1, 2, 3)[step], (1, 0, 2, 3)[step])
-        i = shard(zz, x, y, c)
-        source, receive = out_ref.at[i], recv_sems.at[i, 0]
-        if step == 0:
-            source = x_ref
-        else:
-            landed(out_ref.at[i], receive, mate)
-        sends.start(source, out_ref.at[i], receive, up, (zz <= z) & (z < 3))
-        sends.start(source, out_ref.at[i], receive, down, (zz >= z) & (z > 0))
-        sends.start(source, out_ref.at[i], receive, over)
-        sends.start(source, out_ref.at[i], receive, side)
-        sends.start(source, out_ref.at[i], receive, mate)
-
-    def relay(step):
-        zz = ordered(z, (0, 1, 2, 3)[step], (1, 0, 2, 3)[step])
-        i = shard(zz, 1 - x, y, c)
-        landed(out_ref.at[i], recv_sems.at[i, 0], mate)
-        sends.start(halves(i, 0), halves(i, 0), recv_sems.at[i, 0], side)
-        sends.start(out_ref.at[i], out_ref.at[i], recv_sems.at[i, 0], mate)
-        i = shard(zz, x, 1 - y, c)
-        landed(out_ref.at[i], recv_sems.at[i, 0], mate)
-        sends.start(halves(i, 1), halves(i, 1), recv_sems.at[i, 1], over)
-        sends.start(out_ref.at[i], out_ref.at[i], recv_sems.at[i, 0], mate)
-
-    def corner(step):
-        zz = ordered(z, (0, 1, 2, 3)[step], (1, 0, 2, 3)[step])
-        i = shard(zz, 1 - x, 1 - y, c)
-        for h in range(2):
-            landed(halves(i, h), recv_sems.at[i, h], mate)
-            sends.start(halves(i, h), halves(i, h), recv_sems.at[i, h], mate)
-
-    whole(0)
-    whole(1)
-    relay(0)
-    whole(2)
-    relay(1)
-    corner(0)
-    whole(3)
-    relay(2)
-    corner(1)
-    relay(3)
-    corner(2)
-    corner(3)
-    for step in range(4):
-        zz = ordered(z, (0, 1, 2, 3)[step], (1, 0, 2, 3)[step])
-        for i in (shard(zz, x, y, 1 - c), shard(zz, 1 - x, y, 1 - c), shard(zz, x, 1 - y, 1 - c)):
-            landed(out_ref.at[i], recv_sems.at[i, 0], mate)
-        i = shard(zz, 1 - x, 1 - y, 1 - c)
-        for h in range(2):
-            landed(halves(i, h), recv_sems.at[i, h], mate)
-    sends.finish()
-    keep.wait()
-
-
-def gather_all(value, number):
+    gather = Gather(x_ref, out_ref, sends, recv_sems, local_sem, place)
+
+    def begin():
+        greet(gather_neighbours(place))
+        gather.whole(0)
+
+    def end():
+        gather.whole(3)
+        gather.relay(2)
+        gather.corner(1)
+        gather.relay(3)
+        gather.corner(2)
+        gather.corner(3)
+        gather.last()
+        sends.finish()
+
+    def early():
+        gather.relay(1)
+        gather.corner(0)
+
+    pieces = [
+        begin,
+        lambda: None,
+        functools.partial(gather.whole, 1),
+        functools.partial(gather.relay, 0),
+        functools.partial(gather.whole, 2),
+        lambda: None,
+        early,
+    ]
+    for number, piece in enumerate(pieces):
+        pl.when(turn == number)(piece)
+    inner(turn, ins, outs)
+    pl.when(turn == turns - 1)(end)
+
+
+def gather_all(value, number, inner, turns, ins, outs, flops):
     if lax.axis_size("expert") != 8 or lax.axis_size("weight") != 4:
-        return lax.all_gather(value, ("expert", "weight"), axis=0)
+
+        def alone(*refs):
+            inner(pl.program_id(0), refs[: len(ins)], refs[len(ins) :])
+
+        gathered = lax.all_gather(value, ("expert", "weight"), axis=0)
+        return gathered, call(alone, turns, ins, outs, flops)
     out = jax.ShapeDtypeStruct((32,) + value.shape, value.dtype)
-    return pl.pallas_call(
-        gather_all_kernel,
-        out_shape=out,
-        in_specs=[pl.BlockSpec(memory_space=pltpu.VMEM)],
-        out_specs=pl.BlockSpec(memory_space=pl.ANY),
+    arrays, shapes = [a for a, _ in ins], [o for o, _ in outs]
+    results = pl.pallas_call(
+        functools.partial(gather_all_kernel, inner, len(ins), len(outs)),
+        grid=(turns,),
+        out_shape=[out] + shapes,
+        in_specs=[whole_spec(value)] + [spec for _, spec in ins],
+        out_specs=[pl.BlockSpec(memory_space=pl.ANY)] + [spec for _, spec in outs],
         scratch_shapes=[
             pltpu.SemaphoreType.DMA((44,)),
             pltpu.SemaphoreType.DMA((32, 2)),
             pltpu.SemaphoreType.DMA,
         ],
-        compiler_params=pltpu.CompilerParams(collective_id=number, has_side_effects=True),
-        cost_estimate=cost(0, value, out),
-    )(value)
+        compiler_params=pltpu.CompilerParams(
+            collective_id=number, has_side_effects=True, vmem_limit_bytes=vmem_limit
+        ),
+        cost_estimate=cost(flops, value, out, *arrays, *shapes),
+    )(value, *arrays)
+    return results[0], results[1:]
+
+
+def attention_kernel(
+    score_scale,
+    normed_ref,
+    value_ref,
+    cosine_ref,
+    sine_ref,
+    segment_row_ref,
+    segment_column_ref,
+    gain_ref,
+    query_hbm,
+    latent_hbm,
+    expand_hbm,
+    output_hbm,
+    value_out,
+    normed_out,
+    query_out,
+    latent_out,
+    scale_out,
+    latent_normed_out,
+    key_rope_out,
+    expanded_out,
+    log_out,
+    mixed_out,
+    attended_out,
+    query_matrix,
+    latent_matrix,
+    expand_matrix,
+    output_matrix,
+    partial,
+    mates,
+    sides,
+    carried,
+    send_sems,
+    recv_sems,
+    local_sems,
+    group_sends,
+    group_sems,
+    sum_sends,
+    mate_sems,
+    side_sems,
+):
+    place = places()
+    z, x, y, c = place
+    side, mate = device(z, x, 1 - y, c), device(z, x, y, 1 - c)
+    rows = normed_ref.shape[0]
+    half = rows // 2
+    heads = query_out.shape[0]
+    greet(gather_neighbours(place))
+    near = Sends(group_sends)
+    own, across = y * 2 + c, (1 - y) * 2 + c
+    keep = pltpu.make_async_copy(normed_ref, normed_out.at[own], local_sems.at[0])
+    keep.start()
+
+    def part(i, h):
+        return normed_out.at[i, pl.ds(h * half, half)]
+
+    for to in (side, mate):
+        for h in range(2):
+            piece = normed_ref.at[pl.ds(h * half, half)]
+            near.start(piece, part(own, h), group_sems.at[own, h], to)
+    sends = Sends(send_sems)
+    gather = Gather(value_ref, value_out, sends, recv_sems, local_sems.at[1], place)
+    gather.whole(0)
+    loads = [
+        pltpu.make_async_copy(source, target, local_sems.at[2 + i])
+        for i, (source, target) in enumerate(
+            (
+                (query_hbm, query_matrix),
+                (latent_hbm, latent_matrix),
+                (expand_hbm, expand_matrix),
+                (output_hbm, output_matrix),
+            )
+        )
+    ]
+    for load in loads:
+        load.start()
+    for h in range(2):
+        landed(part(across, h), group_sems.at[across, h], mate)
+        near.start(part(across, h), part(across, h), group_sems.at[across, h], mate)
+    for i in (y * 2 + 1 - c, (1 - y) * 2 + 1 - c):
+        for h in range(2):
+            landed(part(i, h), group_sems.at[i, h], mate)
+    keep.wait()
+    normed = normed_out[...].reshape(4 * rows, normed_out.shape[2])
+    cosine, sine = cosine_ref[...], sine_ref[...]
+    turn_half = ROPE // 2
+
+    def turned(first, second):
+        return jnp.concatenate(
+            [first * cosine - second * sine, second * cosine + first * sine], axis=1
+        )
+
+    loads[0].wait()
+    full = matmul(normed, query_matrix[...])
+    for h in range(heads):
+        start = h * (NOPE + ROPE)
+        first = full[:, start + NOPE : start + NOPE + turn_half]
+        second = full[:, start + NOPE + turn_half : start + NOPE + ROPE]
+        query = jnp.concatenate([full[:, start : start + NOPE], turned(first, second)], axis=1)
+        query_out[h] = query.astype(jnp.bfloat16)
+    gather.whole(1)
+    loads[1].wait()
+    compressed = times_trans(normed, latent_matrix[...])
+    latent = compressed[:, :LATENT]
+    scale = inv_rms(latent)
+    latent_out[...] = latent
+    scale_out[...] = jnp.broadcast_to(scale, scale_out.shape)
+    latent_normed_out[...] = (latent * scale * gain_ref[...]).astype(jnp.bfloat16)
+    first = compressed[:, LATENT : LATENT + turn_half]
+    second = compressed[:, LATENT + turn_half : LATENT + ROPE]
+    key_rope_out[...] = turned(first, second).astype(jnp.bfloat16)
+    gather.relay(0)
+    loads[2].wait()
+    expanded_out[...] = matmul(latent_normed_out[...], expand_matrix[...]).astype(jnp.bfloat16)
+
+    def head(h):
+        start = h * (NOPE + VDIM)
+        query = query_out[h]
+        raw = times_trans(query[:, :NOPE], expanded_out[:, start : start + NOPE])
+        raw = raw + times_trans(query[:, NOPE:], key_rope_out[...])
+        row = lax.broadcasted_iota(jnp.int32, raw.shape, 0)
+        column = lax.broadcasted_iota(jnp.int32, raw.shape, 1)
+        allowed = (segment_column_ref[...] == segment_row_ref[...]) & (column <= row)
+        scores = jnp.where(allowed, raw * score_scale, -1e30)
+        peak = jnp.max(scores, axis=1, keepdims=True)
+        weights = jnp.exp(scores - peak)
+        total = jnp.sum(weights, axis=1, keepdims=True)
+        log_out[h] = jnp.broadcast_to(peak + jnp.log(total), log_out.shape[1:])
+        probs = (weights / total).astype(jnp.bfloat16)
+        mixed = matmul(probs, expanded_out[:, start + NOPE : start + NOPE + VDIM])
+        mixed_out[:, h * VDIM : (h + 1) * VDIM] = mixed.astype(jnp.bfloat16)
+
+    middle = [
+        None,
+        functools.partial(gather.whole, 2),
+        functools.partial(gather.relay, 1),
+        functools.partial(gather.corner, 0),
+    ]
+    for h in range(heads):
+        head(h)
+        if h < 4 and middle[h] is not None:
+            middle[h]()
+    loads[3].wait()
+    for i in range(4):
+        block = matmul(mixed_out[i * rows : (i + 1) * rows], output_matrix[...])
+        partial[i] = block.astype(jnp.bfloat16)
+    sums = Sends(sum_sends)
+    for j, yy in enumerate((1 - y, y)):
+        for h in range(2):
+            some = pl.ds(h * half, half)
+            sums.start(
+                partial.at[yy * 2 + 1 - c, some], mates.at[j, some], mate_sems.at[j, h], mate
+            )
+    gather.whole(3)
+    for h in range(2):
+        some = pl.ds(h * half, half)
+        landed(mates.at[0, some], mate_sems.at[0, h], mate)
+        add_into(carried, [partial.at[(1 - y) * 2 + c], mates.at[0]], h * half, half)
+        sums.start(carried.at[some], sides.at[some], side_sems.at[h], side)
+    gather.relay(2)
+    gather.corner(1)
+    gather.relay(3)
+    gather.corner(2)
+    for h in range(2):
+        some = pl.ds(h * half, half)
+        landed(mates.at[1, some], mate_sems.at[1, h], mate)
+        landed(sides.at[some], side_sems.at[h], mate)
+        add_into(attended_out, [partial.at[y * 2 + c], mates.at[1], sides], h * half, half)
+    gather.corner(3)
+    gather.last()
+    near.finish()
+    sends.finish()
+    sums.finish()
+
+
+def add_into(target, sources, start, rows):
+    step = 16
+
+    def body(i, carry):
+        part = pl.ds(pl.multiple_of(start + i * step, step), step)
+        total = sources[0][part].astype(jnp.float32)
+        for source in sources[1:]:
+            total = total + source[part].astype(jnp.float32)
+        target[part] = total.astype(target.dtype)
+        return carry
+
+    lax.fori_loop(0, rows // step, body, 0)
+
+
+def attention_forward(
+    score_scale, normed, value, cosine, sine, segment, gain, query, latent, expand, output, number
+):
+    rows, width = normed.shape
+    group, heads = 4 * rows, query.shape[1] // (NOPE + ROPE)
+    shape, low = jax.ShapeDtypeStruct, jnp.bfloat16
+    vmem, away = pl.BlockSpec(memory_space=pltpu.VMEM), pl.BlockSpec(memory_space=pl.ANY)
+    segment = segment.astype(jnp.float32)
+    inputs = [normed, value, cosine, sine, segment[None], segment[:, None], gain[None]]
+    matrices = [query, latent.T, expand, output]
+    outs = [
+        shape((32,) + value.shape, low),
+        shape((4, rows, width), low),
+        shape((heads, group, NOPE + ROPE), low),
+        shape((group, LATENT), jnp.float32),
+        shape((group, lanes), jnp.float32),
+        shape((group, LATENT), low),
+        shape((group, ROPE), low),
+        shape((group, heads * (NOPE + VDIM)), low),
+        shape((heads, group, lanes), jnp.float32),
+        shape((group, heads * VDIM), low),
+        shape((rows, width), jnp.float32),
+    ]
+    flops = 2 * group * (width * (query.shape[1] + latent.shape[1]) + output.size + expand.size)
+    return pl.pallas_call(
+        functools.partial(attention_kernel, score_scale),
+        out_shape=outs,
+        in_specs=[vmem] * len(inputs) + [away] * 4,
+        out_specs=[away] + [vmem] * (len(outs) - 1),
+        scratch_shapes=[pltpu.VMEM(m.shape, low) for m in matrices]
+        + [
+            pltpu.VMEM((4, rows, width), low),
+            pltpu.VMEM((2, rows, width), low),
+            pltpu.VMEM((rows, width), low),
+            pltpu.VMEM((rows, width), low),
+            pltpu.SemaphoreType.DMA((44,)),
+            pltpu.SemaphoreType.DMA((32, 2)),
+            pltpu.SemaphoreType.DMA((6,)),
+            pltpu.SemaphoreType.DMA((6,)),
+            pltpu.SemaphoreType.DMA((4, 2)),
+            pltpu.SemaphoreType.DMA((6,)),
+            pltpu.SemaphoreType.DMA((2, 2)),
+            pltpu.SemaphoreType.DMA((2,)),
+        ],
+        compiler_params=pltpu.CompilerParams(
+            collective_id=number, has_side_effects=True, vmem_limit_bytes=vmem_limit
+        ),
+        cost_estimate=cost(flops, *inputs, *matrices, *outs),
+    )(*inputs, *matrices)
 
 
 def sum_all_kernel(inner, cover_ins, cover_outs, p_ref, *refs):
@@ -986,7 +1317,6 @@
     activations = tokens.astype(jnp.float32)
     first_scale = inv_rms(activations)
     normed = (activations * first_scale * first_gain).astype(jnp.bfloat16)
-    normed_all = gather_group(normed, 0)
     both = ("expert", "weight")
     expert_index = lax.axis_index("expert")
     expert_lanes = lax.axis_size("expert")
@@ -1033,38 +1363,62 @@
     slots = shape((local_experts, slot_rows, width), jnp.bfloat16)
     slots_one = shape((local_experts, slot_rows, lanes), jnp.float32)
     gather_flops = 2 * all_rows * width * (2 * CAP * local_experts + shared_wide)
-    cotangent_all = lax.all_gather(cotangent_wide, both, axis=0, tiled=True)
-    marks = (cotangent_all, pl.BlockSpec((quad_rows, lanes), lambda i: (i, width // lanes)))
-    grads_slots, shared_raw = call(
-        functools.partial(grads_kernel, pair_rows),
-        quads,
-        [whole(here), (cotangent_all, pair_spec(cotangent_all, quads)), whole(down_part)],
-        [
-            (slots, slots_spec(slots, quads)),
-            (shape((all_rows, shared_wide), jnp.float32), pl.BlockSpec((quad_rows, shared_wide), lambda i: (i, 0))),
-        ],
-        gather_flops,
-    )
     cosine, sine = rope_tables(segments[0])
     allowed = attention_mask(segments[0])
-    query_full = matmul(normed_all, query_weight).reshape(group_rows, heads_here, query_width)
-    query = jnp.concatenate(
-        [
-            query_full[..., :NOPE],
-            rotate(query_full[..., NOPE:], cosine[:, None, :], sine[:, None, :]),
-        ],
-        axis=-1,
-    ).astype(jnp.bfloat16)
-    compressed = matmul(normed_all, latent_weight)
-    latent = compressed[:, :LATENT]
-    latent_scale = inv_rms(latent)
-    latent_normed = (latent * latent_scale * latent_gain).astype(jnp.bfloat16)
-    key_rope = rotate(compressed[:, LATENT:], cosine, sine).astype(jnp.bfloat16)
-    expanded = (
-        matmul(latent_normed, expand_weight)
-        .astype(jnp.bfloat16)
-        .reshape(group_rows, heads_here, NOPE + VDIM)
-    )
+    sizes = (expert_lanes, weight_count)
+    if sizes == (8, 4):
+        (
+            cotangent_all,
+            normed_all,
+            query,
+            latent,
+            latent_scale,
+            latent_normed,
+            key_rope,
+            expanded,
+            log_total,
+            mixed,
+            attended,
+        ) = attention_forward(
+            score_scale,
+            normed,
+            cotangent_wide,
+            cosine,
+            sine,
+            segments[0],
+            latent_gain,
+            query_weight,
+            latent_weight,
+            expand_weight,
+            output_weight,
+            0,
+        )
+        cotangent_all = cotangent_all.reshape(all_rows, -1)
+        normed_all = normed_all.reshape(group_rows, width)
+        latent_scale, log_total = latent_scale[:, :1], log_total[:, :, :1]
+        query = query.transpose(1, 0, 2)
+        expanded = expanded.reshape(group_rows, heads_here, NOPE + VDIM)
+    else:
+        cotangent_all = lax.all_gather(cotangent_wide, both, axis=0, tiled=True)
+        normed_all = gather_group(normed, 0)
+        query_full = matmul(normed_all, query_weight).reshape(group_rows, heads_here, query_width)
+        query = jnp.concatenate(
+            [
+                query_full[..., :NOPE],
+                rotate(query_full[..., NOPE:], cosine[:, None, :], sine[:, None, :]),
+            ],
+            axis=-1,
+        ).astype(jnp.bfloat16)
+        compressed = matmul(normed_all, latent_weight)
+        latent = compressed[:, :LATENT]
+        latent_scale = inv_rms(latent)
+        latent_normed = (latent * latent_scale * latent_gain).astype(jnp.bfloat16)
+        key_rope = rotate(compressed[:, LATENT:], cosine, sine).astype(jnp.bfloat16)
+        expanded = (
+            matmul(latent_normed, expand_weight)
+            .astype(jnp.bfloat16)
+            .reshape(group_rows, heads_here, NOPE + VDIM)
+        )
     key_nope = expanded[..., :NOPE]
     values = expanded[..., NOPE:]
 
@@ -1077,19 +1431,20 @@
         )
         return jnp.where(allowed[None], raw * score_scale, -1e30)
 
-    scores = score_block()
-    peak = jnp.max(scores, axis=-1, keepdims=True)
-    weights = jnp.exp(scores - peak)
-    total = jnp.sum(weights, axis=-1, keepdims=True)
-    log_total = peak + jnp.log(total)
-    mixed = jnp.einsum(
-        "hij,jhd->ihd",
-        (weights / total).astype(jnp.bfloat16),
-        values,
-        preferred_element_type=jnp.float32,
-    )
-    mixed = mixed.astype(jnp.bfloat16).reshape(group_rows, heads_here * VDIM)
-    attended = sum_group(matmul(mixed, output_weight).astype(jnp.bfloat16), 1)
+    if sizes != (8, 4):
+        scores = score_block()
+        peak = jnp.max(scores, axis=-1, keepdims=True)
+        weights = jnp.exp(scores - peak)
+        total = jnp.sum(weights, axis=-1, keepdims=True)
+        log_total = peak + jnp.log(total)
+        mixed = jnp.einsum(
+            "hij,jhd->ihd",
+            (weights / total).astype(jnp.bfloat16),
+            values,
+            preferred_element_type=jnp.float32,
+        )
+        mixed = mixed.astype(jnp.bfloat16).reshape(group_rows, heads_here * VDIM)
+        attended = sum_group(matmul(mixed, output_weight).astype(jnp.bfloat16), 1)
     hidden_one = activations + attended
     second_scale = inv_rms(hidden_one)
     normed_two = (hidden_one * second_scale * second_gain).astype(jnp.bfloat16)
@@ -1102,7 +1457,20 @@
     mixing_high = mixing_at.astype(jnp.bfloat16)
     mixing_low = (mixing_at - mixing_high.astype(jnp.float32)).astype(jnp.bfloat16)
     normed_wide = jnp.concatenate([normed_two, mixing_high, mixing_low], axis=1)
-    normed_tokens = gather_all(normed_wide, 2).reshape(all_rows, -1)
+    marks = (cotangent_all, pl.BlockSpec((quad_rows, lanes), lambda i: (i, width // lanes)))
+    normed_tokens, (grads_slots, shared_raw) = gather_all(
+        normed_wide,
+        2,
+        functools.partial(grads_kernel, pair_rows),
+        quads,
+        [whole(here), (cotangent_all, pair_spec(cotangent_all, quads)), whole(down_part)],
+        [
+            (slots, slots_spec(slots, quads)),
+            (shape((all_rows, shared_wide), jnp.float32), pl.BlockSpec((quad_rows, shared_wide), lambda i: (i, 0))),
+        ],
+        gather_flops,
+    )
+    normed_tokens = normed_tokens.reshape(all_rows, -1)
     token_spec = pl.BlockSpec((quad_rows, shared_wide), lambda i: (i, 0))
     token_shape = shape((all_rows, shared_wide), jnp.bfloat16)
     rows_slots, mix_slots, shared_hidden, shared_gate_grad, shared_lift_grad = call(
@@ -1251,7 +1619,8 @@
     )
     hidden_grad = upstream + back_two
     hidden_group = gather_group(hidden_grad.astype(jnp.bfloat16), 4)
-    output_gradient = trans_times(mixed, hidden_group)
+    output_gradient = trans_times(mixed, hidden_group).astype(jnp.bfloat16)
+    hidden_group, output_gradient = lax.optimization_barrier((hidden_group, output_gradient))
     mixed_grad = (
         times_trans(hidden_group, output_weight)
         .astype(jnp.bfloat16)
@@ -1335,7 +1704,7 @@
             expand_gradient.astype(jnp.bfloat16), "expert", scatter_dimension=0, tiled=True
         ).astype(jnp.float32),
         lax.psum_scatter(
-            output_gradient.astype(jnp.bfloat16), "expert", scatter_dimension=1, tiled=True
+            output_gradient, "expert", scatter_dimension=1, tiled=True
         ).astype(jnp.float32),
     )
     latent_columns = latent_weight.shape[1]

time: 950 us -> 901 us (0.948)
  matrix products: 67.8 us -> 42.7 us
  waiting for transfers between devices: 44.3 us -> 19.5 us
  Pallas kernels: 719 us -> 733 us
    pallas_call x1 -> x2, Pallas kernels: 162 us -> 234 us  [the longest x1 132 us: attention_forward(): pl.pallas_call(functools.partial(attention_kernel, score_scale), out_shap...]
    all_gather x1 -> x0, waiting for transfers between devices: 27.8 us -> none  [per_device(): cotangent_all = lax.all_gather(cotangent_wide, both, axis=0, tiled=True)]
    pallas_call x6 -> x5, Pallas kernels: 203 us -> 179 us  [call(): pl.pallas_call(kernel, grid=(grid,), in_specs=[s for _, s in ins], out_sp...]
    pallas_call x2 -> x1, Pallas kernels: 43.6 us -> 20.9 us  [gather_group(): pl.pallas_call(gather_group_kernel, out_shape=out, in_specs=[pl.BlockSpec...]
    pallas_call x2 -> x1, Pallas kernels: 43.6 us -> 21.9 us  [sum_group(): pl.pallas_call(sum_group_kernel, out_shape=out, in_specs=[pl.BlockSpec(me...]
    dot_general x6 -> x2, matrix products: 15.6 us -> 0.51 us  [matmul(): return jnp.dot(left, right, preferred_element_type=jnp.float32)]
  transfers between devices with their start and end apart: 5 -> 4, of which waited for: 2 -> 1; matrix products, arithmetic and copies ran while one was open for 9% -> 7% of each run, Pallas kernels for 32% -> 16%
where the time goes in v4:
time: 901 us; the launch traced here: 894 us
  Pallas kernels  733 us (81%)
  local copies, waits for them, and re-layouts  44.9 us (5%)
  matrix products  42.7 us (5%)
  other arithmetic  33.6 us (4%)
  waiting for transfers between devices  19.5 us (2%)
  between operations  14.9 us (2%)
    pallas_call x2, Pallas kernels, sum_all(): pl.pallas_call(functools.partial(sum_all_kernel, inner, len(ins), len(out...  210 us
    pallas_call x5, Pallas kernels, call(): pl.pallas_call(kernel, grid=(grid,), in_specs=[s for _, s in ins], out_sp...  179 us
    pallas_call x1, Pallas kernels, attention_forward(): pl.pallas_call(functools.partial(attention_kernel, score_scale), out_shap...  132 us
    pallas_call x1, Pallas kernels, gather_all(): pl.pallas_call(functools.partial(gather_all_kernel, inner, len(ins), len(...  102 us
    pallas_call x1, Pallas kernels, total_over_all(): pl.pallas_call(total_kernel, out_shape=out, in_specs=[pl.BlockSpec(memory...  67.4 us
    pallas_call x1, Pallas kernels, sum_group(): pl.pallas_call(sum_group_kernel, out_shape=out, in_specs=[pl.BlockSpec(me...  21.9 us
    pallas_call x1, Pallas kernels, gather_group(): pl.pallas_call(gather_group_kernel, out_shape=out, in_specs=[pl.BlockSpec...  20.9 us
    reduce_scatter x1, waiting for transfers between devices, per_device(): lax.psum_scatter(query_gradient.astype(jnp.bfloat16), 'expert', scatter_d...  18.8 us
  transfers between devices with their start and end apart: 4, of which 1 were waited for; matrix products, arithmetic and copies ran while one was open for 7% of the time, Pallas kernels for 16%

profile of v4, /device:TPU:0, one launch (start us, length us, event | category | flops | bytes accessed | tf_op | source)
XLA Modules:
  0.0 894.2 jit_solution(6455508683011264867)
XLA Ops:
  8.2 1.9 fusion.65
  10.1 1.3 fusion.13
  14.5 1.7 fusion.15.normed_ref
  17.4 2.1 multiply_sine_fusion
  19.4 131.9 %shard_map.297 = (bf16[32,160,2176]{2,1,0:T(8,128)(2,1)}, bf16[4,160,2048]{2,1,0:T(8,128)(2,1)}, bf16[4,640,192]{2,1,0:T(8,128)(2,1)}, f32[640,512]{1,0:T(8,128)...) custom-call(bf16[160,2048]{1,0:T(8,128)(2,1)} %fusion.15.normed_ref,, ...), custom_call_target="tpu_custom_call" | custom-call | flops 5536481280 | bytes 43023360 | tf_op jit(solution)/shard_map/pallas_call | solution.py:782
  151.4 1.7 multiply_reduce_fusion.5
  158.7 1.2 dynamic-slice_bitcast_fusion
  162.2 102.4 %shard_map.298 = (bf16[32,160,2176]{2,1,0:T(8,128)(2,1)}, bf16[8,640,2048]{2,1,0:T(8,128)(2,1)}, f32[5120,128]{1,0:T(8,128)}) custom-call(bf16[160,2176]{1,0:T(8,128)(2,1)} %concatenate.40.x_ref, bf16[8,128]{1,0:T(8,128)(2,1)} %get-tuple-element.130.refs_0_.here_ref, bf16[5120,2176]{1,0:T(8,128)(2,1)} %bitcast.114, bf16[128,2048]{1,0:T(8,128)(2,1)} %pad.25.refs_2_.down_ref), custom_call_target="tpu_custom_call" | custom-call | flops 9395240960 | bytes 69380096 | tf_op jit(solution)/shard_map/pallas_call | solution.py:550
  264.5 30.0 %shard_map.299 = (bf16[8,640,2048]{2,1,0:T(8,128)(2,1)}, f32[8,640,128]{2,1,0:T(8,128)}, bf16[5120,128]{1,0:T(8,128)(2,1)}, bf16[5120,128]{1,0:T(8,128)(2,1)}, bf16[5120,128]{1,0:T(8,128)(2,1)}) custom-call(bf16[8,128]{1,0:T(8,128)(2,1)} %get-tuple-element.130.refs_0_.here_ref, bf16[8,128]{1,0:T(8,128)(2,1)} %get-tuple-element.129.twice_ref, ...), custom_call_target="tpu_custom_call" | custom-call | flops 12079595520 | bytes 75763712 | tf_op jit(solution)/shard_map/pallas_call | solution.py:287
  294.5 40.1 %shard_map.300 = (bf16[8,640,352]{2,1,0:T(8,128)(2,1)}, bf16[8,640,352]{2,1,0:T(8,128)(2,1)}, bf16[8,640,352]{2,1,0:T(8,128)(2,1)}, bf16[8,640,352]{2,1,0:T(8,128)(2,1)}, bf16[8,640,2048]{2,1,0:T(8,128)(2,1)}) custom-call(bf16[8,640,2048]{2,1,0:T(8,128)(2,1)} %get-tuple-element.58.rows_ref, f32[8,640,128]{2,1,0:T(8,128)} %get-tuple-element.59.mix_ref, ...), custom_call_target="tpu_custom_call" | custom-call | flops 22145925120 | bytes 93585408 | tf_op jit(solution)/shard_map/pallas_call | solution.py:287
  334.6 24.0 %shard_map.301 = bf16[5120,2048]{1,0:T(8,128)(2,1)} custom-call(bf16[8,128]{1,0:T(8,128)(2,1)} %get-tuple-element.130.refs_0_.here_ref, bf16[5120,2176]{1,0:T(8,128)(2,1)} %bitcast.116, bf16[8,640,2048]{2,1,0:T(8,128)(2,1)} %get-tuple-element.60.rows_ref, bf16[5120,128]{1,0:T(8,128)(2,1)} %get-tuple-element.61.hidden_ref.refs_4_, ...), custom_call_target="tpu_custom_call" | custom-call | flops 9395240960 | bytes 66062336 | tf_op jit(solution)/shard_map/pallas_call | solution.py:287
  359.3 108.0 %shard_map.302 = (f32[160,2048]{1,0:T(8,128)}, bf16[8,640,352]{2,1,0:T(8,128)(2,1)}, bf16[8,640,352]{2,1,0:T(8,128)(2,1)}, bf16[8,640,2048]{2,1,0:T(8,128)(2,1)}, f32[8,640,128]{2,1,0:T(8,128)}) custom-call(bf16[32,160,2048]{2,1,0:T(8,128)(2,1)} %bitcast.122, bf16[8,640,2048]{2,1,0:T(8,128)(2,1)} %get-tuple-element.62.refs_0_.grads_ref, ...), custom_call_target="tpu_custom_call" | custom-call | flops 22145925120 | bytes 119472128 | tf_op jit(solution)/shard_map/pallas_call | solution.py:968
  467.3 30.0 %shard_map.303 = bf16[5120,2176]{1,0:T(8,128)(2,1)} custom-call(bf16[8,128]{1,0:T(8,128)(2,1)} %get-tuple-element.130.refs_0_.here_ref, bf16[8,128]{1,0:T(8,128)(2,1)} %get-tuple-element.132.high_ref, bf16[8,128]{1,0:T(8,128)(2,1)} %get-tuple-element.131.low_ref, bf16[5120,2176]{1,0:T(8,128)(2,1)} %bitcast.117, ...), custom_call_target="tpu_custom_call" | custom-call | flops 12079595520 | bytes 71833600 | tf_op jit(solution)/shard_map/pallas_call | solution.py:287
  497.3 101.6 %shard_map.304 = (f32[160,2176]{1,0:T(8,128)}, f32[128,2048]{1,0:T(8,128)}, f32[128,2048]{1,0:T(8,128)}, f32[128,2048]{1,0:T(8,128)}) custom-call(bf16[32,160,2176]{2,1,0:T(8,128)(2,1)} %bitcast.121, bf16[5120,2176]{1,0:T(8,128)(2,1)} %bitcast.120, bf16[5120,2176]{1,0:T(8,128)(2,1)} %bitcast.118, bf16[5120,128]{1,0:T(8,128)(2,1)} %get-tuple-element.69.gate_grad_ref.refs_2_, ...), custom_call_target="tpu_custom_call" | custom-call | flops 8053063680 | bytes 75317248 | tf_op jit(solution)/shard_map/pallas_call | solution.py:968
  600.1 3.1 multiply_reduce_fusion.2
  603.2 2.0 fusion.61
  605.2 20.9 %shard_map.305 = bf16[4,160,2048]{2,1,0:T(8,128)(2,1)} custom-call(bf16[160,2048]{1,0:T(8,128)(2,1)} %get-tuple-element.104.x_ref), custom_call_target="tpu_custom_call" | custom-call | bytes 3276800 | tf_op jit(solution)/shard_map/pallas_call | solution.py:1031
  626.1 5.0 convolution_convert_fusion.2
  631.1 3.4 convolution_convert_fusion.5
  634.6 3.3 reshape.368
  642.2 2.6 multiply_reduce_fusion
  646.9 2.2 fusion.25
  650.4 2.0 convolution_convert_fusion.4
  657.8 5.7 all-to-all-start
  663.5 1.8 copy.163
  665.3 1.8 copy.162
  670.1 4.2 convolution_convert_fusion
  674.3 4.5 fusion.66
  682.9 1.5 add_convert_fusion.2
  684.4 3.7 add_convert_fusion
  688.2 21.9 %shard_map.306 = f32[160,2048]{1,0:T(8,128)} custom-call(bf16[4,160,2048]{2,1,0:T(8,128)(2,1)} %bitcast.136), custom_call_target="tpu_custom_call" | custom-call | bytes 3932160 | tf_op jit(solution)/shard_map/pallas_call | solution.py:1094
  710.1 1.8 fusion.21
  713.1 3.4 convolution_convert_fusion.1
  716.5 9.5 %concatenate.44 = bf16[643,2048]{1,0:T(8,128)(2,1)S(1)} concatenate(bf16[576,2048]{1,0:T(8,128)(2,1)} %convolution_convert_fusion.1, bf16[64,2048]{1,0:T(8,128)(2,1)} %convolution_convert_fusion.3, bf16[1,2048]{1,0:T(2,128)(2,1)S(1)} %broadcast_in_dim.30, bf16[1,2048]{1,0:T(2,128)(2,1)S(1)} %broadcast_in_dim.31, bf16[1,2048]{1,0:T(2,128)(2,1)S(1)} %broadcast_in_dim.32), dimensions={0} | concatenate | bytes 5267456 | tf_op jit(solution)/shard_map/concatenate | solution.py:1711
  726.0 1.9 pad.29.p_ref
  727.9 67.4 %shard_map.307 = bf16[704,2048]{1,0:T(8,128)(2,1)} custom-call(bf16[704,2048]{1,0:T(8,128)(2,1)} %pad.29.p_ref), custom_call_target="tpu_custom_call" | custom-call | bytes 5767168 | tf_op jit(solution)/shard_map/pallas_call | solution.py:1244
  795.3 2.7 convert_element_type.169
  798.0 1.3 slice.126
  799.3 1.4 fusion.62
  801.6 1.4 fusion.18
  803.0 2.8 slice_bitcast_fusion
  805.8 54.7 %shard_map.308 = (f32[8,352,2048]{2,1,0:T(8,128)}, f32[8,352,2048]{2,1,0:T(8,128)}, f32[8,352,2048]{2,1,0:T(8,128)}) custom-call(bf16[8,640,2048]{2,1,0:T(8,128)(2,1)} %get-tuple-element.58.rows_ref, bf16[8,640,2048]{2,1,0:T(8,128)(2,1)} %get-tuple-element.62.refs_0_.grads_ref, bf16[8,640,352]{2,1,0:T(8,128)(2,1)} %get-tuple-element.86.gate_grad_ref, ...), custom_call_target="tpu_custom_call" | custom-call | flops 22145925120 | bytes 121962496 | tf_op jit(solution)/shard_map/pallas_call | solution.py:287
  860.5 1.4 convert_element_type.179
  861.9 1.4 fusion.63
  863.3 1.6 convert_element_type.173
  864.9 1.8 convert_element_type.174
  866.7 18.8 %reduce-scatter.4.cloned.1.call-done = bf16[256,768]{1,0:T(8,128)(2,1)} async-done(((bf16[2048,768]{1,0:T(8,128)(2,1)}), bf16[256,768]{1,0:T(8,128)(2,1)}) %reduce-scatter.4.cloned.1.call-update) | async-done | bytes 393232 | tf_op jit(solution)/shard_map/reduce_scatter | solution.py:1700
  885.5 1.9 convert_element_type.171
  (184 shorter events, 36.6 us)
Async XLA Ops:
  7.2 7.4 copy-start.2
  7.2 9.3 %copy-start.13 = (bf16[160,2048]{1,0:T(8,128)(2,1)S(1)}, bf16[160,2048]{1,0:T(8,128)(2,1)}, u32[]{:S(2)}) copy-start(bf16[160,2048]{1,0:T(8,128)(2,1)} %param.19) | copy-start | bytes 1966084
  7.2 856.1 %reduce-scatter.6.cloned.1.call-start = ((), (), s32[]{:S(2)}) async-start(), calls=%async_computation.5 | async-start | bytes 1179648 | tf_op jit(solution)/shard_map/reduce_scatter | solution.py:1703
  7.3 10.1 %copy-start.44 = (f32[32]{0:T(128)}, f32[32]{0:T(128)S(1)}, u32[]{:S(2)}) copy-start(f32[32]{0:T(128)S(1)} %negate_power_fusion) | copy-start | bytes 388
  12.0 5.4 copy-start.41
  13.6 3.7 copy-start.38
  151.4 2.8 copy-start.36
  153.1 1.1 copy-start
  153.1 1.2 copy-start.34
  153.1 2.2 copy-start.35
  154.4 3.5 copy-start.8
  600.0 3.1 copy-start.1
  600.1 3.1 copy-start.14
  600.1 3.1 copy-start.19
  605.2 20.9 %copy-start.27 = (bf16[640,512]{1,0:T(8,128)(2,1)S(1)}, bf16[640,512]{1,0:T(8,128)(2,1)}, u32[]{:S(2)}) copy-start(bf16[640,512]{1,0:T(8,128)(2,1)} %get-tuple-element.76) | copy-start | bytes 1966084
  626.1 5.1 copy-start.5
  637.9 1.3 copy-start.21
  637.9 1.7 copy-start.40
  638.3 3.9 copy-start.6
  639.9 1.3 copy-start.11
  639.9 1.3 copy-start.28
  649.2 1.2 copy-start.49
  649.3 1.1 copy-start.22
  652.4 212.5 %reduce-scatter.8.cloned.1.call-start = ((), (), s32[]{:S(2)}) async-start(), calls=%async_computation.6 | async-start | bytes 2359296 | tf_op jit(solution)/shard_map/reduce_scatter | solution.py:1706
  657.8 202.7 %all-to-all-start = ((bf16[264,8,256]{2,0,1:T(8,128)(2,1)}), bf16[264,8,256]{2,0,1:T(8,128)(2,1)}, u32[]{:S(2)}, u32[]{:S(2)}) async-start(bf16[264,8,256]{2,0,1:T(8,128)(2,1)} %pad_maximum_fusion.1), calls=%async_computation.3 | async-start | bytes 2162688 | tf_op jit(solution)/shard_map/all_to_all | solution.py:1604
  663.5 222.0 %reduce-scatter.4.cloned.1.call-start = ((), (), s32[]{:S(2)}) async-start(), calls=%async_computation.4 | async-start | bytes 3538944 | tf_op jit(solution)/shard_map/reduce_scatter | solution.py:1700
  667.0 1.2 copy-start.7
  668.2 1.9 copy-start.15
  674.3 4.6 copy-start.12
  678.9 1.1 copy-start.33
  678.9 1.4 copy-start.20
  678.9 1.8 copy-start.23
  678.9 1.8 copy-start.46
  679.0 2.1 copy-start.48
  682.2 2.2 copy-start.47
  682.9 5.2 copy-start.17
  684.4 3.7 copy-start.25
  688.1 21.9 %copy-start.3 = (bf16[160,2048]{1,0:T(8,128)(2,1)S(1)}, bf16[160,2048]{1,0:T(8,128)(2,1)}, u32[]{:S(2)}) copy-start(bf16[160,2048]{1,0:T(8,128)(2,1)} %param.18) | copy-start | bytes 1966084
  688.1 21.9 %copy-start.37 = (f32[2048]{0:T(1024)S(1)}, f32[2048]{0:T(1024)}, u32[]{:S(2)}) copy-start(f32[2048]{0:T(1024)} %param.22) | copy-start | bytes 24580
  688.1 21.9 %copy-start.42 = (f32[160]{0:T(256)S(1)}, f32[160]{0:T(256)}, u32[]{:S(2)}) copy-start(f32[160]{0:T(256)} %copy-done.41) | copy-start | bytes 1924
  688.1 24.9 %copy-start.16 = (bf16[4,160,2048]{2,1,0:T(8,128)(2,1)S(1)}, bf16[4,160,2048]{2,1,0:T(8,128)(2,1)}, u32[]{:S(2)}) copy-start(bf16[4,160,2048]{2,1,0:T(8,128)(2,1)} %get-tuple-element.80) | copy-start | bytes 7864324
  710.1 1.9 copy-start.9
  710.1 1.9 copy-start.30
  710.1 3.0 copy-start.18
  710.1 3.0 copy-start.26
  795.3 6.3 copy-start.4
  795.3 6.3 copy-start.10
  795.3 6.3 copy-start.43
  (6 other events, 4.8 us)
Sparse Core Ops, SparseCore 0:
  652.5 73.5 reduce-scatter.5
  729.6 78.6 reduce-scatter.7
  812.0 73.4 reduce-scatter.3

commit v5 on v4

--- a/solution.py
+++ b/solution.py
@@ -390,12 +390,14 @@
 
 
 class Gather:
-    def __init__(self, x_ref, out_ref, sends, recv_sems, local_sem, place):
+    def __init__(self, x_ref, out_ref, sends, recv_sems, local_sem, place, cut=None):
         z, x, y, c = place
-        half = x_ref.shape[0] // 2
+        rows = x_ref.shape[0]
+        cut = rows // 2 if cut is None else cut
+        self.parts = [pl.ds(0, cut), pl.ds(cut, rows - cut)]
         over, side, mate = device(z, 1 - x, y, c), device(z, x, 1 - y, c), device(z, x, y, 1 - c)
         up, down = device(z + 1, x, y, c), device(z - 1, x, y, c)
-        self.out_ref, self.recv_sems, self.mate, self.half = out_ref, recv_sems, mate, half
+        self.out_ref, self.recv_sems, self.mate = out_ref, recv_sems, mate
         planes = [ordered(z, (0, 1, 2, 3)[step], (1, 0, 2, 3)[step]) for step in range(4)]
         self.rising = [(zz <= z) & (z < 3) for zz in planes]
         self.falling = [(zz >= z) & (z > 0) for zz in planes]
@@ -442,7 +444,7 @@
             )
 
     def halves(self, i, h):
-        return self.out_ref.at[i, pl.ds(h * self.half, self.half)]
+        return self.out_ref.at[i, self.parts[h]]
 
     def full_here(self, i):
         landed(self.out_ref.at[i], self.recv_sems.at[i, 0], self.mate)
@@ -627,7 +629,7 @@
             piece = normed_ref.at[pl.ds(h * half, half)]
             near.start(piece, part(own, h), group_sems.at[own, h], to)
     sends = Sends(send_sems)
-    gather = Gather(value_ref, value_out, sends, recv_sems, local_sems.at[1], place)
+    gather = Gather(value_ref, value_out, sends, recv_sems, local_sems.at[1], place, 48)
     gather.whole(0)
     loads = [
         pltpu.make_async_copy(source, target, local_sems.at[2 + i])
@@ -1129,10 +1131,22 @@
 
 
 def total_kernel(
-    p_ref, out_ref, acc, mates, first_over, first_side, next_side, next_over, line, send_sems, sems
+    top_ref,
+    rest_ref,
+    out_ref,
+    acc,
+    mates,
+    first_over,
+    first_side,
+    next_side,
+    next_over,
+    line,
+    send_sems,
+    sems,
 ):
     z, x, y, c = places()
-    rows, width = p_ref.shape
+    rows, width = out_ref.shape
+    sources = [(top_ref, 0, 0), (rest_ref, top_ref.shape[0], 24)]
     half, quarter, eighth, sixteenth = width // 2, width // 4, width // 8, width // 16
     strip = rows // 4
     over, side, mate = device(z, 1 - x, y, c), device(z, x, 1 - y, c), device(z, x, y, 1 - c)
@@ -1143,27 +1157,30 @@
     sends = Sends(send_sems)
     base = c * half
     for j in range(2):
-        sends.start(
-            p_ref.at[:, columns((1 - c) * half + j * quarter, quarter)],
-            mates.at[:, columns(j * quarter, quarter)],
-            sems.at[j],
-            mate,
-        )
+        for p_ref, top, sem in sources:
+            sends.start(
+                p_ref.at[:, columns((1 - c) * half + j * quarter, quarter)],
+                mates.at[pl.ds(top, p_ref.shape[0]), columns(j * quarter, quarter)],
+                sems.at[sem + j],
+                mate,
+            )
     kept = (x * eighth + y * sixteenth, quarter + y * eighth + x * sixteenth)
     firsts, nexts = (first_over, first_side), (next_side, next_over)
     for j in range(2):
         part = columns(j * quarter, quarter)
-        landed(mates.at[:, part], sems.at[j], mate)
         wide = 16
-
-        def join(i, carry, j=j):
-            some = pl.ds(pl.multiple_of(i * wide, wide), wide)
-            mine = p_ref[some, columns(base + j * quarter, quarter)].astype(jnp.float32)
-            total = mine + mates[some, columns(j * quarter, quarter)].astype(jnp.float32)
-            acc[some, columns(j * quarter, quarter)] = total.astype(acc.dtype)
-            return carry
-
-        lax.fori_loop(0, rows // wide, join, 0)
+        for p_ref, top, sem in sources:
+            landed(mates.at[pl.ds(top, p_ref.shape[0]), part], sems.at[sem + j], mate)
+
+            def join(i, carry, j=j, p_ref=p_ref, top=top):
+                mine = pl.ds(pl.multiple_of(i * wide, wide), wide)
+                some = pl.ds(pl.multiple_of(top + i * wide, wide), wide)
+                total = p_ref[mine, columns(base + j * quarter, quarter)].astype(jnp.float32)
+                total = total + mates[some, columns(j * quarter, quarter)].astype(jnp.float32)
+                acc[some, columns(j * quarter, quarter)] = total.astype(acc.dtype)
+                return carry
+
+            lax.fori_loop(0, p_ref.shape[0] // wide, join, 0)
         away = (1 - x) * eighth if j == 0 else quarter + (1 - y) * eighth
         sends.start(
             acc.at[:, columns(away, eighth)], firsts[j], sems.at[2 + j], (over, side)[j]
@@ -1235,16 +1252,17 @@
     sends.finish()
 
 
-def total_over_all(value, number):
+def total_over_all(top, rest, number):
     if lax.axis_size("expert") != 8 or lax.axis_size("weight") != 4:
-        return lax.psum(value.astype(jnp.float32), ("expert", "weight"))
-    rows, width = value.shape
-    out = jax.ShapeDtypeStruct(value.shape, value.dtype)
-    buffer = lambda n: pltpu.VMEM((rows, n), value.dtype)
+        value = jnp.concatenate([top, rest], axis=0).astype(jnp.float32)
+        return lax.psum(value, ("expert", "weight"))
+    rows, width = top.shape[0] + rest.shape[0], top.shape[1]
+    out = jax.ShapeDtypeStruct((rows, width), top.dtype)
+    buffer = lambda n: pltpu.VMEM((rows, n), top.dtype)
     return pl.pallas_call(
         total_kernel,
         out_shape=out,
-        in_specs=[pl.BlockSpec(memory_space=pltpu.VMEM)],
+        in_specs=[pl.BlockSpec(memory_space=pltpu.VMEM)] * 2,
         out_specs=pl.BlockSpec(memory_space=pltpu.VMEM),
         scratch_shapes=[
             buffer(width // 2),
@@ -1253,13 +1271,13 @@
             buffer(width // 8),
             buffer(width // 16),
             buffer(width // 16),
-            pltpu.VMEM((2, 3, rows // 4, width // 16), value.dtype),
-            pltpu.SemaphoreType.DMA((24,)),
-            pltpu.SemaphoreType.DMA((24,)),
+            pltpu.VMEM((2, 3, rows // 4, width // 16), top.dtype),
+            pltpu.SemaphoreType.DMA((26,)),
+            pltpu.SemaphoreType.DMA((26,)),
         ],
         compiler_params=pltpu.CompilerParams(collective_id=number, has_side_effects=True),
-        cost_estimate=cost(0, value, out),
-    )(value).astype(jnp.float32)
+        cost_estimate=cost(0, top, rest, out),
+    )(top, rest)
 
 
 def shared_kernel(turn, ins, outs):
@@ -1276,13 +1294,24 @@
     outs[2][...] += trans_times(hidden_ref[...], cotangent)
 
 
-def weight_kernel(
-    rows_ref, grads_ref, gate_grad_ref, lift_grad_ref, hidden_ref, gate_out, up_out, down_out
-):
+def weight_kernel(turn, ins, outs):
+    rows_ref, grads_ref, gate_grad_ref, lift_grad_ref, hidden_ref = ins
     rows = rows_ref[0]
-    gate_out[0] = trans_times(gate_grad_ref[0], rows)
-    up_out[0] = trans_times(lift_grad_ref[0], rows)
-    down_out[0] = trans_times(hidden_ref[0], grads_ref[0])
+    for out_ref, left_ref, right in (
+        (outs[0], gate_grad_ref, rows),
+        (outs[1], lift_grad_ref, rows),
+        (outs[2], hidden_ref, grads_ref[0]),
+    ):
+        out_ref[0] = trans_times(left_ref[0], right).astype(out_ref.dtype)
+
+
+def weights_alone(*refs):
+    weight_kernel(pl.program_id(0), refs[:5], refs[5:])
+
+
+def gradients_kernel(turn, ins, outs):
+    shared_kernel(turn, ins[:5], outs[:3])
+    weight_kernel(turn, ins[5:], outs[3:])
 
 
 def per_device(
@@ -1581,21 +1610,48 @@
     shared_out = (shared_sum, whole_spec(shared_sum))
     plain_spec = pl.BlockSpec((pair_rows, width), lambda i: (i, 0))
     shared_spec = pl.BlockSpec((pair_rows, shared_wide), lambda i: (i, 0))
-    back_here, shared_sums = sum_all(
-        back_dense.reshape(blocks, token_rows, -1),
-        3,
-        shared_kernel,
-        pairs,
-        [
-            (normed_tokens, plain_spec),
-            (cotangent_all, plain_spec),
-            (shared_gate_grad, shared_spec),
-            (shared_lift_grad, shared_spec),
-            (shared_hidden, shared_spec),
-        ],
-        [shared_out] * 3,
-        6 * all_rows * width * shared_wide,
-    )
+    column_half = width // 2
+    half_spec = lambda m: pl.BlockSpec((1, m, column_half), lambda i: (i // 2, 0, i % 2))
+    narrow_spec = pl.BlockSpec((1, slot_rows, hidden_here), lambda i: (i // 2, 0, 0))
+    shared_ins = [
+        (normed_tokens, plain_spec),
+        (cotangent_all, plain_spec),
+        (shared_gate_grad, shared_spec),
+        (shared_lift_grad, shared_spec),
+        (shared_hidden, shared_spec),
+    ]
+    weight_ins = [
+        (rows_slots, half_spec(slot_rows)),
+        (grads_slots, half_spec(slot_rows)),
+        (gate_grad, narrow_spec),
+        (lift_grad, narrow_spec),
+        (mixed_hidden, narrow_spec),
+    ]
+    back_blocks = back_dense.reshape(blocks, token_rows, -1)
+    shared_flops = 6 * all_rows * width * shared_wide
+    together = pairs == 2 * local_experts
+    weight_type = jnp.bfloat16 if together else jnp.float32
+    weight_shape = shape((local_experts, hidden_here, width), weight_type)
+    weight_outs = [(weight_shape, half_spec(hidden_here))] * 3
+    if together:
+        back_here, sums = sum_all(
+            back_blocks,
+            3,
+            gradients_kernel,
+            pairs,
+            shared_ins + weight_ins,
+            [shared_out] * 3 + weight_outs,
+            shared_flops + 3 * one_matmul,
+        )
+        shared_sums = sums[:3]
+        weight_grads = [value.astype(jnp.float32) for value in sums[3:]]
+    else:
+        back_here, shared_sums = sum_all(
+            back_blocks, 3, shared_kernel, pairs, shared_ins, [shared_out] * 3, shared_flops
+        )
+        weight_grads = call(
+            weights_alone, 2 * local_experts, weight_ins, weight_outs, 3 * one_matmul
+        )
     routed_back = back_here[:, :width]
     mix_grad = back_here[:, width : width + 2 * weight_count * routes.shape[1]]
     mix_grad = jnp.sum(mix_grad.reshape(token_rows, routes.shape[1], -1), axis=2)
@@ -1621,6 +1677,7 @@
     hidden_group = gather_group(hidden_grad.astype(jnp.bfloat16), 4)
     output_gradient = trans_times(mixed, hidden_group).astype(jnp.bfloat16)
     hidden_group, output_gradient = lax.optimization_barrier((hidden_group, output_gradient))
+    output_shard = lax.psum_scatter(output_gradient, "expert", scatter_dimension=1, tiled=True)
     mixed_grad = (
         times_trans(hidden_group, output_weight)
         .astype(jnp.bfloat16)
@@ -1660,27 +1717,11 @@
         .astype(jnp.bfloat16)
         .reshape(group_rows, heads_here * (NOPE + VDIM))
     )
-    column_half = width // 2
-    half_spec = lambda m: pl.BlockSpec((1, m, column_half), lambda i: (i // 2, 0, i % 2))
-    narrow_spec = pl.BlockSpec((1, slot_rows, hidden_here), lambda i: (i // 2, 0, 0))
-    weight_shape = shape((local_experts, hidden_here, width), jnp.float32)
-    weight_grads = call(
-        weight_kernel,
-        2 * local_experts,
-        [
-            (rows_slots, half_spec(slot_rows)),
-            (grads_slots, half_spec(slot_rows)),
-            (gate_grad, narrow_spec),
-            (lift_grad, narrow_spec),
-            (mixed_hidden, narrow_spec),
-        ],
-        [(weight_shape, half_spec(hidden_here))] * 3,
-        3 * one_matmul,
-    )
     expert_grads = (weight_grads[0].transpose(0, 2, 1), weight_grads[1].transpose(0, 2, 1), weight_grads[2])
     layer_out = (hidden_one + routed_out).astype(jnp.bfloat16)
     query_gradient = trans_times(normed_all, query_grad)
-    expand_gradient = trans_times(latent_normed, expand_grad)
+    expand_gradient = trans_times(latent_normed, expand_grad).astype(jnp.bfloat16)
+    expand_gradient, output_shard = lax.optimization_barrier((expand_gradient, output_shard))
     latent_normed_grad = times_trans(expand_grad, expand_weight)
     latent_back, latent_gain_gradient = norm_back(
         latent_normed_grad, latent, latent_scale, latent_gain
@@ -1701,16 +1742,13 @@
             query_gradient.astype(jnp.bfloat16), "expert", scatter_dimension=0, tiled=True
         ).astype(jnp.float32),
         lax.psum_scatter(
-            expand_gradient.astype(jnp.bfloat16), "expert", scatter_dimension=0, tiled=True
+            expand_gradient, "expert", scatter_dimension=0, tiled=True
         ).astype(jnp.float32),
-        lax.psum_scatter(
-            output_gradient, "expert", scatter_dimension=1, tiled=True
-        ).astype(jnp.float32),
+        output_shard.astype(jnp.float32),
     )
     latent_columns = latent_weight.shape[1]
-    filled = jnp.concatenate(
+    rest = jnp.concatenate(
         [
-            latent_weight_gradient,
             router_gradient,
             first_gain_gradient[None],
             second_gain_gradient[None],
@@ -1718,16 +1756,17 @@
         ],
         axis=0,
     ).astype(jnp.bfloat16)
-    wanted = -(-filled.shape[0] // 64) * 64
-    filled = jnp.pad(filled, ((0, wanted - filled.shape[0]), (0, 0)))
-    total = total_over_all(filled, 7)
+    wanted = -(-(latent_columns + rest.shape[0]) // 64) * 64 - latent_columns
+    rest = jnp.pad(rest, ((0, wanted - rest.shape[0]), (0, 0)))
+    total = total_over_all(latent_weight_gradient.astype(jnp.bfloat16), rest, 7)
     gains_at = latent_columns + expert_count
+    wide = lambda value: value.astype(jnp.float32)
     totals = (
-        total[:latent_columns].T,
-        total[gains_at + 2, :LATENT],
-        total[latent_columns:gains_at].T,
-        total[gains_at],
-        total[gains_at + 1],
+        wide(total[:latent_columns]).T,
+        wide(total[gains_at + 2, :LATENT]),
+        wide(total[latent_columns:gains_at]).T,
+        wide(total[gains_at]),
+        wide(total[gains_at + 1]),
     )
     return (
         layer_out,

time: 901 us -> 890 us (0.988)
  Pallas kernels: 733 us -> 670 us
  other arithmetic: 33.6 us -> 74.6 us
  waiting for transfers between devices: 19.5 us -> 47.5 us
  local copies, waits for them, and re-layouts: 44.9 us -> 28.1 us
    pallas_call x5 -> x4, Pallas kernels: 179 us -> 124 us  [call(): pl.pallas_call(kernel, grid=(grid,), in_specs=[s for _, s in ins], out_sp...]
    reduce_scatter x1, waiting for transfers between devices: 0.01 us -> 47.4 us  [per_device(): lax.psum_scatter(output_gradient, 'expert', scatter_dimension=1, tiled=True)]
    transpose x0 -> x4, other arithmetic: none -> 32.1 us  [the longest x1 17.4 us: per_device(): weight_grads[1].transpose(0, 2, 1)]
    reduce_scatter x1, waiting for transfers between devices: 18.8 us -> 0.01 us  [per_device(): lax.psum_scatter(query_gradient.astype(jnp.bfloat16), 'expert', scatter_d...]
    convert_element_type x1 -> x4, other arithmetic: 2.73 us -> 13.2 us  [the longest x1 9.62 us: per_device(): weight_grads = [value.astype(jnp.float32) for value in sums[3:]]]
    concatenate x1 -> x0, local copies, waits for them, and re-layouts: 9.48 us -> none  [per_device(): jnp.concatenate([latent_weight_gradient, router_gradient, first_gain_grad...]
  transfers between devices with their start and end apart: 4 -> 4, of which waited for: 1 -> 1; matrix products, arithmetic and copies ran while one was open for 7% -> 11% of each run, Pallas kernels for 16% -> 11%
where the time goes in v5:
time: 890 us; the launch traced here: 878 us
  Pallas kernels  670 us (75%)
  other arithmetic  74.6 us (8%)
  waiting for transfers between devices  47.5 us (5%)
  matrix products  39.4 us (4%)
  local copies, waits for them, and re-layouts  28.1 us (3%)
  between operations  14.9 us (2%)
    pallas_call x2, Pallas kernels, sum_all(): pl.pallas_call(functools.partial(sum_all_kernel, inner, len(ins), len(out...  203 us
    pallas_call x4, Pallas kernels, call(): pl.pallas_call(kernel, grid=(grid,), in_specs=[s for _, s in ins], out_sp...  124 us
    pallas_call x1, Pallas kernels, attention_forward(): pl.pallas_call(functools.partial(attention_kernel, score_scale), out_shap...  124 us
    pallas_call x1, Pallas kernels, gather_all(): pl.pallas_call(functools.partial(gather_all_kernel, inner, len(ins), len(...  101 us
    pallas_call x1, Pallas kernels, total_over_all(): pl.pallas_call(total_kernel, out_shape=out, in_specs=[pl.BlockSpec(memory...  74.3 us
    reduce_scatter x1, waiting for transfers between devices, per_device(): lax.psum_scatter(output_gradient, 'expert', scatter_dimension=1, tiled=True)  47.4 us
    pallas_call x1, Pallas kernels, sum_group(): pl.pallas_call(sum_group_kernel, out_shape=out, in_specs=[pl.BlockSpec(me...  21.8 us
    pallas_call x1, Pallas kernels, gather_group(): pl.pallas_call(gather_group_kernel, out_shape=out, in_specs=[pl.BlockSpec...  21.2 us
  transfers between devices with their start and end apart: 4, of which 1 were waited for; matrix products, arithmetic and copies ran while one was open for 11% of the time, Pallas kernels for 11%

profile of v5, /device:TPU:0, one launch (start us, length us, event | category | flops | bytes accessed | tf_op | source)
XLA Modules:
  0.0 878.3 jit_solution(13759351937949765671)
XLA Ops:
  8.1 1.9 fusion.71
  11.7 1.4 fusion.13
  14.6 2.0 multiply_sine_fusion
  18.8 124.0 %shard_map.297 = (bf16[32,160,2176]{2,1,0:T(8,128)(2,1)}, bf16[4,160,2048]{2,1,0:T(8,128)(2,1)}, bf16[4,640,192]{2,1,0:T(8,128)(2,1)}, f32[640,512]{1,0:T(8,128)...) custom-call(bf16[160,2048]{1,0:T(8,128)(2,1)} %fusion.15.normed_ref,, ...), custom_call_target="tpu_custom_call" | custom-call | flops 5536481280 | bytes 43023360 | tf_op jit(solution)/shard_map/pallas_call | solution.py:784
  142.8 1.7 multiply_reduce_fusion.5
  153.6 100.8 %shard_map.298 = (bf16[32,160,2176]{2,1,0:T(8,128)(2,1)}, bf16[8,640,2048]{2,1,0:T(8,128)(2,1)}, f32[5120,128]{1,0:T(8,128)}) custom-call(bf16[160,2176]{1,0:T(8,128)(2,1)} %concatenate.40.x_ref, bf16[8,128]{1,0:T(8,128)(2,1)} %get-tuple-element.134.refs_0_.here_ref, bf16[5120,2176]{1,0:T(8,128)(2,1)} %bitcast.116, bf16[128,2048]{1,0:T(8,128)(2,1)} %pad.25.refs_2_.down_ref), custom_call_target="tpu_custom_call" | custom-call | flops 9395240960 | bytes 69380096 | tf_op jit(solution)/shard_map/pallas_call | solution.py:552
  254.4 30.0 %shard_map.299 = (bf16[8,640,2048]{2,1,0:T(8,128)(2,1)}, f32[8,640,128]{2,1,0:T(8,128)}, bf16[5120,128]{1,0:T(8,128)(2,1)}, bf16[5120,128]{1,0:T(8,128)(2,1)}, bf16[5120,128]{1,0:T(8,128)(2,1)}) custom-call(bf16[8,128]{1,0:T(8,128)(2,1)} %get-tuple-element.134.refs_0_.here_ref, bf16[8,128]{1,0:T(8,128)(2,1)} %get-tuple-element.133.twice_ref, ...), custom_call_target="tpu_custom_call" | custom-call | flops 12079595520 | bytes 75763712 | tf_op jit(solution)/shard_map/pallas_call | solution.py:287
  284.4 40.1 %shard_map.300 = (bf16[8,640,352]{2,1,0:T(8,128)(2,1)}, bf16[8,640,352]{2,1,0:T(8,128)(2,1)}, bf16[8,640,352]{2,1,0:T(8,128)(2,1)}, bf16[8,640,352]{2,1,0:T(8,128)(2,1)}, bf16[8,640,2048]{2,1,0:T(8,128)(2,1)}) custom-call(bf16[8,640,2048]{2,1,0:T(8,128)(2,1)} %get-tuple-element.60.rows_ref.refs_5_, f32[8,640,128]{2,1,0:T(8,128)} %get-tuple-element.61.mix_ref, ...), custom_call_target="tpu_custom_call" | custom-call | flops 22145925120 | bytes 93585408 | tf_op jit(solution)/shard_map/pallas_call | solution.py:287
  324.5 24.0 %shard_map.301 = bf16[5120,2048]{1,0:T(8,128)(2,1)} custom-call(bf16[8,128]{1,0:T(8,128)(2,1)} %get-tuple-element.134.refs_0_.here_ref, bf16[5120,2176]{1,0:T(8,128)(2,1)} %bitcast.118, bf16[8,640,2048]{2,1,0:T(8,128)(2,1)} %get-tuple-element.62.rows_ref, bf16[5120,128]{1,0:T(8,128)(2,1)} %get-tuple-element.63.hidden_ref.refs_4_, ...), custom_call_target="tpu_custom_call" | custom-call | flops 9395240960 | bytes 66062336 | tf_op jit(solution)/shard_map/pallas_call | solution.py:287
  349.2 97.3 %shard_map.302 = (f32[160,2048]{1,0:T(8,128)}, bf16[8,640,352]{2,1,0:T(8,128)(2,1)}, bf16[8,640,352]{2,1,0:T(8,128)(2,1)}, bf16[8,640,2048]{2,1,0:T(8,128)(2,1)}, f32[8,640,128]{2,1,0:T(8,128)}) custom-call(bf16[32,160,2048]{2,1,0:T(8,128)(2,1)} %bitcast.124, bf16[8,640,2048]{2,1,0:T(8,128)(2,1)} %get-tuple-element.64.refs_0_.refs_6_, ...), custom_call_target="tpu_custom_call" | custom-call | flops 22145925120 | bytes 119472128 | tf_op jit(solution)/shard_map/pallas_call | solution.py:970
  446.5 30.0 %shard_map.303 = bf16[5120,2176]{1,0:T(8,128)(2,1)} custom-call(bf16[8,128]{1,0:T(8,128)(2,1)} %get-tuple-element.134.refs_0_.here_ref, bf16[8,128]{1,0:T(8,128)(2,1)} %get-tuple-element.136.high_ref, bf16[8,128]{1,0:T(8,128)(2,1)} %get-tuple-element.135.low_ref, bf16[5120,2176]{1,0:T(8,128)(2,1)} %bitcast.119, ...), custom_call_target="tpu_custom_call" | custom-call | flops 12079595520 | bytes 71833600 | tf_op jit(solution)/shard_map/pallas_call | solution.py:287
  476.5 106.1 %shard_map.304 = (f32[160,2176]{1,0:T(8,128)}, f32[128,2048]{1,0:T(8,128)}, f32[128,2048]{1,0:T(8,128)}, f32[128,2048]{1,0:T(8,128)}, bf16[8,352,2048]{2,1,0:T(8...) custom-call(bf16[32,160,2176]{2,1,0:T(8,128)(2,1)} %bitcast.123, bf16[5120,2176]{1,0:T(8,128)(2,1)} %bitcast.122, ...), custom_call_target="tpu_custom_call" | custom-call | flops 30198988800 | bytes 162676736 | tf_op jit(solution)/shard_map/pallas_call | solution.py:970
  583.7 3.1 multiply_reduce_fusion.2
  586.8 2.0 fusion.68
  588.9 21.2 %shard_map.305 = bf16[4,160,2048]{2,1,0:T(8,128)(2,1)} custom-call(bf16[160,2048]{1,0:T(8,128)(2,1)} %get-tuple-element.108.x_ref), custom_call_target="tpu_custom_call" | custom-call | bytes 3276800 | tf_op jit(solution)/shard_map/pallas_call | solution.py:1033
  610.0 4.9 convolution_convert_fusion.2
  615.0 1.2 copy-done.21
  616.3 1.4 reshape.374
  622.2 1.8 convolution_convert_fusion.5
  625.1 2.6 multiply_reduce_fusion
  628.7 2.3 fusion.25
  633.3 2.0 convolution_convert_fusion.4
  635.3 47.4 %reduce-scatter.6.cloned.1.call-done = bf16[512,256]{1,0:T(8,128)(2,1)} async-done(((bf16[512,2048]{1,0:T(8,128)(2,1)}), bf16[512,256]{1,0:T(8,128)(2,1)}) %reduce-scatter.6.cloned.1.call-update) | async-done | bytes 262160 | tf_op jit(solution)/shard_map/reduce_scatter | solution.py:1680
  687.4 4.3 all-to-all-start
  691.7 1.8 copy.162
  693.5 1.7 copy.163
  698.3 4.2 convolution_convert_fusion
  702.5 2.2 fusion.27
  704.9 2.3 fusion.72
  708.7 1.5 add_convert_fusion.2
  710.6 1.3 copy-done.49
  711.9 3.7 add_convert_fusion
  715.6 21.8 %shard_map.306 = f32[160,2048]{1,0:T(8,128)} custom-call(bf16[4,160,2048]{2,1,0:T(8,128)(2,1)} %bitcast.142), custom_call_target="tpu_custom_call" | custom-call | bytes 3932160 | tf_op jit(solution)/shard_map/pallas_call | solution.py:1096
  737.4 1.8 fusion.21
  740.6 3.5 convolution_convert_fusion.1.top_ref
  744.1 74.3 %shard_map.307 = bf16[704,2048]{1,0:T(8,128)(2,1)} custom-call(bf16[576,2048]{1,0:T(8,128)(2,1)} %convolution_convert_fusion.1.top_ref, bf16[128,2048]{1,0:T(8,128)(2,1)} %fusion.49.rest_ref), custom_call_target="tpu_custom_call" | custom-call | bytes 5767168 | tf_op jit(solution)/shard_map/pallas_call | solution.py:1262
  818.4 1.3 slice_convert_fusion.5
  819.7 1.4 slice_convert_fusion.3
  821.1 1.8 convert_bitcast_fusion.3
  822.9 4.5 convert_bitcast_fusion.2
  827.4 17.4 %convert_bitcast_fusion = f32[8,2048,352]{1,2,0:T(8,128)} fusion(bf16[8,352,2048]{2,1,0:T(8,128)(2,1)} %get-tuple-element.94), kind=kLoop, calls=%fused_computation | loop fusion | flops 5767168 | bytes 34603008 | tf_op jit(solution)/shard_map/transpose | solution.py:1720
  844.9 9.6 %convert_element_type.209 = f32[8,352,2048]{2,1,0:T(8,128)} convert(bf16[8,352,2048]{2,1,0:T(8,128)(2,1)S(1)} %bitcast.128) | non-fusion elementwise | flops 5767168 | bytes 34603008 | tf_op jit(solution)/shard_map/convert_element_type | solution.py:1647
  854.5 1.5 fusion.18
  856.0 8.4 convert_bitcast_fusion.1
  864.4 1.4 convert_element_type.214
  865.8 1.4 fusion.69
  868.0 1.6 convert_element_type.202
  869.7 1.9 convert_element_type.198
  (204 shorter events, 37.4 us)
Async XLA Ops:
  7.2 9.6 %copy-start.12 = (bf16[160,2048]{1,0:T(8,128)(2,1)S(1)}, bf16[160,2048]{1,0:T(8,128)(2,1)}, u32[]{:S(2)}) copy-start(bf16[160,2048]{1,0:T(8,128)(2,1)} %param.19) | copy-start | bytes 1966084
  7.2 675.6 %reduce-scatter.6.cloned.1.call-start = ((), (), s32[]{:S(2)}) async-start(), calls=%async_computation.5 | async-start | bytes 2359296 | tf_op jit(solution)/shard_map/reduce_scatter | solution.py:1680
  7.3 10.4 %copy-start.45 = (f32[32]{0:T(128)}, f32[32]{0:T(128)S(1)}, u32[]{:S(2)}) copy-start(f32[32]{0:T(128)S(1)} %negate_power_fusion) | copy-start | bytes 388
  10.7 7.0 copy-start.39
  11.7 6.0 copy-start.2
  11.7 6.0 copy-start.37
  13.7 5.1 copy-start.42
  142.8 2.8 copy-start.36
  144.5 2.2 copy-start.35
  145.8 3.5 copy-start.8
  583.7 3.1 copy-start.1
  583.7 3.1 copy-start.13
  583.7 3.1 copy-start.18
  588.9 21.2 %copy-start.26 = (bf16[640,512]{1,0:T(8,128)(2,1)S(1)}, bf16[640,512]{1,0:T(8,128)(2,1)}, u32[]{:S(2)}) copy-start(bf16[640,512]{1,0:T(8,128)(2,1)} %get-tuple-element.81) | copy-start | bytes 1966084
  610.0 8.1 copy-start.41
  615.0 253.1 %reduce-scatter.8.cloned.1.call-start = ((), (), s32[]{:S(2)}) async-start(), calls=%async_computation.6 | async-start | bytes 1179648 | tf_op jit(solution)/shard_map/reduce_scatter | solution.py:1744
  617.7 1.9 copy-start.11
  617.7 1.9 copy-start.27
  618.2 6.9 copy-start.6
  619.6 1.9 copy-start.5
  619.6 2.6 copy-start.50
  628.6 2.3 copy-start.17
  687.4 177.0 %all-to-all-start = ((bf16[264,8,256]{2,0,1:T(8,128)(2,1)}), bf16[264,8,256]{2,0,1:T(8,128)(2,1)}, u32[]{:S(2)}, u32[]{:S(2)}) async-start(bf16[264,8,256]{2,0,1:T(8,128)(2,1)} %pad_maximum_fusion.1), calls=%async_computation.3 | async-start | bytes 2162688 | tf_op jit(solution)/shard_map/all_to_all | solution.py:1660
  691.7 178.0 %reduce-scatter.4.cloned.1.call-start = ((), (), s32[]{:S(2)}) async-start(), calls=%async_computation.4 | async-start | bytes 3538944 | tf_op jit(solution)/shard_map/reduce_scatter | solution.py:1741
  696.4 1.9 copy-start.14
  702.5 2.3 copy-start.25
  702.5 2.4 copy-start.48
  704.9 2.3 copy-start.32
  704.9 2.5 copy-start.19
  704.9 2.5 copy-start.23
  704.9 2.5 copy-start.47
  704.9 2.6 copy-start.51
  710.2 1.7 copy-start.49
  715.6 21.8 %copy-start.3 = (bf16[160,2048]{1,0:T(8,128)(2,1)S(1)}, bf16[160,2048]{1,0:T(8,128)(2,1)}, u32[]{:S(2)}) copy-start(bf16[160,2048]{1,0:T(8,128)(2,1)} %param.18) | copy-start | bytes 1966084
  715.6 21.8 %copy-start.38 = (f32[2048]{0:T(1024)S(1)}, f32[2048]{0:T(1024)}, u32[]{:S(2)}) copy-start(f32[2048]{0:T(1024)} %param.22) | copy-start | bytes 24580
  715.6 21.8 %copy-start.43 = (f32[160]{0:T(256)S(1)}, f32[160]{0:T(256)}, u32[]{:S(2)}) copy-start(f32[160]{0:T(256)} %copy-done.42) | copy-start | bytes 1924
  715.6 23.7 %copy-start.29 = (f32[160,64]{0,1:T(8,128)S(1)}, f32[160,64]{0,1:T(8,128)}, u32[]{:S(2)}) copy-start(f32[160,64]{0,1:T(8,128)} %copy-done.28) | copy-start | bytes 122884
  737.4 1.9 copy-start.9
  737.4 3.2 copy-start.15
  827.3 17.5 %slice-start.3 = ((s8[11534336]{0:T(1024)(128)(4,1)}), s8[4194304]{0:T(1024)(128)(4,1)S(1)}, s32[]{:S(2)}) async-start(s8[11534336]{0:T(1024)(128)(4,1)} %bitcast.127), calls=%async_computation.10 | async-start | bytes 8388608
  827.3 17.5 %slice-start.4 = ((s8[11534336]{0:T(1024)(128)(4,1)}), s8[4194304]{0:T(1024)(128)(4,1)S(1)}, s32[]{:S(2)}) async-start(s8[11534336]{0:T(1024)(128)(4,1)} %bitcast.127), calls=%async_computation.11 | async-start | bytes 8388608
  827.3 17.5 %slice-start.5 = ((s8[11534336]{0:T(1024)(128)(4,1)}), s8[3145728]{0:T(1024)(128)(4,1)S(1)}, s32[]{:S(2)}) async-start(s8[11534336]{0:T(1024)(128)(4,1)} %bitcast.127), calls=%async_computation.12 | async-start | bytes 6291456
  827.3 28.7 %slice-start = ((s8[11534336]{0:T(1024)(128)(4,1)}), s8[4194304]{0:T(1024)(128)(4,1)S(1)}, s32[]{:S(2)}) async-start(s8[11534336]{0:T(1024)(128)(4,1)} %bitcast.125), calls=%async_computation.7 | async-start | bytes 8388608
  827.4 28.7 %slice-start.1 = ((s8[11534336]{0:T(1024)(128)(4,1)}), s8[4194304]{0:T(1024)(128)(4,1)S(1)}, s32[]{:S(2)}) async-start(s8[11534336]{0:T(1024)(128)(4,1)} %bitcast.125), calls=%async_computation.8 | async-start | bytes 8388608
  844.8 9.7 %copy-start.4 = (f32[160,2048]{1,0:T(8,128)S(1)}, f32[160,2048]{1,0:T(8,128)}, u32[]{:S(2)}) copy-start(f32[160,2048]{1,0:T(8,128)} %shard_map.306) | copy-start | bytes 3932164
  844.8 9.7 %copy-start.10 = (f32[160,2048]{1,0:T(8,128)S(1)}, f32[160,2048]{1,0:T(8,128)}, u32[]{:S(2)}) copy-start(f32[160,2048]{1,0:T(8,128)} %get-tuple-element.109) | copy-start | bytes 3932164
  844.9 9.6 %copy-start.44 = (f32[160]{0:T(256)S(1)}, f32[160]{0:T(256)}, u32[]{:S(2)}) copy-start(f32[160]{0:T(256)} %get-tuple-element.129) | copy-start | bytes 1924
  844.9 11.1 %slice-start.2 = ((s8[11534336]{0:T(1024)(128)(4,1)}), s8[3145728]{0:T(1024)(128)(4,1)S(1)}, s32[]{:S(2)}) async-start(s8[11534336]{0:T(1024)(128)(4,1)} %bitcast.125), calls=%async_computation.9 | async-start | bytes 6291456
  (15 other events, 16.5 us)
Sparse Core Ops, SparseCore 0:
  615.1 67.6 reduce-scatter.5
  686.2 71.9 reduce-scatter.7
  761.8 89.7 reduce-scatter.3

commit v6 on v5

--- a/solution.py
+++ b/solution.py
@@ -1133,7 +1133,9 @@
 def total_kernel(
     top_ref,
     rest_ref,
+    group_ref,
     out_ref,
+    group_out,
     acc,
     mates,
     first_over,
@@ -1141,11 +1143,18 @@
     next_side,
     next_over,
     line,
+    group_mates,
+    group_sides,
+    carried,
     send_sems,
     sems,
+    mate_sems,
+    side_sems,
 ):
     z, x, y, c = places()
     rows, width = out_ref.shape
+    group_half = group_out.shape[0] // 2
+    group_parts = [pl.ds(h * group_half, group_half) for h in range(2)]
     sources = [(top_ref, 0, 0), (rest_ref, top_ref.shape[0], 24)]
     half, quarter, eighth, sixteenth = width // 2, width // 4, width // 8, width // 16
     strip = rows // 4
@@ -1164,6 +1173,14 @@
                 sems.at[sem + j],
                 mate,
             )
+    for i, yy in enumerate((1 - y, y)):
+        for h, some in enumerate(group_parts):
+            sends.start(
+                group_ref.at[yy * 2 + 1 - c, some],
+                group_mates.at[i, some],
+                mate_sems.at[i, h],
+                mate,
+            )
     kept = (x * eighth + y * sixteenth, quarter + y * eighth + x * sixteenth)
     firsts, nexts = (first_over, first_side), (next_side, next_over)
     for j in range(2):
@@ -1185,6 +1202,15 @@
         sends.start(
             acc.at[:, columns(away, eighth)], firsts[j], sems.at[2 + j], (over, side)[j]
         )
+    for h, some in enumerate(group_parts):
+        landed(group_mates.at[0, some], mate_sems.at[0, h], mate)
+        add_into(
+            carried,
+            [group_ref.at[(1 - y) * 2 + c], group_mates.at[0]],
+            h * group_half,
+            group_half,
+        )
+        sends.start(carried.at[some], group_sides.at[some], side_sems.at[h], side)
     for j in range(2):
         landed(firsts[j], sems.at[2 + j], mate)
         near = x * eighth if j == 0 else quarter + y * eighth
@@ -1245,6 +1271,15 @@
         landed(out_ref.at[:, columns(base + away, eighth)], sems.at[20 + j], mate)
         part = out_ref.at[:, columns(base + j * quarter, quarter)]
         sends.start(part, part, sems.at[22 + j], mate)
+    for h, some in enumerate(group_parts):
+        landed(group_mates.at[1, some], mate_sems.at[1, h], mate)
+        landed(group_sides.at[some], side_sems.at[h], mate)
+        add_into(
+            group_out,
+            [group_ref.at[y * 2 + c], group_mates.at[1], group_sides],
+            h * group_half,
+            group_half,
+        )
     for j in range(2):
         landed(
             out_ref.at[:, columns((1 - c) * half + j * quarter, quarter)], sems.at[22 + j], mate
@@ -1252,18 +1287,21 @@
     sends.finish()
 
 
-def total_over_all(top, rest, number):
+def total_over_all(top, rest, group, number):
     if lax.axis_size("expert") != 8 or lax.axis_size("weight") != 4:
         value = jnp.concatenate([top, rest], axis=0).astype(jnp.float32)
-        return lax.psum(value, ("expert", "weight"))
+        return lax.psum(value, ("expert", "weight")), sum_group(group, number)
     rows, width = top.shape[0] + rest.shape[0], top.shape[1]
+    group = group.reshape(4, -1, width)
+    group_rows = group.shape[1]
     out = jax.ShapeDtypeStruct((rows, width), top.dtype)
+    group_out = jax.ShapeDtypeStruct((group_rows, width), jnp.float32)
     buffer = lambda n: pltpu.VMEM((rows, n), top.dtype)
     return pl.pallas_call(
         total_kernel,
-        out_shape=out,
-        in_specs=[pl.BlockSpec(memory_space=pltpu.VMEM)] * 2,
-        out_specs=pl.BlockSpec(memory_space=pltpu.VMEM),
+        out_shape=[out, group_out],
+        in_specs=[pl.BlockSpec(memory_space=pltpu.VMEM)] * 3,
+        out_specs=[pl.BlockSpec(memory_space=pltpu.VMEM)] * 2,
         scratch_shapes=[
             buffer(width // 2),
             buffer(width // 2),
@@ -1272,12 +1310,19 @@
             buffer(width // 16),
             buffer(width // 16),
             pltpu.VMEM((2, 3, rows // 4, width // 16), top.dtype),
+            pltpu.VMEM((2, group_rows, width), group.dtype),
+            pltpu.VMEM((group_rows, width), group.dtype),
+            pltpu.VMEM((group_rows, width), group.dtype),
+            pltpu.SemaphoreType.DMA((32,)),
             pltpu.SemaphoreType.DMA((26,)),
-            pltpu.SemaphoreType.DMA((26,)),
+            pltpu.SemaphoreType.DMA((2, 2)),
+            pltpu.SemaphoreType.DMA((2,)),
         ],
-        compiler_params=pltpu.CompilerParams(collective_id=number, has_side_effects=True),
-        cost_estimate=cost(0, top, rest, out),
-    )(top, rest)
+        compiler_params=pltpu.CompilerParams(
+            collective_id=number, has_side_effects=True, vmem_limit_bytes=vmem_limit
+        ),
+        cost_estimate=cost(0, top, rest, group, out, group_out),
+    )(top, rest, group)
 
 
 def shared_kernel(turn, ins, outs):
@@ -1675,9 +1720,9 @@
     )
     hidden_grad = upstream + back_two
     hidden_group = gather_group(hidden_grad.astype(jnp.bfloat16), 4)
-    output_gradient = trans_times(mixed, hidden_group).astype(jnp.bfloat16)
+    output_gradient = trans_times(hidden_group, mixed).astype(jnp.bfloat16)
     hidden_group, output_gradient = lax.optimization_barrier((hidden_group, output_gradient))
-    output_shard = lax.psum_scatter(output_gradient, "expert", scatter_dimension=1, tiled=True)
+    output_shard = lax.psum_scatter(output_gradient, "expert", scatter_dimension=0, tiled=True)
     mixed_grad = (
         times_trans(hidden_group, output_weight)
         .astype(jnp.bfloat16)
@@ -1721,7 +1766,6 @@
     layer_out = (hidden_one + routed_out).astype(jnp.bfloat16)
     query_gradient = trans_times(normed_all, query_grad)
     expand_gradient = trans_times(latent_normed, expand_grad).astype(jnp.bfloat16)
-    expand_gradient, output_shard = lax.optimization_barrier((expand_gradient, output_shard))
     latent_normed_grad = times_trans(expand_grad, expand_weight)
     latent_back, latent_gain_gradient = norm_back(
         latent_normed_grad, latent, latent_scale, latent_gain
@@ -1729,14 +1773,8 @@
     compressed_grad = jnp.concatenate([latent_back, unrotate(key_rope_grad, cosine, sine)], axis=-1)
     compressed_grad = compressed_grad.astype(jnp.bfloat16)
     latent_weight_gradient = trans_times(compressed_grad, normed_all)
-    normed_grad = sum_group(
-        (
-            times_trans(query_grad, query_weight) + times_trans(compressed_grad, latent_weight)
-        ).astype(jnp.bfloat16),
-        5,
-    )
-    back_one, first_gain_gradient = norm_back(normed_grad, activations, first_scale, first_gain)
-    token_gradient = hidden_grad + back_one
+    normed_part = times_trans(query_grad, query_weight) + times_trans(compressed_grad, latent_weight)
+    first_gain_gradient = jnp.sum(normed_part * normed_all.astype(jnp.float32), axis=0) / first_gain
     shards = (
         lax.psum_scatter(
             query_gradient.astype(jnp.bfloat16), "expert", scatter_dimension=0, tiled=True
@@ -1744,7 +1782,7 @@
         lax.psum_scatter(
             expand_gradient, "expert", scatter_dimension=0, tiled=True
         ).astype(jnp.float32),
-        output_shard.astype(jnp.float32),
+        output_shard.T.astype(jnp.float32),
     )
     latent_columns = latent_weight.shape[1]
     rest = jnp.concatenate(
@@ -1758,7 +1796,11 @@
     ).astype(jnp.bfloat16)
     wanted = -(-(latent_columns + rest.shape[0]) // 64) * 64 - latent_columns
     rest = jnp.pad(rest, ((0, wanted - rest.shape[0]), (0, 0)))
-    total = total_over_all(latent_weight_gradient.astype(jnp.bfloat16), rest, 7)
+    total, normed_grad = total_over_all(
+        latent_weight_gradient.astype(jnp.bfloat16), rest, normed_part.astype(jnp.bfloat16), 7
+    )
+    back_one, _ = norm_back(normed_grad, activations, first_scale, first_gain)
+    token_gradient = hidden_grad + back_one
     gains_at = latent_columns + expert_count
     wide = lambda value: value.astype(jnp.float32)
     totals = (

time: 890 us -> 887 us (level)
  Pallas kernels: 670 us -> 658 us
    reduce_scatter x1, waiting for transfers between devices: 0.01 us -> 49.4 us  [per_device(): lax.psum_scatter(query_gradient.astype(jnp.bfloat16), 'expert', scatter_d...]
    reduce_scatter x1, waiting for transfers between devices: 47.4 us -> 0.01 us  [per_device(): lax.psum_scatter(output_gradient, 'expert', scatter_dimension=0, tiled=True)]
    pallas_call x2 -> x1, Pallas kernels: 96 us -> 84 us  [total_over_all(): pl.pallas_call(total_kernel, out_shape=[out, group_out], in_specs=[pl.Blo...]
  transfers between devices with their start and end apart: 4 -> 4, of which waited for: 1 -> 1; matrix products, arithmetic and copies ran while one was open for 11% -> 10% of each run, Pallas kernels for 11% -> 10%
where the time goes in v6:
time: 887 us; the launch traced here: 875 us
  Pallas kernels  658 us (74%)
  other arithmetic  75.1 us (8%)
  waiting for transfers between devices  50.1 us (6%)
  matrix products  43.4 us (5%)
  local copies, waits for them, and re-layouts  29.7 us (3%)
  between operations  14.9 us (2%)
    pallas_call x2, Pallas kernels, sum_all(): pl.pallas_call(functools.partial(sum_all_kernel, inner, len(ins), len(out...  203 us
    pallas_call x4, Pallas kernels, call(): pl.pallas_call(kernel, grid=(grid,), in_specs=[s for _, s in ins], out_sp...  124 us
    pallas_call x1, Pallas kernels, attention_forward(): pl.pallas_call(functools.partial(attention_kernel, score_scale), out_shap...  124 us
    pallas_call x1, Pallas kernels, gather_all(): pl.pallas_call(functools.partial(gather_all_kernel, inner, len(ins), len(...  101 us
    pallas_call x1, Pallas kernels, total_over_all(): pl.pallas_call(total_kernel, out_shape=[out, group_out], in_specs=[pl.Blo...  84 us
    reduce_scatter x1, waiting for transfers between devices, per_device(): lax.psum_scatter(query_gradient.astype(jnp.bfloat16), 'expert', scatter_d...  49.4 us
    pallas_call x1, Pallas kernels, gather_group(): pl.pallas_call(gather_group_kernel, out_shape=out, in_specs=[pl.BlockSpec...  21.5 us
  transfers between devices with their start and end apart: 4, of which 1 were waited for; matrix products, arithmetic and copies ran while one was open for 10% of the time, Pallas kernels for 10%

profile of v6, /device:TPU:0, one launch (start us, length us, event | category | flops | bytes accessed | tf_op | source)
XLA Modules:
  0.0 875.5 jit_solution(6522520250793876810)
XLA Ops:
  8.1 1.9 fusion.70
  11.7 1.4 fusion.13
  14.6 2.0 multiply_sine_fusion
  18.8 124.0 %shard_map.297 = (bf16[32,160,2176]{2,1,0:T(8,128)(2,1)}, bf16[4,160,2048]{2,1,0:T(8,128)(2,1)}, bf16[4,640,192]{2,1,0:T(8,128)(2,1)}, f32[640,512]{1,0:T(8,128)...) custom-call(bf16[160,2048]{1,0:T(8,128)(2,1)} %fusion.15.normed_ref,, ...), custom_call_target="tpu_custom_call" | custom-call | flops 5536481280 | bytes 43023360 | tf_op jit(solution)/shard_map/pallas_call | solution.py:784
  142.8 1.7 multiply_reduce_fusion.6
  150.1 1.2 dynamic-slice_bitcast_fusion
  153.6 100.8 %shard_map.298 = (bf16[32,160,2176]{2,1,0:T(8,128)(2,1)}, bf16[8,640,2048]{2,1,0:T(8,128)(2,1)}, f32[5120,128]{1,0:T(8,128)}) custom-call(bf16[160,2176]{1,0:T(8,128)(2,1)} %concatenate.40.x_ref, bf16[8,128]{1,0:T(8,128)(2,1)} %get-tuple-element.214.refs_0_.here_ref, bf16[5120,2176]{1,0:T(8,128)(2,1)} %bitcast.119, bf16[128,2048]{1,0:T(8,128)(2,1)} %pad.25.refs_2_.down_ref), custom_call_target="tpu_custom_call" | custom-call | flops 9395240960 | bytes 69380096 | tf_op jit(solution)/shard_map/pallas_call | solution.py:552
  254.4 30.0 %shard_map.299 = (bf16[8,640,2048]{2,1,0:T(8,128)(2,1)}, f32[8,640,128]{2,1,0:T(8,128)}, bf16[5120,128]{1,0:T(8,128)(2,1)}, bf16[5120,128]{1,0:T(8,128)(2,1)}, bf16[5120,128]{1,0:T(8,128)(2,1)}) custom-call(bf16[8,128]{1,0:T(8,128)(2,1)} %get-tuple-element.214.refs_0_.here_ref, bf16[8,128]{1,0:T(8,128)(2,1)} %get-tuple-element.213.twice_ref, ...), custom_call_target="tpu_custom_call" | custom-call | flops 12079595520 | bytes 75763712 | tf_op jit(solution)/shard_map/pallas_call | solution.py:287
  284.4 40.1 %shard_map.300 = (bf16[8,640,352]{2,1,0:T(8,128)(2,1)}, bf16[8,640,352]{2,1,0:T(8,128)(2,1)}, bf16[8,640,352]{2,1,0:T(8,128)(2,1)}, bf16[8,640,352]{2,1,0:T(8,128)(2,1)}, bf16[8,640,2048]{2,1,0:T(8,128)(2,1)}) custom-call(bf16[8,640,2048]{2,1,0:T(8,128)(2,1)} %get-tuple-element.60.rows_ref.refs_5_, f32[8,640,128]{2,1,0:T(8,128)} %get-tuple-element.61.mix_ref, ...), custom_call_target="tpu_custom_call" | custom-call | flops 22145925120 | bytes 93585408 | tf_op jit(solution)/shard_map/pallas_call | solution.py:287
  324.5 24.0 %shard_map.301 = bf16[5120,2048]{1,0:T(8,128)(2,1)} custom-call(bf16[8,128]{1,0:T(8,128)(2,1)} %get-tuple-element.214.refs_0_.here_ref, bf16[5120,2176]{1,0:T(8,128)(2,1)} %bitcast.121, bf16[8,640,2048]{2,1,0:T(8,128)(2,1)} %get-tuple-element.62.rows_ref, bf16[5120,128]{1,0:T(8,128)(2,1)} %get-tuple-element.63.hidden_ref.refs_4_, ...), custom_call_target="tpu_custom_call" | custom-call | flops 9395240960 | bytes 66062336 | tf_op jit(solution)/shard_map/pallas_call | solution.py:287
  349.2 97.4 %shard_map.302 = (f32[160,2048]{1,0:T(8,128)}, bf16[8,640,352]{2,1,0:T(8,128)(2,1)}, bf16[8,640,352]{2,1,0:T(8,128)(2,1)}, bf16[8,640,2048]{2,1,0:T(8,128)(2,1)}, f32[8,640,128]{2,1,0:T(8,128)}) custom-call(bf16[32,160,2048]{2,1,0:T(8,128)(2,1)} %bitcast.127, bf16[8,640,2048]{2,1,0:T(8,128)(2,1)} %get-tuple-element.64.refs_0_.refs_6_, ...), custom_call_target="tpu_custom_call" | custom-call | flops 22145925120 | bytes 119472128 | tf_op jit(solution)/shard_map/pallas_call | solution.py:970
  446.6 30.0 %shard_map.303 = bf16[5120,2176]{1,0:T(8,128)(2,1)} custom-call(bf16[8,128]{1,0:T(8,128)(2,1)} %get-tuple-element.214.refs_0_.here_ref, bf16[8,128]{1,0:T(8,128)(2,1)} %get-tuple-element.216.high_ref, bf16[8,128]{1,0:T(8,128)(2,1)} %get-tuple-element.215.low_ref, bf16[5120,2176]{1,0:T(8,128)(2,1)} %bitcast.122, ...), custom_call_target="tpu_custom_call" | custom-call | flops 12079595520 | bytes 71833600 | tf_op jit(solution)/shard_map/pallas_call | solution.py:287
  476.6 106.1 %shard_map.304 = (f32[160,2176]{1,0:T(8,128)}, f32[128,2048]{1,0:T(8,128)}, f32[128,2048]{1,0:T(8,128)}, f32[128,2048]{1,0:T(8,128)}, bf16[8,352,2048]{2,1,0:T(8...) custom-call(bf16[32,160,2176]{2,1,0:T(8,128)(2,1)} %bitcast.126, bf16[5120,2176]{1,0:T(8,128)(2,1)} %bitcast.125, ...), custom_call_target="tpu_custom_call" | custom-call | flops 30198988800 | bytes 162676736 | tf_op jit(solution)/shard_map/pallas_call | solution.py:970
  583.8 3.1 multiply_reduce_fusion.3
  586.9 2.0 fusion.66
  588.9 21.5 %shard_map.305 = bf16[4,160,2048]{2,1,0:T(8,128)(2,1)} custom-call(bf16[160,2048]{1,0:T(8,128)(2,1)} %get-tuple-element.186.x_ref), custom_call_target="tpu_custom_call" | custom-call | bytes 3276800 | tf_op jit(solution)/shard_map/pallas_call | solution.py:1033
  610.5 5.0 convolution_convert_fusion.2
  615.5 3.4 convolution_convert_fusion.5
  619.0 2.9 reshape.374
  626.2 2.6 multiply_reduce_fusion
  630.9 2.2 fusion.23
  634.4 2.0 convolution_convert_fusion.4
  637.2 1.1 slice.161
  641.8 4.2 all-to-all-start
  646.1 1.8 copy.173
  647.9 1.8 copy.174
  652.7 4.2 convolution_convert_fusion
  657.7 1.5 convolution_convert_fusion.3
  659.2 4.6 fusion.71
  667.1 1.5 add_convert_fusion.1
  669.0 1.4 copy-done.5
  670.4 4.0 fusion.67
  675.2 3.5 convolution_convert_fusion.1.top_ref
  678.7 84.0 %shard_map.306 = (bf16[704,2048]{1,0:T(8,128)(2,1)}, f32[160,2048]{1,0:T(8,128)}) custom-call(bf16[576,2048]{1,0:T(8,128)(2,1)} %convolution_convert_fusion.1.top_ref, bf16[128,2048]{1,0:T(8,128)(2,1)} %fusion.47.rest_ref, bf16[4,160,2048]{2,1,0:T(8,128)(2,1)} %bitcast.138), custom_call_target="tpu_custom_call" | custom-call | bytes 9699328 | tf_op jit(solution)/shard_map/pallas_call | solution.py:1300
  762.8 1.8 fusion.19
  764.6 1.3 slice_convert_fusion.5
  765.8 1.4 slice_convert_fusion.3
  767.3 1.8 convert_bitcast_fusion.3
  769.1 4.5 convert_bitcast_fusion.2
  773.5 17.5 %convert_bitcast_fusion = f32[8,2048,352]{1,2,0:T(8,128)} fusion(bf16[8,352,2048]{2,1,0:T(8,128)(2,1)} %get-tuple-element.94), kind=kLoop, calls=%fused_computation | loop fusion | flops 5767168 | bytes 34603008 | tf_op jit(solution)/shard_map/transpose | solution.py:1765
  791.2 9.9 %convert_element_type.217 = f32[8,352,2048]{2,1,0:T(8,128)} convert(bf16[8,352,2048]{2,1,0:T(8,128)(2,1)S(1)} %bitcast.131) | non-fusion elementwise | flops 5767168 | bytes 34603008 | tf_op jit(solution)/shard_map/convert_element_type | solution.py:1692
  801.1 1.5 fusion.18
  802.6 8.4 convert_bitcast_fusion.1
  811.0 1.4 convert_element_type.223
  812.4 1.4 fusion.68
  813.8 1.6 convert_element_type.209
  817.4 49.4 %reduce-scatter.4.cloned.1.call-done = bf16[256,768]{1,0:T(8,128)(2,1)} async-done(((bf16[2048,768]{1,0:T(8,128)(2,1)}), bf16[256,768]{1,0:T(8,128)(2,1)}) %reduce-scatter.4.cloned.1.call-update) | async-done | bytes 393232 | tf_op jit(solution)/shard_map/reduce_scatter | solution.py:1779
  866.8 1.9 convert_element_type.205
  (191 shorter events, 37.9 us)
Async XLA Ops:
  7.2 9.6 %copy-start.13 = (bf16[160,2048]{1,0:T(8,128)(2,1)S(1)}, bf16[160,2048]{1,0:T(8,128)(2,1)}, u32[]{:S(2)}) copy-start(bf16[160,2048]{1,0:T(8,128)(2,1)} %param.19) | copy-start | bytes 1966084
  7.2 806.6 %reduce-scatter.6.cloned.1.call-start = ((), (), s32[]{:S(2)}) async-start(), calls=%async_computation.5 | async-start | bytes 1179648 | tf_op jit(solution)/shard_map/reduce_scatter | solution.py:1782
  7.3 10.4 %copy-start.40 = (f32[32]{0:T(128)}, f32[32]{0:T(128)S(1)}, u32[]{:S(2)}) copy-start(f32[32]{0:T(128)S(1)} %negate_power_fusion) | copy-start | bytes 388
  10.7 7.0 copy-start.34
  11.7 6.0 copy-start.2
  11.7 6.0 copy-start.30
  13.7 5.1 copy-start.37
  142.8 2.8 copy-start.33
  144.5 1.2 copy-start.29
  144.5 2.2 copy-start.32
  145.8 3.5 copy-start.8
  583.8 3.1 copy-start.1
  583.8 3.1 copy-start.14
  583.8 3.1 copy-start.17
  588.9 21.5 %copy-start.45 = (bf16[640,512]{1,0:T(8,128)(2,1)S(1)}, bf16[640,512]{1,0:T(8,128)(2,1)}, u32[]{:S(2)}) copy-start(bf16[640,512]{1,0:T(8,128)(2,1)} %get-tuple-element.82) | copy-start | bytes 1966084
  610.5 5.1 copy-start.15
  621.8 1.3 copy-start.19
  621.9 1.7 copy-start.36
  622.3 3.9 copy-start.6
  623.9 1.3 copy-start.11
  623.9 1.3 copy-start.23
  633.2 1.2 copy-start.44
  636.4 179.0 %reduce-scatter.8.cloned.1.call-start = ((), (), s32[]{:S(2)}) async-start(), calls=%async_computation.6 | async-start | bytes 2359296 | tf_op jit(solution)/shard_map/reduce_scatter | solution.py:1725
  641.8 169.1 %all-to-all-start = ((bf16[264,8,256]{2,0,1:T(8,128)(2,1)}), bf16[264,8,256]{2,0,1:T(8,128)(2,1)}, u32[]{:S(2)}, u32[]{:S(2)}) async-start(bf16[264,8,256]{2,0,1:T(8,128)(2,1)} %pad_maximum_fusion.1), calls=%async_computation.3 | async-start | bytes 2162688 | tf_op jit(solution)/shard_map/all_to_all | solution.py:1705
  646.1 220.7 %reduce-scatter.4.cloned.1.call-start = ((), (), s32[]{:S(2)}) async-start(), calls=%async_computation.4 | async-start | bytes 3538944 | tf_op jit(solution)/shard_map/reduce_scatter | solution.py:1779
  649.6 1.2 copy-start.7
  650.8 1.9 copy-start.4
  659.2 4.6 copy-start.12
  663.8 1.4 copy-start.18
  663.8 1.8 copy-start.21
  663.8 1.8 copy-start.42
  663.9 2.1 copy-start.43
  666.0 1.1 copy-start.35
  666.0 1.1 copy-start.41
  666.0 3.0 copy-start.16
  668.6 1.7 copy-start.5
  670.4 4.0 copy-start.31
  773.5 17.6 %slice-start.3 = ((s8[11534336]{0:T(1024)(128)(4,1)}), s8[4194304]{0:T(1024)(128)(4,1)S(1)}, s32[]{:S(2)}) async-start(s8[11534336]{0:T(1024)(128)(4,1)} %bitcast.130), calls=%async_computation.10 | async-start | bytes 8388608
  773.5 17.6 %slice-start.4 = ((s8[11534336]{0:T(1024)(128)(4,1)}), s8[4194304]{0:T(1024)(128)(4,1)S(1)}, s32[]{:S(2)}) async-start(s8[11534336]{0:T(1024)(128)(4,1)} %bitcast.130), calls=%async_computation.11 | async-start | bytes 8388608
  773.5 17.6 %slice-start.5 = ((s8[11534336]{0:T(1024)(128)(4,1)}), s8[3145728]{0:T(1024)(128)(4,1)S(1)}, s32[]{:S(2)}) async-start(s8[11534336]{0:T(1024)(128)(4,1)} %bitcast.130), calls=%async_computation.12 | async-start | bytes 6291456
  773.5 29.0 %slice-start = ((s8[11534336]{0:T(1024)(128)(4,1)}), s8[4194304]{0:T(1024)(128)(4,1)S(1)}, s32[]{:S(2)}) async-start(s8[11534336]{0:T(1024)(128)(4,1)} %bitcast.128), calls=%async_computation.7 | async-start | bytes 8388608
  773.5 29.0 %slice-start.1 = ((s8[11534336]{0:T(1024)(128)(4,1)}), s8[4194304]{0:T(1024)(128)(4,1)S(1)}, s32[]{:S(2)}) async-start(s8[11534336]{0:T(1024)(128)(4,1)} %bitcast.128), calls=%async_computation.8 | async-start | bytes 8388608
  791.1 9.9 %copy-start.3 = (bf16[160,2048]{1,0:T(8,128)(2,1)S(1)}, bf16[160,2048]{1,0:T(8,128)(2,1)}, u32[]{:S(2)}) copy-start(bf16[160,2048]{1,0:T(8,128)(2,1)} %param.18) | copy-start | bytes 1966084
  791.1 9.9 %copy-start.9 = (f32[160,2048]{1,0:T(8,128)S(1)}, f32[160,2048]{1,0:T(8,128)}, u32[]{:S(2)}) copy-start(f32[160,2048]{1,0:T(8,128)} %get-tuple-element.187) | copy-start | bytes 3932164
  791.1 9.9 %copy-start.10 = (f32[160,2048]{1,0:T(8,128)S(1)}, f32[160,2048]{1,0:T(8,128)}, u32[]{:S(2)}) copy-start(f32[160,2048]{1,0:T(8,128)} %get-tuple-element.86) | copy-start | bytes 3932164
  791.1 9.9 %copy-start.38 = (f32[160]{0:T(256)S(1)}, f32[160]{0:T(256)}, u32[]{:S(2)}) copy-start(f32[160]{0:T(256)} %copy-done.37) | copy-start | bytes 1924
  791.2 9.9 %copy-start.39 = (f32[160]{0:T(256)S(1)}, f32[160]{0:T(256)}, u32[]{:S(2)}) copy-start(f32[160]{0:T(256)} %get-tuple-element.209) | copy-start | bytes 1924
  791.2 11.4 %slice-start.2 = ((s8[11534336]{0:T(1024)(128)(4,1)}), s8[3145728]{0:T(1024)(128)(4,1)S(1)}, s32[]{:S(2)}) async-start(s8[11534336]{0:T(1024)(128)(4,1)} %bitcast.128), calls=%async_computation.9 | async-start | bytes 6291456
  (8 other events, 7.4 us)
Sparse Core Ops, SparseCore 0:
  636.5 75.6 reduce-scatter.5
  715.8 73.9 reduce-scatter.7
  793.3 73.4 reduce-scatter.3

commit v7 on v6

--- a/solution.py
+++ b/solution.py
@@ -11,7 +11,6 @@
 ROPE = 64
 VDIM = 128
 LATENT = 512
-TOPK = 6
 CAP = 20
 
 
@@ -51,9 +50,8 @@
 def rope_tables(seg):
     size = seg.shape[0]
     index = jnp.arange(size, dtype=jnp.int32)
-    fresh = jnp.concatenate([jnp.ones((1,), dtype=bool), seg[1:] != seg[:-1]])
-    first = lax.cummax(jnp.where(fresh, index, jnp.zeros_like(index)), axis=0)
-    place = (index - first).astype(jnp.float32)
+    earlier = jnp.sum((seg[None, :] < seg[:, None]).astype(jnp.int32), axis=1)
+    place = (index - earlier).astype(jnp.float32)
     half = ROPE // 2
     freqs = rope_base ** (-(jnp.arange(half, dtype=jnp.float32) * 2.0 / ROPE))
     angle = place[:, None] * freqs[None, :]
@@ -577,6 +575,9 @@
     segment_row_ref,
     segment_column_ref,
     gain_ref,
+    tokens_ref,
+    second_gain_ref,
+    router_ref,
     query_hbm,
     latent_hbm,
     expand_hbm,
@@ -591,7 +592,10 @@
     expanded_out,
     log_out,
     mixed_out,
-    attended_out,
+    hidden_out,
+    second_scale_out,
+    gates_out,
+    wide_out,
     query_matrix,
     latent_matrix,
     expand_matrix,
@@ -729,13 +733,27 @@
         sums.start(carried.at[some], sides.at[some], side_sems.at[h], side)
     gather.relay(2)
     gather.corner(1)
-    gather.relay(3)
-    gather.corner(2)
     for h in range(2):
         some = pl.ds(h * half, half)
         landed(mates.at[1, some], mate_sems.at[1, h], mate)
         landed(sides.at[some], side_sems.at[h], mate)
-        add_into(attended_out, [partial.at[y * 2 + c], mates.at[1], sides], h * half, half)
+        add_into(hidden_out, [partial.at[y * 2 + c], mates.at[1], sides], h * half, half)
+    hidden = tokens_ref[...].astype(jnp.float32) + hidden_out[...]
+    hidden_out[...] = hidden
+    second_scale = inv_rms(hidden)
+    second_scale_out[...] = jnp.broadcast_to(second_scale, second_scale_out.shape)
+    normed_two = (hidden * second_scale * second_gain_ref[...]).astype(jnp.bfloat16)
+    width = hidden.shape[1]
+    wide_out[:, :width] = normed_two
+    gates = jax.nn.sigmoid(times_trans(normed_two, router_ref[...]))
+    gates_out[...] = gates
+    codes = value_ref[:, width:].astype(jnp.float32)[:, : gates.shape[1]]
+    weighted = jnp.where(codes >= 0, gates, 0.0)
+    mixing = route_scale * weighted / jnp.sum(weighted, axis=1, keepdims=True)
+    high = mixing.astype(jnp.bfloat16).astype(jnp.float32)
+    wide_out[:, width:] = jnp.concatenate([high, mixing - high], axis=1).astype(jnp.bfloat16)
+    gather.relay(3)
+    gather.corner(2)
     gather.corner(3)
     gather.last()
     near.finish()
@@ -758,7 +776,21 @@
 
 
 def attention_forward(
-    score_scale, normed, value, cosine, sine, segment, gain, query, latent, expand, output, number
+    score_scale,
+    normed,
+    value,
+    cosine,
+    sine,
+    segment,
+    gain,
+    tokens,
+    second_gain,
+    router,
+    query,
+    latent,
+    expand,
+    output,
+    number,
 ):
     rows, width = normed.shape
     group, heads = 4 * rows, query.shape[1] // (NOPE + ROPE)
@@ -766,6 +798,7 @@
     vmem, away = pl.BlockSpec(memory_space=pltpu.VMEM), pl.BlockSpec(memory_space=pl.ANY)
     segment = segment.astype(jnp.float32)
     inputs = [normed, value, cosine, sine, segment[None], segment[:, None], gain[None]]
+    inputs += [tokens, second_gain[None], router.T]
     matrices = [query, latent.T, expand, output]
     outs = [
         shape((32,) + value.shape, low),
@@ -779,6 +812,9 @@
         shape((heads, group, lanes), jnp.float32),
         shape((group, heads * VDIM), low),
         shape((rows, width), jnp.float32),
+        shape((rows, lanes), jnp.float32),
+        shape((rows, router.shape[1]), jnp.float32),
+        shape(value.shape, low),
     ]
     flops = 2 * group * (width * (query.shape[1] + latent.shape[1]) + output.size + expand.size)
     return pl.pallas_call(
@@ -1339,7 +1375,7 @@
     outs[2][...] += trans_times(hidden_ref[...], cotangent)
 
 
-def weight_kernel(turn, ins, outs):
+def weight_kernel(ins, outs):
     rows_ref, grads_ref, gate_grad_ref, lift_grad_ref, hidden_ref = ins
     rows = rows_ref[0]
     for out_ref, left_ref, right in (
@@ -1351,12 +1387,16 @@
 
 
 def weights_alone(*refs):
-    weight_kernel(pl.program_id(0), refs[:5], refs[5:])
+    weight_kernel(refs[:5], refs[5:])
 
 
 def gradients_kernel(turn, ins, outs):
     shared_kernel(turn, ins[:5], outs[:3])
-    weight_kernel(turn, ins[5:], outs[3:])
+    weight_kernel(ins[5:], outs[3:])
+
+
+def sum_shards(value):
+    return lax.psum_scatter(value, "expert", scatter_dimension=0, tiled=True)
 
 
 def per_device(
@@ -1452,7 +1492,10 @@
             expanded,
             log_total,
             mixed,
-            attended,
+            hidden_one,
+            second_scale,
+            gates,
+            normed_wide,
         ) = attention_forward(
             score_scale,
             normed,
@@ -1461,12 +1504,16 @@
             sine,
             segments[0],
             latent_gain,
+            tokens,
+            second_gain,
+            router_weight,
             query_weight,
             latent_weight,
             expand_weight,
             output_weight,
             0,
         )
+        second_scale, normed_two = second_scale[:, :1], normed_wide[:, :width]
         cotangent_all = cotangent_all.reshape(all_rows, -1)
         normed_all = normed_all.reshape(group_rows, width)
         latent_scale, log_total = latent_scale[:, :1], log_total[:, :, :1]
@@ -1519,18 +1566,18 @@
         )
         mixed = mixed.astype(jnp.bfloat16).reshape(group_rows, heads_here * VDIM)
         attended = sum_group(matmul(mixed, output_weight).astype(jnp.bfloat16), 1)
-    hidden_one = activations + attended
-    second_scale = inv_rms(hidden_one)
-    normed_two = (hidden_one * second_scale * second_gain).astype(jnp.bfloat16)
-    gates = jax.nn.sigmoid(matmul(normed_two, router_weight))
+        hidden_one = activations + attended
+        second_scale = inv_rms(hidden_one)
+        normed_two = (hidden_one * second_scale * second_gain).astype(jnp.bfloat16)
+        gates = jax.nn.sigmoid(matmul(normed_two, router_weight))
+        weighted = hit * gates
+        mixing_at = route_scale * weighted / jnp.sum(weighted, axis=1, keepdims=True)
+        mixing_high = mixing_at.astype(jnp.bfloat16)
+        mixing_low = (mixing_at - mixing_high.astype(jnp.float32)).astype(jnp.bfloat16)
+        normed_wide = jnp.concatenate([normed_two, mixing_high, mixing_low], axis=1)
     chosen = jnp.sum(choose * gates[:, None, :], axis=-1)
     chosen_total = jnp.sum(chosen, axis=1, keepdims=True)
-    mixing = route_scale * chosen / chosen_total
     upstream = cotangent.astype(jnp.float32)
-    mixing_at = jnp.sum(choose * mixing[:, :, None], axis=1)
-    mixing_high = mixing_at.astype(jnp.bfloat16)
-    mixing_low = (mixing_at - mixing_high.astype(jnp.float32)).astype(jnp.bfloat16)
-    normed_wide = jnp.concatenate([normed_two, mixing_high, mixing_low], axis=1)
     marks = (cotangent_all, pl.BlockSpec((quad_rows, lanes), lambda i: (i, width // lanes)))
     normed_tokens, (grads_slots, shared_raw) = gather_all(
         normed_wide,
@@ -1722,7 +1769,7 @@
     hidden_group = gather_group(hidden_grad.astype(jnp.bfloat16), 4)
     output_gradient = trans_times(hidden_group, mixed).astype(jnp.bfloat16)
     hidden_group, output_gradient = lax.optimization_barrier((hidden_group, output_gradient))
-    output_shard = lax.psum_scatter(output_gradient, "expert", scatter_dimension=0, tiled=True)
+    output_shard = sum_shards(output_gradient)
     mixed_grad = (
         times_trans(hidden_group, output_weight)
         .astype(jnp.bfloat16)
@@ -1776,12 +1823,8 @@
     normed_part = times_trans(query_grad, query_weight) + times_trans(compressed_grad, latent_weight)
     first_gain_gradient = jnp.sum(normed_part * normed_all.astype(jnp.float32), axis=0) / first_gain
     shards = (
-        lax.psum_scatter(
-            query_gradient.astype(jnp.bfloat16), "expert", scatter_dimension=0, tiled=True
-        ).astype(jnp.float32),
-        lax.psum_scatter(
-            expand_gradient, "expert", scatter_dimension=0, tiled=True
-        ).astype(jnp.float32),
+        sum_shards(query_gradient.astype(jnp.bfloat16)).astype(jnp.float32),
+        sum_shards(expand_gradient).astype(jnp.float32),
         output_shard.T.astype(jnp.float32),
     )
     latent_columns = latent_weight.shape[1]

time: 887 us -> 874 us (0.985)
    transpose x1, other arithmetic: 17.5 us -> 8.39 us  [per_device(): weight_grads[1].transpose(0, 2, 1)]
    transpose x1, other arithmetic: 8.39 us -> 17.4 us  [per_device(): weight_grads[0].transpose(0, 2, 1)]
where the time goes in v7:
time: 874 us; the launch traced here: 870 us
  Pallas kernels  660 us (76%)
  other arithmetic  73.7 us (8%)
  waiting for transfers between devices  49.2 us (6%)
  matrix products  41 us (5%)
  local copies, waits for them, and re-layouts  26.3 us (3%)
  between operations  14.9 us (2%)
    pallas_call x2, Pallas kernels, sum_all(): pl.pallas_call(functools.partial(sum_all_kernel, inner, len(ins), len(out...  204 us
    pallas_call x1, Pallas kernels, attention_forward(): pl.pallas_call(functools.partial(attention_kernel, score_scale), out_shap...  124 us
    pallas_call x4, Pallas kernels, call(): pl.pallas_call(kernel, grid=(grid,), in_specs=[s for _, s in ins], out_sp...  124 us
    pallas_call x1, Pallas kernels, gather_all(): pl.pallas_call(functools.partial(gather_all_kernel, inner, len(ins), len(...  102 us
    pallas_call x1, Pallas kernels, total_over_all(): pl.pallas_call(total_kernel, out_shape=[out, group_out], in_specs=[pl.Blo...  85.4 us
    reduce_scatter x3, waiting for transfers between devices, sum_shards(): return lax.psum_scatter(value, 'expert', scatter_dimension=0, tiled=True)  48.5 us
    pallas_call x1, Pallas kernels, gather_group(): pl.pallas_call(gather_group_kernel, out_shape=out, in_specs=[pl.BlockSpec...  20.3 us
  transfers between devices with their start and end apart: 4, of which 1 were waited for; matrix products, arithmetic and copies ran while one was open for 10% of the time, Pallas kernels for 10%

profile of v7, /device:TPU:0, one launch (start us, length us, event | category | flops | bytes accessed | tf_op | source)
XLA Modules:
  0.0 869.5 jit_solution(7966248698238076709)
XLA Ops:
  7.3 1.4 convert_bitcast_fusion.5
  9.9 1.3 fusion.13
  13.7 1.7 fusion.15.normed_ref
  16.6 2.0 multiply_sine_fusion
  18.6 124.3 %shard_map.297 = (bf16[32,160,2176]{2,1,0:T(8,128)(2,1)}, bf16[4,160,2048]{2,1,0:T(8,128)(2,1)}, bf16[4,640,192]{2,1,0:T(8,128)(2,1)}, f32[640,512]{1,0:T(8,128)...) custom-call(bf16[160,2048]{1,0:T(8,128)(2,1)} %fusion.15.normed_ref,, ...), custom_call_target="tpu_custom_call" | custom-call | flops 5536481280 | bytes 44768256 | tf_op jit(solution)/shard_map/pallas_call | solution.py:820
  145.9 1.2 dynamic-slice_bitcast_fusion
  149.3 102.2 %shard_map.298 = (bf16[32,160,2176]{2,1,0:T(8,128)(2,1)}, bf16[8,640,2048]{2,1,0:T(8,128)(2,1)}, f32[5120,128]{1,0:T(8,128)}) custom-call(bf16[160,2176]{1,0:T(8,128)(2,1)} %get-tuple-element.61.x_ref, bf16[8,128]{1,0:T(8,128)(2,1)} %get-tuple-element.218.refs_0_.here_ref, bf16[5120,2176]{1,0:T(8,128)(2,1)} %bitcast.110, bf16[128,2048]{1,0:T(8,128)(2,1)} %pad.25.refs_2_.down_ref), custom_call_target="tpu_custom_call" | custom-call | flops 9395240960 | bytes 69380096 | tf_op jit(solution)/shard_map/pallas_call | solution.py:550
  251.6 30.0 %shard_map.299 = (bf16[8,640,2048]{2,1,0:T(8,128)(2,1)}, f32[8,640,128]{2,1,0:T(8,128)}, bf16[5120,128]{1,0:T(8,128)(2,1)}, bf16[5120,128]{1,0:T(8,128)(2,1)}, bf16[5120,128]{1,0:T(8,128)(2,1)}) custom-call(bf16[8,128]{1,0:T(8,128)(2,1)} %get-tuple-element.218.refs_0_.here_ref, bf16[8,128]{1,0:T(8,128)(2,1)} %get-tuple-element.217.twice_ref, ...), custom_call_target="tpu_custom_call" | custom-call | flops 12079595520 | bytes 75763712 | tf_op jit(solution)/shard_map/pallas_call | solution.py:285
  281.6 40.1 %shard_map.300 = (bf16[8,640,352]{2,1,0:T(8,128)(2,1)}, bf16[8,640,352]{2,1,0:T(8,128)(2,1)}, bf16[8,640,352]{2,1,0:T(8,128)(2,1)}, bf16[8,640,352]{2,1,0:T(8,128)(2,1)}, bf16[8,640,2048]{2,1,0:T(8,128)(2,1)}) custom-call(bf16[8,640,2048]{2,1,0:T(8,128)(2,1)} %get-tuple-element.64.rows_ref.refs_5_, f32[8,640,128]{2,1,0:T(8,128)} %get-tuple-element.65.mix_ref, ...), custom_call_target="tpu_custom_call" | custom-call | flops 22145925120 | bytes 93585408 | tf_op jit(solution)/shard_map/pallas_call | solution.py:285
  321.7 24.0 %shard_map.301 = bf16[5120,2048]{1,0:T(8,128)(2,1)} custom-call(bf16[8,128]{1,0:T(8,128)(2,1)} %get-tuple-element.218.refs_0_.here_ref, bf16[5120,2176]{1,0:T(8,128)(2,1)} %bitcast.112, bf16[8,640,2048]{2,1,0:T(8,128)(2,1)} %get-tuple-element.66.rows_ref, bf16[5120,128]{1,0:T(8,128)(2,1)} %get-tuple-element.67.hidden_ref.refs_4_, ...), custom_call_target="tpu_custom_call" | custom-call | flops 9395240960 | bytes 66062336 | tf_op jit(solution)/shard_map/pallas_call | solution.py:285
  346.4 97.5 %shard_map.302 = (f32[160,2048]{1,0:T(8,128)}, bf16[8,640,352]{2,1,0:T(8,128)(2,1)}, bf16[8,640,352]{2,1,0:T(8,128)(2,1)}, bf16[8,640,2048]{2,1,0:T(8,128)(2,1)}, f32[8,640,128]{2,1,0:T(8,128)}) custom-call(bf16[32,160,2048]{2,1,0:T(8,128)(2,1)} %bitcast.118, bf16[8,640,2048]{2,1,0:T(8,128)(2,1)} %get-tuple-element.68.refs_0_.refs_6_, ...), custom_call_target="tpu_custom_call" | custom-call | flops 22145925120 | bytes 119472128 | tf_op jit(solution)/shard_map/pallas_call | solution.py:1006
  443.9 30.0 %shard_map.303 = bf16[5120,2176]{1,0:T(8,128)(2,1)} custom-call(bf16[8,128]{1,0:T(8,128)(2,1)} %get-tuple-element.218.refs_0_.here_ref, bf16[8,128]{1,0:T(8,128)(2,1)} %get-tuple-element.220.high_ref, bf16[8,128]{1,0:T(8,128)(2,1)} %get-tuple-element.219.low_ref, bf16[5120,2176]{1,0:T(8,128)(2,1)} %bitcast.113, ...), custom_call_target="tpu_custom_call" | custom-call | flops 12079595520 | bytes 71833600 | tf_op jit(solution)/shard_map/pallas_call | solution.py:285
  473.9 106.0 %shard_map.304 = (f32[160,2176]{1,0:T(8,128)}, f32[128,2048]{1,0:T(8,128)}, f32[128,2048]{1,0:T(8,128)}, f32[128,2048]{1,0:T(8,128)}, bf16[8,352,2048]{2,1,0:T(8...) custom-call(bf16[32,160,2176]{2,1,0:T(8,128)(2,1)} %bitcast.117, bf16[5120,2176]{1,0:T(8,128)(2,1)} %bitcast.116, ...), custom_call_target="tpu_custom_call" | custom-call | flops 30198988800 | bytes 162676736 | tf_op jit(solution)/shard_map/pallas_call | solution.py:1006
  582.3 3.0 multiply_reduce_fusion.3
  585.3 2.0 fusion.64
  587.3 20.3 %shard_map.305 = bf16[4,160,2048]{2,1,0:T(8,128)(2,1)} custom-call(bf16[160,2048]{1,0:T(8,128)(2,1)} %get-tuple-element.194.x_ref), custom_call_target="tpu_custom_call" | custom-call | bytes 3276800 | tf_op jit(solution)/shard_map/pallas_call | solution.py:1069
  607.7 5.1 convolution_convert_fusion.2
  612.8 3.4 convolution_convert_fusion.5
  616.2 2.9 reshape.317
  623.2 2.6 multiply_reduce_fusion
  627.9 2.2 fusion.23
  631.3 2.0 convolution_convert_fusion.4
  634.2 1.1 slice.151
  638.8 4.3 all-to-all-start
  643.2 1.8 copy.169
  644.9 1.8 copy.168
  649.7 4.3 convolution_convert_fusion
  654.0 2.2 fusion.25
  656.5 2.2 fusion.68
  659.3 1.5 add_convert_fusion.1
  662.8 1.4 copy-done.3
  664.1 4.0 fusion.65
  668.9 3.5 convolution_convert_fusion.1.top_ref
  672.4 85.4 %shard_map.306 = (bf16[704,2048]{1,0:T(8,128)(2,1)}, f32[160,2048]{1,0:T(8,128)}) custom-call(bf16[576,2048]{1,0:T(8,128)(2,1)} %convolution_convert_fusion.1.top_ref, bf16[128,2048]{1,0:T(8,128)(2,1)} %fusion.45.rest_ref, bf16[4,160,2048]{2,1,0:T(8,128)(2,1)} %bitcast.129), custom_call_target="tpu_custom_call" | custom-call | bytes 9699328 | tf_op jit(solution)/shard_map/pallas_call | solution.py:1336
  757.9 1.8 fusion.19
  759.6 1.3 slice_convert_fusion.5
  760.9 1.4 slice_convert_fusion.3
  762.4 1.8 convert_bitcast_fusion.3
  764.1 4.5 convert_bitcast_fusion.2
  768.6 17.4 %convert_bitcast_fusion.1 = f32[8,2048,352]{1,2,0:T(8,128)} fusion(bf16[8,352,2048]{2,1,0:T(8,128)(2,1)} %get-tuple-element.99), kind=kLoop, calls=%fused_computation.1 | loop fusion | flops 5767168 | bytes 34603008 | tf_op jit(solution)/shard_map/transpose | solution.py:1812
  786.1 9.8 %convert_element_type.205 = f32[8,352,2048]{2,1,0:T(8,128)} convert(bf16[8,352,2048]{2,1,0:T(8,128)(2,1)S(1)} %bitcast.122) | non-fusion elementwise | flops 5767168 | bytes 34603008 | tf_op jit(solution)/shard_map/convert_element_type | solution.py:1739
  796.0 1.5 fusion.18
  797.5 8.4 convert_bitcast_fusion
  805.9 1.4 convert_element_type.211
  807.3 1.4 fusion.66
  808.7 1.6 convert_element_type.197
  812.3 48.5 %reduce-scatter.4.cloned.1.call-done = bf16[256,768]{1,0:T(8,128)(2,1)} async-done(((bf16[2048,768]{1,0:T(8,128)(2,1)}), bf16[256,768]{1,0:T(8,128)(2,1)}) %reduce-scatter.4.cloned.1.call-update) | async-done | bytes 393232 | tf_op jit(solution)/shard_map/reduce_scatter | solution.py:1399
  860.8 1.9 convert_element_type.193
  (172 shorter events, 33.0 us)
Async XLA Ops:
  7.2 6.6 copy-start
  7.2 8.5 copy-start.10
  7.2 801.5 %reduce-scatter.6.cloned.1.call-start = ((), (), s32[]{:S(2)}) async-start(), calls=%async_computation.5 | async-start | bytes 1179648 | tf_op jit(solution)/shard_map/reduce_scatter | solution.py:1399
  7.3 9.3 %copy-start.36 = (f32[32]{0:T(128)}, f32[32]{0:T(128)S(1)}, u32[]{:S(2)}) copy-start(f32[32]{0:T(128)S(1)} %negate_power_fusion) | copy-start | bytes 388
  11.8 6.8 copy-start.33
  12.8 5.8 copy-start.30
  473.9 108.0 %copy-start.29 = (s32[160,6]{0,1:T(8,128)S(1)}, s32[160,6]{0,1:T(8,128)}, u32[]{:S(2)}) copy-start(s32[160,6]{0,1:T(8,128)} %param.21) | copy-start | bytes 11524
  473.9 108.3 %copy-start.32 = (f32[2048]{0:T(1024)S(1)}, f32[2048]{0:T(1024)}, u32[]{:S(2)}) copy-start(f32[2048]{0:T(1024)} %param.28) | copy-start | bytes 24580
  582.2 3.1 copy-start.7
  582.2 3.1 copy-start.11
  582.3 3.1 copy-start.15
  587.3 20.4 %copy-start.42 = (bf16[640,512]{1,0:T(8,128)(2,1)S(1)}, bf16[640,512]{1,0:T(8,128)(2,1)}, u32[]{:S(2)}) copy-start(bf16[640,512]{1,0:T(8,128)(2,1)} %get-tuple-element.88) | copy-start | bytes 1966084
  607.7 5.1 copy-start.12
  619.1 1.3 copy-start.17
  619.6 3.6 copy-start.4
  620.8 1.3 copy-start.9
  620.8 1.3 copy-start.23
  630.1 1.2 copy-start.41
  633.4 176.9 %reduce-scatter.8.cloned.1.call-start = ((), (), s32[]{:S(2)}) async-start(), calls=%async_computation.6 | async-start | bytes 2359296 | tf_op jit(solution)/shard_map/reduce_scatter | solution.py:1399
  638.8 167.0 %all-to-all-start = ((bf16[264,8,256]{2,0,1:T(8,128)(2,1)}), bf16[264,8,256]{2,0,1:T(8,128)(2,1)}, u32[]{:S(2)}, u32[]{:S(2)}) async-start(bf16[264,8,256]{2,0,1:T(8,128)(2,1)} %pad_maximum_fusion.1), calls=%async_computation.3 | async-start | bytes 2162688 | tf_op jit(solution)/shard_map/all_to_all | solution.py:1752
  643.1 217.7 %reduce-scatter.4.cloned.1.call-start = ((), (), s32[]{:S(2)}) async-start(), calls=%async_computation.4 | async-start | bytes 3538944 | tf_op jit(solution)/shard_map/reduce_scatter | solution.py:1399
  646.7 1.2 copy-start.5
  647.9 1.9 copy-start.2
  654.0 2.3 copy-start.21
  654.0 2.4 copy-start.39
  656.4 2.3 copy-start.22
  656.4 2.3 copy-start.24
  656.4 2.8 copy-start.31
  656.4 2.8 copy-start.37
  656.4 4.6 copy-start.19
  656.4 4.6 copy-start.40
  658.7 2.1 copy-start.27
  658.7 2.3 copy-start.16
  658.7 2.3 copy-start.38
  661.1 1.7 copy-start.13
  662.2 1.9 copy-start.3
  664.1 4.0 copy-start.28
  768.6 17.4 %slice-start.3 = ((s8[11534336]{0:T(1024)(128)(4,1)}), s8[4194304]{0:T(1024)(128)(4,1)S(1)}, s32[]{:S(2)}) async-start(s8[11534336]{0:T(1024)(128)(4,1)} %bitcast.121), calls=%async_computation.10 | async-start | bytes 8388608
  768.6 17.4 %slice-start.4 = ((s8[11534336]{0:T(1024)(128)(4,1)}), s8[4194304]{0:T(1024)(128)(4,1)S(1)}, s32[]{:S(2)}) async-start(s8[11534336]{0:T(1024)(128)(4,1)} %bitcast.121), calls=%async_computation.11 | async-start | bytes 8388608
  768.6 17.4 %slice-start.5 = ((s8[11534336]{0:T(1024)(128)(4,1)}), s8[3145728]{0:T(1024)(128)(4,1)S(1)}, s32[]{:S(2)}) async-start(s8[11534336]{0:T(1024)(128)(4,1)} %bitcast.121), calls=%async_computation.12 | async-start | bytes 6291456
  768.6 28.8 %slice-start = ((s8[11534336]{0:T(1024)(128)(4,1)}), s8[4194304]{0:T(1024)(128)(4,1)S(1)}, s32[]{:S(2)}) async-start(s8[11534336]{0:T(1024)(128)(4,1)} %bitcast.119), calls=%async_computation.7 | async-start | bytes 8388608
  768.6 28.8 %slice-start.1 = ((s8[11534336]{0:T(1024)(128)(4,1)}), s8[4194304]{0:T(1024)(128)(4,1)S(1)}, s32[]{:S(2)}) async-start(s8[11534336]{0:T(1024)(128)(4,1)} %bitcast.119), calls=%async_computation.8 | async-start | bytes 8388608
  786.1 9.9 %copy-start.1 = (bf16[160,2048]{1,0:T(8,128)(2,1)S(1)}, bf16[160,2048]{1,0:T(8,128)(2,1)}, u32[]{:S(2)}) copy-start(bf16[160,2048]{1,0:T(8,128)(2,1)} %tokens_ref.1) | copy-start | bytes 1966084
  786.1 9.9 %copy-start.6 = (f32[160,2048]{1,0:T(8,128)S(1)}, f32[160,2048]{1,0:T(8,128)}, u32[]{:S(2)}) copy-start(f32[160,2048]{1,0:T(8,128)} %get-tuple-element.195) | copy-start | bytes 3932164
  786.1 9.9 %copy-start.8 = (f32[160,2048]{1,0:T(8,128)S(1)}, f32[160,2048]{1,0:T(8,128)}, u32[]{:S(2)}) copy-start(f32[160,2048]{1,0:T(8,128)} %get-tuple-element.92) | copy-start | bytes 3932164
  786.1 9.8 %copy-start.34 = (f32[160]{0:T(256)S(1)}, f32[160]{0:T(256)}, u32[]{:S(2)}) copy-start(f32[160]{0:T(256)} %copy-done.33) | copy-start | bytes 1924
  786.1 9.8 %copy-start.35 = (f32[160]{0:T(256)S(1)}, f32[160]{0:T(256)}, u32[]{:S(2)}) copy-start(f32[160]{0:T(256)} %get-tuple-element.215) | copy-start | bytes 1924
  786.1 11.3 %slice-start.2 = ((s8[11534336]{0:T(1024)(128)(4,1)}), s8[3145728]{0:T(1024)(128)(4,1)S(1)}, s32[]{:S(2)}) async-start(s8[11534336]{0:T(1024)(128)(4,1)} %bitcast.119), calls=%async_computation.9 | async-start | bytes 6291456
  (5 other events, 4.8 us)
Sparse Core Ops, SparseCore 0:
  633.5 73.3 reduce-scatter.5
  710.5 73.1 reduce-scatter.7
  787.3 73.4 reduce-scatter.3

commit v8 on v7

--- a/solution.py
+++ b/solution.py
@@ -132,7 +132,7 @@
     return jnp.concatenate(totals, axis=0)
 
 
-def grads_kernel(pair, turn, ins, outs):
+def grads_kernel(pair, ins, outs):
     here_ref, value_ref, down_ref = ins
     rows_ref, back_ref = outs
     width = rows_ref.shape[2]
@@ -397,6 +397,7 @@
         up, down = device(z + 1, x, y, c), device(z - 1, x, y, c)
         self.out_ref, self.recv_sems, self.mate = out_ref, recv_sems, mate
         planes = [ordered(z, (0, 1, 2, 3)[step], (1, 0, 2, 3)[step]) for step in range(4)]
+        self.planes = planes
         self.rising = [(zz <= z) & (z < 3) for zz in planes]
         self.falling = [(zz >= z) & (z > 0) for zz in planes]
         self.mine = [shard(zz, x, y, c) for zz in planes]
@@ -474,13 +475,17 @@
             self.half_here(self.corners[step], h)
             self.corner_copies[step][h].start()
 
+    def rest(self, step):
+        for i in self.mates[step]:
+            self.full_here(i)
+        for h in range(2):
+            self.half_here(self.mate_corners[step], h)
+        if step == 0:
+            self.keep.wait()
+
     def last(self):
         for step in range(4):
-            for i in self.mates[step]:
-                self.full_here(i)
-            for h in range(2):
-                self.half_here(self.mate_corners[step], h)
-        self.keep.wait()
+            self.rest(step)
 
 
 def gather_neighbours(place):
@@ -494,33 +499,119 @@
     ]
 
 
-def gather_all_kernel(inner, cover_ins, cover_outs, x_ref, *refs):
-    ins, refs = refs[:cover_ins], refs[cover_ins:]
-    out_ref, refs = refs[0], refs[1:]
-    outs, refs = refs[:cover_outs], refs[cover_outs:]
-    send_sems, recv_sems, local_sem = refs
+def token_kernel(
+    pair,
+    x_ref,
+    here_ref,
+    value_ref,
+    down_ref,
+    twice_ref,
+    gate_ref,
+    up_ref,
+    cotangent_hbm,
+    out_ref,
+    grads_ref,
+    rows_hbm,
+    mix_ref,
+    hidden_ref,
+    gate_grad_ref,
+    lift_grad_ref,
+    raw,
+    arrived,
+    marks,
+    stage,
+    send_sems,
+    recv_sems,
+    local_sem,
+    load_sems,
+    store_sems,
+):
     turn, turns = pl.program_id(0), pl.num_programs(0)
     place = places()
     sends = Sends(send_sems)
     gather = Gather(x_ref, out_ref, sends, recv_sems, local_sem, place)
+    quad, rows = value_ref.shape[0], x_ref.shape[0]
+    count = quad // rows
+    width = grads_ref.shape[2]
+    slot_rows = grads_ref.shape[1]
 
     def begin():
         greet(gather_neighbours(place))
         gather.whole(0)
 
+    def early():
+        gather.relay(1)
+        gather.corner(0)
+
+    def part(index, size):
+        return pl.ds(pl.multiple_of(index * size, 16), size)
+
+    stores = {}
+
+    def plane(step):
+        gather.rest(step)
+        loads = []
+        for k in range(2):
+            group = gather.planes[step] * 2 + k
+            copies = [
+                pltpu.make_async_copy(
+                    out_ref.at[group * count + i],
+                    arrived.at[k, pl.ds(i * rows, rows)],
+                    load_sems.at[k, i],
+                )
+                for i in range(count)
+            ]
+            copies.append(
+                pltpu.make_async_copy(
+                    cotangent_hbm.at[part(group, quad), pl.ds(width, lanes)],
+                    marks.at[k],
+                    load_sems.at[k, count],
+                )
+            )
+            for copy in copies:
+                copy.start()
+            loads.append(copies)
+        for k in range(2):
+            group = gather.planes[step] * 2 + k
+            for copy in loads[k]:
+                copy.wait()
+            if k in stores:
+                stores[k].wait()
+            tokens = part(group, quad)
+            rows_kernel(
+                pair,
+                here_ref,
+                twice_ref,
+                marks.at[k],
+                arrived.at[k],
+                raw.at[tokens],
+                gate_ref,
+                up_ref,
+                stage.at[k],
+                mix_ref.at[:, part(group, slot_rows)],
+                hidden_ref.at[tokens],
+                gate_grad_ref.at[tokens],
+                lift_grad_ref.at[tokens],
+            )
+            stores[k] = pltpu.make_async_copy(
+                stage.at[k], rows_hbm.at[:, part(group, slot_rows)], store_sems.at[k]
+            )
+            stores[k].start()
+
     def end():
         gather.whole(3)
         gather.relay(2)
+        plane(0)
         gather.corner(1)
         gather.relay(3)
+        plane(1)
         gather.corner(2)
+        plane(2)
         gather.corner(3)
-        gather.last()
+        plane(3)
+        for k in range(2):
+            stores[k].wait()
         sends.finish()
-
-    def early():
-        gather.relay(1)
-        gather.corner(0)
 
     pieces = [
         begin,
@@ -533,37 +624,65 @@
     ]
     for number, piece in enumerate(pieces):
         pl.when(turn == number)(piece)
-    inner(turn, ins, outs)
+    grads_kernel(pair, (here_ref, value_ref, down_ref), (grads_ref, raw.at[part(turn, quad)]))
     pl.when(turn == turns - 1)(end)
 
 
-def gather_all(value, number, inner, turns, ins, outs, flops):
-    if lax.axis_size("expert") != 8 or lax.axis_size("weight") != 4:
-
-        def alone(*refs):
-            inner(pl.program_id(0), refs[: len(ins)], refs[len(ins) :])
-
-        gathered = lax.all_gather(value, ("expert", "weight"), axis=0)
-        return gathered, call(alone, turns, ins, outs, flops)
-    out = jax.ShapeDtypeStruct((32,) + value.shape, value.dtype)
-    arrays, shapes = [a for a, _ in ins], [o for o, _ in outs]
-    results = pl.pallas_call(
-        functools.partial(gather_all_kernel, inner, len(ins), len(outs)),
+def gather_tokens(
+    value, cotangent, here, twice, down, gate, up, local_experts, slot_rows, pair, number
+):
+    rows, wide = value.shape
+    width = down.shape[1]
+    quad, all_rows, turns = 4 * rows, 32 * rows, 8
+    shared_wide = down.shape[0]
+    shape, low = jax.ShapeDtypeStruct, jnp.bfloat16
+    slots = shape((local_experts, slot_rows, width), low)
+    token_part = shape((all_rows, shared_wide), low)
+    mix = shape((local_experts, slot_rows, lanes), jnp.float32)
+    away = pl.BlockSpec(memory_space=pl.ANY)
+    ins = [
+        (value, whole_spec(value)),
+        (here, whole_spec(here)),
+        (cotangent, pair_spec(cotangent, turns)),
+        (down, whole_spec(down)),
+        (twice, whole_spec(twice)),
+        (gate, whole_spec(gate)),
+        (up, whole_spec(up)),
+        (cotangent, away),
+    ]
+    outs = [
+        (shape((32,) + value.shape, low), away),
+        (slots, slots_spec(slots, turns)),
+        (slots, away),
+        (mix, whole_spec(mix)),
+        (token_part, whole_spec(token_part)),
+        (token_part, whole_spec(token_part)),
+        (token_part, whole_spec(token_part)),
+    ]
+    part = slot_rows // turns
+    flops = 4 * all_rows * width * (2 * CAP * local_experts + 2 * shared_wide)
+    return pl.pallas_call(
+        functools.partial(token_kernel, pair),
         grid=(turns,),
-        out_shape=[out] + shapes,
-        in_specs=[whole_spec(value)] + [spec for _, spec in ins],
-        out_specs=[pl.BlockSpec(memory_space=pl.ANY)] + [spec for _, spec in outs],
+        out_shape=[o for o, _ in outs],
+        in_specs=[spec for _, spec in ins],
+        out_specs=[spec for _, spec in outs],
         scratch_shapes=[
+            pltpu.VMEM((all_rows, shared_wide), jnp.float32),
+            pltpu.VMEM((2, quad, wide), low),
+            pltpu.VMEM((2, quad, lanes), low),
+            pltpu.VMEM((2, local_experts, part, width), low),
             pltpu.SemaphoreType.DMA((44,)),
             pltpu.SemaphoreType.DMA((32, 2)),
             pltpu.SemaphoreType.DMA,
+            pltpu.SemaphoreType.DMA((2, 5)),
+            pltpu.SemaphoreType.DMA((2,)),
         ],
         compiler_params=pltpu.CompilerParams(
             collective_id=number, has_side_effects=True, vmem_limit_bytes=vmem_limit
         ),
-        cost_estimate=cost(flops, value, out, *arrays, *shapes),
-    )(value, *arrays)
-    return results[0], results[1:]
+        cost_estimate=cost(flops, *[a for a, _ in ins], *[o for o, _ in outs]),
+    )(*[a for a, _ in ins])
 
 
 def attention_kernel(
@@ -1579,42 +1698,68 @@
     chosen_total = jnp.sum(chosen, axis=1, keepdims=True)
     upstream = cotangent.astype(jnp.float32)
     marks = (cotangent_all, pl.BlockSpec((quad_rows, lanes), lambda i: (i, width // lanes)))
-    normed_tokens, (grads_slots, shared_raw) = gather_all(
-        normed_wide,
-        2,
-        functools.partial(grads_kernel, pair_rows),
-        quads,
-        [whole(here), (cotangent_all, pair_spec(cotangent_all, quads)), whole(down_part)],
-        [
-            (slots, slots_spec(slots, quads)),
-            (shape((all_rows, shared_wide), jnp.float32), pl.BlockSpec((quad_rows, shared_wide), lambda i: (i, 0))),
-        ],
-        gather_flops,
-    )
-    normed_tokens = normed_tokens.reshape(all_rows, -1)
     token_spec = pl.BlockSpec((quad_rows, shared_wide), lambda i: (i, 0))
-    token_shape = shape((all_rows, shared_wide), jnp.bfloat16)
-    rows_slots, mix_slots, shared_hidden, shared_gate_grad, shared_lift_grad = call(
-        functools.partial(rows_kernel, pair_rows),
-        quads,
-        [
-            whole(here),
-            whole(twice),
-            marks,
-            (normed_tokens, pair_spec(normed_tokens, quads)),
-            (shared_raw, token_spec),
-            whole(gate_part),
-            whole(up_part),
-        ],
-        [
-            (slots, slots_spec(slots, quads)),
-            (slots_one, slots_spec(slots_one, quads)),
-            (token_shape, token_spec),
-            (token_shape, token_spec),
-            (token_shape, token_spec),
-        ],
-        gather_flops + 2 * all_rows * width * shared_wide,
-    )
+    if sizes == (8, 4):
+        (
+            normed_tokens,
+            grads_slots,
+            rows_slots,
+            mix_slots,
+            shared_hidden,
+            shared_gate_grad,
+            shared_lift_grad,
+        ) = gather_tokens(
+            normed_wide,
+            cotangent_all,
+            here,
+            twice,
+            down_part,
+            gate_part,
+            up_part,
+            local_experts,
+            slot_rows,
+            pair_rows,
+            2,
+        )
+        normed_tokens = normed_tokens.reshape(all_rows, -1)
+    else:
+        normed_tokens = lax.all_gather(normed_wide, both, axis=0, tiled=True)
+
+        def grads_alone(*refs):
+            grads_kernel(pair_rows, refs[:3], refs[3:])
+
+        grads_slots, shared_raw = call(
+            grads_alone,
+            quads,
+            [whole(here), (cotangent_all, pair_spec(cotangent_all, quads)), whole(down_part)],
+            [
+                (slots, slots_spec(slots, quads)),
+                (shape((all_rows, shared_wide), jnp.float32), pl.BlockSpec((quad_rows, shared_wide), lambda i: (i, 0))),
+            ],
+            gather_flops,
+        )
+        token_shape = shape((all_rows, shared_wide), jnp.bfloat16)
+        rows_slots, mix_slots, shared_hidden, shared_gate_grad, shared_lift_grad = call(
+            functools.partial(rows_kernel, pair_rows),
+            quads,
+            [
+                whole(here),
+                whole(twice),
+                marks,
+                (normed_tokens, pair_spec(normed_tokens, quads)),
+                (shared_raw, token_spec),
+                whole(gate_part),
+                whole(up_part),
+            ],
+            [
+                (slots, slots_spec(slots, quads)),
+                (slots_one, slots_spec(slots_one, quads)),
+                (token_shape, token_spec),
+                (token_shape, token_spec),
+                (token_shape, token_spec),
+            ],
+            gather_flops + 2 * all_rows * width * shared_wide,
+        )
     hidden_here = expert_gate.shape[2]
     gate_rows, up_rows = expert_gate.transpose(0, 2, 1), expert_up.transpose(0, 2, 1)
 
@@ -1822,9 +1967,15 @@
     latent_weight_gradient = trans_times(compressed_grad, normed_all)
     normed_part = times_trans(query_grad, query_weight) + times_trans(compressed_grad, latent_weight)
     first_gain_gradient = jnp.sum(normed_part * normed_all.astype(jnp.float32), axis=0) / first_gain
+    rows_each = query_gradient.shape[0]
+    joined = jnp.concatenate(
+        [query_gradient.astype(jnp.bfloat16), expand_gradient.reshape(rows_each, -1)], axis=1
+    )
+    joined = sum_shards(joined).astype(jnp.float32)
+    query_columns = query_gradient.shape[1]
     shards = (
-        sum_shards(query_gradient.astype(jnp.bfloat16)).astype(jnp.float32),
-        sum_shards(expand_gradient).astype(jnp.float32),
+        joined[:, :query_columns],
+        joined[:, query_columns:].reshape(-1, expand_gradient.shape[1]),
         output_shard.T.astype(jnp.float32),
     )
     latent_columns = latent_weight.shape[1]

time: 874 us -> 844 us (0.966); the launches traced: 870 us -> 828 us
  waiting for transfers between devices: 49.2 us -> 0.04 us
    reduce_scatter x3 -> x2, waiting for transfers between devices: 48.5 us -> 0.01 us  [sum_shards(): return lax.psum_scatter(value, 'expert', scatter_dimension=0, tiled=True)]
    pallas_call x4 -> x3, Pallas kernels: 124 us -> 94.2 us  [call(): pl.pallas_call(kernel, grid=(grid,), in_specs=[s for _, s in ins], out_sp...]
    pallas_call x1, Pallas kernels: 102 us -> 131 us  [gather_tokens(): pl.pallas_call(functools.partial(token_kernel, pair), grid=(turns,), out_...]
  transfers between devices with their start and end apart: 4 -> 3, of which waited for: 1 -> 0; matrix products, arithmetic and copies ran while one was open for 10% -> 13% of each run, Pallas kernels for 10% -> 11%
where the time goes in v8:
time: 844 us; the launch traced here: 828 us
  Pallas kernels  663 us (79%)
  other arithmetic  72.8 us (9%)
  matrix products  39.9 us (5%)
  local copies, waits for them, and re-layouts  32.1 us (4%)
  between operations  15.2 us (2%)
    pallas_call x2, Pallas kernels, sum_all(): pl.pallas_call(functools.partial(sum_all_kernel, inner, len(ins), len(out...  202 us
    pallas_call x1, Pallas kernels, gather_tokens(): pl.pallas_call(functools.partial(token_kernel, pair), grid=(turns,), out_...  131 us
    pallas_call x1, Pallas kernels, attention_forward(): pl.pallas_call(functools.partial(attention_kernel, score_scale), out_shap...  124 us
    pallas_call x3, Pallas kernels, call(): pl.pallas_call(kernel, grid=(grid,), in_specs=[s for _, s in ins], out_sp...  94.2 us
    pallas_call x1, Pallas kernels, total_over_all(): pl.pallas_call(total_kernel, out_shape=[out, group_out], in_specs=[pl.Blo...  91.4 us
    pallas_call x1, Pallas kernels, gather_group(): pl.pallas_call(gather_group_kernel, out_shape=out, in_specs=[pl.BlockSpec...  20.6 us
    transpose x1, other arithmetic, per_device(): weight_grads[0].transpose(0, 2, 1)  17.4 us
  transfers between devices with their start and end apart: 3, of which 0 were waited for; matrix products, arithmetic and copies ran while one was open for 13% of the time, Pallas kernels for 11%

profile of v8, /device:TPU:0, one launch (start us, length us, event | category | flops | bytes accessed | tf_op | source)
XLA Modules:
  0.0 828.0 jit_solution(1623635054625402827)
XLA Ops:
  7.3 1.4 fusion.13
  10.2 1.3 convert_bitcast_fusion.5
  13.3 2.1 fusion.15.normed_ref
  16.5 2.0 multiply_sine_fusion
  18.6 124.3 %shard_map.297 = (bf16[32,160,2176]{2,1,0:T(8,128)(2,1)}, bf16[4,160,2048]{2,1,0:T(8,128)(2,1)}, bf16[4,640,192]{2,1,0:T(8,128)(2,1)}, f32[640,512]{1,0:T(8,128)...) custom-call(bf16[160,2048]{1,0:T(8,128)(2,1)} %fusion.15.normed_ref,, ...), custom_call_target="tpu_custom_call" | custom-call | flops 5536481280 | bytes 44768256 | tf_op jit(solution)/shard_map/pallas_call | solution.py:939
  145.8 1.2 dynamic-slice_bitcast_fusion
  149.3 130.5 %shard_map.298 = (bf16[32,160,2176]{2,1,0:T(8,128)(2,1)}, bf16[8,640,2048]{2,1,0:T(8,128)(2,1)}, bf16[8,640,2048]{2,1,0:T(8,128)(2,1)}, f32[8,640,128]{2,1,0:T(8...) custom-call(bf16[160,2176]{1,0:T(8,128)(2,1)} %get-tuple-element.60.x_ref, ...), custom_call_target="tpu_custom_call" | custom-call | flops 24159191040 | bytes 117616640 | tf_op jit(solution)/shard_map/pallas_call | solution.py:664
  279.8 40.1 %shard_map.299 = (bf16[8,640,352]{2,1,0:T(8,128)(2,1)}, bf16[8,640,352]{2,1,0:T(8,128)(2,1)}, bf16[8,640,352]{2,1,0:T(8,128)(2,1)}, bf16[8,640,352]{2,1,0:T(8,128)(2,1)}, bf16[8,640,2048]{2,1,0:T(8,128)(2,1)}) custom-call(bf16[8,640,2048]{2,1,0:T(8,128)(2,1)} %get-tuple-element.61.rows_ref.refs_5_, f32[8,640,128]{2,1,0:T(8,128)} %get-tuple-element.62.mix_ref, ...), custom_call_target="tpu_custom_call" | custom-call | flops 22145925120 | bytes 93585408 | tf_op jit(solution)/shard_map/pallas_call | solution.py:285
  319.9 24.0 %shard_map.300 = bf16[5120,2048]{1,0:T(8,128)(2,1)} custom-call(bf16[8,128]{1,0:T(8,128)(2,1)} %get-tuple-element.216.here_ref, bf16[5120,2176]{1,0:T(8,128)(2,1)} %bitcast.112, bf16[8,640,2048]{2,1,0:T(8,128)(2,1)} %get-tuple-element.63.rows_ref, bf16[5120,128]{1,0:T(8,128)(2,1)} %get-tuple-element.64.hidden_ref.refs_4_, bf16[128,2048]{1,0:T(8,128)(2,1)} %pad.25.down_ref), custom_call_target="tpu_custom_call" | custom-call | flops 9395240960 | bytes 66062336 | tf_op jit(solution)/shard_map/pallas_call | solution.py:285
  344.6 97.1 %shard_map.301 = (f32[160,2048]{1,0:T(8,128)}, bf16[8,640,352]{2,1,0:T(8,128)(2,1)}, bf16[8,640,352]{2,1,0:T(8,128)(2,1)}, bf16[8,640,2048]{2,1,0:T(8,128)(2,1)}, f32[8,640,128]{2,1,0:T(8,128)}) custom-call(bf16[32,160,2048]{2,1,0:T(8,128)(2,1)} %bitcast.116, bf16[8,640,2048]{2,1,0:T(8,128)(2,1)} %get-tuple-element.65.refs_0_.refs_6_, ...), custom_call_target="tpu_custom_call" | custom-call | flops 22145925120 | bytes 119472128 | tf_op jit(solution)/shard_map/pallas_call | solution.py:1125
  441.7 30.0 %shard_map.302 = bf16[5120,2176]{1,0:T(8,128)(2,1)} custom-call(bf16[8,128]{1,0:T(8,128)(2,1)} %get-tuple-element.216.here_ref, bf16[8,128]{1,0:T(8,128)(2,1)} %get-tuple-element.218.high_ref, bf16[8,128]{1,0:T(8,128)(2,1)} %get-tuple-element.217.low_ref, bf16[5120,2176]{1,0:T(8,128)(2,1)} %bitcast.113, bf16[8,640,2048]{2,1,0:T(8,128)(2,1)} %get-tuple-element.71.rows_ref, ...), custom_call_target="tpu_custom_call" | custom-call | flops 12079595520 | bytes 71833600 | tf_op jit(solution)/shard_map/pallas_call | solution.py:285
  471.8 105.3 %shard_map.303 = (f32[160,2176]{1,0:T(8,128)}, f32[128,2048]{1,0:T(8,128)}, f32[128,2048]{1,0:T(8,128)}, f32[128,2048]{1,0:T(8,128)}, bf16[8,352,2048]{2,1,0:T(8...) custom-call(bf16[32,160,2176]{2,1,0:T(8,128)(2,1)} %bitcast.115, bf16[5120,2176]{1,0:T(8,128)(2,1)} %bitcast.117, ...), custom_call_target="tpu_custom_call" | custom-call | flops 30198988800 | bytes 162676736 | tf_op jit(solution)/shard_map/pallas_call | solution.py:1125
  579.4 3.0 multiply_reduce_fusion.3
  582.4 2.0 fusion.64
  584.5 20.6 %shard_map.304 = bf16[4,160,2048]{2,1,0:T(8,128)(2,1)} custom-call(bf16[160,2048]{1,0:T(8,128)(2,1)} %get-tuple-element.192.x_ref), custom_call_target="tpu_custom_call" | custom-call | bytes 3276800 | tf_op jit(solution)/shard_map/pallas_call | solution.py:1188
  605.0 4.9 convolution_convert_fusion.2
  610.0 1.1 slice.161
  611.2 1.1 slice.162
  612.4 1.1 slice.163
  614.7 4.5 all-to-all-start
  621.9 3.4 convolution_convert_fusion.5
  625.3 3.1 reshape.323
  632.5 2.6 multiply_reduce_fusion
  636.1 2.3 fusion.23
  638.5 1.1 fusion.20
  640.8 2.0 convolution_convert_fusion.4
  642.8 2.5 reshape.328
  645.3 2.3 copy.181
  650.6 3.2 convolution_convert_fusion
  653.8 2.2 pad_maximum_fusion
  656.2 2.3 fusion.25
  660.5 1.5 add_convert_fusion.1
  662.1 2.3 fusion.68
  664.6 4.0 fusion.65
  670.0 3.5 convolution_convert_fusion.1.top_ref
  673.4 91.4 %shard_map.305 = (bf16[704,2048]{1,0:T(8,128)(2,1)}, f32[160,2048]{1,0:T(8,128)}) custom-call(bf16[576,2048]{1,0:T(8,128)(2,1)} %convolution_convert_fusion.1.top_ref, bf16[128,2048]{1,0:T(8,128)(2,1)} %fusion.45.rest_ref, bf16[4,160,2048]{2,1,0:T(8,128)(2,1)} %bitcast.128), custom_call_target="tpu_custom_call" | custom-call | bytes 9699328 | tf_op jit(solution)/shard_map/pallas_call | solution.py:1455
  764.8 1.8 fusion.19
  766.6 1.3 slice_convert_fusion.5
  767.9 1.4 slice_convert_fusion.3
  769.4 1.8 convert_bitcast_fusion.3
  771.1 4.5 convert_bitcast_fusion.2
  775.6 17.4 %convert_bitcast_fusion.1 = f32[8,2048,352]{1,2,0:T(8,128)} fusion(bf16[8,352,2048]{2,1,0:T(8,128)(2,1)} %get-tuple-element.97), kind=kLoop, calls=%fused_computation.1 | loop fusion | flops 5767168 | bytes 34603008 | tf_op jit(solution)/shard_map/transpose | solution.py:1957
  793.1 9.9 %convert_element_type.201 = f32[8,352,2048]{2,1,0:T(8,128)} convert(bf16[8,352,2048]{2,1,0:T(8,128)(2,1)S(1)} %bitcast.121) | non-fusion elementwise | flops 5767168 | bytes 34603008 | tf_op jit(solution)/shard_map/convert_element_type | solution.py:1884
  803.0 1.5 fusion.18
  804.5 8.4 %convert_bitcast_fusion = f32[8,2048,352]{1,2,0:T(8,128)} fusion(bf16[8,352,2048]{2,1,0:T(8,128)(2,1)S(1)} %bitcast.119), kind=kLoop, calls=%fused_computation | loop fusion | flops 5767168 | bytes 34603008 | tf_op jit(solution)/shard_map/transpose | solution.py:1957
  812.9 1.4 convert_element_type.207
  814.3 1.4 fusion.66
  818.9 1.1 copy.186
  (188 shorter events, 33.3 us)
Async XLA Ops:
  7.2 8.4 %copy-start.10 = (bf16[160,2048]{1,0:T(8,128)(2,1)S(1)}, bf16[160,2048]{1,0:T(8,128)(2,1)}, u32[]{:S(2)}) copy-start(bf16[160,2048]{1,0:T(8,128)(2,1)} %param.19) | copy-start | bytes 1966084
  7.2 808.5 %reduce-scatter.5.cloned.1.call-start = ((), (), s32[]{:S(2)}) async-start(), calls=%async_computation.4 | async-start | bytes 2359296 | tf_op jit(solution)/shard_map/reduce_scatter | solution.py:1518
  7.3 9.3 %copy-start.43 = (f32[32]{0:T(128)}, f32[32]{0:T(128)S(1)}, u32[]{:S(2)}) copy-start(f32[32]{0:T(128)S(1)} %negate_power_fusion) | copy-start | bytes 388
  9.2 9.4 %copy-start.40 = (f32[160]{0:T(256)}, f32[160]{0:T(256)S(1)}, u32[]{:S(2)}) copy-start(f32[160]{0:T(256)S(1)} %get-tuple-element.214) | copy-start | bytes 1924
  12.4 6.2 copy-start.37
  471.8 107.3 %copy-start.36 = (s32[160,6]{0,1:T(8,128)S(1)}, s32[160,6]{0,1:T(8,128)}, u32[]{:S(2)}) copy-start(s32[160,6]{0,1:T(8,128)} %param.21) | copy-start | bytes 11524
  471.8 107.6 %copy-start.39 = (f32[2048]{0:T(1024)S(1)}, f32[2048]{0:T(1024)}, u32[]{:S(2)}) copy-start(f32[2048]{0:T(1024)} %param.28) | copy-start | bytes 24580
  579.3 3.1 copy-start.6
  579.4 3.1 copy-start.11
  579.4 3.1 copy-start.18
  584.5 20.6 %copy-start.49 = (bf16[640,512]{1,0:T(8,128)(2,1)S(1)}, bf16[640,512]{1,0:T(8,128)(2,1)}, u32[]{:S(2)}) copy-start(bf16[640,512]{1,0:T(8,128)(2,1)} %get-tuple-element.86) | copy-start | bytes 1966084
  613.6 5.7 copy-start.35
  613.6 6.7 copy-start.24
  614.7 6.4 copy-start.23
  614.7 7.2 copy-start.12
  614.7 198.2 %all-to-all-start = ((bf16[264,8,256]{2,0,1:T(8,128)(2,1)}), bf16[264,8,256]{2,0,1:T(8,128)(2,1)}, u32[]{:S(2)}, u32[]{:S(2)}) async-start(bf16[264,8,256]{2,0,1:T(8,128)(2,1)} %pad_maximum_fusion.2), calls=%async_computation.2 | async-start | bytes 2162688 | tf_op jit(solution)/shard_map/all_to_all | solution.py:1897
  619.2 198.5 %reduce-scatter.3.cloned.1.call-start = ((), (), s32[]{:S(2)}) async-start(), calls=%async_computation.3 | async-start | bytes 4718592 | tf_op jit(solution)/shard_map/reduce_scatter | solution.py:1518
  625.3 4.9 copy-start.13
  628.4 1.3 copy-start.20
  628.9 3.6 copy-start.3
  630.2 1.3 copy-start.9
  636.1 2.3 copy-start.14
  648.7 1.9 copy-start.1
  650.6 3.2 copy-start.8
  656.1 2.3 copy-start.32
  656.1 2.6 copy-start.19
  656.1 2.6 copy-start.22
  656.1 2.6 copy-start.45
  656.1 2.6 copy-start.47
  659.9 2.2 copy-start.26
  659.9 2.2 copy-start.46
  662.1 2.3 copy-start.2
  662.1 2.5 copy-start.15
  664.6 4.0 copy-start.33
  664.6 4.0 copy-start.27
  664.6 4.0 copy-start.29
  775.6 17.4 %slice-start.3 = ((s8[11534336]{0:T(1024)(128)(4,1)}), s8[4194304]{0:T(1024)(128)(4,1)S(1)}, s32[]{:S(2)}) async-start(s8[11534336]{0:T(1024)(128)(4,1)} %bitcast.120), calls=%async_computation.8 | async-start | bytes 8388608
  775.6 17.4 %slice-start.4 = ((s8[11534336]{0:T(1024)(128)(4,1)}), s8[4194304]{0:T(1024)(128)(4,1)S(1)}, s32[]{:S(2)}) async-start(s8[11534336]{0:T(1024)(128)(4,1)} %bitcast.120), calls=%async_computation.9 | async-start | bytes 8388608
  775.6 17.4 %slice-start.5 = ((s8[11534336]{0:T(1024)(128)(4,1)}), s8[3145728]{0:T(1024)(128)(4,1)S(1)}, s32[]{:S(2)}) async-start(s8[11534336]{0:T(1024)(128)(4,1)} %bitcast.120), calls=%async_computation.10 | async-start | bytes 6291456
  775.6 28.9 %slice-start = ((s8[11534336]{0:T(1024)(128)(4,1)}), s8[4194304]{0:T(1024)(128)(4,1)S(1)}, s32[]{:S(2)}) async-start(s8[11534336]{0:T(1024)(128)(4,1)} %bitcast.118), calls=%async_computation.5 | async-start | bytes 8388608
  775.6 28.9 %slice-start.1 = ((s8[11534336]{0:T(1024)(128)(4,1)}), s8[4194304]{0:T(1024)(128)(4,1)S(1)}, s32[]{:S(2)}) async-start(s8[11534336]{0:T(1024)(128)(4,1)} %bitcast.118), calls=%async_computation.6 | async-start | bytes 8388608
  793.0 10.0 %copy-start = (bf16[160,2048]{1,0:T(8,128)(2,1)S(1)}, bf16[160,2048]{1,0:T(8,128)(2,1)}, u32[]{:S(2)}) copy-start(bf16[160,2048]{1,0:T(8,128)(2,1)} %tokens_ref.1) | copy-start | bytes 1966084
  793.0 10.0 %copy-start.5 = (f32[160,2048]{1,0:T(8,128)S(1)}, f32[160,2048]{1,0:T(8,128)}, u32[]{:S(2)}) copy-start(f32[160,2048]{1,0:T(8,128)} %get-tuple-element.193) | copy-start | bytes 3932164
  793.1 10.0 %copy-start.7 = (f32[160,2048]{1,0:T(8,128)S(1)}, f32[160,2048]{1,0:T(8,128)}, u32[]{:S(2)}) copy-start(f32[160,2048]{1,0:T(8,128)} %get-tuple-element.90) | copy-start | bytes 3932164
  793.1 10.0 %copy-start.41 = (f32[160]{0:T(256)S(1)}, f32[160]{0:T(256)}, u32[]{:S(2)}) copy-start(f32[160]{0:T(256)} %copy-done.40) | copy-start | bytes 1924
  793.1 10.0 %copy-start.42 = (f32[160]{0:T(256)S(1)}, f32[160]{0:T(256)}, u32[]{:S(2)}) copy-start(f32[160]{0:T(256)} %get-tuple-element.213) | copy-start | bytes 1924
  793.1 11.4 %slice-start.2 = ((s8[11534336]{0:T(1024)(128)(4,1)}), s8[3145728]{0:T(1024)(128)(4,1)S(1)}, s32[]{:S(2)}) async-start(s8[11534336]{0:T(1024)(128)(4,1)} %bitcast.118), calls=%async_computation.7 | async-start | bytes 6291456
  817.7 2.3 copy-start.16
  (11 other events, 10.5 us)
Sparse Core Ops, SparseCore 0:
  610.1 82.4 reduce-scatter.4
  696.3 107.9 reduce-scatter.2

commit v9 on v8

--- a/solution.py
+++ b/solution.py
@@ -397,7 +397,6 @@
         up, down = device(z + 1, x, y, c), device(z - 1, x, y, c)
         self.out_ref, self.recv_sems, self.mate = out_ref, recv_sems, mate
         planes = [ordered(z, (0, 1, 2, 3)[step], (1, 0, 2, 3)[step]) for step in range(4)]
-        self.planes = planes
         self.rising = [(zz <= z) & (z < 3) for zz in planes]
         self.falling = [(zz >= z) & (z > 0) for zz in planes]
         self.mine = [shard(zz, x, y, c) for zz in planes]
@@ -546,37 +545,46 @@
     def part(index, size):
         return pl.ds(pl.multiple_of(index * size, 16), size)
 
-    stores = {}
-
-    def plane(step):
-        gather.rest(step)
-        loads = []
+    first_plane = turns - 4
+    step = turn - first_plane
+    second = step + (1 - 2 * step) * (1 - lax.div(step, 2))
+    zz = ordered(place[0], step, second)
+
+    def store(k):
+        group = zz * 2 + k
+        return pltpu.make_async_copy(
+            stage.at[k], rows_hbm.at[:, part(group, slot_rows)], store_sems.at[k]
+        )
+
+    def loads(k):
+        group = zz * 2 + k
+        copies = [
+            pltpu.make_async_copy(
+                out_ref.at[group * count + i],
+                arrived.at[k, pl.ds(i * rows, rows)],
+                load_sems.at[k, i],
+            )
+            for i in range(count)
+        ]
+        copies.append(
+            pltpu.make_async_copy(
+                cotangent_hbm.at[part(group, quad), pl.ds(width, lanes)],
+                marks.at[k],
+                load_sems.at[k, count],
+            )
+        )
+        return copies
+
+    def plane():
         for k in range(2):
-            group = gather.planes[step] * 2 + k
-            copies = [
-                pltpu.make_async_copy(
-                    out_ref.at[group * count + i],
-                    arrived.at[k, pl.ds(i * rows, rows)],
-                    load_sems.at[k, i],
-                )
-                for i in range(count)
-            ]
-            copies.append(
-                pltpu.make_async_copy(
-                    cotangent_hbm.at[part(group, quad), pl.ds(width, lanes)],
-                    marks.at[k],
-                    load_sems.at[k, count],
-                )
-            )
-            for copy in copies:
+            for copy in loads(k):
                 copy.start()
-            loads.append(copies)
-        for k in range(2):
-            group = gather.planes[step] * 2 + k
-            for copy in loads[k]:
+
+        def one(k, carry):
+            for copy in loads(k):
                 copy.wait()
-            if k in stores:
-                stores[k].wait()
+            pl.when(step > 0)(lambda: store(k).wait())
+            group = zz * 2 + k
             tokens = part(group, quad)
             rows_kernel(
                 pair,
@@ -593,24 +601,28 @@
                 gate_grad_ref.at[tokens],
                 lift_grad_ref.at[tokens],
             )
-            stores[k] = pltpu.make_async_copy(
-                stage.at[k], rows_hbm.at[:, part(group, slot_rows)], store_sems.at[k]
-            )
-            stores[k].start()
+            store(k).start()
+            return carry
+
+        lax.fori_loop(0, 2, one, 0)
+
+    def second_plane():
+        gather.relay(2)
+        gather.corner(1)
+        gather.rest(1)
+
+    def third_plane():
+        gather.relay(3)
+        gather.corner(2)
+        gather.rest(2)
+
+    def fourth_plane():
+        gather.corner(3)
+        gather.rest(3)
 
     def end():
-        gather.whole(3)
-        gather.relay(2)
-        plane(0)
-        gather.corner(1)
-        gather.relay(3)
-        plane(1)
-        gather.corner(2)
-        plane(2)
-        gather.corner(3)
-        plane(3)
         for k in range(2):
-            stores[k].wait()
+            store(k).wait()
         sends.finish()
 
     pieces = [
@@ -621,10 +633,20 @@
         functools.partial(gather.whole, 2),
         lambda: None,
         early,
+        functools.partial(gather.whole, 3),
+        functools.partial(gather.rest, 0),
+        second_plane,
+        third_plane,
+        fourth_plane,
     ]
     for number, piece in enumerate(pieces):
         pl.when(turn == number)(piece)
-    grads_kernel(pair, (here_ref, value_ref, down_ref), (grads_ref, raw.at[part(turn, quad)]))
+
+    @pl.when(turn < first_plane)
+    def _():
+        grads_kernel(pair, (here_ref, value_ref, down_ref), (grads_ref, raw.at[part(turn, quad)]))
+
+    pl.when(turn >= first_plane)(plane)
     pl.when(turn == turns - 1)(end)
 
 
@@ -640,10 +662,14 @@
     token_part = shape((all_rows, shared_wide), low)
     mix = shape((local_experts, slot_rows, lanes), jnp.float32)
     away = pl.BlockSpec(memory_space=pl.ANY)
+    last = turns - 1
+    quad_spec = pl.BlockSpec((quad, cotangent.shape[1]), lambda i: (jnp.minimum(i, last), 0))
+    part = slot_rows // turns
+    slot_spec = pl.BlockSpec((local_experts, part, width), lambda i: (0, jnp.minimum(i, last), 0))
     ins = [
         (value, whole_spec(value)),
         (here, whole_spec(here)),
-        (cotangent, pair_spec(cotangent, turns)),
+        (cotangent, quad_spec),
         (down, whole_spec(down)),
         (twice, whole_spec(twice)),
         (gate, whole_spec(gate)),
@@ -652,18 +678,17 @@
     ]
     outs = [
         (shape((32,) + value.shape, low), away),
-        (slots, slots_spec(slots, turns)),
+        (slots, slot_spec),
         (slots, away),
         (mix, whole_spec(mix)),
         (token_part, whole_spec(token_part)),
         (token_part, whole_spec(token_part)),
         (token_part, whole_spec(token_part)),
     ]
-    part = slot_rows // turns
     flops = 4 * all_rows * width * (2 * CAP * local_experts + 2 * shared_wide)
     return pl.pallas_call(
         functools.partial(token_kernel, pair),
-        grid=(turns,),
+        grid=(turns + 4,),
         out_shape=[o for o, _ in outs],
         in_specs=[spec for _, spec in ins],
         out_specs=[spec for _, spec in outs],
@@ -809,7 +834,7 @@
     def head(h):
         start = h * (NOPE + VDIM)
         query = query_out[h]
-        raw = times_trans(query[:, :NOPE], expanded_out[:, start : start + NOPE])
+        raw = times_trans(query[:, :NOPE], expanded_out[:, columns(start, NOPE)])
         raw = raw + times_trans(query[:, NOPE:], key_rope_out[...])
         row = lax.broadcasted_iota(jnp.int32, raw.shape, 0)
         column = lax.broadcasted_iota(jnp.int32, raw.shape, 1)
@@ -820,8 +845,8 @@
         total = jnp.sum(weights, axis=1, keepdims=True)
         log_out[h] = jnp.broadcast_to(peak + jnp.log(total), log_out.shape[1:])
         probs = (weights / total).astype(jnp.bfloat16)
-        mixed = matmul(probs, expanded_out[:, start + NOPE : start + NOPE + VDIM])
-        mixed_out[:, h * VDIM : (h + 1) * VDIM] = mixed.astype(jnp.bfloat16)
+        mixed = matmul(probs, expanded_out[:, columns(start + NOPE, VDIM)])
+        mixed_out[:, columns(h * VDIM, VDIM)] = mixed.astype(jnp.bfloat16)
 
     middle = [
         None,
@@ -829,10 +854,15 @@
         functools.partial(gather.relay, 1),
         functools.partial(gather.corner, 0),
     ]
-    for h in range(heads):
+
+    def step(h, carry):
         head(h)
-        if h < 4 and middle[h] is not None:
-            middle[h]()
+        for number, piece in enumerate(middle):
+            if piece is not None:
+                pl.when(h == number)(piece)
+        return carry
+
+    lax.fori_loop(0, heads, step, 0)
     loads[3].wait()
     for i in range(4):
         block = matmul(mixed_out[i * rows : (i + 1) * rows], output_matrix[...])

time: 844 us -> 828 us (0.981)
  Pallas kernels: 663 us -> 649 us
    pallas_call x1, Pallas kernels: 131 us -> 115 us  [gather_tokens(): pl.pallas_call(functools.partial(token_kernel, pair), grid=(turns + 4,),...]
where the time goes in v9:
time: 828 us; the launch traced here: 814 us
  Pallas kernels  649 us (78%)
  other arithmetic  72.7 us (9%)
  matrix products  39.7 us (5%)
  local copies, waits for them, and re-layouts  32.1 us (4%)
  between operations  15.5 us (2%)
    pallas_call x2, Pallas kernels, sum_all(): pl.pallas_call(functools.partial(sum_all_kernel, inner, len(ins), len(out...  204 us
    pallas_call x1, Pallas kernels, attention_forward(): pl.pallas_call(functools.partial(attention_kernel, score_scale), out_shap...  125 us
    pallas_call x1, Pallas kernels, gather_tokens(): pl.pallas_call(functools.partial(token_kernel, pair), grid=(turns + 4,),...  115 us
    pallas_call x3, Pallas kernels, call(): pl.pallas_call(kernel, grid=(grid,), in_specs=[s for _, s in ins], out_sp...  94.2 us
    pallas_call x1, Pallas kernels, total_over_all(): pl.pallas_call(total_kernel, out_shape=[out, group_out], in_specs=[pl.Blo...  89.5 us
    pallas_call x1, Pallas kernels, gather_group(): pl.pallas_call(gather_group_kernel, out_shape=out, in_specs=[pl.BlockSpec...  20.8 us
    transpose x1, other arithmetic, per_device(): weight_grads[0].transpose(0, 2, 1)  17.4 us
  transfers between devices with their start and end apart: 3, of which 0 were waited for; matrix products, arithmetic and copies ran while one was open for 13% of the time, Pallas kernels for 11%

profile of v9, /device:TPU:0, one launch (start us, length us, event | category | flops | bytes accessed | tf_op | source)
XLA Modules:
  0.0 813.6 jit_solution(16735319513201389720)
XLA Ops:
  7.3 1.4 fusion.13
  10.2 1.3 convert_bitcast_fusion.5
  13.3 2.1 fusion.15.normed_ref
  16.5 2.0 multiply_sine_fusion
  18.6 125.0 %shard_map.297 = (bf16[32,160,2176]{2,1,0:T(8,128)(2,1)}, bf16[4,160,2048]{2,1,0:T(8,128)(2,1)}, bf16[4,640,192]{2,1,0:T(8,128)(2,1)}, f32[640,512]{1,0:T(8,128)...) custom-call(bf16[160,2048]{1,0:T(8,128)(2,1)} %fusion.15.normed_ref,, ...), custom_call_target="tpu_custom_call" | custom-call | flops 5536481280 | bytes 44768256 | tf_op jit(solution)/shard_map/pallas_call | solution.py:969
  146.5 1.2 dynamic-slice_bitcast_fusion
  150.0 115.4 %shard_map.298 = (bf16[32,160,2176]{2,1,0:T(8,128)(2,1)}, bf16[8,640,2048]{2,1,0:T(8,128)(2,1)}, bf16[8,640,2048]{2,1,0:T(8,128)(2,1)}, f32[8,640,128]{2,1,0:T(8...) custom-call(bf16[160,2176]{1,0:T(8,128)(2,1)} %get-tuple-element.60.x_ref, ...), custom_call_target="tpu_custom_call" | custom-call | flops 24159191040 | bytes 117616640 | tf_op jit(solution)/shard_map/pallas_call | solution.py:689
  265.4 40.1 %shard_map.299 = (bf16[8,640,352]{2,1,0:T(8,128)(2,1)}, bf16[8,640,352]{2,1,0:T(8,128)(2,1)}, bf16[8,640,352]{2,1,0:T(8,128)(2,1)}, bf16[8,640,352]{2,1,0:T(8,128)(2,1)}, bf16[8,640,2048]{2,1,0:T(8,128)(2,1)}) custom-call(bf16[8,640,2048]{2,1,0:T(8,128)(2,1)} %get-tuple-element.61.rows_ref.refs_5_, f32[8,640,128]{2,1,0:T(8,128)} %get-tuple-element.62.mix_ref, ...), custom_call_target="tpu_custom_call" | custom-call | flops 22145925120 | bytes 93585408 | tf_op jit(solution)/shard_map/pallas_call | solution.py:285
  305.5 24.0 %shard_map.300 = bf16[5120,2048]{1,0:T(8,128)(2,1)} custom-call(bf16[8,128]{1,0:T(8,128)(2,1)} %get-tuple-element.216.here_ref, bf16[5120,2176]{1,0:T(8,128)(2,1)} %bitcast.112, bf16[8,640,2048]{2,1,0:T(8,128)(2,1)} %get-tuple-element.63.rows_ref, bf16[5120,128]{1,0:T(8,128)(2,1)} %get-tuple-element.64.hidden_ref.refs_4_, bf16[128,2048]{1,0:T(8,128)(2,1)} %pad.25.down_ref), custom_call_target="tpu_custom_call" | custom-call | flops 9395240960 | bytes 66062336 | tf_op jit(solution)/shard_map/pallas_call | solution.py:285
  330.2 98.7 %shard_map.301 = (f32[160,2048]{1,0:T(8,128)}, bf16[8,640,352]{2,1,0:T(8,128)(2,1)}, bf16[8,640,352]{2,1,0:T(8,128)(2,1)}, bf16[8,640,2048]{2,1,0:T(8,128)(2,1)}, f32[8,640,128]{2,1,0:T(8,128)}) custom-call(bf16[32,160,2048]{2,1,0:T(8,128)(2,1)} %bitcast.116, bf16[8,640,2048]{2,1,0:T(8,128)(2,1)} %get-tuple-element.65.refs_0_.refs_6_, ...), custom_call_target="tpu_custom_call" | custom-call | flops 22145925120 | bytes 119472128 | tf_op jit(solution)/shard_map/pallas_call | solution.py:1155
  428.9 30.0 %shard_map.302 = bf16[5120,2176]{1,0:T(8,128)(2,1)} custom-call(bf16[8,128]{1,0:T(8,128)(2,1)} %get-tuple-element.216.here_ref, bf16[8,128]{1,0:T(8,128)(2,1)} %get-tuple-element.218.high_ref, bf16[8,128]{1,0:T(8,128)(2,1)} %get-tuple-element.217.low_ref, bf16[5120,2176]{1,0:T(8,128)(2,1)} %bitcast.113, bf16[8,640,2048]{2,1,0:T(8,128)(2,1)} %get-tuple-element.71.rows_ref, ...), custom_call_target="tpu_custom_call" | custom-call | flops 12079595520 | bytes 71833600 | tf_op jit(solution)/shard_map/pallas_call | solution.py:285
  458.9 105.5 %shard_map.303 = (f32[160,2176]{1,0:T(8,128)}, f32[128,2048]{1,0:T(8,128)}, f32[128,2048]{1,0:T(8,128)}, f32[128,2048]{1,0:T(8,128)}, bf16[8,352,2048]{2,1,0:T(8...) custom-call(bf16[32,160,2176]{2,1,0:T(8,128)(2,1)} %bitcast.115, bf16[5120,2176]{1,0:T(8,128)(2,1)} %bitcast.117, ...), custom_call_target="tpu_custom_call" | custom-call | flops 30198988800 | bytes 162676736 | tf_op jit(solution)/shard_map/pallas_call | solution.py:1155
  566.8 3.0 multiply_reduce_fusion.3
  569.8 2.0 fusion.64
  571.8 20.8 %shard_map.304 = bf16[4,160,2048]{2,1,0:T(8,128)(2,1)} custom-call(bf16[160,2048]{1,0:T(8,128)(2,1)} %get-tuple-element.192.x_ref), custom_call_target="tpu_custom_call" | custom-call | bytes 3276800 | tf_op jit(solution)/shard_map/pallas_call | solution.py:1218
  592.6 4.9 convolution_convert_fusion.2
  597.6 1.1 slice.161
  598.8 1.1 slice.162
  600.0 1.1 slice.163
  602.3 4.5 all-to-all-start
  609.4 3.4 convolution_convert_fusion.5
  612.9 3.1 reshape.323
  620.1 2.6 multiply_reduce_fusion
  623.7 2.3 fusion.23
  626.1 1.1 fusion.20
  628.4 2.0 convolution_convert_fusion.4
  630.4 2.5 reshape.328
  632.9 2.3 copy.181
  638.2 3.0 convolution_convert_fusion
  641.2 2.2 pad_maximum_fusion
  643.6 2.3 fusion.25
  648.0 1.5 add_convert_fusion.1
  649.5 2.3 fusion.68
  652.0 4.0 fusion.65
  657.4 3.5 convolution_convert_fusion.1.top_ref
  660.9 89.5 %shard_map.305 = (bf16[704,2048]{1,0:T(8,128)(2,1)}, f32[160,2048]{1,0:T(8,128)}) custom-call(bf16[576,2048]{1,0:T(8,128)(2,1)} %convolution_convert_fusion.1.top_ref, bf16[128,2048]{1,0:T(8,128)(2,1)} %fusion.45.rest_ref, bf16[4,160,2048]{2,1,0:T(8,128)(2,1)} %bitcast.128), custom_call_target="tpu_custom_call" | custom-call | bytes 9699328 | tf_op jit(solution)/shard_map/pallas_call | solution.py:1485
  750.3 1.8 fusion.19
  752.1 1.3 slice_convert_fusion.5
  753.4 1.4 slice_convert_fusion.3
  754.9 1.8 convert_bitcast_fusion.3
  756.6 4.5 convert_bitcast_fusion.2
  761.1 17.4 %convert_bitcast_fusion.1 = f32[8,2048,352]{1,2,0:T(8,128)} fusion(bf16[8,352,2048]{2,1,0:T(8,128)(2,1)} %get-tuple-element.97), kind=kLoop, calls=%fused_computation.1 | loop fusion | flops 5767168 | bytes 34603008 | tf_op jit(solution)/shard_map/transpose | solution.py:1987
  778.7 9.7 %convert_element_type.201 = f32[8,352,2048]{2,1,0:T(8,128)} convert(bf16[8,352,2048]{2,1,0:T(8,128)(2,1)S(1)} %bitcast.121) | non-fusion elementwise | flops 5767168 | bytes 34603008 | tf_op jit(solution)/shard_map/convert_element_type | solution.py:1914
  788.4 1.5 fusion.18
  789.9 8.4 %convert_bitcast_fusion = f32[8,2048,352]{1,2,0:T(8,128)} fusion(bf16[8,352,2048]{2,1,0:T(8,128)(2,1)S(1)} %bitcast.119), kind=kLoop, calls=%fused_computation | loop fusion | flops 5767168 | bytes 34603008 | tf_op jit(solution)/shard_map/transpose | solution.py:1987
  798.3 1.4 convert_element_type.207
  799.7 1.4 fusion.66
  804.2 1.1 copy.186
  (188 shorter events, 33.3 us)
Async XLA Ops:
  7.2 8.4 %copy-start.10 = (bf16[160,2048]{1,0:T(8,128)(2,1)S(1)}, bf16[160,2048]{1,0:T(8,128)(2,1)}, u32[]{:S(2)}) copy-start(bf16[160,2048]{1,0:T(8,128)(2,1)} %param.19) | copy-start | bytes 1966084
  7.2 793.9 %reduce-scatter.5.cloned.1.call-start = ((), (), s32[]{:S(2)}) async-start(), calls=%async_computation.4 | async-start | bytes 2359296 | tf_op jit(solution)/shard_map/reduce_scatter | solution.py:1548
  7.3 9.3 %copy-start.43 = (f32[32]{0:T(128)}, f32[32]{0:T(128)S(1)}, u32[]{:S(2)}) copy-start(f32[32]{0:T(128)S(1)} %negate_power_fusion) | copy-start | bytes 388
  9.2 9.4 %copy-start.40 = (f32[160]{0:T(256)}, f32[160]{0:T(256)S(1)}, u32[]{:S(2)}) copy-start(f32[160]{0:T(256)S(1)} %get-tuple-element.214) | copy-start | bytes 1924
  12.4 6.2 copy-start.37
  458.9 107.5 %copy-start.36 = (s32[160,6]{0,1:T(8,128)S(1)}, s32[160,6]{0,1:T(8,128)}, u32[]{:S(2)}) copy-start(s32[160,6]{0,1:T(8,128)} %param.21) | copy-start | bytes 11524
  458.9 107.8 %copy-start.39 = (f32[2048]{0:T(1024)S(1)}, f32[2048]{0:T(1024)}, u32[]{:S(2)}) copy-start(f32[2048]{0:T(1024)} %param.28) | copy-start | bytes 24580
  566.7 3.1 copy-start.6
  566.7 3.1 copy-start.11
  566.8 3.1 copy-start.18
  571.8 20.8 %copy-start.49 = (bf16[640,512]{1,0:T(8,128)(2,1)S(1)}, bf16[640,512]{1,0:T(8,128)(2,1)}, u32[]{:S(2)}) copy-start(bf16[640,512]{1,0:T(8,128)(2,1)} %get-tuple-element.86) | copy-start | bytes 1966084
  601.2 5.7 copy-start.35
  601.2 6.7 copy-start.24
  602.3 6.4 copy-start.23
  602.3 7.2 copy-start.12
  602.3 196.0 %all-to-all-start = ((bf16[264,8,256]{2,0,1:T(8,128)(2,1)}), bf16[264,8,256]{2,0,1:T(8,128)(2,1)}, u32[]{:S(2)}, u32[]{:S(2)}) async-start(bf16[264,8,256]{2,0,1:T(8,128)(2,1)} %pad_maximum_fusion.2), calls=%async_computation.2 | async-start | bytes 2162688 | tf_op jit(solution)/shard_map/all_to_all | solution.py:1927
  606.8 196.3 %reduce-scatter.3.cloned.1.call-start = ((), (), s32[]{:S(2)}) async-start(), calls=%async_computation.3 | async-start | bytes 4718592 | tf_op jit(solution)/shard_map/reduce_scatter | solution.py:1548
  612.9 4.9 copy-start.13
  616.0 1.3 copy-start.20
  616.5 3.6 copy-start.3
  617.8 1.3 copy-start.9
  623.7 2.4 copy-start.14
  636.4 1.9 copy-start.1
  638.2 3.0 copy-start.8
  643.5 2.3 copy-start.32
  643.5 2.6 copy-start.19
  643.5 2.6 copy-start.22
  643.6 2.6 copy-start.45
  643.6 2.6 copy-start.47
  647.3 2.2 copy-start.26
  647.3 2.2 copy-start.46
  649.5 2.3 copy-start.2
  649.5 2.5 copy-start.15
  652.0 4.0 copy-start.33
  652.0 4.0 copy-start.27
  652.0 4.0 copy-start.29
  761.1 17.5 %slice-start.3 = ((s8[11534336]{0:T(1024)(128)(4,1)}), s8[4194304]{0:T(1024)(128)(4,1)S(1)}, s32[]{:S(2)}) async-start(s8[11534336]{0:T(1024)(128)(4,1)} %bitcast.120), calls=%async_computation.8 | async-start | bytes 8388608
  761.1 17.5 %slice-start.4 = ((s8[11534336]{0:T(1024)(128)(4,1)}), s8[4194304]{0:T(1024)(128)(4,1)S(1)}, s32[]{:S(2)}) async-start(s8[11534336]{0:T(1024)(128)(4,1)} %bitcast.120), calls=%async_computation.9 | async-start | bytes 8388608
  761.1 17.5 %slice-start.5 = ((s8[11534336]{0:T(1024)(128)(4,1)}), s8[3145728]{0:T(1024)(128)(4,1)S(1)}, s32[]{:S(2)}) async-start(s8[11534336]{0:T(1024)(128)(4,1)} %bitcast.120), calls=%async_computation.10 | async-start | bytes 6291456
  761.1 28.7 %slice-start = ((s8[11534336]{0:T(1024)(128)(4,1)}), s8[4194304]{0:T(1024)(128)(4,1)S(1)}, s32[]{:S(2)}) async-start(s8[11534336]{0:T(1024)(128)(4,1)} %bitcast.118), calls=%async_computation.5 | async-start | bytes 8388608
  761.1 28.7 %slice-start.1 = ((s8[11534336]{0:T(1024)(128)(4,1)}), s8[4194304]{0:T(1024)(128)(4,1)S(1)}, s32[]{:S(2)}) async-start(s8[11534336]{0:T(1024)(128)(4,1)} %bitcast.118), calls=%async_computation.6 | async-start | bytes 8388608
  778.6 9.7 %copy-start = (bf16[160,2048]{1,0:T(8,128)(2,1)S(1)}, bf16[160,2048]{1,0:T(8,128)(2,1)}, u32[]{:S(2)}) copy-start(bf16[160,2048]{1,0:T(8,128)(2,1)} %tokens_ref.1) | copy-start | bytes 1966084
  778.6 9.7 %copy-start.5 = (f32[160,2048]{1,0:T(8,128)S(1)}, f32[160,2048]{1,0:T(8,128)}, u32[]{:S(2)}) copy-start(f32[160,2048]{1,0:T(8,128)} %get-tuple-element.193) | copy-start | bytes 3932164
  778.6 9.7 %copy-start.7 = (f32[160,2048]{1,0:T(8,128)S(1)}, f32[160,2048]{1,0:T(8,128)}, u32[]{:S(2)}) copy-start(f32[160,2048]{1,0:T(8,128)} %get-tuple-element.90) | copy-start | bytes 3932164
  778.6 9.7 %copy-start.41 = (f32[160]{0:T(256)S(1)}, f32[160]{0:T(256)}, u32[]{:S(2)}) copy-start(f32[160]{0:T(256)} %copy-done.40) | copy-start | bytes 1924
  778.6 9.7 %copy-start.42 = (f32[160]{0:T(256)S(1)}, f32[160]{0:T(256)}, u32[]{:S(2)}) copy-start(f32[160]{0:T(256)} %get-tuple-element.213) | copy-start | bytes 1924
  778.7 11.2 %slice-start.2 = ((s8[11534336]{0:T(1024)(128)(4,1)}), s8[3145728]{0:T(1024)(128)(4,1)S(1)}, s32[]{:S(2)}) async-start(s8[11534336]{0:T(1024)(128)(4,1)} %bitcast.118), calls=%async_computation.7 | async-start | bytes 6291456
  803.1 2.3 copy-start.16
  (11 other events, 10.5 us)
Sparse Core Ops, SparseCore 0:
  597.7 83.9 reduce-scatter.4
  685.4 106.4 reduce-scatter.2
